TPU v7x, 32 devices: a whole 2x2x4 slice. The times are simulated.
32 devices in a mesh: row: 8 (over z, x), col: 4 (over y, core).
Axes of the slice: x: 2, y: 2, z: 4, core: 2. Of those that a mesh axis runs over, the one named last changes fastest.
Arguments:
- stream: float32 [1024, 2048], P('row', 'col'), may hold values from -6 to 6
- grad_out: float32 [1024, 2048], P('row', 'col'), may hold values from -6 to 6
- wqkv: bfloat16 [2, 2048, 4, 640], P(None, 'row', 'col'), may hold values from -0.125 to 0.125
- wo: bfloat16 [2, 2048, 2048], P(None, 'row', 'col'), may hold values from -2 to 2
- wgu: bfloat16 [2, 2048, 2, 5632], P(None, 'row', None, 'col'), may hold values from -0.125 to 0.125
- wd: bfloat16 [2, 2048, 5632], P(None, 'row', 'col'), may hold values from -0.078125 to 0.078125
- gain_attn: float32 [2, 2048], P(None, 'col'), may hold values from 0.5 to 1.5
- gain_ffn: float32 [2, 2048], P(None, 'col'), may hold values from 0.5 to 1.5
Outputs:
- out_stream: float32 [1024, 2048], P('row', 'col')
- grad_stream: float32 [1024, 2048], P('row', 'col')
- grad_wqkv: float32 [2, 2048, 4, 640], P(None, 'row', 'col')
- grad_wo: float32 [2, 2048, 2048], P(None, 'row', 'col')
- grad_wgu: float32 [2, 2048, 2, 5632], P(None, 'row', None, 'col')
- grad_wd: float32 [2, 2048, 5632], P(None, 'row', 'col')
- grad_gain_attn: float32 [2, 2048], P(None, 'col')
- grad_gain_ffn: float32 [2, 2048], P(None, 'col')
All inputs are finite; a program needn't handle non-finite values.
Results may differ from a plain program's by a relative error of at most 0.028.
Values may be sent and summed in bfloat16 or wider, within the bound.
A program may use at most 256 MiB of HBM per device.

v0:
```python
import math

import jax
import jax.numpy as jnp
from jax import lax
from jax.sharding import PartitionSpec as P

D = 2048
HEAD = 64
GROUP = 8


EPS = 1e-05
THETA = 10000.0


def rope_turn(tensor, cosine, sine):
    half = tensor.shape[-1] // 2
    first = tensor[..., :half]
    second = tensor[..., half:]
    return jnp.concatenate(
        [first * cosine - second * sine, second * cosine + first * sine], axis=-1
    )


def feature_sum(values):
    return lax.psum(values, "col")


def gather_features(rows_in):
    return lax.all_gather(rows_in, "col", axis=1, tiled=True)


def sum_features(partials):
    return lax.psum_scatter(
        partials.astype(jnp.bfloat16), "col", scatter_dimension=1, tiled=True
    ).astype(jnp.float32)


def add_rows(left, piece):
    return jnp.dot(left, piece, preferred_element_type=jnp.float32)


def project_in(left, shard):
    return add_rows(left, lax.all_gather(shard, "row", axis=0, tiled=True))


def columns_of(left, piece):
    return jnp.einsum("tj,dj->td", left, piece, preferred_element_type=jnp.float32)


def project_out(left, shard):
    return columns_of(left, lax.all_gather(shard, "row", axis=0, tiled=True))


def weight_grad(left, right):
    return lax.psum_scatter(
        lax.dot_general(
            left, right, (((0,), (0,)), ((), ())), preferred_element_type=jnp.float32
        ).astype(jnp.bfloat16),
        "row",
        scatter_dimension=0,
        tiled=True,
    ).astype(jnp.float32)


def norm_forward(values, gain):
    total = feature_sum(jnp.sum(values * values, axis=1))
    factor = lax.rsqrt(total / D + EPS)
    normed = values * factor[:, None]
    return (normed, factor, (normed * gain).astype(jnp.bfloat16))


def norm_backward(grad_normed, normed, factor, gain):
    scaled = grad_normed * gain
    inner = feature_sum(jnp.sum(scaled * normed, axis=1))
    grad_in = factor[:, None] * (scaled - normed * (inner / D)[:, None])
    return (grad_in, jnp.sum(grad_normed * normed, axis=0))


def masked_scores(queries, keys, query_pos, key_pos):
    scores = jnp.einsum("qgd,kd->gqk", queries, keys, preferred_element_type=jnp.float32) * (
        1.0 / math.sqrt(queries.shape[-1])
    )
    return jnp.where(key_pos[None, None, :] <= query_pos[None, :, None], scores, -1e30)


def local(stream, grad_out, wqkv, wo, wgu, wd, gain_attn, gain_ffn):
    tok = stream.shape[0]
    layers = wqkv.shape[0]
    count_rows = wqkv.shape[1]
    head = HEAD
    query_cols = GROUP * head
    seq_len = lax.axis_size("row") * tok
    query_pos = lax.axis_index("row") * tok + jnp.arange(tok, dtype=jnp.int32)
    key_pos = jnp.arange(seq_len, dtype=jnp.int32)
    freq = THETA ** (-(jnp.arange(head // 2, dtype=jnp.float32) * 2.0 / head))
    angle = query_pos.astype(jnp.float32)[:, None] * freq[None, :]
    cosine = jnp.cos(angle)
    sine = jnp.sin(angle)
    saved = []
    current = stream
    for index in range(layers):
        weight_qkv = wqkv[index].reshape(count_rows, -1)
        weight_out = wo[index]
        weight_gu = wgu[index].reshape(count_rows, -1)
        weight_down = wd[index]
        wholes = (None, None, None, None)
        normed_a, factor_a, xnormed = norm_forward(current, gain_attn[index])
        xfull = gather_features(xnormed)
        qkv = project_in(xfull, weight_qkv)
        queries = rope_turn(
            qkv[:, :query_cols].reshape(tok, GROUP, head), cosine[:, None, :], sine[:, None, :]
        ).astype(jnp.bfloat16)
        keys = rope_turn(qkv[:, query_cols : query_cols + head], cosine, sine).astype(jnp.bfloat16)
        values = qkv[:, query_cols + head :].astype(jnp.bfloat16)
        seqkv = lax.all_gather(jnp.concatenate([keys, values], axis=1), "row", axis=0, tiled=True)
        seq_keys = seqkv[:, :head]
        seq_values = seqkv[:, head:]
        scores = masked_scores(queries, seq_keys, query_pos, key_pos)
        top = jnp.max(scores, axis=2, keepdims=True)
        expo = jnp.exp(scores - top)
        denom = jnp.sum(expo, axis=2, keepdims=True)
        probs = (expo / denom).astype(jnp.bfloat16)
        log_total = top + jnp.log(denom)
        mixed = (
            jnp.einsum("gqk,kd->qgd", probs, seq_values, preferred_element_type=jnp.float32)
            .reshape(tok, query_cols)
            .astype(jnp.bfloat16)
        )
        hidden_in = current + sum_features(project_out(mixed, weight_out))
        normed_f, factor_f, hnormed = norm_forward(hidden_in, gain_ffn[index])
        hfull = gather_features(hnormed)
        gate_up = project_in(hfull, weight_gu)
        hidden_cols = gate_up.shape[1] // 2
        gate = gate_up[:, :hidden_cols]
        upper = gate_up[:, hidden_cols:]
        active = (jax.nn.silu(gate) * upper).astype(jnp.bfloat16)
        current = hidden_in + sum_features(project_out(active, weight_down))
        saved.append(
            (
                weight_qkv,
                weight_out,
                weight_gu,
                weight_down,
                wholes,
                normed_a,
                factor_a,
                xfull,
                queries,
                seq_keys,
                seq_values,
                log_total,
                mixed,
                normed_f,
                factor_f,
                hfull,
                gate,
                upper,
                active,
            )
        )
    grad_now = grad_out
    list_qkv, list_out, list_gu, list_down, list_ga, list_gf = ([], [], [], [], [], [])
    for index in reversed(range(layers)):
        (
            weight_qkv,
            weight_out,
            weight_gu,
            weight_down,
            wholes,
            normed_a,
            factor_a,
            xfull,
            queries,
            seq_keys,
            seq_values,
            log_total,
            mixed,
            normed_f,
            factor_f,
            hfull,
            gate,
            upper,
            active,
        ) = saved[index]
        grad_full = gather_features(grad_now.astype(jnp.bfloat16))
        grad_active = project_in(grad_full, weight_down)
        list_down.append(weight_grad(grad_full, active))
        sig = jax.nn.sigmoid(gate)
        grad_gate = grad_active * upper * sig * (1.0 + gate * (1.0 - sig))
        grad_up = grad_active * gate * sig
        grad_gu = jnp.concatenate([grad_gate, grad_up], axis=1).astype(jnp.bfloat16)
        grad_hn = sum_features(project_out(grad_gu, weight_gu))
        list_gu.append(weight_grad(hfull, grad_gu).reshape(count_rows, 2, -1))
        grad_mid, gain_f_grad = norm_backward(grad_hn, normed_f, factor_f, gain_ffn[index])
        list_gf.append(gain_f_grad)
        grad_hidden = grad_now + grad_mid
        hidden_full = gather_features(grad_hidden.astype(jnp.bfloat16))
        grad_mixed = project_in(hidden_full, weight_out).astype(jnp.bfloat16)
        list_out.append(weight_grad(hidden_full, mixed))
        grad_heads = grad_mixed.reshape(tok, GROUP, head)
        scores = masked_scores(queries, seq_keys, query_pos, key_pos)
        probs_full = jnp.exp(scores - log_total)
        probs = probs_full.astype(jnp.bfloat16)
        grad_probs = jnp.einsum(
            "qgd,kd->gqk", grad_heads, seq_values, preferred_element_type=jnp.float32
        )
        delta = jnp.sum(probs_full * grad_probs, axis=2, keepdims=True)
        grad_scores = (probs_full * (grad_probs - delta)).astype(jnp.bfloat16)
        inverse = 1.0 / math.sqrt(head)
        grad_queries = (
            jnp.einsum("gqk,kd->qgd", grad_scores, seq_keys, preferred_element_type=jnp.float32)
            * inverse
        )
        grad_keys = (
            jnp.einsum("gqk,qgd->kd", grad_scores, queries, preferred_element_type=jnp.float32)
            * inverse
        )
        grad_values = jnp.einsum(
            "gqk,qgd->kd", probs, grad_heads, preferred_element_type=jnp.float32
        )
        grad_kv = lax.psum_scatter(
            jnp.concatenate([grad_keys, grad_values], axis=1).astype(jnp.bfloat16),
            "row",
            scatter_dimension=0,
            tiled=True,
        ).astype(jnp.float32)
        grad_k = rope_turn(grad_kv[:, :head], cosine, -sine)
        grad_v = grad_kv[:, head:]
        grad_q = rope_turn(grad_queries, cosine[:, None, :], -sine[:, None, :]).reshape(
            tok, query_cols
        )
        grad_qkv = jnp.concatenate([grad_q, grad_k, grad_v], axis=1).astype(jnp.bfloat16)
        grad_xn = sum_features(project_out(grad_qkv, weight_qkv))
        list_qkv.append(weight_grad(xfull, grad_qkv).reshape(count_rows, 1, -1))
        grad_in, gain_a_grad = norm_backward(grad_xn, normed_a, factor_a, gain_attn[index])
        list_ga.append(gain_a_grad)
        grad_now = grad_hidden + grad_in
    gains_a, gains_f = lax.psum((jnp.stack(list_ga[::-1]), jnp.stack(list_gf[::-1])), "row")
    return (
        current,
        grad_now,
        jnp.stack(list_qkv[::-1]),
        jnp.stack(list_out[::-1]),
        jnp.stack(list_gu[::-1]),
        jnp.stack(list_down[::-1]),
        gains_a,
        gains_f,
    )


def solution(mesh):
    in_specs = (
        P("row", "col"),
        P("row", "col"),
        P(None, "row", "col", None),
        P(None, "row", "col"),
        P(None, "row", None, "col"),
        P(None, "row", "col"),
        P(None, "col"),
        P(None, "col"),
    )
    out_specs = (
        P("row", "col"),
        P("row", "col"),
        P(None, "row", "col", None),
        P(None, "row", "col"),
        P(None, "row", None, "col"),
        P(None, "row", "col"),
        P(None, "col"),
        P(None, "col"),
    )
    return jax.shard_map(local, mesh=mesh, in_specs=in_specs, out_specs=out_specs, check_vma=False)
```

profile of v0, /device:TPU:4, one launch (start us, length us, event | category | flops | bytes accessed | tf_op | source)
XLA Modules:
  0.0 2084.1 jit_solution(1052592607271940637)
XLA Ops:
  12.3 5.8 psum.70
  20.5 7.3 all_gather.62
  28.0 38.4 %all-gather.19.cloned.1.call-done = bf16[1,2048,1,640]{3,1,2,0:T(8,128)(2,1)} async-done(((bf16[1,256,1,640]{3,1,2,0:T(8,128)(2,1)}), bf16[1,2048,1,640]{3,1,2,0:T(8,128)(2,1)}) %all-gather.19.cloned.1.call-update) | async-done | bytes 2621456 | tf_op jit(solution)/shard_map/all_gather | solution.py:45
  70.3 31.4 %all_gather.64 = bf16[1024,128]{1,0:T(8,128)(2,1)S(1)} all-gather(bf16[128,128]{1,0:T(8,128)(2,1)S(1)} %pad_maximum_fusion.18), channel_id=1, replica_groups=mesh['row'=8,'col'=4] {'row'}, dimensions={0}, use_global_device_ids=true | all-gather | bytes 294912 | tf_op jit(solution)/shard_map/all_gather | solution.py:117
  105.4 12.0 all-gather.21.cloned.1.call-done
  117.4 3.2 convolution_convert_fusion.11
  127.4 12.9 reduce-scatter.23.cloned.1.call-done
  141.3 6.6 psum.71
  148.9 6.5 all_gather.66
  155.4 151.9 %all-gather.15.cloned.1.call-done = bf16[2048,2816]{1,0:T(8,128)(2,1)} async-done(((bf16[256,2816]{1,0:T(8,128)(2,1)}), bf16[2048,2816]{1,0:T(8,128)(2,1)}) %all-gather.15.cloned.1.call-update) | async-done | bytes 11534352 | tf_op jit(solution)/shard_map/all_gather | solution.py:45
  307.4 5.9 fusion.165
  313.6 86.9 %all-gather.23.cloned.1.call-done = bf16[1,2048,1408]{2,1,0:T(8,128)(2,1)} async-done(((bf16[1,256,1408]{2,1,0:T(8,128)(2,1)}), bf16[1,2048,1408]{2,1,0:T(8,128)(2,1)}) %all-gather.23.cloned.1.call-update) | async-done | bytes 5767184 | tf_op jit(solution)/shard_map/all_gather | solution.py:53
  400.5 5.4 fusion.33
  407.5 17.3 reduce-scatter.25.cloned.1.call-done
  425.8 6.6 psum.72
  432.6 6.5 all_gather.69
  439.1 43.5 %all-gather.25.cloned.1.call-done = bf16[1,2048,1,640]{3,1,2,0:T(8,128)(2,1)} async-done(((bf16[1,256,1,640]{3,1,2,0:T(8,128)(2,1)}), bf16[1,2048,1,640]{3,1,2,0:T(8,128)(2,1)}) %all-gather.25.cloned.1.call-update) | async-done | bytes 2621456 | tf_op jit(solution)/shard_map/all_gather | solution.py:45
  485.9 31.9 %all_gather.71 = bf16[1024,128]{1,0:T(8,128)(2,1)S(1)} all-gather(bf16[128,128]{1,0:T(8,128)(2,1)S(1)} %pad_maximum_fusion.19), channel_id=1, replica_groups=mesh['row'=8,'col'=4] {'row'}, dimensions={0}, use_global_device_ids=true | all-gather | bytes 294912 | tf_op jit(solution)/shard_map/all_gather | solution.py:117
  521.5 12.2 all-gather.27.cloned.1.call-done
  533.7 3.2 convolution_convert_fusion.10
  539.1 6.5 all_gather.76
  545.6 10.7 reduce-scatter.27.cloned.1.call-done
  557.3 6.6 psum.73
  565.0 6.5 all_gather.73
  571.5 151.9 %all-gather.17.cloned.1.call-done = bf16[2048,2816]{1,0:T(8,128)(2,1)} async-done(((bf16[256,2816]{1,0:T(8,128)(2,1)}), bf16[2048,2816]{1,0:T(8,128)(2,1)}) %all-gather.17.cloned.1.call-update) | async-done | bytes 11534352 | tf_op jit(solution)/shard_map/all_gather | solution.py:45
  723.4 7.0 fusion.166
  730.5 86.2 %all-gather.29.cloned.1.call-done = bf16[1,2048,1408]{2,1,0:T(8,128)(2,1)} async-done(((bf16[1,256,1408]{2,1,0:T(8,128)(2,1)}), bf16[1,2048,1408]{2,1,0:T(8,128)(2,1)}) %all-gather.29.cloned.1.call-update) | async-done | bytes 5767184 | tf_op jit(solution)/shard_map/all_gather | solution.py:53
  816.7 4.9 multiply_convert_fusion.3
  822.5 9.0 convolution_convert_fusion.9
  832.9 17.5 reduce-scatter.31.cloned.1.call-done
  852.2 7.2 psum.74
  861.8 6.7 all_gather.77
  883.3 61.0 %reduce-scatter.55.cloned.1.call-done = bf16[128,128]{1,0:T(8,128)(2,1)} async-done(((bf16[1024,128]{1,0:T(8,128)(2,1)}), bf16[128,128]{1,0:T(8,128)(2,1)}) %reduce-scatter.55.cloned.1.call-update) | async-done | bytes 32784
  946.0 3.5 fusion.30
  949.6 5.6 fusion.36
  955.3 13.9 reduce-scatter.33.cloned.1.call-done
  970.9 6.6 psum.75
  978.0 15.9 reduce-scatter.29.cloned.1.call-done
  995.9 7.4 all_gather.78
  1003.2 3.9 multiply_convert_fusion.1
  1008.0 9.0 convolution_convert_fusion.8
  1018.4 20.2 reduce-scatter.35.cloned.1.call-done
  1040.4 7.2 psum.76
  1049.8 6.7 all_gather.79
  1070.2 61.9 %reduce-scatter.57.cloned.1.call-done = bf16[128,128]{1,0:T(8,128)(2,1)} async-done(((bf16[1024,128]{1,0:T(8,128)(2,1)}), bf16[128,128]{1,0:T(8,128)(2,1)}) %reduce-scatter.57.cloned.1.call-update) | async-done | bytes 32784
  1133.9 3.6 fusion.27
  1137.6 3.1 convolution_convert_fusion.6
  1147.9 4.2 fusion
  1153.3 4.2 convolution_convert_fusion.3
  1158.8 5.9 convolution_convert_fusion
  1165.8 5.9 convolution_convert_fusion.1
  1173.4 6.1 psum.77
  1179.5 20.7 all-reduce
  1202.1 28.5 %reduce-scatter.45.cloned.1.call-done = bf16[256,512]{1,0:T(8,128)(2,1)} async-done(((bf16[2048,512]{1,0:T(8,128)(2,1)}), bf16[256,512]{1,0:T(8,128)(2,1)}) %reduce-scatter.45.cloned.1.call-update) | async-done | bytes 262160 | tf_op jit(solution)/shard_map/reduce_scatter | solution.py:57
  1230.5 70.8 %reduce-scatter.43.cloned.1.call-done = bf16[256,512]{1,0:T(8,128)(2,1)} async-done(((bf16[2048,512]{1,0:T(8,128)(2,1)}), bf16[256,512]{1,0:T(8,128)(2,1)}) %reduce-scatter.43.cloned.1.call-update) | async-done | bytes 262160 | tf_op jit(solution)/shard_map/reduce_scatter | solution.py:57
  1303.4 72.0 %reduce-scatter.41.cloned.1.call-done = bf16[256,640]{1,0:T(8,128)(2,1)} async-done(((bf16[2048,640]{1,0:T(8,128)(2,1)}), bf16[256,640]{1,0:T(8,128)(2,1)}) %reduce-scatter.41.cloned.1.call-update) | async-done | bytes 327696 | tf_op jit(solution)/shard_map/reduce_scatter | solution.py:57
  1375.4 73.6 %reduce-scatter.39.cloned.1.call-done = bf16[256,640]{1,0:T(8,128)(2,1)} async-done(((bf16[2048,640]{1,0:T(8,128)(2,1)}), bf16[256,640]{1,0:T(8,128)(2,1)}) %reduce-scatter.39.cloned.1.call-update) | async-done | bytes 327696 | tf_op jit(solution)/shard_map/reduce_scatter | solution.py:57
  1452.5 110.4 %reduce-scatter.53.cloned.1.call-done = bf16[256,1408]{1,0:T(8,128)(2,1)} async-done(((bf16[2048,1408]{1,0:T(8,128)(2,1)}), bf16[256,1408]{1,0:T(8,128)(2,1)}) %reduce-scatter.53.cloned.1.call-update) | async-done | bytes 720912 | tf_op jit(solution)/shard_map/reduce_scatter | solution.py:57
  1563.0 113.5 %reduce-scatter.51.cloned.1.call-done = bf16[256,1408]{1,0:T(8,128)(2,1)} async-done(((bf16[2048,1408]{1,0:T(8,128)(2,1)}), bf16[256,1408]{1,0:T(8,128)(2,1)}) %reduce-scatter.51.cloned.1.call-update) | async-done | bytes 720912 | tf_op jit(solution)/shard_map/reduce_scatter | solution.py:57
  1679.5 192.7 %reduce-scatter.49.cloned.1.call-done = bf16[256,2816]{1,0:T(8,128)(2,1)} async-done(((bf16[2048,2816]{1,0:T(8,128)(2,1)}), bf16[256,2816]{1,0:T(8,128)(2,1)}) %reduce-scatter.49.cloned.1.call-update) | async-done | bytes 1441808 | tf_op jit(solution)/shard_map/reduce_scatter | solution.py:57
  1872.2 3.2 stack_reshape.19
  1875.4 192.2 %reduce-scatter.47.cloned.1.call-done = bf16[256,2816]{1,0:T(8,128)(2,1)} async-done(((bf16[2048,2816]{1,0:T(8,128)(2,1)}), bf16[256,2816]{1,0:T(8,128)(2,1)}) %reduce-scatter.47.cloned.1.call-update) | async-done | bytes 1441808 | tf_op jit(solution)/shard_map/reduce_scatter | solution.py:57
  2067.6 3.2 stack_reshape.18
  2070.9 6.2 maximum_convert_fusion
  (359 shorter events, 108.9 us)
Async XLA Ops:
  7.2 59.2 %all-gather.19.cloned.1.call-start = ((), (), s32[]{:S(2)}) async-start(), calls=%async_computation.36 | async-start | bytes 2949120 | tf_op jit(solution)/shard_map/all_gather | solution.py:45
  9.2 108.2 %all-gather.21.cloned.1.call-start = ((), (), s32[]{:S(2)}) async-start(), calls=%async_computation.37 | async-start | bytes 2359296 | tf_op jit(solution)/shard_map/all_gather | solution.py:53
  11.1 129.1 %reduce-scatter.23.cloned.1.call-start = ((), (), s32[]{:S(2)}) async-start(), calls=%async_computation.18 | async-start | bytes 655360 | tf_op jit(solution)/shard_map/reduce_scatter | solution.py:35
  11.2 91.3 %copy-start.81 = (f32[128]{0:T(128)}, f32[128]{0:T(128)S(1)}, u32[]{:S(2)}) copy-start(f32[128]{0:T(128)S(1)} %fusion.150) | copy-start | bytes 1540
  18.1 84.4 %copy-start.83 = (f32[32]{0:T(128)}, f32[32]{0:T(128)S(1)}, u32[]{:S(2)}) copy-start(f32[32]{0:T(128)S(1)} %negate_power_fusion) | copy-start | bytes 388
  27.8 74.7 %copy-start.12 = (bf16[128,2048]{1,0:T(8,128)(2,1)}, bf16[128,2048]{1,0:T(8,128)(2,1)S(1)}, u32[]{:S(2)}) copy-start(bf16[128,2048]{1,0:T(8,128)(2,1)S(1)} %all_gather.62) | copy-start | bytes 1572868
  27.9 74.6 %copy-start.44 = (pred[128,1024]{0,1:T(8,128)(4,1)}, pred[128,1024]{0,1:T(8,128)(4,1)S(1)}, u32[]{:S(2)}) copy-start(pred[128,1024]{0,1:T(8,128)(4,1)S(1)} %iota_compare_fusion) | copy-start | bytes 393220
  69.9 33.2 %copy-start.62 = (f32[128,32]{0,1:T(8,128)}, f32[128,32]{0,1:T(8,128)S(1)}, u32[]{:S(2)}) copy-start(f32[128,32]{0,1:T(8,128)S(1)} %get-tuple-element.93) | copy-start | bytes 49156
  105.4 18.2 copy-start.56
  120.7 186.7 %all-gather.15.cloned.1.call-start = ((), (), s32[]{:S(2)}) async-start(), calls=%async_computation.19 | async-start | bytes 12976128 | tf_op jit(solution)/shard_map/all_gather | solution.py:45
  124.9 275.5 %all-gather.23.cloned.1.call-start = ((), (), s32[]{:S(2)}) async-start(), calls=%async_computation.38 | async-start | bytes 6488064 | tf_op jit(solution)/shard_map/all_gather | solution.py:53
  126.8 298.0 %reduce-scatter.25.cloned.1.call-start = ((), (), s32[]{:S(2)}) async-start(), calls=%async_computation.20 | async-start | bytes 655360 | tf_op jit(solution)/shard_map/reduce_scatter | solution.py:35
  127.4 28.1 %copy-start.70 = (f32[1,512]{1,0:T(1,128)}, f32[1,512]{1,0:T(1,128)S(1)}, u32[]{:S(2)}) copy-start(f32[1,512]{1,0:T(1,128)S(1)} %get-tuple-element.90) | copy-start | bytes 6148
  313.3 92.6 %copy-start.9 = (f32[128,2816]{1,0:T(8,128)}, f32[128,2816]{1,0:T(8,128)S(1)}, u32[]{:S(2)}) copy-start(f32[128,2816]{1,0:T(8,128)S(1)} %fusion.165) | copy-start | bytes 4325380
  313.5 112.3 %copy-start.24 = (bf16[128,1408]{1,0:T(8,128)(2,1)}, bf16[128,1408]{1,0:T(8,128)(2,1)S(1)}, u32[]{:S(2)}) copy-start(bf16[128,1408]{1,0:T(8,128)(2,1)S(1)} %multiply_convert_fusion.5) | copy-start | bytes 1081348
  313.5 111.2 %copy-start.16 = (bf16[128,512]{1,0:T(8,128)(2,1)S(1)}, bf16[128,512]{1,0:T(8,128)(2,1)}, u32[]{:S(2)}) copy-start(bf16[128,512]{1,0:T(8,128)(2,1)} %reduce-scatter.23.cloned.1.call-done) | copy-start | bytes 393220
  313.5 118.9 %copy-start.77 = (f32[1,512]{1,0:T(1,128)S(1)}, f32[1,512]{1,0:T(1,128)}, u32[]{:S(2)}) copy-start(f32[1,512]{1,0:T(1,128)} %get-tuple-element.88) | copy-start | bytes 6148
  405.9 79.5 %copy-start.82 = (f32[128]{0:T(128)S(1)}, f32[128]{0:T(128)}, u32[]{:S(2)}) copy-start(f32[128]{0:T(128)} %copy-done.81) | copy-start | bytes 1540
  405.9 79.5 %copy-start.84 = (f32[32]{0:T(128)S(1)}, f32[32]{0:T(128)}, u32[]{:S(2)}) copy-start(f32[32]{0:T(128)} %copy-done.83) | copy-start | bytes 388
  405.9 111.9 %copy-start.63 = (f32[128,32]{0,1:T(8,128)S(1)}, f32[128,32]{0,1:T(8,128)}, u32[]{:S(2)}) copy-start(f32[128,32]{0,1:T(8,128)} %copy-done.62) | copy-start | bytes 49156
  405.9 76.6 %all-gather.25.cloned.1.call-start = ((), (), s32[]{:S(2)}) async-start(), calls=%async_computation.39 | async-start | bytes 2949120 | tf_op jit(solution)/shard_map/all_gather | solution.py:45
  406.0 111.9 %copy-start.45 = (pred[128,1024]{0,1:T(8,128)(4,1)S(1)}, pred[128,1024]{0,1:T(8,128)(4,1)}, u32[]{:S(2)}) copy-start(pred[128,1024]{0,1:T(8,128)(4,1)} %copy-done.44) | copy-start | bytes 393220
  406.7 127.0 %all-gather.27.cloned.1.call-start = ((), (), s32[]{:S(2)}) async-start(), calls=%async_computation.40 | async-start | bytes 2359296 | tf_op jit(solution)/shard_map/all_gather | solution.py:53
  407.4 148.9 %reduce-scatter.27.cloned.1.call-start = ((), (), s32[]{:S(2)}) async-start(), calls=%async_computation.21 | async-start | bytes 655360 | tf_op jit(solution)/shard_map/reduce_scatter | solution.py:35
  432.4 52.7 %copy-start.93 = (f32[128]{0:T(128)}, f32[128]{0:T(128)S(1)}, u32[]{:S(2)}) copy-start(f32[128]{0:T(128)S(1)} %add_rsqrt_fusion.1) | copy-start | bytes 1540
  439.1 79.4 %copy-start.14 = (bf16[128,2048]{1,0:T(8,128)(2,1)}, bf16[128,2048]{1,0:T(8,128)(2,1)S(1)}, u32[]{:S(2)}) copy-start(bf16[128,2048]{1,0:T(8,128)(2,1)S(1)} %all_gather.69) | copy-start | bytes 1572868
  521.5 17.6 copy-start.58
  521.5 17.5 copy-start.27
  536.9 27.1 %copy-start.72 = (f32[1,512]{1,0:T(1,128)S(1)}, f32[1,512]{1,0:T(1,128)}, u32[]{:S(2)}) copy-start(f32[1,512]{1,0:T(1,128)} %get-tuple-element.91) | copy-start | bytes 6148
  536.9 186.5 %all-gather.17.cloned.1.call-start = ((), (), s32[]{:S(2)}) async-start(), calls=%async_computation.22 | async-start | bytes 12976128 | tf_op jit(solution)/shard_map/all_gather | solution.py:45
  538.3 278.4 %all-gather.29.cloned.1.call-start = ((), (), s32[]{:S(2)}) async-start(), calls=%async_computation.41 | async-start | bytes 6488064 | tf_op jit(solution)/shard_map/all_gather | solution.py:53
  539.0 311.4 %reduce-scatter.31.cloned.1.call-start = ((), (), s32[]{:S(2)}) async-start(), calls=%async_computation.24 | async-start | bytes 655360 | tf_op jit(solution)/shard_map/reduce_scatter | solution.py:35
  545.6 271.1 %copy-start.31 = (bf16[128,2048]{1,0:T(8,128)(2,1)}, bf16[128,2048]{1,0:T(8,128)(2,1)S(1)}, u32[]{:S(2)}) copy-start(bf16[128,2048]{1,0:T(8,128)(2,1)S(1)} %all_gather.76) | copy-start | bytes 1572868
  564.0 166.5 %copy-start.90 = (f32[128]{0:T(128)}, f32[128]{0:T(128)S(1)}, u32[]{:S(2)}) copy-start(f32[128]{0:T(128)S(1)} %add_rsqrt_fusion) | copy-start | bytes 1540
  571.5 159.0 %copy-start.7 = (bf16[128,2048]{1,0:T(8,128)(2,1)}, bf16[128,2048]{1,0:T(8,128)(2,1)S(1)}, u32[]{:S(2)}) copy-start(bf16[128,2048]{1,0:T(8,128)(2,1)S(1)} %all_gather.73) | copy-start | bytes 1572868
  822.5 46.8 %copy-start.6 = (bf16[1,2048,512]{2,1,0:T(8,128)(2,1)S(1)}, bf16[1,2048,512]{2,1,0:T(8,128)(2,1)}, u32[]{:S(2)}) copy-start(bf16[1,2048,512]{2,1,0:T(8,128)(2,1)} %all-gather.27.cloned.1.call-done) | copy-start | bytes 6291460
  831.5 112.7 %reduce-scatter.55.cloned.1.call-start = ((), (), s32[]{:S(2)}) async-start(), calls=%async_computation.42 | async-start | bytes 294912
  881.0 88.3 %reduce-scatter.33.cloned.1.call-start = ((), (), s32[]{:S(2)}) async-start(), calls=%async_computation.25 | async-start | bytes 655360 | tf_op jit(solution)/shard_map/reduce_scatter | solution.py:35
  883.3 66.3 %copy-start.42 = (bf16[128,8,64]{0,2,1:T(8,128)(2,1)}, bf16[128,8,64]{0,2,1:T(8,128)(2,1)S(1)}, u32[]{:S(2)}) copy-start(bf16[128,8,64]{0,2,1:T(8,128)(2,1)S(1)} %pad_maximum_fusion.12) | copy-start | bytes 393220
  949.5 19.8 copy-start.78
  949.5 19.8 copy-start.94
  949.5 44.4 %copy-start.23 = (bf16[128,512]{1,0:T(8,128)(2,1)S(1)}, bf16[128,512]{1,0:T(8,128)(2,1)}, u32[]{:S(2)}) copy-start(bf16[128,512]{1,0:T(8,128)(2,1)} %reduce-scatter.27.cloned.1.call-done) | copy-start | bytes 393220
  949.5 44.4 %copy-start.28 = (f32[128,512]{1,0:T(8,128)S(1)}, f32[128,512]{1,0:T(8,128)}, u32[]{:S(2)}) copy-start(f32[128,512]{1,0:T(8,128)} %param.9) | copy-start | bytes 786436
  949.5 44.4 %copy-start.47 = (bf16[128,512]{1,0:T(8,128)(2,1)S(1)}, bf16[128,512]{1,0:T(8,128)(2,1)}, u32[]{:S(2)}) copy-start(bf16[128,512]{1,0:T(8,128)(2,1)} %reduce-scatter.31.cloned.1.call-done) | copy-start | bytes 393220
  949.5 44.3 %reduce-scatter.29.cloned.1.call-start = ((), (), s32[]{:S(2)}) async-start(), calls=%async_computation.23 | async-start | bytes 655360 | tf_op jit(solution)/shard_map/reduce_scatter | solution.py:35
  949.6 53.6 %copy-start.10 = (f32[128,2816]{1,0:T(8,128)S(1)}, f32[128,2816]{1,0:T(8,128)}, u32[]{:S(2)}) copy-start(f32[128,2816]{1,0:T(8,128)} %copy-done.9) | copy-start | bytes 4325380
  955.3 83.4 %reduce-scatter.35.cloned.1.call-start = ((), (), s32[]{:S(2)}) async-start(), calls=%async_computation.26 | async-start | bytes 655360 | tf_op jit(solution)/shard_map/reduce_scatter | solution.py:35
  1008.0 40.8 %copy-start.29 = (f32[128,512]{1,0:T(8,128)S(1)}, f32[128,512]{1,0:T(8,128)}, u32[]{:S(2)}) copy-start(f32[128,512]{1,0:T(8,128)} %get-tuple-element.51) | copy-start | bytes 786436
  1008.0 49.3 %copy-start.5 = (bf16[1,2048,512]{2,1,0:T(8,128)(2,1)S(1)}, bf16[1,2048,512]{2,1,0:T(8,128)(2,1)}, u32[]{:S(2)}) copy-start(bf16[1,2048,512]{2,1,0:T(8,128)(2,1)} %all-gather.21.cloned.1.call-done) | copy-start | bytes 6291460
  1017.1 115.1 %reduce-scatter.57.cloned.1.call-start = ((), (), s32[]{:S(2)}) async-start(), calls=%async_computation.43 | async-start | bytes 294912
  1068.8 103.0 %reduce-scatter.37.cloned.1.call-start = ((), (), s32[]{:S(2)}) async-start(), calls=%async_computation.27 | async-start | bytes 655360 | tf_op jit(solution)/shard_map/reduce_scatter | solution.py:35
  1069.4 68.2 %copy-start.59 = (bf16[64,8,128]{2,0,1:T(8,128)(2,1)S(1)}, bf16[64,8,128]{2,0,1:T(8,128)(2,1)}, u32[]{:S(2)}) copy-start(bf16[64,8,128]{2,0,1:T(8,128)(2,1)} %copy-done.58) | copy-start | bytes 393220
  1137.5 93.0 %reduce-scatter.45.cloned.1.call-start = ((), (), s32[]{:S(2)}) async-start(), calls=%async_computation.31 | async-start | bytes 2359296 | tf_op jit(solution)/shard_map/reduce_scatter | solution.py:57
  1140.8 160.6 %reduce-scatter.43.cloned.1.call-start = ((), (), s32[]{:S(2)}) async-start(), calls=%async_computation.30 | async-start | bytes 2359296 | tf_op jit(solution)/shard_map/reduce_scatter | solution.py:57
  1142.9 232.5 %reduce-scatter.41.cloned.1.call-start = ((), (), s32[]{:S(2)}) async-start(), calls=%async_computation.29 | async-start | bytes 2949120 | tf_op jit(solution)/shard_map/reduce_scatter | solution.py:57
  1145.4 303.6 %reduce-scatter.39.cloned.1.call-start = ((), (), s32[]{:S(2)}) async-start(), calls=%async_computation.28 | async-start | bytes 2949120 | tf_op jit(solution)/shard_map/reduce_scatter | solution.py:57
  1147.8 415.1 %reduce-scatter.53.cloned.1.call-start = ((), (), s32[]{:S(2)}) async-start(), calls=%async_computation.35 | async-start | bytes 6488064 | tf_op jit(solution)/shard_map/reduce_scatter | solution.py:57
  1152.2 524.3 %reduce-scatter.51.cloned.1.call-start = ((), (), s32[]{:S(2)}) async-start(), calls=%async_computation.34 | async-start | bytes 6488064 | tf_op jit(solution)/shard_map/reduce_scatter | solution.py:57
  1157.6 714.7 %reduce-scatter.49.cloned.1.call-start = ((), (), s32[]{:S(2)}) async-start(), calls=%async_computation.33 | async-start | bytes 12976128 | tf_op jit(solution)/shard_map/reduce_scatter | solution.py:57
  1164.7 902.9 %reduce-scatter.47.cloned.1.call-start = ((), (), s32[]{:S(2)}) async-start(), calls=%async_computation.32 | async-start | bytes 12976128 | tf_op jit(solution)/shard_map/reduce_scatter | solution.py:57
  1171.7 28.6 %copy-start.46 = (bf16[128,512]{1,0:T(8,128)(2,1)S(1)}, bf16[128,512]{1,0:T(8,128)(2,1)}, u32[]{:S(2)}) copy-start(bf16[128,512]{1,0:T(8,128)(2,1)} %reduce-scatter.35.cloned.1.call-done) | copy-start | bytes 393220
  1171.7 28.6 %copy-start.71 = (f32[1,512]{1,0:T(1,128)S(1)}, f32[1,512]{1,0:T(1,128)}, u32[]{:S(2)}) copy-start(f32[1,512]{1,0:T(1,128)} %copy-done.70) | copy-start | bytes 6148
  1171.7 28.5 %copy-start.89 = (f32[128]{0:T(128)S(1)}, f32[128]{0:T(128)}, u32[]{:S(2)}) copy-start(f32[128]{0:T(128)} %copy-done.88) | copy-start | bytes 1540
  1171.7 28.5 %copy-start.97 = (f32[128]{0:T(128)S(1)}, f32[128]{0:T(128)}, u32[]{:S(2)}) copy-start(f32[128]{0:T(128)} %copy-done.96) | copy-start | bytes 1540
  (61 other events, 213.6 us)
Sparse Core Ops, SparseCore 0:
  10.7 55.5 all-gather.18
  69.1 48.3 all-gather.20
  120.8 19.4 reduce-scatter.22
  142.9 164.4 all-gather.14
  310.0 90.4 all-gather.22
  406.0 18.7 reduce-scatter.24
  427.0 55.5 all-gather.24
  485.2 48.4 all-gather.26
  537.0 19.2 reduce-scatter.26
  558.9 164.4 all-gather.16
  726.2 90.4 all-gather.28
  831.6 18.7 reduce-scatter.30
  881.1 63.1 reduce-scatter.54
  949.7 19.5 reduce-scatter.32
  972.2 21.6 reduce-scatter.28
  1017.2 21.4 reduce-scatter.34
  1069.0 63.1 reduce-scatter.56
  1137.6 19.5 reduce-scatter.36
  1160.7 69.7 reduce-scatter.44
  1233.9 67.3 reduce-scatter.42
  1305.4 69.9 reduce-scatter.40
  1378.9 70.0 reduce-scatter.38
  1453.2 109.7 reduce-scatter.52
  1566.5 109.9 reduce-scatter.50
  1680.0 192.1 reduce-scatter.48
  1875.7 191.9 reduce-scatter.46
where the time goes:
time: 2100 us; the launch traced here: 2080 us
  waiting for transfers between devices  1670 us (80%)
  blocking collectives  191 us (9%)
  matrix products  118 us (6%)
  other arithmetic  45.5 us (2%)
  local copies, waits for them, and re-layouts  42.2 us (2%)
    reduce_scatter x8, waiting for transfers between devices, weight_grad(): lax.psum_scatter(lax.dot_general(left, right, (((0,), (0,)), ((), ())), p...  854 us
    all_gather x4, waiting for transfers between devices, project_in(): return add_rows(left, lax.all_gather(shard, 'row', axis=0, tiled=True))  386 us
    all_gather x4, waiting for transfers between devices, project_out(): return columns_of(left, lax.all_gather(shard, 'row', axis=0, tiled=True))  197 us
    unnamed x28, waiting for transfers between devices  125 us
    reduce_scatter x8, waiting for transfers between devices, sum_features(): lax.psum_scatter(partials.astype(jnp.bfloat16), 'col', scatter_dimension=...  109 us
    all_gather x2, blocking collectives, local(): lax.all_gather(jnp.concatenate([keys, values], axis=1), 'row', axis=0, ti...  63.3 us
    all_gather x8, blocking collectives, gather_features(): return lax.all_gather(rows_in, 'col', axis=1, tiled=True)  54.1 us
    psum x8, blocking collectives, feature_sum(): return lax.psum(values, 'col')  52.7 us
  transfers between devices with their start and end apart: 26, of which 25 were waited for; matrix products, arithmetic and copies ran while one was open for 5% of the time, Pallas kernels for 0%

commit v1 on v0

--- a/solution.py
+++ b/solution.py
@@ -3,6 +3,7 @@
 import jax
 import jax.numpy as jnp
 from jax import lax
+from jax.sharding import Mesh
 from jax.sharding import PartitionSpec as P
 
 D = 2048
@@ -250,25 +251,232 @@
     )
 
 
+def share_out(mesh):
+    rows, cols = mesh.shape["row"], mesh.shape["col"]
+    return Mesh(
+        mesh.devices.reshape(rows // 2, 2, cols // 2, 2), ("z", "x", "y", "c")
+    )
+
+
+GRID = ("y", "c")
+
+
+def swap_grid(values, depth):
+    width = lax.axis_size("c")
+    pairs = [(z * depth + g, g * depth + z) for z in range(depth) for g in range(depth)]
+    return lax.ppermute(values, ("z", "y", "c"), pairs)
+
+
+def gather_grid(rows_in):
+    return lax.all_gather(rows_in, GRID, axis=0, tiled=True)
+
+
+def sum_grid(partials):
+    return lax.psum_scatter(
+        partials.astype(jnp.bfloat16), GRID, scatter_dimension=0, tiled=True
+    ).astype(jnp.float32)
+
+
+def gather_line(rows_in):
+    return lax.all_gather(rows_in, "z", axis=0, tiled=True)
+
+
+def sum_line(partials):
+    return lax.psum_scatter(
+        partials.astype(jnp.bfloat16), "z", scatter_dimension=0, tiled=True
+    ).astype(jnp.float32)
+
+
+def pair_grad(left, right):
+    return lax.psum_scatter(
+        lax.dot_general(
+            left, right, (((0,), (0,)), ((), ())), preferred_element_type=jnp.float32
+        ).astype(jnp.bfloat16),
+        "x",
+        scatter_dimension=0,
+        tiled=True,
+    ).astype(jnp.float32)
+
+
+def line_norm(values, gain):
+    total = lax.psum(jnp.sum(values * values, axis=1), "z")
+    factor = lax.rsqrt(total / D + EPS)
+    normed = values * factor[:, None]
+    return (normed, factor, (normed * gain).astype(jnp.bfloat16))
+
+
+def line_norm_back(grad_normed, normed, factor, gain):
+    scaled = grad_normed * gain
+    inner = lax.psum(jnp.sum(scaled * normed, axis=1), "z")
+    grad_in = factor[:, None] * (scaled - normed * (inner / D)[:, None])
+    return (grad_in, jnp.sum(grad_normed * normed, axis=0))
+
+
+def times_t(left, piece):
+    return jnp.einsum("tj,dj->td", left, piece, preferred_element_type=jnp.float32)
+
+
+def stationary(stream, grad_out, wqkv, wo, wgu, wd, gain_attn, gain_ffn):
+    tok = stream.shape[0]
+    layers = wqkv.shape[0]
+    count_rows = wqkv.shape[1]
+    depth = lax.axis_size("z")
+    head = HEAD
+    query_cols = GROUP * head
+    inverse = 1.0 / math.sqrt(head)
+    row = lax.axis_index("z") * 2 + lax.axis_index("x")
+    query_pos = row * tok + jnp.arange(tok, dtype=jnp.int32)
+    key_pos = jnp.arange(2 * depth * tok, dtype=jnp.int32)
+    freq = THETA ** (-(jnp.arange(head // 2, dtype=jnp.float32) * 2.0 / head))
+    angle = query_pos.astype(jnp.float32)[:, None] * freq[None, :]
+    cosine = jnp.cos(angle)
+    sine = jnp.sin(angle)
+    whole = lambda shard: lax.all_gather(shard, "x", axis=0, tiled=True)
+    current = swap_grid(stream, depth)
+    grad_now = swap_grid(grad_out, depth)
+    gain_a = swap_grid(gain_attn, depth)
+    gain_f = swap_grid(gain_ffn, depth)
+    saved = []
+    for index in range(layers):
+        weight_qkv = whole(wqkv[index].reshape(count_rows, -1))
+        weight_out = whole(wo[index])
+        weight_gu = whole(wgu[index].reshape(count_rows, -1))
+        weight_down = whole(wd[index])
+        normed_a, factor_a, xnormed = line_norm(current, gain_a[index])
+        xfull = gather_grid(xnormed)
+        qkv = sum_line(add_rows(xfull, weight_qkv))
+        queries = rope_turn(
+            qkv[:, :query_cols].reshape(tok, GROUP, head), cosine[:, None, :], sine[:, None, :]
+        ).astype(jnp.bfloat16)
+        keys = rope_turn(qkv[:, query_cols : query_cols + head], cosine, sine).astype(jnp.bfloat16)
+        values = qkv[:, query_cols + head :].astype(jnp.bfloat16)
+        seqkv = lax.all_gather(
+            jnp.concatenate([keys, values], axis=1), ("z", "x"), axis=0, tiled=True
+        )
+        seq_keys = seqkv[:, :head]
+        seq_values = seqkv[:, head:]
+        scores = masked_scores(queries, seq_keys, query_pos, key_pos)
+        top = jnp.max(scores, axis=2, keepdims=True)
+        expo = jnp.exp(scores - top)
+        denom = jnp.sum(expo, axis=2, keepdims=True)
+        probs = (expo / denom).astype(jnp.bfloat16)
+        log_total = top + jnp.log(denom)
+        mixed = (
+            jnp.einsum("gqk,kd->qgd", probs, seq_values, preferred_element_type=jnp.float32)
+            .reshape(tok, query_cols)
+            .astype(jnp.bfloat16)
+        )
+        mixed_full = gather_line(mixed)
+        hidden_in = current + sum_grid(times_t(mixed_full, weight_out))
+        normed_f, factor_f, hnormed = line_norm(hidden_in, gain_f[index])
+        hfull = gather_grid(hnormed)
+        gate_up = sum_line(add_rows(hfull, weight_gu))
+        hidden_cols = gate_up.shape[1] // 2
+        gate = gate_up[:, :hidden_cols]
+        upper = gate_up[:, hidden_cols:]
+        active = gather_line((jax.nn.silu(gate) * upper).astype(jnp.bfloat16))
+        current = hidden_in + sum_grid(times_t(active, weight_down))
+        saved.append(
+            (weight_qkv, weight_out, weight_gu, weight_down, normed_a, factor_a, xfull, queries,
+             seq_keys, seq_values, log_total, mixed_full, normed_f, factor_f, hfull, gate, upper, active)
+        )
+    list_qkv, list_out, list_gu, list_down, list_ga, list_gf = ([], [], [], [], [], [])
+    for index in reversed(range(layers)):
+        (weight_qkv, weight_out, weight_gu, weight_down, normed_a, factor_a, xfull, queries,
+         seq_keys, seq_values, log_total, mixed_full, normed_f, factor_f, hfull, gate, upper, active) = saved[index]
+        grad_full = gather_grid(grad_now.astype(jnp.bfloat16))
+        grad_active = sum_line(add_rows(grad_full, weight_down))
+        list_down.append(pair_grad(grad_full, active))
+        sig = jax.nn.sigmoid(gate)
+        grad_gate = grad_active * upper * sig * (1.0 + gate * (1.0 - sig))
+        grad_up = grad_active * gate * sig
+        grad_gu = gather_line(jnp.concatenate([grad_gate, grad_up], axis=1).astype(jnp.bfloat16))
+        grad_hn = sum_grid(times_t(grad_gu, weight_gu))
+        list_gu.append(pair_grad(hfull, grad_gu).reshape(count_rows, 2, -1))
+        grad_mid, gain_f_grad = line_norm_back(grad_hn, normed_f, factor_f, gain_f[index])
+        list_gf.append(gain_f_grad)
+        grad_hidden = grad_now + grad_mid
+        hidden_full = gather_grid(grad_hidden.astype(jnp.bfloat16))
+        grad_mixed = sum_line(add_rows(hidden_full, weight_out)).astype(jnp.bfloat16)
+        list_out.append(pair_grad(hidden_full, mixed_full))
+        grad_heads = grad_mixed.reshape(tok, GROUP, head)
+        scores = masked_scores(queries, seq_keys, query_pos, key_pos)
+        probs_full = jnp.exp(scores - log_total)
+        probs = probs_full.astype(jnp.bfloat16)
+        grad_probs = jnp.einsum(
+            "qgd,kd->gqk", grad_heads, seq_values, preferred_element_type=jnp.float32
+        )
+        delta = jnp.sum(probs_full * grad_probs, axis=2, keepdims=True)
+        grad_scores = (probs_full * (grad_probs - delta)).astype(jnp.bfloat16)
+        grad_queries = (
+            jnp.einsum("gqk,kd->qgd", grad_scores, seq_keys, preferred_element_type=jnp.float32)
+            * inverse
+        )
+        grad_keys = (
+            jnp.einsum("gqk,qgd->kd", grad_scores, queries, preferred_element_type=jnp.float32)
+            * inverse
+        )
+        grad_values = jnp.einsum(
+            "gqk,qgd->kd", probs, grad_heads, preferred_element_type=jnp.float32
+        )
+        grad_kv = lax.psum_scatter(
+            jnp.concatenate([grad_keys, grad_values], axis=1).astype(jnp.bfloat16),
+            ("z", "x"),
+            scatter_dimension=0,
+            tiled=True,
+        ).astype(jnp.float32)
+        grad_k = rope_turn(grad_kv[:, :head], cosine, -sine)
+        grad_v = grad_kv[:, head:]
+        grad_q = rope_turn(grad_queries, cosine[:, None, :], -sine[:, None, :]).reshape(
+            tok, query_cols
+        )
+        grad_qkv = gather_line(
+            jnp.concatenate([grad_q, grad_k, grad_v], axis=1).astype(jnp.bfloat16)
+        )
+        grad_xn = sum_grid(times_t(grad_qkv, weight_qkv))
+        list_qkv.append(pair_grad(xfull, grad_qkv).reshape(count_rows, 1, -1))
+        grad_in, gain_a_grad = line_norm_back(grad_xn, normed_a, factor_a, gain_a[index])
+        list_ga.append(gain_a_grad)
+        grad_now = grad_hidden + grad_in
+    gains = lax.psum(jnp.concatenate([jnp.stack(list_ga[::-1]), jnp.stack(list_gf[::-1])]), ("x", "y", "c"))
+    gains = swap_grid(gains, depth)
+    return (
+        swap_grid(current, depth),
+        swap_grid(grad_now, depth),
+        jnp.stack(list_qkv[::-1]),
+        jnp.stack(list_out[::-1]),
+        jnp.stack(list_gu[::-1]),
+        jnp.stack(list_down[::-1]),
+        gains[:layers],
+        gains[layers:],
+    )
+
+
 def solution(mesh):
+    rows, cols = ("row", "col")
+    body = local
+    if (mesh.shape["row"], mesh.shape["col"]) == (8, 4):
+        mesh = share_out(mesh)
+        rows, cols = (("z", "x"), ("y", "c"))
+        body = stationary
     in_specs = (
-        P("row", "col"),
-        P("row", "col"),
-        P(None, "row", "col", None),
-        P(None, "row", "col"),
-        P(None, "row", None, "col"),
-        P(None, "row", "col"),
-        P(None, "col"),
-        P(None, "col"),
+        P(rows, cols),
+        P(rows, cols),
+        P(None, rows, cols, None),
+        P(None, rows, cols),
+        P(None, rows, None, cols),
+        P(None, rows, cols),
+        P(None, cols),
+        P(None, cols),
     )
     out_specs = (
-        P("row", "col"),
-        P("row", "col"),
-        P(None, "row", "col", None),
-        P(None, "row", "col"),
-        P(None, "row", None, "col"),
-        P(None, "row", "col"),
-        P(None, "col"),
-        P(None, "col"),
-    )
-    return jax.shard_map(local, mesh=mesh, in_specs=in_specs, out_specs=out_specs, check_vma=False)
+        P(rows, cols),
+        P(rows, cols),
+        P(None, rows, cols, None),
+        P(None, rows, cols),
+        P(None, rows, None, cols),
+        P(None, rows, cols),
+        P(None, cols),
+        P(None, cols),
+    )
+    return jax.shard_map(body, mesh=mesh, in_specs=in_specs, out_specs=out_specs, check_vma=False)

time: 2100 us -> 1300 us (0.62)
  waiting for transfers between devices: 1670 us -> 754 us
  blocking collectives: 191 us -> 313 us
  starting transfers between devices: 1.32 us -> 29.5 us
  matrix products: 118 us -> 91.1 us
    reduce_scatter x16 -> x22, waiting for transfers between devices: 962 us -> 406 us  [the longest x6 180 us: sum_line(): lax.psum_scatter(partials.astype(jnp.bfloat16), 'z', scatter_dimension=0,...]
    all_gather x8, waiting for transfers between devices: 583 us -> 173 us  [the longest x4 165 us: gather_line(): return lax.all_gather(rows_in, 'z', axis=0, tiled=True)]
    all_gather x10 -> x18, blocking collectives: 117 us -> 213 us  [the longest x4 63.6 us: gather_line(): return lax.all_gather(rows_in, 'z', axis=0, tiled=True)]
    ppermute x0 -> x7, waiting for transfers between devices: none -> 52.8 us  [swap_grid(): return lax.ppermute(values, ('z', 'y', 'c'), pairs)]
    ppermute x0 -> x7, starting transfers between devices: none -> 27.7 us  [swap_grid(): return lax.ppermute(values, ('z', 'y', 'c'), pairs)]
    psum x9, blocking collectives: 73.4 us -> 99.2 us  [the longest x4 44.1 us: line_norm(): total = lax.psum(jnp.sum(values * values, axis=1), 'z')]
    dot_general x26, matrix products: 87.8 us -> 65.6 us  [the longest x8 27.3 us: pair_grad(): lax.dot_general(left, right, (((0,), (0,)), ((), ())), preferred_element_...]
    unnamed x28 -> x38, waiting for transfers between devices: 125 us -> 123 us
  transfers between devices with their start and end apart: 26 -> 41, of which waited for: 25 -> 35; matrix products, arithmetic and copies ran while one was open for 5% -> 7% of each run, Pallas kernels for 0% -> 0%
where the time goes in v1:
time: 1300 us; the launch traced here: 1290 us
  waiting for transfers between devices  754 us (58%)
  blocking collectives  313 us (24%)
  matrix products  91.1 us (7%)
  other arithmetic  46.5 us (4%)
  local copies, waits for them, and re-layouts  37.9 us (3%)
  starting transfers between devices  29.5 us (2%)
  between operations  17.6 us (1%)
    reduce_scatter x6, waiting for transfers between devices, sum_line(): lax.psum_scatter(partials.astype(jnp.bfloat16), 'z', scatter_dimension=0,...  180 us
    all_gather x4, waiting for transfers between devices, gather_line(): return lax.all_gather(rows_in, 'z', axis=0, tiled=True)  165 us
    unnamed x38, waiting for transfers between devices  123 us
    reduce_scatter x8, waiting for transfers between devices, pair_grad(): lax.psum_scatter(lax.dot_general(left, right, (((0,), (0,)), ((), ())), p...  118 us
    reduce_scatter x8, waiting for transfers between devices, sum_grid(): lax.psum_scatter(partials.astype(jnp.bfloat16), GRID, scatter_dimension=0...  108 us
    all_gather x4, blocking collectives, gather_line(): return lax.all_gather(rows_in, 'z', axis=0, tiled=True)  63.6 us
    all_gather x8, blocking collectives, gather_grid(): return lax.all_gather(rows_in, GRID, axis=0, tiled=True)  57.2 us
    all_gather x2, blocking collectives, stationary(): lax.all_gather(jnp.concatenate([keys, values], axis=1), ('z', 'x'), axis=...  53.8 us
  transfers between devices with their start and end apart: 41, of which 35 were waited for; matrix products, arithmetic and copies ran while one was open for 7% of the time, Pallas kernels for 0%

profile of v1, /device:TPU:4, one launch (start us, length us, event | category | flops | bytes accessed | tf_op | source)
XLA Modules:
  0.0 1289.5 jit_solution(12548844694438112647)
XLA Ops:
  16.8 10.7 all-gather
  29.3 8.4 psum.63
  37.8 7.6 all_gather.78
  48.0 9.2 all-gather.1
  57.3 10.7 reduce-scatter.79.cloned.1.call-done
  70.0 26.7 %all_gather.80 = bf16[1024,128]{0,1:T(8,128)(2,1)S(1)} all-gather(bf16[128,128]{0,1:T(8,128)(2,1)S(1)} %pad_maximum_fusion.14), channel_id=1, replica_groups=mesh['z'=4,'x'=2,'y'=2,'c'=2] {'z','x'}, dimensions={0}, use_global_device_ids=true | all-gather | bytes 294912 | tf_op jit(solution)/shard_map/all_gather | solution.py:353
  99.5 13.8 %all_gather.81 = bf16[512,512]{0,1:T(8,128)(2,1)S(1)} all-gather(bf16[128,512]{0,1:T(8,128)(2,1)S(1)} %bitcast.204), channel_id=1, replica_groups=mesh['z'=4,'x'=2,'y'=2,'c'=2] {'z'}, dimensions={0}, use_global_device_ids=true | all-gather | bytes 655360 | tf_op jit(solution)/shard_map/all_gather | solution.py:281
  127.6 5.2 reduce-scatter.35.cloned.1.call-done
  133.8 11.9 psum.64
  146.8 7.2 all_gather.83
  153.9 5.2 all-gather.15.cloned.1.call-done
  166.9 53.8 %reduce-scatter.37.cloned.1.call-done = bf16[128,2816]{1,0:T(8,128)(2,1)} async-done(((bf16[512,2816]{1,0:T(8,128)(2,1)}), bf16[128,2816]{1,0:T(8,128)(2,1)}) %reduce-scatter.37.cloned.1.call-update) | async-done | bytes 720912 | tf_op jit(solution)/shard_map/reduce_scatter | solution.py:285
  224.1 34.3 %all-gather.17.cloned.1.call-done = bf16[512,1408]{1,0:T(8,128)(2,1)} async-done(((bf16[128,1408]{1,0:T(8,128)(2,1)}), bf16[512,1408]{1,0:T(8,128)(2,1)}) %all-gather.17.cloned.1.call-update) | async-done | bytes 1441808 | tf_op jit(solution)/shard_map/all_gather | solution.py:281
  262.1 9.4 all-gather.3
  271.5 10.2 reduce-scatter.39.cloned.1.call-done
  282.8 11.9 psum.65
  295.4 7.2 all_gather.87
  305.3 9.3 all-gather.4
  314.6 11.5 reduce-scatter.81.cloned.1.call-done
  328.8 27.2 %all_gather.89 = bf16[1024,128]{0,1:T(8,128)(2,1)S(1)} all-gather(bf16[128,128]{0,1:T(8,128)(2,1)S(1)} %pad_maximum_fusion.15), channel_id=1, replica_groups=mesh['z'=4,'x'=2,'y'=2,'c'=2] {'z','x'}, dimensions={0}, use_global_device_ids=true | all-gather | bytes 294912 | tf_op jit(solution)/shard_map/all_gather | solution.py:353
  358.8 13.8 %all_gather.90 = bf16[512,512]{0,1:T(8,128)(2,1)S(1)} all-gather(bf16[128,512]{0,1:T(8,128)(2,1)S(1)} %bitcast.205), channel_id=1, replica_groups=mesh['z'=4,'x'=2,'y'=2,'c'=2] {'z'}, dimensions={0}, use_global_device_ids=true | all-gather | bytes 655360 | tf_op jit(solution)/shard_map/all_gather | solution.py:281
  376.0 16.1 %reduce-scatter.41.cloned.1.call-done = bf16[128,512]{1,0:T(8,128)(2,1)} async-done(((bf16[512,512]{1,0:T(8,128)(2,1)}), bf16[128,512]{1,0:T(8,128)(2,1)}) %reduce-scatter.41.cloned.1.call-update) | async-done | bytes 131088 | tf_op jit(solution)/shard_map/reduce_scatter | solution.py:275
  393.1 11.9 psum.66
  406.1 7.1 all_gather.92
  426.5 30.8 %collective-permute-done.4 = f32[128,512]{1,0:T(8,128)S(1)} collective-permute-done((f32[128,512]{1,0:T(8,128)S(1)}, f32[128,512]{1,0:T(8,128)S(1)}, u32[]{:S(2)}, u32[]{:S(2)}) %collective-permute-start.4) | collective-permute-done | bytes 262176 | tf_op jit(solution)/shard_map/ppermute | solution.py:267
  457.4 6.5 all_gather.96
  467.6 13.5 %reduce-scatter.43.cloned.1.call-done = bf16[128,2816]{1,0:T(8,128)(2,1)} async-done(((bf16[512,2816]{1,0:T(8,128)(2,1)}), bf16[128,2816]{1,0:T(8,128)(2,1)}) %reduce-scatter.43.cloned.1.call-update) | async-done | bytes 720912 | tf_op jit(solution)/shard_map/reduce_scatter | solution.py:285
  482.3 38.2 %reduce-scatter.47.cloned.1.call-done = bf16[128,1408]{1,0:T(8,128)(2,1)} async-done(((bf16[512,1408]{1,0:T(8,128)(2,1)}), bf16[128,1408]{1,0:T(8,128)(2,1)}) %reduce-scatter.47.cloned.1.call-update) | async-done | bytes 360464 | tf_op jit(solution)/shard_map/reduce_scatter | solution.py:285
  523.7 57.8 %all-gather.23.cloned.1.call-done = bf16[512,2816]{1,0:T(8,128)(2,1)} async-done(((bf16[128,2816]{1,0:T(8,128)(2,1)}), bf16[512,2816]{1,0:T(8,128)(2,1)}) %all-gather.23.cloned.1.call-update) | async-done | bytes 2883600 | tf_op jit(solution)/shard_map/all_gather | solution.py:281
  581.4 5.2 convolution_convert_fusion.19
  586.7 19.3 %reduce-scatter.49.cloned.1.call-done = bf16[128,512]{1,0:T(8,128)(2,1)} async-done(((bf16[512,512]{1,0:T(8,128)(2,1)}), bf16[128,512]{1,0:T(8,128)(2,1)}) %reduce-scatter.49.cloned.1.call-update) | async-done | bytes 131088 | tf_op jit(solution)/shard_map/reduce_scatter | solution.py:275
  607.6 11.9 psum.67
  620.6 7.2 all_gather.98
  629.1 20.0 %reduce-scatter.51.cloned.1.call-done = bf16[128,512]{1,0:T(8,128)(2,1)} async-done(((bf16[512,512]{1,0:T(8,128)(2,1)}), bf16[128,512]{1,0:T(8,128)(2,1)}) %reduce-scatter.51.cloned.1.call-update) | async-done | bytes 131088 | tf_op jit(solution)/shard_map/reduce_scatter | solution.py:285
  662.4 57.3 %reduce-scatter.83.cloned.1.call-done = bf16[128,128]{1,0:T(8,128)(2,1)} async-done(((bf16[1024,128]{1,0:T(8,128)(2,1)}), bf16[128,128]{1,0:T(8,128)(2,1)}) %reduce-scatter.83.cloned.1.call-update) | async-done | bytes 32784
  721.4 20.2 %all_gather.99 = bf16[512,640]{0,1:T(8,128)(2,1)S(1)} all-gather(bf16[128,640]{0,1:T(8,128)(2,1)S(1)} %pad_maximum_fusion.4), channel_id=1, replica_groups=mesh['z'=4,'x'=2,'y'=2,'c'=2] {'z'}, dimensions={0}, use_global_device_ids=true | all-gather | bytes 819200 | tf_op jit(solution)/shard_map/all_gather | solution.py:281
  744.5 14.6 %all-gather.21.cloned.1.call-done = bf16[512,1408]{1,0:T(8,128)(2,1)} async-done(((bf16[128,1408]{1,0:T(8,128)(2,1)}), bf16[512,1408]{1,0:T(8,128)(2,1)}) %all-gather.21.cloned.1.call-update) | async-done | bytes 1441808 | tf_op jit(solution)/shard_map/all_gather | solution.py:281
  762.7 5.6 reduce-scatter.53.cloned.1.call-done
  770.0 11.9 psum.68
  781.9 11.0 reduce-scatter.45.cloned.1.call-done
  794.8 7.3 all_gather.100
  805.9 34.3 %reduce-scatter.55.cloned.1.call-done = bf16[128,1408]{1,0:T(8,128)(2,1)} async-done(((bf16[512,1408]{1,0:T(8,128)(2,1)}), bf16[128,1408]{1,0:T(8,128)(2,1)}) %reduce-scatter.55.cloned.1.call-update) | async-done | bytes 360464 | tf_op jit(solution)/shard_map/reduce_scatter | solution.py:285
  842.6 57.9 %all-gather.25.cloned.1.call-done = bf16[512,2816]{1,0:T(8,128)(2,1)} async-done(((bf16[128,2816]{1,0:T(8,128)(2,1)}), bf16[512,2816]{1,0:T(8,128)(2,1)}) %all-gather.25.cloned.1.call-update) | async-done | bytes 2883600 | tf_op jit(solution)/shard_map/all_gather | solution.py:281
  900.5 5.2 convolution_convert_fusion.16
  905.7 19.3 %reduce-scatter.57.cloned.1.call-done = bf16[128,512]{1,0:T(8,128)(2,1)} async-done(((bf16[512,512]{1,0:T(8,128)(2,1)}), bf16[128,512]{1,0:T(8,128)(2,1)}) %reduce-scatter.57.cloned.1.call-update) | async-done | bytes 131088 | tf_op jit(solution)/shard_map/reduce_scatter | solution.py:275
  926.7 11.9 psum.69
  939.6 7.2 all_gather.102
  948.1 19.9 %reduce-scatter.59.cloned.1.call-done = bf16[128,512]{1,0:T(8,128)(2,1)} async-done(((bf16[512,512]{1,0:T(8,128)(2,1)}), bf16[128,512]{1,0:T(8,128)(2,1)}) %reduce-scatter.59.cloned.1.call-update) | async-done | bytes 131088 | tf_op jit(solution)/shard_map/reduce_scatter | solution.py:285
  976.0 5.3 convolution_convert_fusion
  994.5 41.9 %reduce-scatter.85.cloned.1.call-done = bf16[128,128]{1,0:T(8,128)(2,1)} async-done(((bf16[1024,128]{1,0:T(8,128)(2,1)}), bf16[128,128]{1,0:T(8,128)(2,1)}) %reduce-scatter.85.cloned.1.call-update) | async-done | bytes 32784
  1037.5 15.8 %all_gather.103 = bf16[512,640]{0,1:T(8,128)(2,1)S(1)} all-gather(bf16[128,640]{0,1:T(8,128)(2,1)S(1)} %pad_maximum_fusion.5), channel_id=1, replica_groups=mesh['z'=4,'x'=2,'y'=2,'c'=2] {'z'}, dimensions={0}, use_global_device_ids=true | all-gather | bytes 819200 | tf_op jit(solution)/shard_map/all_gather | solution.py:281
  1070.6 11.0 collective-permute-done.3
  1084.8 21.0 %reduce-scatter.77.cloned.1.call-done = bf16[256,1408]{1,0:T(8,128)(2,1)} async-done(((bf16[512,1408]{1,0:T(8,128)(2,1)}), bf16[256,1408]{1,0:T(8,128)(2,1)}) %reduce-scatter.77.cloned.1.call-update) | async-done | bytes 720912 | tf_op jit(solution)/shard_map/reduce_scatter | solution.py:291
  1105.8 27.0 %reduce-scatter.75.cloned.1.call-done = bf16[256,1408]{1,0:T(8,128)(2,1)} async-done(((bf16[512,1408]{1,0:T(8,128)(2,1)}), bf16[256,1408]{1,0:T(8,128)(2,1)}) %reduce-scatter.75.cloned.1.call-update) | async-done | bytes 720912 | tf_op jit(solution)/shard_map/reduce_scatter | solution.py:291
  1135.9 13.6 %reduce-scatter.69.cloned.1.call-done = bf16[256,512]{1,0:T(8,128)(2,1)} async-done(((bf16[512,512]{1,0:T(8,128)(2,1)}), bf16[256,512]{1,0:T(8,128)(2,1)}) %reduce-scatter.69.cloned.1.call-update) | async-done | bytes 262160 | tf_op jit(solution)/shard_map/reduce_scatter | solution.py:291
  1149.6 16.9 %reduce-scatter.67.cloned.1.call-done = bf16[256,512]{1,0:T(8,128)(2,1)} async-done(((bf16[512,512]{1,0:T(8,128)(2,1)}), bf16[256,512]{1,0:T(8,128)(2,1)}) %reduce-scatter.67.cloned.1.call-update) | async-done | bytes 262160 | tf_op jit(solution)/shard_map/reduce_scatter | solution.py:291
  1168.5 20.8 %reduce-scatter.61.cloned.1.call-done = bf16[128,512]{1,0:T(8,128)(2,1)} async-done(((bf16[512,512]{1,0:T(8,128)(2,1)}), bf16[128,512]{1,0:T(8,128)(2,1)}) %reduce-scatter.61.cloned.1.call-update) | async-done | bytes 131088 | tf_op jit(solution)/shard_map/reduce_scatter | solution.py:275
  1190.5 11.2 psum.71
  1201.7 7.4 collective-permute-start.6
  1209.1 8.4 psum.70
  1221.9 5.8 reduce-scatter.63.cloned.1.call-done
  1231.2 5.5 collective-permute-done.5
  1236.7 34.1 %reduce-scatter.71.cloned.1.call-done = bf16[256,2816]{1,0:T(8,128)(2,1)} async-done(((bf16[512,2816]{1,0:T(8,128)(2,1)}), bf16[256,2816]{1,0:T(8,128)(2,1)}) %reduce-scatter.71.cloned.1.call-update) | async-done | bytes 1441808 | tf_op jit(solution)/shard_map/reduce_scatter | solution.py:291
  1274.0 6.2 maximum_convert_fusion
  (382 shorter events, 186.2 us)
Async XLA Ops:
  8.0 60.0 %reduce-scatter.79.cloned.1.call-start = ((), (), s32[]{:S(2)}) async-start(), calls=%async_computation.56 | async-start | bytes 819200
  8.0 19.5 %collective-permute-start.1 = (f32[2,512]{1,0:T(2,128)}, f32[2,512]{1,0:T(2,128)S(1)}, u32[]{:S(2)}, u32[]{:S(2)}) collective-permute-start(f32[2,512]{1,0:T(2,128)} %param.14), channel_id=1, source_target_pairs={{0,0},{1,8},{2,16},{3,24},{8,1},{9,9},{10,17},{11,25},{16,2},{17,1... | collective-permute-start | bytes 12296 | tf_op jit(solution)/shard_map/ppermute | solution.py:267
  12.5 16.7 %collective-permute-start = (f32[128,512]{1,0:T(8,128)}, f32[128,512]{1,0:T(8,128)S(1)}, u32[]{:S(2)}, u32[]{:S(2)}) collective-permute-start(f32[128,512]{1,0:T(8,128)} %param.8), channel_id=1, source_target_pairs={{0,0},{1,8},{2,16},{3,24},{8,1},{9,9},{10,17},{11,25},{16,2},{17,1... | collective-permute-start | bytes 786440 | tf_op jit(solution)/shard_map/ppermute | solution.py:267
  46.8 86.0 %reduce-scatter.35.cloned.1.call-start = ((), (), s32[]{:S(2)}) async-start(), calls=%async_computation.26 | async-start | bytes 655360 | tf_op jit(solution)/shard_map/reduce_scatter | solution.py:275
  57.2 56.1 %copy-start.9 = (bf16[1,512,512]{2,1,0:T(8,128)(2,1)}, bf16[1,512,512]{2,1,0:T(8,128)(2,1)S(1)}, u32[]{:S(2)}) copy-start(bf16[1,512,512]{2,1,0:T(8,128)(2,1)S(1)} %all-gather.1) | copy-start | bytes 1572868
  114.6 44.5 %all-gather.15.cloned.1.call-start = ((), (), s32[]{:S(2)}) async-start(), calls=%async_computation.27 | async-start | bytes 4325376 | tf_op jit(solution)/shard_map/all_gather | solution.py:334
  119.7 101.0 %reduce-scatter.37.cloned.1.call-start = ((), (), s32[]{:S(2)}) async-start(), calls=%async_computation.28 | async-start | bytes 3604480 | tf_op jit(solution)/shard_map/reduce_scatter | solution.py:285
  119.7 7.3 collective-permute-start.2
  164.2 59.9 %all-gather.27.cloned.1.call-start = ((), (), s32[]{:S(2)}) async-start(), calls=%async_computation.54 | async-start | bytes 2162688 | tf_op jit(solution)/shard_map/all_gather | solution.py:334
  166.8 91.6 %all-gather.17.cloned.1.call-start = ((), (), s32[]{:S(2)}) async-start(), calls=%async_computation.29 | async-start | bytes 1802240 | tf_op jit(solution)/shard_map/all_gather | solution.py:281
  224.0 57.8 %copy-start.13 = (bf16[128,512]{1,0:T(8,128)(2,1)S(1)}, bf16[128,512]{1,0:T(8,128)(2,1)}, u32[]{:S(2)}) copy-start(bf16[128,512]{1,0:T(8,128)(2,1)} %reduce-scatter.35.cloned.1.call-done) | copy-start | bytes 393220
  224.0 71.2 %copy-start.53 = (f32[1,512]{1,0:T(1,128)S(1)}, f32[1,512]{1,0:T(1,128)}, u32[]{:S(2)}) copy-start(f32[1,512]{1,0:T(1,128)} %get-tuple-element.84) | copy-start | bytes 6148
  224.0 57.7 %reduce-scatter.39.cloned.1.call-start = ((), (), s32[]{:S(2)}) async-start(), calls=%async_computation.30 | async-start | bytes 655360 | tf_op jit(solution)/shard_map/reduce_scatter | solution.py:275
  262.1 64.0 %reduce-scatter.81.cloned.1.call-start = ((), (), s32[]{:S(2)}) async-start(), calls=%async_computation.57 | async-start | bytes 819200
  302.5 53.5 %copy-start.43 = (pred[128,1024]{0,1:T(8,128)(4,1)S(1)}, pred[128,1024]{0,1:T(8,128)(4,1)}, u32[]{:S(2)}) copy-start(pred[128,1024]{0,1:T(8,128)(4,1)} %copy-done.42) | copy-start | bytes 393220
  305.2 86.9 %reduce-scatter.41.cloned.1.call-start = ((), (), s32[]{:S(2)}) async-start(), calls=%async_computation.31 | async-start | bytes 655360 | tf_op jit(solution)/shard_map/reduce_scatter | solution.py:275
  373.9 42.3 %all-gather.19.cloned.1.call-start = ((), (), s32[]{:S(2)}) async-start(), calls=%async_computation.32 | async-start | bytes 4325376 | tf_op jit(solution)/shard_map/all_gather | solution.py:334
  375.2 88.6 %all-gather.29.cloned.1.call-start = ((), (), s32[]{:S(2)}) async-start(), calls=%async_computation.55 | async-start | bytes 2162688 | tf_op jit(solution)/shard_map/all_gather | solution.py:334
  376.0 105.1 %reduce-scatter.43.cloned.1.call-start = ((), (), s32[]{:S(2)}) async-start(), calls=%async_computation.33 | async-start | bytes 3604480 | tf_op jit(solution)/shard_map/reduce_scatter | solution.py:285
  421.3 99.2 %reduce-scatter.47.cloned.1.call-start = ((), (), s32[]{:S(2)}) async-start(), calls=%async_computation.36 | async-start | bytes 1802240 | tf_op jit(solution)/shard_map/reduce_scatter | solution.py:285
  422.2 35.1 %collective-permute-start.4 = (f32[128,512]{1,0:T(8,128)S(1)}, f32[128,512]{1,0:T(8,128)S(1)}, u32[]{:S(2)}, u32[]{:S(2)}) collective-permute-start(f32[128,512]{1,0:T(8,128)S(1)} %copy-done.84), channel_id=1, source_target_pairs={{0,0},{1,8},{2,16},{3,24},{8,1},{9,9},{10,17},{11,25},{16,2},{17,1... | collective-permute-start | bytes 786440 | tf_op jit(solution)/shard_map/ppermute | solution.py:267
  457.3 162.2 %copy-start.16 = (f32[128,512]{1,0:T(8,128)}, f32[128,512]{1,0:T(8,128)S(1)}, u32[]{:S(2)}) copy-start(f32[128,512]{1,0:T(8,128)S(1)} %collective-permute-done.4) | copy-start | bytes 786436
  467.6 113.9 %all-gather.23.cloned.1.call-start = ((), (), s32[]{:S(2)}) async-start(), calls=%async_computation.37 | async-start | bytes 3604480 | tf_op jit(solution)/shard_map/all_gather | solution.py:281
  523.6 82.4 %copy-start.14 = (bf16[128,512]{1,0:T(8,128)(2,1)S(1)}, bf16[128,512]{1,0:T(8,128)(2,1)}, u32[]{:S(2)}) copy-start(bf16[128,512]{1,0:T(8,128)(2,1)} %reduce-scatter.41.cloned.1.call-done) | copy-start | bytes 393220
  523.6 82.4 %copy-start.49 = (f32[1,512]{1,0:T(1,128)S(1)}, f32[1,512]{1,0:T(1,128)}, u32[]{:S(2)}) copy-start(f32[1,512]{1,0:T(1,128)} %get-tuple-element.87) | copy-start | bytes 6148
  523.6 82.4 %copy-start.74 = (f32[128]{0:T(128)S(1)}, f32[128]{0:T(128)}, u32[]{:S(2)}) copy-start(f32[128]{0:T(128)} %copy-done.73) | copy-start | bytes 1540
  523.6 104.1 %copy-start.12 = (bf16[1,512,512]{2,1,0:T(8,128)(2,1)S(1)}, bf16[1,512,512]{2,1,0:T(8,128)(2,1)}, u32[]{:S(2)}) copy-start(bf16[1,512,512]{2,1,0:T(8,128)(2,1)} %all-gather.4) | copy-start | bytes 1572868
  523.6 82.4 %reduce-scatter.49.cloned.1.call-start = ((), (), s32[]{:S(2)}) async-start(), calls=%async_computation.38 | async-start | bytes 655360 | tf_op jit(solution)/shard_map/reduce_scatter | solution.py:275
  586.6 62.4 %reduce-scatter.51.cloned.1.call-start = ((), (), s32[]{:S(2)}) async-start(), calls=%async_computation.39 | async-start | bytes 655360 | tf_op jit(solution)/shard_map/reduce_scatter | solution.py:285
  629.0 90.7 %reduce-scatter.83.cloned.1.call-start = ((), (), s32[]{:S(2)}) async-start(), calls=%async_computation.58 | async-start | bytes 294912
  659.3 99.8 %all-gather.21.cloned.1.call-start = ((), (), s32[]{:S(2)}) async-start(), calls=%async_computation.34 | async-start | bytes 1802240 | tf_op jit(solution)/shard_map/all_gather | solution.py:281
  660.0 108.3 %reduce-scatter.53.cloned.1.call-start = ((), (), s32[]{:S(2)}) async-start(), calls=%async_computation.40 | async-start | bytes 655360 | tf_op jit(solution)/shard_map/reduce_scatter | solution.py:275
  744.5 48.5 %reduce-scatter.45.cloned.1.call-start = ((), (), s32[]{:S(2)}) async-start(), calls=%async_computation.35 | async-start | bytes 655360 | tf_op jit(solution)/shard_map/reduce_scatter | solution.py:275
  762.7 77.6 %reduce-scatter.55.cloned.1.call-start = ((), (), s32[]{:S(2)}) async-start(), calls=%async_computation.41 | async-start | bytes 1802240 | tf_op jit(solution)/shard_map/reduce_scatter | solution.py:285
  794.8 143.8 %copy-start.18 = (f32[128,512]{1,0:T(8,128)}, f32[128,512]{1,0:T(8,128)S(1)}, u32[]{:S(2)}) copy-start(f32[128,512]{1,0:T(8,128)S(1)} %get-tuple-element.49) | copy-start | bytes 786436
  805.8 94.6 %all-gather.25.cloned.1.call-start = ((), (), s32[]{:S(2)}) async-start(), calls=%async_computation.42 | async-start | bytes 3604480 | tf_op jit(solution)/shard_map/all_gather | solution.py:281
  842.5 82.5 %copy-start.46 = (f32[1,512]{1,0:T(1,128)S(1)}, f32[1,512]{1,0:T(1,128)}, u32[]{:S(2)}) copy-start(f32[1,512]{1,0:T(1,128)} %copy-done.45) | copy-start | bytes 6148
  842.5 82.5 %copy-start.71 = (f32[128]{0:T(128)S(1)}, f32[128]{0:T(128)}, u32[]{:S(2)}) copy-start(f32[128]{0:T(128)} %copy-done.70) | copy-start | bytes 1540
  842.5 104.3 %copy-start.10 = (bf16[1,512,512]{2,1,0:T(8,128)(2,1)S(1)}, bf16[1,512,512]{2,1,0:T(8,128)(2,1)}, u32[]{:S(2)}) copy-start(bf16[1,512,512]{2,1,0:T(8,128)(2,1)} %copy-done.9) | copy-start | bytes 1572868
  842.5 82.5 %reduce-scatter.57.cloned.1.call-start = ((), (), s32[]{:S(2)}) async-start(), calls=%async_computation.43 | async-start | bytes 655360 | tf_op jit(solution)/shard_map/reduce_scatter | solution.py:275
  905.7 62.4 %reduce-scatter.59.cloned.1.call-start = ((), (), s32[]{:S(2)}) async-start(), calls=%async_computation.44 | async-start | bytes 655360 | tf_op jit(solution)/shard_map/reduce_scatter | solution.py:285
  948.0 88.4 %reduce-scatter.85.cloned.1.call-start = ((), (), s32[]{:S(2)}) async-start(), calls=%async_computation.59 | async-start | bytes 294912
  975.9 105.6 %reduce-scatter.73.cloned.1.call-start = ((), (), s32[]{:S(2)}) async-start(), calls=%async_computation.51 | async-start | bytes 4325376 | tf_op jit(solution)/shard_map/reduce_scatter | solution.py:291
  981.3 124.5 %reduce-scatter.77.cloned.1.call-start = ((), (), s32[]{:S(2)}) async-start(), calls=%async_computation.53 | async-start | bytes 2162688 | tf_op jit(solution)/shard_map/reduce_scatter | solution.py:291
  985.0 147.7 %reduce-scatter.75.cloned.1.call-start = ((), (), s32[]{:S(2)}) async-start(), calls=%async_computation.52 | async-start | bytes 2162688 | tf_op jit(solution)/shard_map/reduce_scatter | solution.py:291
  988.9 160.6 %reduce-scatter.69.cloned.1.call-start = ((), (), s32[]{:S(2)}) async-start(), calls=%async_computation.49 | async-start | bytes 786432 | tf_op jit(solution)/shard_map/reduce_scatter | solution.py:291
  991.5 174.9 %reduce-scatter.67.cloned.1.call-start = ((), (), s32[]{:S(2)}) async-start(), calls=%async_computation.48 | async-start | bytes 786432 | tf_op jit(solution)/shard_map/reduce_scatter | solution.py:291
  993.9 195.4 %reduce-scatter.61.cloned.1.call-start = ((), (), s32[]{:S(2)}) async-start(), calls=%async_computation.45 | async-start | bytes 655360 | tf_op jit(solution)/shard_map/reduce_scatter | solution.py:275
  1056.7 165.2 %reduce-scatter.65.cloned.1.call-start = ((), (), s32[]{:S(2)}) async-start(), calls=%async_computation.47 | async-start | bytes 983040 | tf_op jit(solution)/shard_map/reduce_scatter | solution.py:291
  1059.6 168.0 %reduce-scatter.63.cloned.1.call-start = ((), (), s32[]{:S(2)}) async-start(), calls=%async_computation.46 | async-start | bytes 983040 | tf_op jit(solution)/shard_map/reduce_scatter | solution.py:291
  1062.4 208.4 %reduce-scatter.71.cloned.1.call-start = ((), (), s32[]{:S(2)}) async-start(), calls=%async_computation.50 | async-start | bytes 4325376 | tf_op jit(solution)/shard_map/reduce_scatter | solution.py:291
  1067.7 13.8 %collective-permute-start.3 = (f32[128,512]{1,0:T(8,128)S(1)}, f32[128,512]{1,0:T(8,128)S(1)}, u32[]{:S(2)}, u32[]{:S(2)}) collective-permute-start(f32[128,512]{1,0:T(8,128)S(1)} %copy-done.39), channel_id=1, source_target_pairs={{0,0},{1,8},{2,16},{3,24},{8,1},{9,9},{10,17},{11,25},{16,2},{17,1... | collective-permute-start | bytes 786440 | tf_op jit(solution)/shard_map/ppermute | solution.py:267
  1132.7 56.6 %copy-start.52 = (f32[1,512]{1,0:T(1,128)S(1)}, f32[1,512]{1,0:T(1,128)}, u32[]{:S(2)}) copy-start(f32[1,512]{1,0:T(1,128)} %copy-done.51) | copy-start | bytes 6148
  1132.7 56.6 %copy-start.77 = (f32[128]{0:T(128)S(1)}, f32[128]{0:T(128)}, u32[]{:S(2)}) copy-start(f32[128]{0:T(128)} %copy-done.76) | copy-start | bytes 1540
  1132.7 57.7 %copy-start.67 = (f32[512]{0:T(512)S(1)}, f32[512]{0:T(512)}, u32[]{:S(2)}) copy-start(f32[512]{0:T(512)} %get-tuple-element.42) | copy-start | bytes 6148
  1132.7 57.7 %copy-start.68 = (f32[512]{0:T(512)S(1)}, f32[512]{0:T(512)}, u32[]{:S(2)}) copy-start(f32[512]{0:T(512)} %get-tuple-element.46) | copy-start | bytes 6148
  1132.7 57.7 %copy-start.69 = (f32[512]{0:T(512)S(1)}, f32[512]{0:T(512)}, u32[]{:S(2)}) copy-start(f32[512]{0:T(512)} %get-tuple-element.40) | copy-start | bytes 6148
  1132.7 84.7 %copy-start.19 = (f32[128,512]{1,0:T(8,128)S(1)}, f32[128,512]{1,0:T(8,128)}, u32[]{:S(2)}) copy-start(f32[128,512]{1,0:T(8,128)} %copy-done.18) | copy-start | bytes 786436
  1132.7 84.7 %copy-start.22 = (bf16[128,512]{1,0:T(8,128)(2,1)S(1)}, bf16[128,512]{1,0:T(8,128)(2,1)}, u32[]{:S(2)}) copy-start(bf16[128,512]{1,0:T(8,128)(2,1)} %reduce-scatter.57.cloned.1.call-done) | copy-start | bytes 393220
  1132.8 84.7 %copy-start.47 = (f32[1,512]{1,0:T(1,128)S(1)}, f32[1,512]{1,0:T(1,128)}, u32[]{:S(2)}) copy-start(f32[1,512]{1,0:T(1,128)} %copy-done.45) | copy-start | bytes 6148
  1132.8 84.7 %copy-start.72 = (f32[128]{0:T(128)S(1)}, f32[128]{0:T(128)}, u32[]{:S(2)}) copy-start(f32[128]{0:T(128)} %copy-done.70) | copy-start | bytes 1540
  1132.8 84.7 %copy-start.81 = (f32[128]{0:T(128)S(1)}, f32[128]{0:T(128)}, u32[]{:S(2)}) copy-start(f32[128]{0:T(128)} %copy-done.80) | copy-start | bytes 1540
  1201.7 19.6 %collective-permute-start.6 = (f32[4,512]{1,0:T(4,128)S(1)}, f32[4,512]{1,0:T(4,128)S(1)}, u32[]{:S(2)}, u32[]{:S(2)}) collective-permute-start(f32[4,512]{1,0:T(4,128)S(1)} %psum.71), channel_id=1, source_target_pairs={{0,0},{1,8},{2,16},{3,24},{8,1},{9,9},{10,17},{11,25},{16,2},{17,1... | collective-permute-start | bytes 24584 | tf_op jit(solution)/shard_map/ppermute | solution.py:267
  1218.6 18.1 %collective-permute-start.5 = (f32[128,512]{1,0:T(8,128)S(1)}, f32[128,512]{1,0:T(8,128)S(1)}, u32[]{:S(2)}, u32[]{:S(2)}) collective-permute-start(f32[128,512]{1,0:T(8,128)S(1)} %fusion.79), channel_id=1, source_target_pairs={{0,0},{1,8},{2,16},{3,24},{8,1},{9,9},{10,17},{11,25},{16,2},{17,1... | collective-permute-start | bytes 786440 | tf_op jit(solution)/shard_map/ppermute | solution.py:267
  (63 other events, 1218.7 us)
Sparse Core Ops, SparseCore 0:
  46.9 21.0 reduce-scatter.78
  114.7 18.0 reduce-scatter.34
  164.4 56.3 reduce-scatter.36
  262.2 19.5 reduce-scatter.38
  374.0 18.0 reduce-scatter.40
  421.4 59.6 reduce-scatter.42
  483.4 37.0 reduce-scatter.46
  586.8 19.1 reduce-scatter.48
  744.5 23.7 reduce-scatter.52
  771.2 21.6 reduce-scatter.44
  842.6 57.8 all-gather.24
  905.8 19.1 reduce-scatter.56
Sparse Core Ops, SparseCore 1:
  119.8 39.3 all-gather.14
  166.9 25.5 all-gather.26
  224.1 34.3 all-gather.16
  305.3 20.7 reduce-scatter.80
  376.8 39.3 all-gather.18
  418.4 25.5 all-gather.28
  523.7 57.7 all-gather.22
  629.1 19.9 reduce-scatter.50
  659.4 60.3 reduce-scatter.82
  721.9 37.1 all-gather.20
  805.9 34.3 reduce-scatter.54
  948.1 19.8 reduce-scatter.58
  976.0 60.4 reduce-scatter.84
  1039.3 39.5 reduce-scatter.72
  1081.1 24.6 reduce-scatter.76
  1108.0 24.6 reduce-scatter.74
  1135.0 14.5 reduce-scatter.68
  1151.8 14.5 reduce-scatter.66
  1168.8 20.4 reduce-scatter.60
  1191.6 17.3 reduce-scatter.64
  1211.6 16.0 reduce-scatter.62
  1230.3 40.4 reduce-scatter.70

commit v2 on v1

--- a/solution.py
+++ b/solution.py
@@ -3,6 +3,8 @@
 import jax
 import jax.numpy as jnp
 from jax import lax
+from jax.experimental import pallas as pl
+from jax.experimental.pallas import tpu as pltpu
 from jax.sharding import Mesh
 from jax.sharding import PartitionSpec as P
 
@@ -316,6 +318,411 @@
     return jnp.einsum("tj,dj->td", left, piece, preferred_element_type=jnp.float32)
 
 
+MESH_ID = pl.DeviceIdType.MESH
+ROWS = 16
+SKEW = 2
+GROUP_CHUNKS = 4
+EXTRA = 128
+
+
+def spread(column):
+    high = column.astype(jnp.bfloat16)
+    low = (column - high.astype(jnp.float32)).astype(jnp.bfloat16)
+    lane = lax.broadcasted_iota(jnp.int32, (column.shape[0], EXTRA), 1)
+    wide = jnp.where(lane == 0, high.astype(jnp.float32), jnp.where(lane == 1, low.astype(jnp.float32), 0.0))
+    return wide.astype(jnp.bfloat16)
+
+
+def unspread(block):
+    return jnp.sum(block.astype(jnp.float32), axis=1, keepdims=True)
+
+
+def transposed_dot(left, right):
+    return lax.dot_general(left, right, (((1,), (1,)), ((), ())), preferred_element_type=jnp.float32)
+
+
+class Line:
+    def __init__(self, tok, depth):
+        self.z, self.x = lax.axis_index("z"), lax.axis_index("x")
+        self.y, self.c = lax.axis_index("y"), lax.axis_index("c")
+        self.tok, self.depth = tok, depth
+        self.half = 2 * tok
+        self.chunks = self.half // ROWS
+        self.own = pl.multiple_of((2 * self.y + self.c) * tok, tok)
+        self.peers = (
+            {"y": self.y, "c": 1 - self.c},
+            {"y": 1 - self.y, "c": self.c},
+            {"y": 1 - self.y, "c": 1 - self.c},
+        )
+
+    def greet(self):
+        barrier = pltpu.get_barrier_semaphore()
+        for peer in self.peers:
+            pl.semaphore_signal(barrier, 1, device_id=peer, device_id_type=MESH_ID)
+
+        @pl.when(self.z > 0)
+        def _():
+            pl.semaphore_signal(barrier, 1, device_id={"z": self.z - 1}, device_id_type=MESH_ID)
+
+        @pl.when(self.z < self.depth - 1)
+        def _():
+            pl.semaphore_signal(barrier, 1, device_id={"z": self.z + 1}, device_id_type=MESH_ID)
+
+        inner = jnp.where(self.z > 0, 1, 0) + jnp.where(self.z < self.depth - 1, 1, 0)
+        pl.semaphore_wait(barrier, 3 + inner)
+
+    def place(self, stream):
+        return self.z if stream == 0 else self.depth - 1 - self.z
+
+    def onward(self, stream):
+        return {"z": self.z + 1} if stream == 0 else {"z": self.z - 1}
+
+    def backward(self, stream):
+        return {"z": self.z - 1} if stream == 0 else {"z": self.z + 1}
+
+    def row_of(self, stream, chunk):
+        per = self.chunks // 2
+        far = chunk // per
+        y = self.y + far * (1 - 2 * self.y)
+        return pl.multiple_of((2 * y + stream) * self.tok + lax.rem(chunk, per) * ROWS, ROWS)
+
+
+def make_line(tok, depth, width_in, width_out, carry_in, carry_out, features):
+    chunks = 2 * tok // ROWS
+    groups = chunks // GROUP_CHUNKS
+    span = GROUP_CHUNKS * ROWS
+    half_groups = groups // 2
+
+    def run(line, taken, prepare, finish, second, close, product, carried, chain_out, chain_in, wide, own_part, rs_out, rs_in,
+            ag_s, ag_r, ch_s, ch_r, bc_s, bc_r, rs_s, rs_r):
+        line.greet()
+        gather = [
+            pltpu.make_async_remote_copy(
+                src_ref=taken.at[pl.ds(line.own, tok)],
+                dst_ref=taken.at[pl.ds(line.own, tok)],
+                send_sem=ag_s.at[at],
+                recv_sem=ag_r.at[at],
+                device_id=peer,
+                device_id_type=MESH_ID,
+            )
+            for at, peer in enumerate(line.peers)
+        ]
+        for copy in gather:
+            copy.start()
+        gather[0].wait_recv()
+        prepare(pl.multiple_of(line.y * 2 * tok, 2 * tok))
+
+        def chain_copy(stream, chunk):
+            return pltpu.make_async_remote_copy(
+                src_ref=chain_out.at[stream, chunk],
+                dst_ref=chain_in.at[stream, chunk],
+                send_sem=ch_s.at[stream, chunk],
+                recv_sem=ch_r.at[stream, chunk],
+                device_id=line.onward(stream),
+                device_id_type=MESH_ID,
+            )
+
+        def wide_copy(stream, chunk):
+            rows = pl.ds(line.row_of(stream, chunk), ROWS)
+            return pltpu.make_async_remote_copy(
+                src_ref=wide.at[rows],
+                dst_ref=wide.at[rows],
+                send_sem=bc_s.at[stream, chunk],
+                recv_sem=bc_r.at[stream, chunk],
+                device_id=line.backward(stream),
+                device_id_type=MESH_ID,
+            )
+
+        def sum_copy(stream, group):
+            far = group // half_groups
+            y = line.y + far * (1 - 2 * line.y)
+            other = stream + line.c - 2 * stream * line.c
+            slot = 2 * far + other - 1
+            part = lax.rem(group, half_groups)
+            return (slot >= 0, part, pltpu.make_async_remote_copy(
+                src_ref=rs_out.at[stream, group],
+                dst_ref=rs_in.at[jnp.maximum(slot, 0), pl.ds(pl.multiple_of(part * span, span), span)],
+                send_sem=rs_s.at[stream, group],
+                recv_sem=rs_r.at[jnp.maximum(slot, 0), part],
+                device_id={"y": y, "c": stream},
+                device_id_type=MESH_ID,
+            ))
+
+        def step(i, _):
+            @pl.when(i == SKEW)
+            def _():
+                gather[1].wait_recv()
+                gather[2].wait_recv()
+                prepare(pl.multiple_of((1 - line.y) * 2 * tok, 2 * tok))
+
+            for stream in (0, 1):
+                place = line.place(stream)
+                chunk = i - SKEW * place
+
+                @pl.when((chunk >= 0) & (chunk < chunks))
+                def _():
+                    row = line.row_of(stream, chunk)
+
+                    @pl.when(place > 0)
+                    def _():
+                        chain_copy(stream, chunk).wait_recv()
+
+                    @pl.when(place == 0)
+                    def _():
+                        chain_out[stream, chunk, :, :width_in] = product[pl.ds(row, ROWS), :].astype(jnp.bfloat16)
+                        if carry_in:
+                            chain_out[stream, chunk, :, width_in:] = spread(carried[pl.ds(row, ROWS), :1])
+
+                    @pl.when((place > 0) & (place < depth - 1))
+                    def _():
+                        chain_out[stream, chunk, :, :width_in] = (
+                            product[pl.ds(row, ROWS), :] + chain_in[stream, chunk, :, :width_in].astype(jnp.float32)
+                        ).astype(jnp.bfloat16)
+                        if carry_in:
+                            chain_out[stream, chunk, :, width_in:] = spread(
+                                carried[pl.ds(row, ROWS), :1] + unspread(chain_in[stream, chunk, :, width_in:])
+                            )
+
+                    @pl.when(place < depth - 1)
+                    def _():
+                        chain_copy(stream, chunk).start()
+
+                    @pl.when(place == depth - 1)
+                    def _():
+                        total = product[pl.ds(row, ROWS), :] + chain_in[stream, chunk, :, :width_in].astype(jnp.float32)
+                        extra = None
+                        if carry_in:
+                            extra = carried[pl.ds(row, ROWS), :1] + unspread(chain_in[stream, chunk, :, width_in:])
+                        finish(row, pl.multiple_of(chunk * ROWS, ROWS), total, extra)
+                        wide_copy(stream, chunk).start()
+
+                ready = i - SKEW * (2 * (depth - 1) - place)
+
+                @pl.when((ready >= 0) & (ready < chunks))
+                def _():
+                    @pl.when(place < depth - 1)
+                    def _():
+                        wide_copy(stream, ready).wait_recv()
+
+                        @pl.when(place > 0)
+                        def _():
+                            wide_copy(stream, ready).start()
+
+                    @pl.when(lax.rem(ready, GROUP_CHUNKS) == GROUP_CHUNKS - 1)
+                    def _():
+                        group = ready // GROUP_CHUNKS
+                        row = pl.multiple_of(line.row_of(stream, ready) - (span - ROWS), span)
+                        away, part, copy = sum_copy(stream, group)
+                        value = second(row, span)
+
+                        @pl.when(away)
+                        def _():
+                            rs_out[stream, group, :, :features] = value.astype(jnp.bfloat16)
+                            if carry_out:
+                                rs_out[stream, group, :, features:] = wide[pl.ds(row, span), width_out:]
+                            copy.start()
+
+                        @pl.when(jnp.logical_not(away))
+                        def _():
+                            own_part[pl.ds(pl.multiple_of(part * span, span), span), :] = value
+
+            return 0
+
+        lax.fori_loop(0, chunks + 2 * SKEW * (depth - 1), step, 0)
+
+        def drain(i, _):
+            for stream in (0, 1):
+                place = line.place(stream)
+
+                @pl.when(place < depth - 1)
+                def _():
+                    chain_copy(stream, i).wait_send()
+
+                @pl.when(place > 0)
+                def _():
+                    wide_copy(stream, i).wait_send()
+
+            return 0
+
+        def drain_sums(i, _):
+            for stream in (0, 1):
+                away, part, copy = sum_copy(stream, i)
+
+                @pl.when(away)
+                def _():
+                    copy.wait_send()
+            return 0
+
+        for slot in range(3):
+            for part in range(half_groups):
+                pltpu.make_async_remote_copy(
+                    src_ref=rs_out.at[0, 0],
+                    dst_ref=rs_in.at[slot, pl.ds(part * span, span)],
+                    send_sem=rs_s.at[0, 0],
+                    recv_sem=rs_r.at[slot, part],
+                    device_id=line.peers[slot],
+                    device_id_type=MESH_ID,
+                ).wait_recv()
+        close()
+        for copy in gather:
+            copy.wait_send()
+        lax.fori_loop(0, chunks, drain, 0)
+        lax.fori_loop(0, groups, drain_sums, 0)
+
+    wide_in = width_in + (EXTRA if carry_in else 0)
+    scratch = [
+        pltpu.VMEM((4 * tok, width_in), jnp.float32),
+        pltpu.VMEM((4 * tok, EXTRA), jnp.float32),
+        pltpu.VMEM((2, chunks, ROWS, wide_in), jnp.bfloat16),
+        pltpu.VMEM((2, chunks, ROWS, wide_in), jnp.bfloat16),
+        pltpu.VMEM((tok, features), jnp.float32),
+        pltpu.VMEM((2, groups, span, features + (EXTRA if carry_out else 0)), jnp.bfloat16),
+        pltpu.VMEM((3, tok, features + (EXTRA if carry_out else 0)), jnp.bfloat16),
+        pltpu.SemaphoreType.DMA((3,)),
+        pltpu.SemaphoreType.DMA((3,)),
+        pltpu.SemaphoreType.DMA((2, chunks)),
+        pltpu.SemaphoreType.DMA((2, chunks)),
+        pltpu.SemaphoreType.DMA((2, chunks)),
+        pltpu.SemaphoreType.DMA((2, chunks)),
+        pltpu.SemaphoreType.DMA((2, groups)),
+        pltpu.SemaphoreType.DMA((3, half_groups)),
+    ]
+    return run, scratch
+
+
+TILE = 256
+
+
+def ffn_forward(hidden, gain, weight_gu, weight_down, depth):
+    tok, features = hidden.shape
+    width = weight_down.shape[1]
+    run, scratch = make_line(tok, depth, 2 * width, width, True, False, features)
+
+    def kernel(h_ref, gain_ref, w1_ref, w2_ref, out_ref, taken, kept, wide, scaled, product, carried, chain_out, chain_in,
+               own_part, rs_out, rs_in, *sems):
+        line = Line(tok, depth)
+        taken[pl.ds(line.own, tok), :] = h_ref[...].astype(jnp.bfloat16)
+
+        def prepare(row):
+            rows = pl.ds(row, 2 * tok)
+            block = taken[rows, :].astype(jnp.float32)
+            carried[rows, :] = jnp.broadcast_to(jnp.sum(block * block, axis=1, keepdims=True), (2 * tok, EXTRA))
+            scaled[...] = (block * gain_ref[...]).astype(jnp.bfloat16)
+
+            def tile(j, _):
+                cols = pl.ds(pl.multiple_of(j * TILE, TILE), TILE)
+                product[rows, cols] = jnp.dot(scaled[...], w1_ref[:, cols], preferred_element_type=jnp.float32)
+                return 0
+
+            lax.fori_loop(0, 2 * width // TILE, tile, 0)
+
+        def finish(row, at, total, extra):
+            factor = lax.rsqrt(extra / D + EPS)
+            gate = total[:, :width] * factor
+            upper = total[:, width:] * factor
+            kept[pl.ds(at, ROWS), :width] = gate
+            kept[pl.ds(at, ROWS), width:] = upper
+            active = gate * jax.nn.sigmoid(gate) * upper
+            wide[pl.ds(row, ROWS), :width] = active.astype(jnp.bfloat16)
+            wide[pl.ds(row, ROWS), width:] = spread(factor)
+
+        def second(row, span):
+            return transposed_dot(wide[pl.ds(row, span), :width], w2_ref[...])
+
+        def close():
+            total = own_part[...]
+            for slot in range(3):
+                total = total + rs_in[slot].astype(jnp.float32)
+            out_ref[...] = h_ref[...] + total
+
+        run(line, taken, prepare, finish, second, close, product, carried, chain_out, chain_in, wide, own_part, rs_out, rs_in,
+            *sems)
+
+    shapes = (
+        jax.ShapeDtypeStruct((tok, features), jnp.float32),
+        jax.ShapeDtypeStruct((4 * tok, features), jnp.bfloat16),
+        jax.ShapeDtypeStruct((2 * tok, 2 * width), jnp.float32),
+        jax.ShapeDtypeStruct((4 * tok, width + EXTRA), jnp.bfloat16),
+    )
+    return pl.pallas_call(
+        kernel,
+        out_shape=shapes,
+        in_specs=[pl.BlockSpec(memory_space=pltpu.VMEM)] * 4,
+        out_specs=[pl.BlockSpec(memory_space=pltpu.VMEM)] * 4,
+        scratch_shapes=[pltpu.VMEM((2 * tok, features), jnp.bfloat16)] + scratch,
+        compiler_params=pltpu.CompilerParams(collective_id=1, has_side_effects=True, vmem_limit_bytes=60 << 20),
+        cost_estimate=pl.CostEstimate(flops=60_000_000_000, bytes_accessed=8_000_000, transcendentals=0),
+        name="ffn_forward",
+    )(hidden, gain.reshape(1, -1), weight_gu, weight_down)
+
+
+def ffn_backward(grad, hidden, gain, kept, wide_forward, weight_gu, weight_down, depth):
+    tok, features = hidden.shape
+    width = weight_down.shape[1]
+    run, scratch = make_line(tok, depth, width, 2 * width, False, True, features)
+
+    def kernel(dy_ref, h_ref, gain_ref, kept_ref, before_ref, w1_ref, w2_ref, out_ref, taken, wide, gain_out, product, carried,
+               chain_out, chain_in, own_part, rs_out, rs_in, *sems):
+        line = Line(tok, depth)
+        taken[pl.ds(line.own, tok), :] = dy_ref[...].astype(jnp.bfloat16)
+
+        def prepare(row):
+            rows = pl.ds(row, 2 * tok)
+
+            def tile(j, _):
+                cols = pl.ds(pl.multiple_of(j * 128, 128), 128)
+                product[rows, cols] = jnp.dot(taken[rows, :], w2_ref[:, cols], preferred_element_type=jnp.float32)
+                return 0
+
+            lax.fori_loop(0, width // 128, tile, 0)
+
+        def finish(row, at, total, extra):
+            gate = kept_ref[pl.ds(at, ROWS), :width]
+            upper = kept_ref[pl.ds(at, ROWS), width:]
+            sig = jax.nn.sigmoid(gate)
+            silu = gate * sig
+            grad_gate = total * upper * (sig + silu * (1.0 - sig))
+            grad_up = total * silu
+            wide[pl.ds(row, ROWS), :width] = grad_gate.astype(jnp.bfloat16)
+            wide[pl.ds(row, ROWS), width : 2 * width] = grad_up.astype(jnp.bfloat16)
+            inner = jnp.sum(grad_gate * gate + grad_up * upper, axis=1, keepdims=True)
+            wide[pl.ds(row, ROWS), 2 * width :] = spread(inner)
+
+        def second(row, span):
+            return transposed_dot(wide[pl.ds(row, span), : 2 * width], w1_ref[...])
+
+        def close():
+            total = own_part[...]
+            inner = unspread(wide[pl.ds(line.own, tok), 2 * width :])
+            for slot in range(3):
+                total = total + rs_in[slot, :, :features].astype(jnp.float32)
+                inner = inner + unspread(rs_in[slot, :, features:])
+            factor = unspread(before_ref[pl.ds(line.own, tok), width:])
+            normed = h_ref[...] * factor
+            gain_out[...] = jnp.broadcast_to(jnp.sum(total * normed, axis=0, keepdims=True), gain_out.shape)
+            out_ref[...] = dy_ref[...] + factor * (total * gain_ref[...] - normed * (inner / D))
+
+        run(line, taken, prepare, finish, second, close, product, carried, chain_out, chain_in, wide, own_part, rs_out, rs_in,
+            *sems)
+
+    shapes = (
+        jax.ShapeDtypeStruct((tok, features), jnp.float32),
+        jax.ShapeDtypeStruct((4 * tok, features), jnp.bfloat16),
+        jax.ShapeDtypeStruct((4 * tok, 2 * width + EXTRA), jnp.bfloat16),
+        jax.ShapeDtypeStruct((8, features), jnp.float32),
+    )
+    return pl.pallas_call(
+        kernel,
+        out_shape=shapes,
+        in_specs=[pl.BlockSpec(memory_space=pltpu.VMEM)] * 7,
+        out_specs=[pl.BlockSpec(memory_space=pltpu.VMEM)] * 4,
+        scratch_shapes=scratch,
+        compiler_params=pltpu.CompilerParams(collective_id=2, has_side_effects=True, vmem_limit_bytes=60 << 20),
+        cost_estimate=pl.CostEstimate(flops=60_000_000_000, bytes_accessed=8_000_000, transcendentals=0),
+        name="ffn_backward",
+    )(grad, hidden, gain.reshape(1, -1), kept, wide_forward, weight_gu, weight_down)
+
+
 def stationary(stream, grad_out, wqkv, wo, wgu, wd, gain_attn, gain_ffn):
     tok = stream.shape[0]
     layers = wqkv.shape[0]
@@ -368,34 +775,24 @@
         )
         mixed_full = gather_line(mixed)
         hidden_in = current + sum_grid(times_t(mixed_full, weight_out))
-        normed_f, factor_f, hnormed = line_norm(hidden_in, gain_f[index])
-        hfull = gather_grid(hnormed)
-        gate_up = sum_line(add_rows(hfull, weight_gu))
-        hidden_cols = gate_up.shape[1] // 2
-        gate = gate_up[:, :hidden_cols]
-        upper = gate_up[:, hidden_cols:]
-        active = gather_line((jax.nn.silu(gate) * upper).astype(jnp.bfloat16))
-        current = hidden_in + sum_grid(times_t(active, weight_down))
+        current, hfull, kept, active = ffn_forward(hidden_in, gain_f[index], weight_gu, weight_down, depth)
         saved.append(
             (weight_qkv, weight_out, weight_gu, weight_down, normed_a, factor_a, xfull, queries,
-             seq_keys, seq_values, log_total, mixed_full, normed_f, factor_f, hfull, gate, upper, active)
+             seq_keys, seq_values, log_total, mixed_full, hidden_in, hfull, kept, active)
         )
     list_qkv, list_out, list_gu, list_down, list_ga, list_gf = ([], [], [], [], [], [])
     for index in reversed(range(layers)):
         (weight_qkv, weight_out, weight_gu, weight_down, normed_a, factor_a, xfull, queries,
-         seq_keys, seq_values, log_total, mixed_full, normed_f, factor_f, hfull, gate, upper, active) = saved[index]
-        grad_full = gather_grid(grad_now.astype(jnp.bfloat16))
-        grad_active = sum_line(add_rows(grad_full, weight_down))
-        list_down.append(pair_grad(grad_full, active))
-        sig = jax.nn.sigmoid(gate)
-        grad_gate = grad_active * upper * sig * (1.0 + gate * (1.0 - sig))
-        grad_up = grad_active * gate * sig
-        grad_gu = gather_line(jnp.concatenate([grad_gate, grad_up], axis=1).astype(jnp.bfloat16))
-        grad_hn = sum_grid(times_t(grad_gu, weight_gu))
-        list_gu.append(pair_grad(hfull, grad_gu).reshape(count_rows, 2, -1))
-        grad_mid, gain_f_grad = line_norm_back(grad_hn, normed_f, factor_f, gain_f[index])
-        list_gf.append(gain_f_grad)
-        grad_hidden = grad_now + grad_mid
+         seq_keys, seq_values, log_total, mixed_full, hidden_in, hfull, kept, active) = saved[index]
+        width = weight_down.shape[1]
+        grad_hidden, grad_full, grad_gu, gain_f_grad = ffn_backward(
+            grad_now, hidden_in, gain_f[index], kept, active, weight_gu, weight_down, depth
+        )
+        list_down.append(pair_grad(grad_full, active[:, :width]))
+        factor_f = jnp.sum(active[:, width:].astype(jnp.float32), axis=1, keepdims=True)
+        hnormed = (hfull.astype(jnp.float32) * factor_f * gain_f[index]).astype(jnp.bfloat16)
+        list_gu.append(pair_grad(hnormed, grad_gu[:, : 2 * width]).reshape(count_rows, 2, -1))
+        list_gf.append(gain_f_grad[0])
         hidden_full = gather_grid(grad_hidden.astype(jnp.bfloat16))
         grad_mixed = sum_line(add_rows(hidden_full, weight_out)).astype(jnp.bfloat16)
         list_out.append(pair_grad(hidden_full, mixed_full))

time: 1300 us -> 1190 us (0.915)
  Pallas kernels: 0 us -> 323 us
  waiting for transfers between devices: 754 us -> 456 us
  blocking collectives: 313 us -> 237 us
  matrix products: 91.1 us -> 48.8 us
    pallas_call x0 -> x4, Pallas kernels: none -> 323 us  [the longest x2 163 us: ffn_forward(): pl.pallas_call(kernel, out_shape=shapes, in_specs=[pl.BlockSpec(memory_sp...]
    all_gather x4 -> x0, waiting for transfers between devices: 165 us -> none  [gather_line(): return lax.all_gather(rows_in, 'z', axis=0, tiled=True)]
    reduce_scatter x6 -> x2, waiting for transfers between devices: 180 us -> 42.5 us  [sum_line(): lax.psum_scatter(partials.astype(jnp.bfloat16), 'z', scatter_dimension=0,...]
    all_gather x4, waiting for transfers between devices: 8.23 us -> 96 us  [stationary(): whole = lambda shard: lax.all_gather(shard, 'x', axis=0, tiled=True)]
    reduce_scatter x8 -> x4, waiting for transfers between devices: 108 us -> 32.5 us  [sum_grid(): lax.psum_scatter(partials.astype(jnp.bfloat16), GRID, scatter_dimension=0...]
    ppermute x7, waiting for transfers between devices: 52.8 us -> 15.9 us  [swap_grid(): return lax.ppermute(values, ('z', 'y', 'c'), pairs)]
    all_gather x8 -> x4, blocking collectives: 57.2 us -> 27.1 us  [gather_grid(): return lax.all_gather(rows_in, GRID, axis=0, tiled=True)]
    psum x4 -> x2, blocking collectives: 44.1 us -> 18.1 us  [line_norm(): total = lax.psum(jnp.sum(values * values, axis=1), 'z')]
  transfers between devices with their start and end apart: 41 -> 29, of which waited for: 35 -> 20; matrix products, arithmetic and copies ran while one was open for 7% -> 5% of each run, Pallas kernels for 0% -> 7%
where the time goes in v2:
time: 1190 us; the launch traced here: 1180 us
  waiting for transfers between devices  456 us (38%)
  Pallas kernels  323 us (27%)
  blocking collectives  237 us (20%)
  matrix products  48.8 us (4%)
  local copies, waits for them, and re-layouts  39.2 us (3%)
  other arithmetic  34.3 us (3%)
  starting transfers between devices  25.1 us (2%)
  between operations  17.5 us (1%)
    pallas_call x2, Pallas kernels, ffn_forward(): pl.pallas_call(kernel, out_shape=shapes, in_specs=[pl.BlockSpec(memory_sp...  163 us
    pallas_call x2, Pallas kernels, ffn_backward(): pl.pallas_call(kernel, out_shape=shapes, in_specs=[pl.BlockSpec(memory_sp...  160 us
    unnamed x26, waiting for transfers between devices  137 us
    reduce_scatter x8, waiting for transfers between devices, pair_grad(): lax.psum_scatter(lax.dot_general(left, right, (((0,), (0,)), ((), ())), p...  131 us
    all_gather x4, waiting for transfers between devices, stationary(): whole = lambda shard: lax.all_gather(shard, 'x', axis=0, tiled=True)  96 us
    all_gather x4, blocking collectives, gather_line(): return lax.all_gather(rows_in, 'z', axis=0, tiled=True)  59.9 us
    all_gather x2, blocking collectives, stationary(): lax.all_gather(jnp.concatenate([keys, values], axis=1), ('z', 'x'), axis=...  53.5 us
    all_gather x4, blocking collectives, stationary(): whole = lambda shard: lax.all_gather(shard, 'x', axis=0, tiled=True)  46.8 us
  transfers between devices with their start and end apart: 29, of which 20 were waited for; matrix products, arithmetic and copies ran while one was open for 5% of the time, Pallas kernels for 7%

profile of v2, /device:TPU:4, one launch (start us, length us, event | category | flops | bytes accessed | tf_op | source)
XLA Modules:
  0.0 1180.0 jit_solution(6650552420671757354)
XLA Ops:
  8.1 4.6 collective-permute-start.1
  12.6 3.2 collective-permute-start
  17.0 10.7 all-gather
  29.4 8.4 psum.35
  37.9 7.6 all_gather.54
  47.2 9.2 all-gather.1
  56.5 11.7 reduce-scatter.55.cloned.1.call-done
  70.1 26.8 %all_gather.56 = bf16[1024,128]{0,1:T(8,128)(2,1)S(1)} all-gather(bf16[128,128]{0,1:T(8,128)(2,1)S(1)} %pad_maximum_fusion.12), channel_id=1, replica_groups=mesh['z'=4,'x'=2,'y'=2,'c'=2] {'z','x'}, dimensions={0}, use_global_device_ids=true | all-gather | bytes 294912 | tf_op jit(solution)/shard_map/all_gather | solution.py:760
  99.7 14.0 %all_gather.57 = bf16[512,512]{0,1:T(8,128)(2,1)S(1)} all-gather(bf16[128,512]{0,1:T(8,128)(2,1)S(1)} %bitcast.170), channel_id=1, replica_groups=mesh['z'=4,'x'=2,'y'=2,'c'=2] {'z'}, dimensions={0}, use_global_device_ids=true | all-gather | bytes 655360 | tf_op jit(solution)/shard_map/all_gather | solution.py:283
  117.1 3.7 fusion.106
  122.2 2.8 collective-permute-start.2
  125.0 17.6 %all-gather.3 = bf16[1,512,1,640]{3,1,2,0:T(8,128)(2,1)S(1)} all-gather(bf16[1,256,1,640]{3,1,2,0:T(8,128)(2,1)S(1)} %get-tuple-element.80), channel_id=5, replica_groups=mesh['z'=4,'x'=2,'y'=2,'c'=2] {'x'}, dimensions={1}, use_global_device_ids=true | all-gather | bytes 983040 | tf_op jit(solution)/shard_map/all_gather | solution.py:741
  144.8 3.7 all-gather.15.cloned.1.call-done
  148.5 42.5 %all-gather.11.cloned.1.call-done.w1_ref = bf16[512,2816]{1,0:T(8,128)(2,1)} async-done(((bf16[256,2816]{1,0:T(8,128)(2,1)}), bf16[512,2816]{1,0:T(8,128)(2,1)}) %all-gather.11.cloned.1.call-update) | async-done | bytes 2883600 | tf_op jit(solution)/shard_map/all_gather | solution.py:741
  191.0 81.5 %ffn_forward.2 = (f32[128,512]{1,0:T(8,128)}, bf16[512,512]{1,0:T(8,128)(2,1)}, f32[256,2816]{1,0:T(8,128)}, bf16[512,1536]{1,0:T(8,128)(2,1)}) custom-call(f32[128,512]{1,0:T(8,128)} %convert_add_fusion.1.h_ref, f32[1,512]{1,0:T(1,128)} %get-tuple-element.103.gain_ref, bf16[512,2816]{1,0:T(8,128)(2,1)} %all-gather.11.cloned.1.call-done.w1_ref, ...), custom_call_target="tpu_custom_call" | custom-call | flops 60000002048 | bytes 8000000 | tf_op jit(solution)/shard_map/ffn_forward/pallas_call | solution.py:647
  273.6 9.7 psum.36
  284.3 6.5 all_gather.61
  292.3 9.2 all-gather.4
  301.6 11.5 reduce-scatter.57.cloned.1.call-done
  314.4 26.8 %all_gather.63 = bf16[1024,128]{0,1:T(8,128)(2,1)S(1)} all-gather(bf16[128,128]{0,1:T(8,128)(2,1)S(1)} %pad_maximum_fusion.13), channel_id=1, replica_groups=mesh['z'=4,'x'=2,'y'=2,'c'=2] {'z','x'}, dimensions={0}, use_global_device_ids=true | all-gather | bytes 294912 | tf_op jit(solution)/shard_map/all_gather | solution.py:760
  344.8 14.0 %all_gather.64 = bf16[512,512]{0,1:T(8,128)(2,1)S(1)} all-gather(bf16[128,512]{0,1:T(8,128)(2,1)S(1)} %bitcast.171), channel_id=1, replica_groups=mesh['z'=4,'x'=2,'y'=2,'c'=2] {'z'}, dimensions={0}, use_global_device_ids=true | all-gather | bytes 655360 | tf_op jit(solution)/shard_map/all_gather | solution.py:283
  362.9 2.8 collective-permute-start.4
  365.8 13.5 %reduce-scatter.29.cloned.1.call-done = bf16[128,512]{1,0:T(8,128)(2,1)} async-done(((bf16[512,512]{1,0:T(8,128)(2,1)}), bf16[128,512]{1,0:T(8,128)(2,1)}) %reduce-scatter.29.cloned.1.call-update) | async-done | bytes 131088 | tf_op jit(solution)/shard_map/reduce_scatter | solution.py:277
  380.9 5.9 all-gather.17.cloned.1.call-done
  386.7 44.0 %all-gather.13.cloned.1.call-done.w1_ref = bf16[512,2816]{1,0:T(8,128)(2,1)} async-done(((bf16[256,2816]{1,0:T(8,128)(2,1)}), bf16[512,2816]{1,0:T(8,128)(2,1)}) %all-gather.13.cloned.1.call-update) | async-done | bytes 2883600 | tf_op jit(solution)/shard_map/all_gather | solution.py:741
  430.7 81.4 %ffn_forward.3 = (f32[128,512]{1,0:T(8,128)}, bf16[512,512]{1,0:T(8,128)(2,1)}, f32[256,2816]{1,0:T(8,128)}, bf16[512,1536]{1,0:T(8,128)(2,1)}) custom-call(f32[128,512]{1,0:T(8,128)} %convert_add_fusion.h_ref, f32[1,512]{1,0:T(1,128)} %get-tuple-element.102.gain_ref, bf16[512,2816]{1,0:T(8,128)(2,1)} %all-gather.13.cloned.1.call-done.w1_ref, ...), custom_call_target="tpu_custom_call" | custom-call | flops 60000002048 | bytes 8000000 | tf_op jit(solution)/shard_map/ffn_forward/pallas_call | solution.py:647
  512.9 79.9 %ffn_backward.2 = (f32[128,512]{1,0:T(8,128)}, bf16[512,512]{1,0:T(8,128)(2,1)}, bf16[512,2944]{1,0:T(8,128)(2,1)}, f32[8,512]{1,0:T(8,128)}) custom-call(f32[128,512]{1,0:T(8,128)} %copy-done.59, f32[128,512]{1,0:T(8,128)} %convert_add_fusion.h_ref, f32[1,512]{1,0:T(1,128)} %get-tuple-element.102.gain_ref, f32[256,2816]{1,0:T(8,128)} %get-tuple-element.26.kept_ref, ...), custom_call_target="tpu_custom_call" | custom-call | flops 60000002048 | bytes 8000000 | tf_op jit(solution)/shard_map/ffn_backward/pallas_call | solution.py:714
  593.8 6.5 all_gather.68
  602.4 21.0 %reduce-scatter.31.cloned.1.call-done = bf16[128,512]{1,0:T(8,128)(2,1)} async-done(((bf16[512,512]{1,0:T(8,128)(2,1)}), bf16[128,512]{1,0:T(8,128)(2,1)}) %reduce-scatter.31.cloned.1.call-update) | async-done | bytes 131088 | tf_op jit(solution)/shard_map/reduce_scatter | solution.py:287
  624.4 3.1 fusion.37
  632.6 59.1 %reduce-scatter.59.cloned.1.call-done = bf16[128,128]{1,0:T(8,128)(2,1)} async-done(((bf16[1024,128]{1,0:T(8,128)(2,1)}), bf16[128,128]{1,0:T(8,128)(2,1)}) %reduce-scatter.59.cloned.1.call-update) | async-done | bytes 32784
  692.8 15.9 %all_gather.69 = bf16[512,640]{0,1:T(8,128)(2,1)S(1)} all-gather(bf16[128,640]{0,1:T(8,128)(2,1)S(1)} %pad_maximum_fusion.2), channel_id=1, replica_groups=mesh['z'=4,'x'=2,'y'=2,'c'=2] {'z'}, dimensions={0}, use_global_device_ids=true | all-gather | bytes 819200 | tf_op jit(solution)/shard_map/all_gather | solution.py:283
  711.0 19.1 %reduce-scatter.33.cloned.1.call-done = bf16[128,512]{1,0:T(8,128)(2,1)} async-done(((bf16[512,512]{1,0:T(8,128)(2,1)}), bf16[128,512]{1,0:T(8,128)(2,1)}) %reduce-scatter.33.cloned.1.call-update) | async-done | bytes 131088 | tf_op jit(solution)/shard_map/reduce_scatter | solution.py:277
  731.8 11.9 %psum.37 = f32[128]{0:T(128)S(1)} all-reduce(f32[128]{0:T(128)S(1)} %get-tuple-element.75), channel_id=1, replica_groups=mesh['z'=4,'x'=2,'y'=2,'c'=2] {'z'}, use_global_device_ids=true, to_apply=%region_17.18 | all-reduce | flops 128 | bytes 1024 | tf_op jit(solution)/shard_map/psum | solution.py:312
  745.4 80.0 %ffn_backward.3 = (f32[128,512]{1,0:T(8,128)}, bf16[512,512]{1,0:T(8,128)(2,1)}, bf16[512,2944]{1,0:T(8,128)(2,1)}, f32[8,512]{1,0:T(8,128)}) custom-call(f32[128,512]{1,0:T(8,128)} %fusion.63.dy_ref, f32[128,512]{1,0:T(8,128)} %convert_add_fusion.1.h_ref, f32[1,512]{1,0:T(1,128)} %get-tuple-element.103.gain_ref, f32[256,2816]{1,0:T(8,128)} %get-tuple-element.29.kept_ref, ...), custom_call_target="tpu_custom_call" | custom-call | flops 60000002048 | bytes 8000000 | tf_op jit(solution)/shard_map/ffn_backward/pallas_call | solution.py:714
  826.4 6.5 all_gather.70
  835.0 21.6 %reduce-scatter.35.cloned.1.call-done = bf16[128,512]{1,0:T(8,128)(2,1)} async-done(((bf16[512,512]{1,0:T(8,128)(2,1)}), bf16[128,512]{1,0:T(8,128)(2,1)}) %reduce-scatter.35.cloned.1.call-update) | async-done | bytes 131088 | tf_op jit(solution)/shard_map/reduce_scatter | solution.py:287
  857.6 3.1 fusion.34
  866.2 2.3 convolution_convert_fusion.8
  868.6 2.3 convolution_convert_fusion.9
  872.4 54.2 %reduce-scatter.61.cloned.1.call-done = bf16[128,128]{1,0:T(8,128)(2,1)} async-done(((bf16[1024,128]{1,0:T(8,128)(2,1)}), bf16[128,128]{1,0:T(8,128)(2,1)}) %reduce-scatter.61.cloned.1.call-update) | async-done | bytes 32784
  928.4 16.0 %all_gather.71 = bf16[512,640]{0,1:T(8,128)(2,1)S(1)} all-gather(bf16[128,640]{0,1:T(8,128)(2,1)S(1)} %pad_maximum_fusion.3), channel_id=1, replica_groups=mesh['z'=4,'x'=2,'y'=2,'c'=2] {'z'}, dimensions={0}, use_global_device_ids=true | all-gather | bytes 819200 | tf_op jit(solution)/shard_map/all_gather | solution.py:283
  949.0 3.6 convolution_convert_fusion.2
  952.8 2.1 convolution_convert_fusion.3
  956.2 5.2 convolution_convert_fusion
  962.5 5.1 convolution_convert_fusion.1
  968.6 2.7 collective-permute-start.3
  972.0 10.1 collective-permute-done.3
  982.9 2.1 maximum_convert_fusion.3
  986.1 11.0 psum.39
  997.1 5.7 collective-permute-start.6
  1002.8 8.4 psum.38
  1012.2 2.1 collective-permute-start.5
  1015.0 5.9 reduce-scatter.39.cloned.1.call-done
  1022.1 2.4 copy.113
  1024.5 4.8 collective-permute-done.5
  1029.3 19.1 %reduce-scatter.53.cloned.1.call-done = bf16[256,1408]{1,0:T(8,128)(2,1)} async-done(((bf16[512,1408]{1,0:T(8,128)(2,1)}), bf16[256,1408]{1,0:T(8,128)(2,1)}) %reduce-scatter.53.cloned.1.call-update) | async-done | bytes 720912 | tf_op jit(solution)/shard_map/reduce_scatter | solution.py:293
  1048.3 26.8 %reduce-scatter.51.cloned.1.call-done = bf16[256,1408]{1,0:T(8,128)(2,1)} async-done(((bf16[512,1408]{1,0:T(8,128)(2,1)}), bf16[256,1408]{1,0:T(8,128)(2,1)}) %reduce-scatter.51.cloned.1.call-update) | async-done | bytes 720912 | tf_op jit(solution)/shard_map/reduce_scatter | solution.py:293
  1075.2 3.1 maximum_convert_fusion.1
  1078.3 40.1 %reduce-scatter.49.cloned.1.call-done = bf16[256,2816]{1,0:T(8,128)(2,1)} async-done(((bf16[512,2816]{1,0:T(8,128)(2,1)}), bf16[256,2816]{1,0:T(8,128)(2,1)}) %reduce-scatter.49.cloned.1.call-update) | async-done | bytes 1441808 | tf_op jit(solution)/shard_map/reduce_scatter | solution.py:293
  1118.4 3.2 stack_reshape.19
  1121.6 39.4 %reduce-scatter.47.cloned.1.call-done = bf16[256,2816]{1,0:T(8,128)(2,1)} async-done(((bf16[512,2816]{1,0:T(8,128)(2,1)}), bf16[256,2816]{1,0:T(8,128)(2,1)}) %reduce-scatter.47.cloned.1.call-update) | async-done | bytes 1441808 | tf_op jit(solution)/shard_map/reduce_scatter | solution.py:293
  1161.1 3.2 stack_reshape.18
  1164.3 6.2 maximum_convert_fusion
  (280 shorter events, 74.4 us)
Async XLA Ops:
  8.0 39.1 %copy-start.28 = (bf16[2,256,512]{2,1,0:T(8,128)(2,1)S(1)}, bf16[2,256,512]{2,1,0:T(8,128)(2,1)}, u32[]{:S(2)}) copy-start(bf16[2,256,512]{2,1,0:T(8,128)(2,1)} %param.11) | copy-start | bytes 1572868
  8.0 60.2 %reduce-scatter.55.cloned.1.call-start = ((), (), s32[]{:S(2)}) async-start(), calls=%async_computation.36 | async-start | bytes 819200
  8.1 19.7 %collective-permute-start.1 = (f32[2,512]{1,0:T(2,128)}, f32[2,512]{1,0:T(2,128)S(1)}, u32[]{:S(2)}, u32[]{:S(2)}) collective-permute-start(f32[2,512]{1,0:T(2,128)} %param.14), channel_id=1, source_target_pairs={{0,0},{1,8},{2,16},{3,24},{8,1},{9,9},{10,17},{11,25},{16,2},{17,1... | collective-permute-start | bytes 12296 | tf_op jit(solution)/shard_map/ppermute | solution.py:269
  12.6 16.7 %collective-permute-start = (f32[128,512]{1,0:T(8,128)}, f32[128,512]{1,0:T(8,128)S(1)}, u32[]{:S(2)}, u32[]{:S(2)}) collective-permute-start(f32[128,512]{1,0:T(8,128)} %param.8), channel_id=1, source_target_pairs={{0,0},{1,8},{2,16},{3,24},{8,1},{9,9},{10,17},{11,25},{16,2},{17,1... | collective-permute-start | bytes 786440 | tf_op jit(solution)/shard_map/ppermute | solution.py:269
  27.7 19.3 %copy-start.22 = (bf16[1,512,1,640]{3,1,2,0:T(8,128)(2,1)}, bf16[1,512,1,640]{3,1,2,0:T(8,128)(2,1)S(1)}, u32[]{:S(2)}) copy-start(bf16[1,512,1,640]{3,1,2,0:T(8,128)(2,1)S(1)} %all-gather) | copy-start | bytes 1966084
  28.3 18.8 %copy-start.36 = (f32[1,512]{1,0:T(1,128)}, f32[1,512]{1,0:T(1,128)S(1)}, u32[]{:S(2)}) copy-start(f32[1,512]{1,0:T(1,128)S(1)} %get-tuple-element.105) | copy-start | bytes 6148
  29.3 113.9 %copy-start.4 = (f32[128,512]{1,0:T(8,128)}, f32[128,512]{1,0:T(8,128)S(1)}, u32[]{:S(2)}) copy-start(f32[128,512]{1,0:T(8,128)S(1)} %collective-permute-done) | copy-start | bytes 786436
  45.5 23.7 %copy-start.24 = (bf16[512,512]{1,0:T(8,128)(2,1)}, bf16[512,512]{1,0:T(8,128)(2,1)S(1)}, u32[]{:S(2)}) copy-start(bf16[512,512]{1,0:T(8,128)(2,1)S(1)} %all_gather.54) | copy-start | bytes 1572868
  46.9 96.2 %reduce-scatter.27.cloned.1.call-start = ((), (), s32[]{:S(2)}) async-start(), calls=%async_computation.18 | async-start | bytes 655360 | tf_op jit(solution)/shard_map/reduce_scatter | solution.py:277
  47.0 50.6 %copy-start.45 = (f32[128]{0:T(128)}, f32[128]{0:T(128)S(1)}, u32[]{:S(2)}) copy-start(f32[128]{0:T(128)S(1)} %fusion.105) | copy-start | bytes 1540
  47.1 50.6 %copy-start.48 = (f32[32]{0:T(128)}, f32[32]{0:T(128)S(1)}, u32[]{:S(2)}) copy-start(f32[32]{0:T(128)S(1)} %negate_power_fusion) | copy-start | bytes 388
  56.4 57.3 %copy-start.13 = (bf16[1,512,512]{2,1,0:T(8,128)(2,1)}, bf16[1,512,512]{2,1,0:T(8,128)(2,1)S(1)}, u32[]{:S(2)}) copy-start(bf16[1,512,512]{2,1,0:T(8,128)(2,1)S(1)} %all-gather.1) | copy-start | bytes 1572868
  56.5 41.2 %copy-start.35 = (pred[128,1024]{0,1:T(8,128)(4,1)}, pred[128,1024]{0,1:T(8,128)(4,1)S(1)}, u32[]{:S(2)}) copy-start(pred[128,1024]{0,1:T(8,128)(4,1)S(1)} %iota_compare_fusion) | copy-start | bytes 393220
  70.1 28.2 %copy-start.33 = (f32[128,32]{0,1:T(8,128)}, f32[128,32]{0,1:T(8,128)S(1)}, u32[]{:S(2)}) copy-start(f32[128,32]{0,1:T(8,128)S(1)} %get-tuple-element.107) | copy-start | bytes 49156
  99.7 16.1 %copy-start.15 = (bf16[2,256,1408]{2,1,0:T(8,128)(2,1)S(1)}, bf16[2,256,1408]{2,1,0:T(8,128)(2,1)}, u32[]{:S(2)}) copy-start(bf16[2,256,1408]{2,1,0:T(8,128)(2,1)} %param.13) | copy-start | bytes 4325380
  115.8 32.8 %all-gather.15.cloned.1.call-start = ((), (), s32[]{:S(2)}) async-start(), calls=%async_computation.34 | async-start | bytes 2162688 | tf_op jit(solution)/shard_map/all_gather | solution.py:741
  117.1 74.0 %all-gather.11.cloned.1.call-start = ((), (), s32[]{:S(2)}) async-start(), calls=%async_computation.19 | async-start | bytes 4325376 | tf_op jit(solution)/shard_map/all_gather | solution.py:741
  122.1 190.9 %reduce-scatter.57.cloned.1.call-start = ((), (), s32[]{:S(2)}) async-start(), calls=%async_computation.37 | async-start | bytes 819200
  122.2 20.4 %collective-permute-start.2 = (f32[2,512]{1,0:T(2,128)S(1)}, f32[2,512]{1,0:T(2,128)S(1)}, u32[]{:S(2)}, u32[]{:S(2)}) collective-permute-start(f32[2,512]{1,0:T(2,128)S(1)} %copy-done.60), channel_id=1, source_target_pairs={{0,0},{1,8},{2,16},{3,24},{8,1},{9,9},{10,17},{11,25},{16,2},{17,1... | collective-permute-start | bytes 12296 | tf_op jit(solution)/shard_map/ppermute | solution.py:269
  191.0 92.3 %copy-start.38 = (f32[1,512]{1,0:T(1,128)S(1)}, f32[1,512]{1,0:T(1,128)}, u32[]{:S(2)}) copy-start(f32[1,512]{1,0:T(1,128)} %get-tuple-element.104) | copy-start | bytes 6148
  273.6 40.6 %copy-start.34 = (f32[128,32]{0,1:T(8,128)S(1)}, f32[128,32]{0,1:T(8,128)}, u32[]{:S(2)}) copy-start(f32[128,32]{0,1:T(8,128)} %copy-done.33) | copy-start | bytes 49156
  283.3 29.8 %copy-start.54 = (f32[128]{0:T(128)}, f32[128]{0:T(128)S(1)}, u32[]{:S(2)}) copy-start(f32[128]{0:T(128)S(1)} %add_rsqrt_fusion) | copy-start | bytes 1540
  284.3 29.9 %copy-start.46 = (f32[128]{0:T(128)S(1)}, f32[128]{0:T(128)}, u32[]{:S(2)}) copy-start(f32[128]{0:T(128)} %copy-done.45) | copy-start | bytes 1540
  284.3 29.9 %copy-start.49 = (f32[32]{0:T(128)S(1)}, f32[32]{0:T(128)}, u32[]{:S(2)}) copy-start(f32[32]{0:T(128)} %copy-done.48) | copy-start | bytes 388
  292.3 86.9 %reduce-scatter.29.cloned.1.call-start = ((), (), s32[]{:S(2)}) async-start(), calls=%async_computation.20 | async-start | bytes 655360 | tf_op jit(solution)/shard_map/reduce_scatter | solution.py:277
  360.9 18.3 %copy-start.6 = (f32[128,512]{1,0:T(8,128)S(1)}, f32[128,512]{1,0:T(8,128)}, u32[]{:S(2)}) copy-start(f32[128,512]{1,0:T(8,128)} %get-tuple-element.24) | copy-start | bytes 786436
  361.0 25.8 %all-gather.17.cloned.1.call-start = ((), (), s32[]{:S(2)}) async-start(), calls=%async_computation.35 | async-start | bytes 2162688 | tf_op jit(solution)/shard_map/all_gather | solution.py:741
  361.5 69.2 %all-gather.13.cloned.1.call-start = ((), (), s32[]{:S(2)}) async-start(), calls=%async_computation.21 | async-start | bytes 4325376 | tf_op jit(solution)/shard_map/all_gather | solution.py:741
  362.9 260.5 %reduce-scatter.31.cloned.1.call-start = ((), (), s32[]{:S(2)}) async-start(), calls=%async_computation.22 | async-start | bytes 655360 | tf_op jit(solution)/shard_map/reduce_scatter | solution.py:287
  362.9 149.3 %collective-permute-start.4 = (f32[128,512]{1,0:T(8,128)}, f32[128,512]{1,0:T(8,128)S(1)}, u32[]{:S(2)}, u32[]{:S(2)}) collective-permute-start(f32[128,512]{1,0:T(8,128)} %param.9), channel_id=1, source_target_pairs={{0,0},{1,8},{2,16},{3,24},{8,1},{9,9},{10,17},{11,25},{16,2},{17,1... | collective-permute-start | bytes 786440 | tf_op jit(solution)/shard_map/ppermute | solution.py:269
  602.3 89.4 %reduce-scatter.59.cloned.1.call-start = ((), (), s32[]{:S(2)}) async-start(), calls=%async_computation.38 | async-start | bytes 294912
  631.2 61.4 %copy-start.47 = (f32[128]{0:T(128)S(1)}, f32[128]{0:T(128)}, u32[]{:S(2)}) copy-start(f32[128]{0:T(128)} %copy-done.45) | copy-start | bytes 1540
  631.2 61.4 %copy-start.50 = (f32[32]{0:T(128)S(1)}, f32[32]{0:T(128)}, u32[]{:S(2)}) copy-start(f32[32]{0:T(128)} %copy-done.48) | copy-start | bytes 388
  631.2 98.8 %reduce-scatter.33.cloned.1.call-start = ((), (), s32[]{:S(2)}) async-start(), calls=%async_computation.23 | async-start | bytes 655360 | tf_op jit(solution)/shard_map/reduce_scatter | solution.py:277
  631.8 98.3 %copy-start.39 = (f32[1,512]{1,0:T(1,128)S(1)}, f32[1,512]{1,0:T(1,128)}, u32[]{:S(2)}) copy-start(f32[1,512]{1,0:T(1,128)} %get-tuple-element.104) | copy-start | bytes 6148
  631.8 98.3 %copy-start.55 = (f32[128]{0:T(128)S(1)}, f32[128]{0:T(128)}, u32[]{:S(2)}) copy-start(f32[128]{0:T(128)} %copy-done.54) | copy-start | bytes 1540
  631.8 111.9 %copy-start.19 = (f32[128,512]{1,0:T(8,128)S(1)}, f32[128,512]{1,0:T(8,128)}, u32[]{:S(2)}) copy-start(f32[128,512]{1,0:T(8,128)} %get-tuple-element.28) | copy-start | bytes 786436
  711.0 145.7 %reduce-scatter.35.cloned.1.call-start = ((), (), s32[]{:S(2)}) async-start(), calls=%async_computation.24 | async-start | bytes 655360 | tf_op jit(solution)/shard_map/reduce_scatter | solution.py:287
  745.4 88.3 %copy-start.14 = (bf16[1,512,512]{2,1,0:T(8,128)(2,1)S(1)}, bf16[1,512,512]{2,1,0:T(8,128)(2,1)}, u32[]{:S(2)}) copy-start(bf16[1,512,512]{2,1,0:T(8,128)(2,1)} %copy-done.13) | copy-start | bytes 1572868
  825.4 9.6 copy-start.41
  825.4 9.6 copy-start.43
  834.9 25.8 %copy-start.17 = (bf16[1024,128]{0,1:T(8,128)(2,1)S(1)}, bf16[1024,128]{0,1:T(8,128)(2,1)}, u32[]{:S(2)}) copy-start(bf16[1024,128]{0,1:T(8,128)(2,1)} %copy-done.16) | copy-start | bytes 786436
  835.0 91.6 %reduce-scatter.61.cloned.1.call-start = ((), (), s32[]{:S(2)}) async-start(), calls=%async_computation.39 | async-start | bytes 294912
  866.2 116.7 %reduce-scatter.45.cloned.1.call-start = ((), (), s32[]{:S(2)}) async-start(), calls=%async_computation.29 | async-start | bytes 786432 | tf_op jit(solution)/shard_map/reduce_scatter | solution.py:293
  868.6 114.3 %reduce-scatter.43.cloned.1.call-start = ((), (), s32[]{:S(2)}) async-start(), calls=%async_computation.28 | async-start | bytes 786432 | tf_op jit(solution)/shard_map/reduce_scatter | solution.py:293
  871.0 73.4 %copy-start.23 = (bf16[1,512,1,640]{3,1,2,0:T(8,128)(2,1)S(1)}, bf16[1,512,1,640]{3,1,2,0:T(8,128)(2,1)}, u32[]{:S(2)}) copy-start(bf16[1,512,1,640]{3,1,2,0:T(8,128)(2,1)} %copy-done.22) | copy-start | bytes 1966084
  871.0 113.9 %reduce-scatter.37.cloned.1.call-start = ((), (), s32[]{:S(2)}) async-start(), calls=%async_computation.25 | async-start | bytes 655360 | tf_op jit(solution)/shard_map/reduce_scatter | solution.py:277
  871.6 74.4 %copy-start.21 = (bf16[512,640]{0,1:T(8,128)(2,1)S(1)}, bf16[512,640]{0,1:T(8,128)(2,1)}, u32[]{:S(2)}) copy-start(bf16[512,640]{0,1:T(8,128)(2,1)} %copy-done.20) | copy-start | bytes 1966084
  871.6 74.4 %copy-start.27 = (bf16[512,512]{1,0:T(8,128)(2,1)S(1)}, bf16[512,512]{1,0:T(8,128)(2,1)}, u32[]{:S(2)}) copy-start(bf16[512,512]{1,0:T(8,128)(2,1)} %copy-done.26) | copy-start | bytes 1572868
  928.4 19.1 %copy-start.25 = (bf16[512,512]{1,0:T(8,128)(2,1)S(1)}, bf16[512,512]{1,0:T(8,128)(2,1)}, u32[]{:S(2)}) copy-start(bf16[512,512]{1,0:T(8,128)(2,1)} %copy-done.24) | copy-start | bytes 1572868
  945.9 69.1 %reduce-scatter.41.cloned.1.call-start = ((), (), s32[]{:S(2)}) async-start(), calls=%async_computation.27 | async-start | bytes 983040 | tf_op jit(solution)/shard_map/reduce_scatter | solution.py:293
  947.4 73.5 %reduce-scatter.39.cloned.1.call-start = ((), (), s32[]{:S(2)}) async-start(), calls=%async_computation.26 | async-start | bytes 983040 | tf_op jit(solution)/shard_map/reduce_scatter | solution.py:293
  949.0 99.4 %reduce-scatter.53.cloned.1.call-start = ((), (), s32[]{:S(2)}) async-start(), calls=%async_computation.33 | async-start | bytes 2162688 | tf_op jit(solution)/shard_map/reduce_scatter | solution.py:293
  952.7 122.5 %reduce-scatter.51.cloned.1.call-start = ((), (), s32[]{:S(2)}) async-start(), calls=%async_computation.32 | async-start | bytes 2162688 | tf_op jit(solution)/shard_map/reduce_scatter | solution.py:293
  954.9 163.5 %reduce-scatter.49.cloned.1.call-start = ((), (), s32[]{:S(2)}) async-start(), calls=%async_computation.31 | async-start | bytes 4325376 | tf_op jit(solution)/shard_map/reduce_scatter | solution.py:293
  961.5 199.6 %reduce-scatter.47.cloned.1.call-start = ((), (), s32[]{:S(2)}) async-start(), calls=%async_computation.30 | async-start | bytes 4325376 | tf_op jit(solution)/shard_map/reduce_scatter | solution.py:293
  967.6 17.3 %copy-start.5 = (f32[128,512]{1,0:T(8,128)S(1)}, f32[128,512]{1,0:T(8,128)}, u32[]{:S(2)}) copy-start(f32[128,512]{1,0:T(8,128)} %copy-done.4) | copy-start | bytes 786436
  967.6 17.3 %copy-start.37 = (f32[1,512]{1,0:T(1,128)S(1)}, f32[1,512]{1,0:T(1,128)}, u32[]{:S(2)}) copy-start(f32[1,512]{1,0:T(1,128)} %copy-done.36) | copy-start | bytes 6148
  967.6 17.3 %copy-start.53 = (f32[128]{0:T(128)S(1)}, f32[128]{0:T(128)}, u32[]{:S(2)}) copy-start(f32[128]{0:T(128)} %copy-done.52) | copy-start | bytes 1540
  967.6 18.4 %copy-start.51 = (f32[512]{0:T(512)S(1)}, f32[512]{0:T(512)}, u32[]{:S(2)}) copy-start(f32[512]{0:T(512)} %get-tuple-element.74) | copy-start | bytes 6148
  967.7 43.5 %copy-start.18 = (f32[128,512]{1,0:T(8,128)S(1)}, f32[128,512]{1,0:T(8,128)}, u32[]{:S(2)}) copy-start(f32[128,512]{1,0:T(8,128)} %get-tuple-element.31) | copy-start | bytes 786436
  968.6 13.6 %collective-permute-start.3 = (f32[128,512]{1,0:T(8,128)S(1)}, f32[128,512]{1,0:T(8,128)S(1)}, u32[]{:S(2)}, u32[]{:S(2)}) collective-permute-start(f32[128,512]{1,0:T(8,128)S(1)} %copy-done.58), channel_id=1, source_target_pairs={{0,0},{1,8},{2,16},{3,24},{8,1},{9,9},{10,17},{11,25},{16,2},{17,1... | collective-permute-start | bytes 786440 | tf_op jit(solution)/shard_map/ppermute | solution.py:269
  997.1 17.3 %collective-permute-start.6 = (f32[4,512]{1,0:T(4,128)S(1)}, f32[4,512]{1,0:T(4,128)S(1)}, u32[]{:S(2)}, u32[]{:S(2)}) collective-permute-start(f32[4,512]{1,0:T(4,128)S(1)} %psum.39), channel_id=1, source_target_pairs={{0,0},{1,8},{2,16},{3,24},{8,1},{9,9},{10,17},{11,25},{16,2},{17,1... | collective-permute-start | bytes 24584 | tf_op jit(solution)/shard_map/ppermute | solution.py:269
  1012.2 17.0 %collective-permute-start.5 = (f32[128,512]{1,0:T(8,128)S(1)}, f32[128,512]{1,0:T(8,128)S(1)}, u32[]{:S(2)}, u32[]{:S(2)}) collective-permute-start(f32[128,512]{1,0:T(8,128)S(1)} %fusion.60), channel_id=1, source_target_pairs={{0,0},{1,8},{2,16},{3,24},{8,1},{9,9},{10,17},{11,25},{16,2},{17,1... | collective-permute-start | bytes 786440 | tf_op jit(solution)/shard_map/ppermute | solution.py:269
  (30 other events, 66.5 us)
Sparse Core Ops, SparseCore 0:
  47.1 21.0 reduce-scatter.54
  115.9 18.0 reduce-scatter.26
  292.4 20.5 reduce-scatter.56
  361.1 18.0 reduce-scatter.28
  602.5 20.8 reduce-scatter.30
  631.4 60.3 reduce-scatter.58
  711.1 18.9 reduce-scatter.32
  835.1 21.4 reduce-scatter.34
  866.3 60.2 reduce-scatter.60
  928.7 13.6 reduce-scatter.44
  944.7 14.6 reduce-scatter.42
  961.7 22.4 reduce-scatter.36
  987.0 15.6 reduce-scatter.40
  1004.8 16.0 reduce-scatter.38
  1023.6 24.6 reduce-scatter.52
  1050.4 24.6 reduce-scatter.50
  1077.8 40.5 reduce-scatter.48
  1120.5 40.5 reduce-scatter.46
Sparse Core Ops, SparseCore 1:
  118.4 30.1 all-gather.14
  150.5 40.4 all-gather.10
  363.6 23.1 all-gather.16
  388.9 41.8 all-gather.12

commit v3 on v2

--- a/solution.py
+++ b/solution.py
@@ -260,33 +260,9 @@
     )
 
 
-GRID = ("y", "c")
-
-
 def swap_grid(values, depth):
-    width = lax.axis_size("c")
     pairs = [(z * depth + g, g * depth + z) for z in range(depth) for g in range(depth)]
     return lax.ppermute(values, ("z", "y", "c"), pairs)
-
-
-def gather_grid(rows_in):
-    return lax.all_gather(rows_in, GRID, axis=0, tiled=True)
-
-
-def sum_grid(partials):
-    return lax.psum_scatter(
-        partials.astype(jnp.bfloat16), GRID, scatter_dimension=0, tiled=True
-    ).astype(jnp.float32)
-
-
-def gather_line(rows_in):
-    return lax.all_gather(rows_in, "z", axis=0, tiled=True)
-
-
-def sum_line(partials):
-    return lax.psum_scatter(
-        partials.astype(jnp.bfloat16), "z", scatter_dimension=0, tiled=True
-    ).astype(jnp.float32)
 
 
 def pair_grad(left, right):
@@ -298,24 +274,6 @@
         scatter_dimension=0,
         tiled=True,
     ).astype(jnp.float32)
-
-
-def line_norm(values, gain):
-    total = lax.psum(jnp.sum(values * values, axis=1), "z")
-    factor = lax.rsqrt(total / D + EPS)
-    normed = values * factor[:, None]
-    return (normed, factor, (normed * gain).astype(jnp.bfloat16))
-
-
-def line_norm_back(grad_normed, normed, factor, gain):
-    scaled = grad_normed * gain
-    inner = lax.psum(jnp.sum(scaled * normed, axis=1), "z")
-    grad_in = factor[:, None] * (scaled - normed * (inner / D)[:, None])
-    return (grad_in, jnp.sum(grad_normed * normed, axis=0))
-
-
-def times_t(left, piece):
-    return jnp.einsum("tj,dj->td", left, piece, preferred_element_type=jnp.float32)
 
 
 MESH_ID = pl.DeviceIdType.MESH
@@ -723,21 +681,465 @@
     )(grad, hidden, gain.reshape(1, -1), kept, wide_forward, weight_gu, weight_down)
 
 
+def to_row(column):
+    return jnp.transpose(jnp.broadcast_to(column, (column.shape[0], EXTRA)))[:8]
+
+
+def to_column(row):
+    return jnp.transpose(jnp.broadcast_to(row[:1], (row.shape[1], row.shape[1])))[:, :1]
+
+
+def turn(values, cosine, sine):
+    lane = lax.broadcasted_iota(jnp.int32, values.shape, 1)
+    width = values.shape[1]
+    back = pltpu.roll(values, width - HEAD // 2, 1)
+    forth = pltpu.roll(values, HEAD // 2, 1)
+    partner = jnp.where(lax.rem(lane, HEAD) < HEAD // 2, back, forth)
+    return values * cosine + partner * sine
+
+
+def split_pair(block):
+    lane = lax.broadcasted_iota(jnp.int32, block.shape, 1)
+    zero = jnp.zeros_like(block)
+    return jnp.concatenate([jnp.where(lane < HEAD, block, zero), jnp.where(lane < HEAD, zero, block)], axis=0)
+
+
+def join_pair(turned, tok):
+    return jnp.transpose(jnp.concatenate([turned[:HEAD, :tok], turned[HEAD:, tok:]], axis=0))
+
+
+def twice(kv):
+    wide = kv.astype(jnp.float32)
+    lane = lax.broadcasted_iota(jnp.int32, wide.shape, 1)
+    other = pltpu.roll(wide, HEAD, 1)
+    return jnp.where(lane < HEAD, wide, other), jnp.where(lane < HEAD, other, wide)
+
+
+class Square:
+    def __init__(self, tok, depth):
+        self.z, self.x = lax.axis_index("z"), lax.axis_index("x")
+        self.y, self.c = lax.axis_index("y"), lax.axis_index("c")
+        self.tok, self.depth = tok, depth
+        self.g = 2 * self.y + self.c
+        self.row = 2 * self.z + self.x
+        self.own = pl.multiple_of(self.g * tok, tok)
+        self.mine = pl.multiple_of(self.z * tok, tok)
+        self.peers = (
+            {"y": self.y, "c": 1 - self.c},
+            {"y": 1 - self.y, "c": self.c},
+            {"y": 1 - self.y, "c": 1 - self.c},
+        )
+
+    def row_peer(self, step):
+        at = lax.rem(self.row + step, 2 * self.depth)
+        return {"z": at // 2, "x": lax.rem(at, 2)}
+
+    def greet(self):
+        barrier = pltpu.get_barrier_semaphore()
+        for peer in self.peers:
+            pl.semaphore_signal(barrier, 1, device_id=peer, device_id_type=MESH_ID)
+        for step in range(1, 2 * self.depth):
+            pl.semaphore_signal(barrier, 1, device_id=self.row_peer(step), device_id_type=MESH_ID)
+        pl.semaphore_wait(barrier, 3 + 2 * self.depth - 1)
+
+
+def remote(src, dst, send, recv, device):
+    return pltpu.make_async_remote_copy(
+        src_ref=src, dst_ref=dst, send_sem=send, recv_sem=recv, device_id=device, device_id_type=MESH_ID
+    )
+
+
+def start_gather(square, taken, send, recv):
+    copies = [
+        remote(taken.at[pl.ds(square.own, square.tok)], taken.at[pl.ds(square.own, square.tok)], send.at[at], recv.at[at], peer)
+        for at, peer in enumerate(square.peers)
+    ]
+    for copy in copies:
+        copy.start()
+    return copies
+
+
+def line_sum(square, gather, product, own, own_row, outs, ins, row_outs, row_ins, send, recv, row_send, row_recv):
+    tok, depth = square.tok, square.depth
+
+    def one(order):
+        block = lax.rem(2 * square.y + order, depth)
+        step = lax.rem(block - square.z + depth, depth)
+        slot = jnp.maximum(depth - 1 - step, 0)
+        value, column = product(pl.multiple_of(block * tok, tok))
+
+        @pl.when(step == 0)
+        def _():
+            own[...] = value
+            if column is not None:
+                own_row[...] = to_row(column)
+
+        copy = remote(outs.at[order], ins.at[slot], send.at[order], recv.at[slot], {"z": block})
+        row_copy = None
+        if column is not None:
+            row_copy = remote(row_outs.at[order], row_ins.at[slot], row_send.at[order], row_recv.at[slot], {"z": block})
+
+        @pl.when(step != 0)
+        def _():
+            outs[order] = value.astype(jnp.bfloat16)
+            copy.start()
+            if column is not None:
+                row_outs[order] = to_row(column)
+                row_copy.start()
+
+        return step, copy, row_copy
+
+    gather[0].wait_recv()
+    sent = [one(0), one(1)]
+    gather[1].wait_recv()
+    gather[2].wait_recv()
+    sent += [one(2), one(3)]
+    for slot in range(depth - 1):
+        remote(outs.at[0], ins.at[slot], send.at[0], recv.at[slot], {"z": square.z}).wait_recv()
+        if row_ins is not None:
+            remote(row_outs.at[0], row_ins.at[slot], row_send.at[0], row_recv.at[slot], {"z": square.z}).wait_recv()
+    return sent
+
+
+def line_gather(square, array, rows, send, recv, row_send, row_recv):
+    depth = square.depth
+    sent = []
+    for step in range(1, depth):
+        peer = {"z": lax.rem(square.z + step, depth)}
+        here = array.at[pl.ds(square.mine, square.tok)]
+        copy = remote(here, here, send.at[step - 1], recv.at[depth - 1 - step], peer)
+        line = rows.at[square.z]
+        row_copy = remote(line, line, row_send.at[step - 1], row_recv.at[depth - 1 - step], peer)
+        copy.start()
+        row_copy.start()
+        sent += [copy, row_copy]
+    return sent
+
+
+def grid_sum(square, array, rows, second, own, outs, ins, row_ins, arrive, row_arrive, send, recv, row_send, row_recv):
+    tok, depth = square.tok, square.depth
+    sent = []
+    for step in range(depth):
+        block = lax.rem(square.z + step, depth)
+        if step:
+            rows_of = pl.ds(pl.multiple_of(block * tok, tok), tok)
+            remote(array.at[rows_of], array.at[rows_of], send.at[0], arrive.at[step - 1], {"z": square.z}).wait_recv()
+            remote(rows.at[block], rows.at[block], send.at[0], row_arrive.at[step - 1], {"z": square.z}).wait_recv()
+        value = second(pl.multiple_of(block * tok, tok))
+        away = lax.rem(block - square.g + depth, depth)
+        slot = jnp.maximum(depth - 1 - away, 0)
+        device = {"y": block // 2, "c": lax.rem(block, 2)}
+        copy = remote(outs.at[step], ins.at[slot], send.at[step], recv.at[slot], device)
+        row_copy = None
+        if row_ins is not None:
+            row_copy = remote(rows.at[block], row_ins.at[slot], row_send.at[step], row_recv.at[slot], device)
+
+        @pl.when(away == 0)
+        def _():
+            own[...] = value
+
+        @pl.when(away != 0)
+        def _():
+            outs[step] = value.astype(jnp.bfloat16)
+            copy.start()
+            if row_ins is not None:
+                row_copy.start()
+
+        sent.append((away, copy, row_copy))
+    for slot in range(depth - 1):
+        remote(outs.at[0], ins.at[slot], send.at[0], recv.at[slot], square.peers[0]).wait_recv()
+        if row_ins is not None:
+            remote(rows.at[0], row_ins.at[slot], row_send.at[0], row_recv.at[slot], square.peers[0]).wait_recv()
+    return sent
+
+
+def drain(sent):
+    for away, copy, row_copy in sent:
+
+        @pl.when(away != 0)
+        def _():
+            copy.wait_send()
+            if row_copy is not None:
+                row_copy.wait_send()
+
+
+def sem(*shape):
+    return pltpu.SemaphoreType.DMA(shape)
+
+
+def attention_forward(hidden, gain, weight_qkv, weight_out, cosine, sine, depth):
+    tok, features = hidden.shape
+    cols = weight_qkv.shape[1]
+    query_cols = GROUP * HEAD
+    seq = 2 * depth * tok
+    pairs = query_cols // EXTRA
+    scale = 1.0 / math.sqrt(HEAD)
+
+    def kernel(h_ref, gain_ref, wqkv_ref, wo_ref, cos_ref, sin_ref, out_ref, taken, queries, kv, lse, mixed, factors,
+               own, own_row, z_out, z_in, zr_out, zr_in, values_t, g_own, g_out, g_in,
+               ag_s, ag_r, zs_s, zs_r, zr_s, zr_r, kv_s, kv_r, zg_s, zg_r, zgr_s, zgr_r, gs_s, gs_r):
+        square = Square(tok, depth)
+        taken[pl.ds(square.own, tok), :] = h_ref[...].astype(jnp.bfloat16)
+        square.greet()
+        gather = start_gather(square, taken, ag_s, ag_r)
+
+        def product(row):
+            block = taken[pl.ds(row, tok), :].astype(jnp.float32)
+            scaled = (block * gain_ref[...]).astype(jnp.bfloat16)
+            return (
+                jnp.dot(scaled, wqkv_ref[...], preferred_element_type=jnp.float32),
+                jnp.sum(block * block, axis=1, keepdims=True),
+            )
+
+        sent = line_sum(square, gather, product, own, own_row, z_out, z_in, zr_out, zr_in, zs_s, zs_r, zr_s, zr_r)
+        total, squares = own[...], own_row[...]
+        for slot in range(depth - 1):
+            total = total + z_in[slot].astype(jnp.float32)
+            squares = squares + zr_in[slot]
+        factor_row = lax.rsqrt(squares / D + EPS)
+        factors[square.z] = factor_row
+        turned = turn(total * to_column(factor_row), cos_ref[...], sin_ref[...])
+        here = pl.ds(pl.multiple_of(square.row * tok, tok), tok)
+        kv[here, :] = turned[:, query_cols:].astype(jnp.bfloat16)
+        queries[...] = turned[:, :query_cols].astype(jnp.bfloat16)
+        spreads = []
+        for step in range(1, 2 * depth):
+            copy = remote(kv.at[here], kv.at[here], kv_s.at[step - 1], kv_r.at[2 * depth - 1 - step], square.row_peer(step))
+            copy.start()
+            spreads.append(copy)
+        for copy in spreads:
+            copy.wait_recv()
+        keys, both = twice(kv[...])
+        values_t[...] = jnp.transpose(both).astype(jnp.bfloat16)
+        keys = keys.astype(jnp.bfloat16)
+
+        def pair(t, _):
+            lanes = pl.ds(pl.multiple_of(t * EXTRA, EXTRA), EXTRA)
+            scores = transposed_dot(keys, split_pair(queries[:, lanes])) * scale
+            key_at = lax.broadcasted_iota(jnp.int32, scores.shape, 0)
+            query_at = lax.rem(lax.broadcasted_iota(jnp.int32, scores.shape, 1), tok) + square.row * tok
+            scores = jnp.where(key_at <= query_at, scores, -1e30)
+            top = jnp.max(scores, axis=0, keepdims=True)
+            expo = jnp.exp(scores - top)
+            denom = jnp.sum(expo, axis=0, keepdims=True)
+            lse[t] = jnp.broadcast_to(top + jnp.log(denom), (8, 2 * tok))
+            probs = (expo * (1.0 / denom)).astype(jnp.bfloat16)
+            out_t = jnp.dot(values_t[...], probs, preferred_element_type=jnp.float32)
+            mixed[pl.ds(square.mine, tok), lanes] = join_pair(out_t, tok).astype(jnp.bfloat16)
+            return 0
+
+        lax.fori_loop(0, pairs, pair, 0)
+        given = line_gather(square, mixed, factors, zg_s, zg_r, zgr_s, zgr_r)
+
+        def second(row):
+            return transposed_dot(mixed[pl.ds(row, tok), :], wo_ref[...])
+
+        sums = grid_sum(square, mixed, factors, second, g_own, g_out, g_in, None, zg_r, zgr_r, gs_s, gs_r, None, None)
+        total = g_own[...]
+        for slot in range(depth - 1):
+            total = total + g_in[slot].astype(jnp.float32)
+        out_ref[...] = h_ref[...] + total
+        drain(sent)
+        drain(sums)
+        for copy in gather + spreads + given:
+            copy.wait_send()
+
+    low, full = jnp.bfloat16, jnp.float32
+    shapes = (
+        jax.ShapeDtypeStruct((tok, features), full),
+        jax.ShapeDtypeStruct((depth * tok, features), low),
+        jax.ShapeDtypeStruct((tok, query_cols), low),
+        jax.ShapeDtypeStruct((seq, 2 * HEAD), low),
+        jax.ShapeDtypeStruct((pairs, 8, 2 * tok), full),
+        jax.ShapeDtypeStruct((depth * tok, query_cols), low),
+        jax.ShapeDtypeStruct((depth, 8, tok), full),
+    )
+    return pl.pallas_call(
+        kernel,
+        out_shape=shapes,
+        in_specs=[pl.BlockSpec(memory_space=pltpu.VMEM)] * 6,
+        out_specs=[pl.BlockSpec(memory_space=pltpu.VMEM)] * 7,
+        scratch_shapes=[
+            pltpu.VMEM((tok, cols), full),
+            pltpu.VMEM((8, tok), full),
+            pltpu.VMEM((depth, tok, cols), low),
+            pltpu.VMEM((depth - 1, tok, cols), low),
+            pltpu.VMEM((depth, 8, tok), full),
+            pltpu.VMEM((depth - 1, 8, tok), full),
+            pltpu.VMEM((2 * HEAD, seq), low),
+            pltpu.VMEM((tok, features), full),
+            pltpu.VMEM((depth, tok, features), low),
+            pltpu.VMEM((depth - 1, tok, features), low),
+            sem(3), sem(3), sem(depth), sem(depth - 1), sem(depth), sem(depth - 1),
+            sem(2 * depth - 1), sem(2 * depth - 1), sem(depth - 1), sem(depth - 1), sem(depth - 1), sem(depth - 1),
+            sem(depth), sem(depth - 1),
+        ],
+        compiler_params=pltpu.CompilerParams(collective_id=3, has_side_effects=True, vmem_limit_bytes=60 << 20),
+        cost_estimate=pl.CostEstimate(flops=50_000_000_000, bytes_accessed=8_000_000, transcendentals=0),
+        name="attention_forward",
+    )(hidden, gain.reshape(1, -1), weight_qkv, weight_out, cosine, sine)
+
+
+def attention_backward(grad, hidden, gain, weight_qkv, weight_out, cosine, sine, queries, kv, lse, factors, depth):
+    tok, features = hidden.shape
+    cols = weight_qkv.shape[1]
+    query_cols = GROUP * HEAD
+    seq = 2 * depth * tok
+    pairs = query_cols // EXTRA
+    scale = 1.0 / math.sqrt(HEAD)
+
+    def kernel(dy_ref, h_ref, gain_ref, wqkv_ref, wo_ref, cos_ref, sin_ref, q_ref, kv_ref, lse_ref, factor_ref,
+               out_ref, taken, spun, gain_out,
+               own, heads, z_out, z_in, keys_t, dk, dv, kv_out, kv_own, kv_in, dq, inner_rows, g_own, g_out, g_in, g_rows,
+               ag_s, ag_r, zs_s, zs_r, kv_s, kv_r, zg_s, zg_r, zgr_s, zgr_r, gs_s, gs_r, gr_s, gr_r):
+        square = Square(tok, depth)
+        taken[pl.ds(square.own, tok), :] = dy_ref[...].astype(jnp.bfloat16)
+        square.greet()
+        gather = start_gather(square, taken, ag_s, ag_r)
+
+        def product(row):
+            return jnp.dot(taken[pl.ds(row, tok), :], wo_ref[...], preferred_element_type=jnp.float32), None
+
+        sent = line_sum(square, gather, product, own, None, z_out, z_in, None, None, zs_s, zs_r, None, None)
+        total = own[...]
+        for slot in range(depth - 1):
+            total = total + z_in[slot].astype(jnp.float32)
+        heads[...] = total.astype(jnp.bfloat16)
+        keys, both = twice(kv_ref[...])
+        keys_t[...] = jnp.transpose(keys).astype(jnp.bfloat16)
+        keys = keys.astype(jnp.bfloat16)
+        both = both.astype(jnp.bfloat16)
+        dk[...] = jnp.zeros_like(dk)
+        dv[...] = jnp.zeros_like(dv)
+
+        def pair(t, _):
+            lanes = pl.ds(pl.multiple_of(t * EXTRA, EXTRA), EXTRA)
+            query = split_pair(q_ref[:, lanes])
+            head = split_pair(heads[:, lanes])
+            scores = transposed_dot(keys, query) * scale
+            key_at = lax.broadcasted_iota(jnp.int32, scores.shape, 0)
+            query_at = lax.rem(lax.broadcasted_iota(jnp.int32, scores.shape, 1), tok) + square.row * tok
+            probs = jnp.exp(jnp.where(key_at <= query_at, scores, -1e30) - lse_ref[t, :1, :])
+            grad_probs = transposed_dot(both, head)
+            delta = jnp.sum(probs * grad_probs, axis=0, keepdims=True)
+            grad_scores = (probs * (grad_probs - delta)).astype(jnp.bfloat16)
+            dk[...] += jnp.dot(grad_scores, query, preferred_element_type=jnp.float32)
+            dv[...] += jnp.dot(probs.astype(jnp.bfloat16), head, preferred_element_type=jnp.float32)
+            turned = jnp.dot(keys_t[...], grad_scores, preferred_element_type=jnp.float32)
+            dq[:, lanes] = join_pair(turned, tok) * scale
+            return 0
+
+        lax.fori_loop(0, pairs, pair, 0)
+        lane = lax.broadcasted_iota(jnp.int32, (seq, EXTRA), 1)
+        left = dk[...]
+        right = dv[...]
+        both_kv = jnp.where(
+            lane < HEAD, (left + pltpu.roll(left, HEAD, 1)) * scale, right + pltpu.roll(right, HEAD, 1)
+        )
+        dk[...] = both_kv
+        kv_out[...] = both_kv.astype(jnp.bfloat16)
+        here = pl.ds(pl.multiple_of(square.row * tok, tok), tok)
+        spreads = []
+        for step in range(1, 2 * depth):
+            at = lax.rem(square.row + step, 2 * depth)
+            copy = remote(
+                kv_out.at[pl.ds(pl.multiple_of(at * tok, tok), tok)],
+                kv_in.at[2 * depth - 1 - step],
+                kv_s.at[step - 1],
+                kv_r.at[2 * depth - 1 - step],
+                square.row_peer(step),
+            )
+            copy.start()
+            spreads.append(copy)
+        total_kv = dk[here, :]
+        for copy in spreads:
+            copy.wait_recv()
+        for slot in range(2 * depth - 1):
+            total_kv = total_kv + kv_in[slot].astype(jnp.float32)
+        inner = jnp.sum(dq[...] * q_ref[...].astype(jnp.float32), axis=1, keepdims=True) + jnp.sum(
+            total_kv * kv_ref[here, :].astype(jnp.float32), axis=1, keepdims=True
+        )
+        inner_rows[square.z] = to_row(inner)
+        whole = jnp.concatenate([dq[...], total_kv], axis=1)
+        spun[pl.ds(square.mine, tok), :] = turn(whole, cos_ref[...], -sin_ref[...]).astype(jnp.bfloat16)
+        given = line_gather(square, spun, inner_rows, zg_s, zg_r, zgr_s, zgr_r)
+
+        def second(row):
+            return transposed_dot(spun[pl.ds(row, tok), :], wqkv_ref[...])
+
+        sums = grid_sum(
+            square, spun, inner_rows, second, g_own, g_out, g_in, g_rows, zg_r, zgr_r, gs_s, gs_r, gr_s, gr_r
+        )
+        total = g_own[...]
+        inner = inner_rows[square.g]
+        for slot in range(depth - 1):
+            total = total + g_in[slot].astype(jnp.float32)
+            inner = inner + g_rows[slot]
+        factor = to_column(factor_ref[square.g])
+        normed = h_ref[...] * factor
+        gain_out[...] = jnp.broadcast_to(jnp.sum(total * normed, axis=0, keepdims=True), gain_out.shape)
+        out_ref[...] = dy_ref[...] + factor * (total * gain_ref[...] - normed * (to_column(inner) / D))
+        drain(sent)
+        drain(sums)
+        for copy in gather + spreads + given:
+            copy.wait_send()
+
+    low, full = jnp.bfloat16, jnp.float32
+    shapes = (
+        jax.ShapeDtypeStruct((tok, features), full),
+        jax.ShapeDtypeStruct((depth * tok, features), low),
+        jax.ShapeDtypeStruct((depth * tok, cols), low),
+        jax.ShapeDtypeStruct((8, features), full),
+    )
+    return pl.pallas_call(
+        kernel,
+        out_shape=shapes,
+        in_specs=[pl.BlockSpec(memory_space=pltpu.VMEM)] * 11,
+        out_specs=[pl.BlockSpec(memory_space=pltpu.VMEM)] * 4,
+        scratch_shapes=[
+            pltpu.VMEM((tok, query_cols), full),
+            pltpu.VMEM((tok, query_cols), low),
+            pltpu.VMEM((depth, tok, query_cols), low),
+            pltpu.VMEM((depth - 1, tok, query_cols), low),
+            pltpu.VMEM((2 * HEAD, seq), low),
+            pltpu.VMEM((seq, 2 * HEAD), full),
+            pltpu.VMEM((seq, 2 * HEAD), full),
+            pltpu.VMEM((seq, 2 * HEAD), low),
+            pltpu.VMEM((tok, 2 * HEAD), full),
+            pltpu.VMEM((2 * depth - 1, tok, 2 * HEAD), low),
+            pltpu.VMEM((tok, query_cols), full),
+            pltpu.VMEM((depth, 8, tok), full),
+            pltpu.VMEM((tok, features), full),
+            pltpu.VMEM((depth, tok, features), low),
+            pltpu.VMEM((depth - 1, tok, features), low),
+            pltpu.VMEM((depth - 1, 8, tok), full),
+            sem(3), sem(3), sem(depth), sem(depth - 1),
+            sem(2 * depth - 1), sem(2 * depth - 1), sem(depth - 1), sem(depth - 1), sem(depth - 1), sem(depth - 1),
+            sem(depth), sem(depth - 1), sem(depth), sem(depth - 1),
+        ],
+        compiler_params=pltpu.CompilerParams(collective_id=4, has_side_effects=True, vmem_limit_bytes=60 << 20),
+        cost_estimate=pl.CostEstimate(flops=50_000_000_000, bytes_accessed=8_000_000, transcendentals=0),
+        name="attention_backward",
+    )(grad, hidden, gain.reshape(1, -1), weight_qkv, weight_out, cosine, sine, queries, kv, lse, factors)
+
+
 def stationary(stream, grad_out, wqkv, wo, wgu, wd, gain_attn, gain_ffn):
     tok = stream.shape[0]
     layers = wqkv.shape[0]
     count_rows = wqkv.shape[1]
     depth = lax.axis_size("z")
     head = HEAD
-    query_cols = GROUP * head
-    inverse = 1.0 / math.sqrt(head)
     row = lax.axis_index("z") * 2 + lax.axis_index("x")
     query_pos = row * tok + jnp.arange(tok, dtype=jnp.int32)
-    key_pos = jnp.arange(2 * depth * tok, dtype=jnp.int32)
     freq = THETA ** (-(jnp.arange(head // 2, dtype=jnp.float32) * 2.0 / head))
     angle = query_pos.astype(jnp.float32)[:, None] * freq[None, :]
     cosine = jnp.cos(angle)
     sine = jnp.sin(angle)
+    turns = GROUP + 1
+    cosine = jnp.concatenate([jnp.tile(cosine, (1, 2 * turns)), jnp.ones((tok, head), jnp.float32)], axis=1)
+    sine = jnp.concatenate(
+        [jnp.tile(jnp.concatenate([-sine, sine], axis=1), (1, turns)), jnp.zeros((tok, head), jnp.float32)], axis=1
+    )
     whole = lambda shard: lax.all_gather(shard, "x", axis=0, tiled=True)
     current = swap_grid(stream, depth)
     grad_now = swap_grid(grad_out, depth)
@@ -749,41 +1151,19 @@
         weight_out = whole(wo[index])
         weight_gu = whole(wgu[index].reshape(count_rows, -1))
         weight_down = whole(wd[index])
-        normed_a, factor_a, xnormed = line_norm(current, gain_a[index])
-        xfull = gather_grid(xnormed)
-        qkv = sum_line(add_rows(xfull, weight_qkv))
-        queries = rope_turn(
-            qkv[:, :query_cols].reshape(tok, GROUP, head), cosine[:, None, :], sine[:, None, :]
-        ).astype(jnp.bfloat16)
-        keys = rope_turn(qkv[:, query_cols : query_cols + head], cosine, sine).astype(jnp.bfloat16)
-        values = qkv[:, query_cols + head :].astype(jnp.bfloat16)
-        seqkv = lax.all_gather(
-            jnp.concatenate([keys, values], axis=1), ("z", "x"), axis=0, tiled=True
-        )
-        seq_keys = seqkv[:, :head]
-        seq_values = seqkv[:, head:]
-        scores = masked_scores(queries, seq_keys, query_pos, key_pos)
-        top = jnp.max(scores, axis=2, keepdims=True)
-        expo = jnp.exp(scores - top)
-        denom = jnp.sum(expo, axis=2, keepdims=True)
-        probs = (expo / denom).astype(jnp.bfloat16)
-        log_total = top + jnp.log(denom)
-        mixed = (
-            jnp.einsum("gqk,kd->qgd", probs, seq_values, preferred_element_type=jnp.float32)
-            .reshape(tok, query_cols)
-            .astype(jnp.bfloat16)
-        )
-        mixed_full = gather_line(mixed)
-        hidden_in = current + sum_grid(times_t(mixed_full, weight_out))
+        before = current
+        hidden_in, xfull, queries, kv, lse, mixed_full, factors = attention_forward(
+            before, gain_a[index], weight_qkv, weight_out, cosine, sine, depth
+        )
         current, hfull, kept, active = ffn_forward(hidden_in, gain_f[index], weight_gu, weight_down, depth)
         saved.append(
-            (weight_qkv, weight_out, weight_gu, weight_down, normed_a, factor_a, xfull, queries,
-             seq_keys, seq_values, log_total, mixed_full, hidden_in, hfull, kept, active)
+            (weight_qkv, weight_out, weight_gu, weight_down, before, xfull, queries, kv, lse, mixed_full, factors,
+             hidden_in, hfull, kept, active)
         )
     list_qkv, list_out, list_gu, list_down, list_ga, list_gf = ([], [], [], [], [], [])
     for index in reversed(range(layers)):
-        (weight_qkv, weight_out, weight_gu, weight_down, normed_a, factor_a, xfull, queries,
-         seq_keys, seq_values, log_total, mixed_full, hidden_in, hfull, kept, active) = saved[index]
+        (weight_qkv, weight_out, weight_gu, weight_down, before, xfull, queries, kv, lse, mixed_full, factors,
+         hidden_in, hfull, kept, active) = saved[index]
         width = weight_down.shape[1]
         grad_hidden, grad_full, grad_gu, gain_f_grad = ffn_backward(
             grad_now, hidden_in, gain_f[index], kept, active, weight_gu, weight_down, depth
@@ -793,48 +1173,14 @@
         hnormed = (hfull.astype(jnp.float32) * factor_f * gain_f[index]).astype(jnp.bfloat16)
         list_gu.append(pair_grad(hnormed, grad_gu[:, : 2 * width]).reshape(count_rows, 2, -1))
         list_gf.append(gain_f_grad[0])
-        hidden_full = gather_grid(grad_hidden.astype(jnp.bfloat16))
-        grad_mixed = sum_line(add_rows(hidden_full, weight_out)).astype(jnp.bfloat16)
+        grad_now, hidden_full, grad_qkv, gain_a_grad = attention_backward(
+            grad_hidden, before, gain_a[index], weight_qkv, weight_out, cosine, sine, queries, kv, lse, factors, depth
+        )
         list_out.append(pair_grad(hidden_full, mixed_full))
-        grad_heads = grad_mixed.reshape(tok, GROUP, head)
-        scores = masked_scores(queries, seq_keys, query_pos, key_pos)
-        probs_full = jnp.exp(scores - log_total)
-        probs = probs_full.astype(jnp.bfloat16)
-        grad_probs = jnp.einsum(
-            "qgd,kd->gqk", grad_heads, seq_values, preferred_element_type=jnp.float32
-        )
-        delta = jnp.sum(probs_full * grad_probs, axis=2, keepdims=True)
-        grad_scores = (probs_full * (grad_probs - delta)).astype(jnp.bfloat16)
-        grad_queries = (
-            jnp.einsum("gqk,kd->qgd", grad_scores, seq_keys, preferred_element_type=jnp.float32)
-            * inverse
-        )
-        grad_keys = (
-            jnp.einsum("gqk,qgd->kd", grad_scores, queries, preferred_element_type=jnp.float32)
-            * inverse
-        )
-        grad_values = jnp.einsum(
-            "gqk,qgd->kd", probs, grad_heads, preferred_element_type=jnp.float32
-        )
-        grad_kv = lax.psum_scatter(
-            jnp.concatenate([grad_keys, grad_values], axis=1).astype(jnp.bfloat16),
-            ("z", "x"),
-            scatter_dimension=0,
-            tiled=True,
-        ).astype(jnp.float32)
-        grad_k = rope_turn(grad_kv[:, :head], cosine, -sine)
-        grad_v = grad_kv[:, head:]
-        grad_q = rope_turn(grad_queries, cosine[:, None, :], -sine[:, None, :]).reshape(
-            tok, query_cols
-        )
-        grad_qkv = gather_line(
-            jnp.concatenate([grad_q, grad_k, grad_v], axis=1).astype(jnp.bfloat16)
-        )
-        grad_xn = sum_grid(times_t(grad_qkv, weight_qkv))
-        list_qkv.append(pair_grad(xfull, grad_qkv).reshape(count_rows, 1, -1))
-        grad_in, gain_a_grad = line_norm_back(grad_xn, normed_a, factor_a, gain_a[index])
-        list_ga.append(gain_a_grad)
-        grad_now = grad_hidden + grad_in
+        factor_a = factors[:, 0, :].reshape(-1, 1)
+        xnormed = (xfull.astype(jnp.float32) * factor_a * gain_a[index]).astype(jnp.bfloat16)
+        list_qkv.append(pair_grad(xnormed, grad_qkv).reshape(count_rows, 1, -1))
+        list_ga.append(gain_a_grad[0])
     gains = lax.psum(jnp.concatenate([jnp.stack(list_ga[::-1]), jnp.stack(list_gf[::-1])]), ("x", "y", "c"))
     gains = swap_grid(gains, depth)
     return (

time: 1190 us -> 895 us (0.75)
  waiting for transfers between devices: 456 us -> 147 us
  Pallas kernels: 323 us -> 563 us
  blocking collectives: 237 us -> 65 us
  matrix products: 48.8 us -> 23.8 us
  other arithmetic: 34.3 us -> 13 us
    pallas_call x0 -> x4, Pallas kernels: none -> 228 us  [the longest x2 115 us: attention_forward(): pl.pallas_call(kernel, out_shape=shapes, in_specs=[pl.BlockSpec(memory_sp...]
    all_gather x10 -> x0, blocking collectives: 140 us -> none  [the longest x4 59.9 us: gather_line(): return lax.all_gather(rows_in, 'z', axis=0, tiled=True)]
    unnamed x26 -> x12, waiting for transfers between devices: 137 us -> 0.86 us
    all_gather x4, waiting for transfers between devices: 96 us -> 0.08 us  [stationary(): whole = lambda shard: lax.all_gather(shard, 'x', axis=0, tiled=True)]
    reduce_scatter x6 -> x0, waiting for transfers between devices: 75.1 us -> none  [the longest x2 42.5 us: sum_line(): lax.psum_scatter(partials.astype(jnp.bfloat16), 'z', scatter_dimension=0,...]
    psum x4 -> x0, blocking collectives: 38.3 us -> none  [the longest x2 20.3 us: line_norm_back(): inner = lax.psum(jnp.sum(scaled * normed, axis=1), 'z')]
    dot_general x20 -> x0, matrix products: 25.1 us -> none  [the longest x2 6.21 us: stationary(): jnp.einsum('gqk,qgd->kd', probs, grad_heads, preferred_element_type=jnp.f...]
    ppermute x7, waiting for transfers between devices: 15.9 us -> 2.64 us  [swap_grid(): return lax.ppermute(values, ('z', 'y', 'c'), pairs)]
  transfers between devices with their start and end apart: 29 -> 19, of which waited for: 20 -> 6; matrix products, arithmetic and copies ran while one was open for 5% -> 5% of each run, Pallas kernels for 7% -> 32%
where the time goes in v3:
time: 895 us; the launch traced here: 884 us
  Pallas kernels  563 us (63%)
  waiting for transfers between devices  147 us (16%)
  blocking collectives  65 us (7%)
  local copies, waits for them, and re-layouts  29.2 us (3%)
  starting transfers between devices  28.5 us (3%)
  matrix products  23.8 us (3%)
  between operations  15.1 us (2%)
  other arithmetic  13 us (1%)
    pallas_call x2, Pallas kernels, ffn_forward(): pl.pallas_call(kernel, out_shape=shapes, in_specs=[pl.BlockSpec(memory_sp...  170 us
    pallas_call x2, Pallas kernels, ffn_backward(): pl.pallas_call(kernel, out_shape=shapes, in_specs=[pl.BlockSpec(memory_sp...  165 us
    reduce_scatter x8, waiting for transfers between devices, pair_grad(): lax.psum_scatter(lax.dot_general(left, right, (((0,), (0,)), ((), ())), p...  143 us
    pallas_call x2, Pallas kernels, attention_forward(): pl.pallas_call(kernel, out_shape=shapes, in_specs=[pl.BlockSpec(memory_sp...  115 us
    pallas_call x2, Pallas kernels, attention_backward(): pl.pallas_call(kernel, out_shape=shapes, in_specs=[pl.BlockSpec(memory_sp...  113 us
    all_gather x4, blocking collectives, stationary(): whole = lambda shard: lax.all_gather(shard, 'x', axis=0, tiled=True)  51 us
    ppermute x7, starting transfers between devices, swap_grid(): return lax.ppermute(values, ('z', 'y', 'c'), pairs)  28 us
    dot_general x8, matrix products, pair_grad(): lax.dot_general(left, right, (((0,), (0,)), ((), ())), preferred_element_...  23.8 us
  transfers between devices with their start and end apart: 19, of which 6 were waited for; matrix products, arithmetic and copies ran while one was open for 5% of the time, Pallas kernels for 32%

profile of v3, /device:TPU:4, one launch (start us, length us, event | category | flops | bytes accessed | tf_op | source)
XLA Modules:
  0.0 884.3 jit_solution(8459308520302644563)
XLA Ops:
  7.2 2.5 fusion.14
  9.8 3.7 fusion.13
  13.5 1.3 copy.20
  14.9 0.7 all-gather.17.cloned.1.call-update
  15.6 4.4 collective-permute-start.1
  20.1 3.2 collective-permute-start
  23.3 4.4 collective-permute-start.2
  27.7 3.2 collective-permute-start.4
  31.0 1.3 copy.21
  32.4 11.5 %all-gather = bf16[1,512,1,640]{3,1,2,0:T(8,128)(2,1)} all-gather(bf16[1,256,1,640]{3,1,2,0:T(8,128)(2,1)S(1)} %get-tuple-element.105), channel_id=2, replica_groups=mesh['z'=4,'x'=2,'y'=2,'c'=2] {'x'}, dimensions={1}, use_global_device_ids=true | all-gather | bytes 983040 | tf_op jit(solution)/shard_map/all_gather | solution.py:1143
  43.9 9.1 %all-gather.1 = bf16[1,512,512]{2,1,0:T(8,128)(2,1)} all-gather(bf16[1,256,512]{2,1,0:T(8,128)(2,1)S(1)} %get-tuple-element.107), channel_id=3, replica_groups=mesh['z'=4,'x'=2,'y'=2,'c'=2] {'x'}, dimensions={1}, use_global_device_ids=true | all-gather | bytes 786432 | tf_op jit(solution)/shard_map/all_gather | solution.py:1143
  53.0 16.6 %all-gather.3 = bf16[1,512,1,640]{3,1,2,0:T(8,128)(2,1)} all-gather(bf16[1,256,1,640]{3,1,2,0:T(8,128)(2,1)S(1)} %get-tuple-element.104), channel_id=5, replica_groups=mesh['z'=4,'x'=2,'y'=2,'c'=2] {'x'}, dimensions={1}, use_global_device_ids=true | all-gather | bytes 983040 | tf_op jit(solution)/shard_map/all_gather | solution.py:1143
  69.6 13.9 %all-gather.4 = bf16[1,512,512]{2,1,0:T(8,128)(2,1)} all-gather(bf16[1,256,512]{2,1,0:T(8,128)(2,1)S(1)} %get-tuple-element.106), channel_id=6, replica_groups=mesh['z'=4,'x'=2,'y'=2,'c'=2] {'x'}, dimensions={1}, use_global_device_ids=true | all-gather | bytes 786432 | tf_op jit(solution)/shard_map/all_gather | solution.py:1143
  83.9 0.2 copy.17
  84.0 0.8 concatenate.14.sin_ref
  84.8 0.8 concatenate.12.cos_ref
  85.5 0.6 fusion.19
  86.1 0.6 fusion.18
  86.7 0.7 copy-done.10
  87.4 58.4 %attention_forward.2 = (f32[128,512]{1,0:T(8,128)}, bf16[512,512]{1,0:T(8,128)(2,1)}, bf16[128,512]{1,0:T(8,128)(2,1)}, bf16[1024,128]{1,0:T(8,128)(2,1)}, f32[4...) custom-call(f32[128,512]{1,0:T(8,128)} %copy-done.10, f32[1,512]{1,0:T(1,128)} %get-tuple-element.113.gain_ref, ...), custom_call_target="tpu_custom_call" | custom-call | flops 49999998976 | bytes 8000000 | tf_op jit(solution)/shard_map/attention_forward/pallas_call | solution.py:957
  145.9 85.4 %ffn_forward.2 = (f32[128,512]{1,0:T(8,128)}, bf16[512,512]{1,0:T(8,128)(2,1)}, f32[256,2816]{1,0:T(8,128)}, bf16[512,1536]{1,0:T(8,128)(2,1)}) custom-call(f32[128,512]{1,0:T(8,128)} %get-tuple-element.46.h_ref, f32[1,512]{1,0:T(1,128)} %get-tuple-element.111.gain_ref, bf16[512,2816]{1,0:T(8,128)(2,1)} %all-gather.11.cloned.1.call-done.w1_ref, ...), custom_call_target="tpu_custom_call" | custom-call | flops 60000002048 | bytes 8000000 | tf_op jit(solution)/shard_map/ffn_forward/pallas_call | solution.py:605
  231.3 57.0 %attention_forward.3 = (f32[128,512]{1,0:T(8,128)}, bf16[512,512]{1,0:T(8,128)(2,1)}, bf16[128,512]{1,0:T(8,128)(2,1)}, bf16[1024,128]{1,0:T(8,128)(2,1)}, f32[4...) custom-call(f32[128,512]{1,0:T(8,128)} %get-tuple-element.47.h_ref, ...), custom_call_target="tpu_custom_call" | custom-call | flops 49999998976 | bytes 8000000 | tf_op jit(solution)/shard_map/attention_forward/pallas_call | solution.py:957
  288.3 84.3 %ffn_forward.3 = (f32[128,512]{1,0:T(8,128)}, bf16[512,512]{1,0:T(8,128)(2,1)}, f32[256,2816]{1,0:T(8,128)}, bf16[512,1536]{1,0:T(8,128)(2,1)}) custom-call(f32[128,512]{1,0:T(8,128)} %get-tuple-element.48.h_ref, f32[1,512]{1,0:T(1,128)} %get-tuple-element.110.gain_ref, bf16[512,2816]{1,0:T(8,128)(2,1)} %all-gather.13.cloned.1.call-done.w1_ref, ...), custom_call_target="tpu_custom_call" | custom-call | flops 60000002048 | bytes 8000000 | tf_op jit(solution)/shard_map/ffn_forward/pallas_call | solution.py:605
  372.6 80.3 %ffn_backward.2 = (f32[128,512]{1,0:T(8,128)}, bf16[512,512]{1,0:T(8,128)(2,1)}, bf16[512,2944]{1,0:T(8,128)(2,1)}, f32[8,512]{1,0:T(8,128)}) custom-call(f32[128,512]{1,0:T(8,128)} %collective-permute-done.4.dy_ref, f32[128,512]{1,0:T(8,128)} %get-tuple-element.48.h_ref, f32[1,512]{1,0:T(1,128)} %get-tuple-element.110.gain_ref, ...), custom_call_target="tpu_custom_call" | custom-call | flops 60000002048 | bytes 8000000 | tf_op jit(solution)/shard_map/ffn_backward/pallas_call | solution.py:672
  453.0 56.8 %attention_backward.2 = (f32[128,512]{1,0:T(8,128)}, bf16[512,512]{1,0:T(8,128)(2,1)}, bf16[512,640]{1,0:T(8,128)(2,1)}, f32[8,512]{1,0:T(8,128)}) custom-call(f32[128,512]{1,0:T(8,128)} %get-tuple-element.52.dy_ref, f32[128,512]{1,0:T(8,128)} %get-tuple-element.47.h_ref, f32[1,512]{1,0:T(1,128)} %get-tuple-element.112.gain_ref, bf16[512,640]{1,0:T(8,128)(2,1)} %bitcast.45, ...), custom_call_target="tpu_custom_call" | custom-call | flops 49999998976 | bytes 8000000 | tf_op jit(solution)/shard_map/attention_backward/pallas_call | solution.py:1094
  509.8 84.8 %ffn_backward.3 = (f32[128,512]{1,0:T(8,128)}, bf16[512,512]{1,0:T(8,128)(2,1)}, bf16[512,2944]{1,0:T(8,128)(2,1)}, f32[8,512]{1,0:T(8,128)}) custom-call(f32[128,512]{1,0:T(8,128)} %get-tuple-element.57.dy_ref, f32[128,512]{1,0:T(8,128)} %get-tuple-element.46.h_ref, f32[1,512]{1,0:T(1,128)} %get-tuple-element.111.gain_ref, ...), custom_call_target="tpu_custom_call" | custom-call | flops 60000002048 | bytes 8000000 | tf_op jit(solution)/shard_map/ffn_backward/pallas_call | solution.py:672
  594.6 55.8 %attention_backward.3 = (f32[128,512]{1,0:T(8,128)}, bf16[512,512]{1,0:T(8,128)(2,1)}, bf16[512,640]{1,0:T(8,128)(2,1)}, f32[8,512]{1,0:T(8,128)}) custom-call(f32[128,512]{1,0:T(8,128)} %get-tuple-element.60.dy_ref, f32[128,512]{1,0:T(8,128)} %copy-done.10, f32[1,512]{1,0:T(1,128)} %get-tuple-element.113.gain_ref, bf16[512,640]{1,0:T(8,128)(2,1)} %bitcast.43, ...), custom_call_target="tpu_custom_call" | custom-call | flops 49999998976 | bytes 8000000 | tf_op jit(solution)/shard_map/attention_backward/pallas_call | solution.py:1094
  650.4 2.4 convolution_convert_fusion.7
  652.9 1.3 convolution_convert_fusion.6
  654.2 0.7 slice.98
  655.0 1.6 convolution_convert_fusion.5
  656.6 0.7 slice.99
  657.3 1.6 convolution_convert_fusion.4
  659.0 3.3 convolution_convert_fusion.2
  662.4 3.2 convolution_convert_fusion.3
  665.7 0.4 copy-done.5
  666.2 5.4 convolution_convert_fusion.1
  671.8 0.5 copy-done.4
  672.3 0.4 copy-done.21
  672.6 5.2 convolution_convert_fusion
  677.9 0.8 slice.106
  678.6 0.7 slice.108
  679.3 0.7 slice.107
  680.1 0.7 slice.109
  680.8 6.0 collective-permute-start.5
  686.8 1.9 collective-permute-start.3
  688.7 14.0 %psum.7 = f32[4,512]{1,0:T(4,128)S(1)} all-reduce(f32[4,512]{1,0:T(4,128)S(1)} %pad_maximum_fusion.1), channel_id=1, replica_groups=mesh['z'=4,'x'=2,'y'=2,'c'=2] {'x','y','c'}, use_global_device_ids=true, to_apply=%region_10.0 | all-reduce | flops 2048 | bytes 16384 | tf_op jit(solution)/shard_map/psum | solution.py:1184
  702.7 4.8 collective-permute-start.6
  707.5 2.6 collective-permute-done.6
  710.2 0.6 fusion.17
  710.8 2.1 maximum_convert_fusion.3
  712.9 12.7 %reduce-scatter.11.cloned.1.call-done = bf16[256,640]{1,0:T(8,128)(2,1)} async-done(((bf16[512,640]{1,0:T(8,128)(2,1)}), bf16[256,640]{1,0:T(8,128)(2,1)}) %reduce-scatter.11.cloned.1.call-update) | async-done | bytes 327696 | tf_op jit(solution)/shard_map/reduce_scatter | solution.py:269
  725.6 1.2 maximum_convert_fusion.2
  726.8 2.4 copy.19
  729.2 24.0 %reduce-scatter.23.cloned.1.call-done = bf16[256,1408]{1,0:T(8,128)(2,1)} async-done(((bf16[512,1408]{1,0:T(8,128)(2,1)}), bf16[256,1408]{1,0:T(8,128)(2,1)}) %reduce-scatter.23.cloned.1.call-update) | async-done | bytes 720912 | tf_op jit(solution)/shard_map/reduce_scatter | solution.py:269
  753.2 26.8 %reduce-scatter.21.cloned.1.call-done = bf16[256,1408]{1,0:T(8,128)(2,1)} async-done(((bf16[512,1408]{1,0:T(8,128)(2,1)}), bf16[256,1408]{1,0:T(8,128)(2,1)}) %reduce-scatter.21.cloned.1.call-update) | async-done | bytes 720912 | tf_op jit(solution)/shard_map/reduce_scatter | solution.py:269
  780.0 3.1 maximum_convert_fusion.1
  783.1 39.8 %reduce-scatter.17.cloned.1.call-done = bf16[256,2816]{1,0:T(8,128)(2,1)} async-done(((bf16[512,2816]{1,0:T(8,128)(2,1)}), bf16[256,2816]{1,0:T(8,128)(2,1)}) %reduce-scatter.17.cloned.1.call-update) | async-done | bytes 1441808 | tf_op jit(solution)/shard_map/reduce_scatter | solution.py:269
  822.9 3.2 stack_reshape.18
  826.1 40.0 %reduce-scatter.19.cloned.1.call-done = bf16[256,2816]{1,0:T(8,128)(2,1)} async-done(((bf16[512,2816]{1,0:T(8,128)(2,1)}), bf16[256,2816]{1,0:T(8,128)(2,1)}) %reduce-scatter.19.cloned.1.call-update) | async-done | bytes 1441808 | tf_op jit(solution)/shard_map/reduce_scatter | solution.py:269
  866.1 3.2 stack_reshape.19
  869.3 6.2 maximum_convert_fusion
  875.6 0.7 copy.24
  876.3 0.7 copy.25
  (88 shorter events, 1.6 us)
Async XLA Ops:
  7.2 138.7 %all-gather.15.cloned.1.call-start = ((), (), s32[]{:S(2)}) async-start(), calls=%async_computation.18 | async-start | bytes 2162688 | tf_op jit(solution)/shard_map/all_gather | solution.py:1143
  9.8 136.1 %all-gather.11.cloned.1.call-start = ((), (), s32[]{:S(2)}) async-start(), calls=%async_computation.8 | async-start | bytes 4325376 | tf_op jit(solution)/shard_map/all_gather | solution.py:1143
  14.8 0.8 copy-start.12
  14.8 5.3 copy-start.8
  14.8 8.5 copy-start.13
  14.8 273.5 %all-gather.17.cloned.1.call-start = ((), (), s32[]{:S(2)}) async-start(), calls=%async_computation.19 | async-start | bytes 2162688 | tf_op jit(solution)/shard_map/all_gather | solution.py:1143
  15.6 272.8 %all-gather.13.cloned.1.call-start = ((), (), s32[]{:S(2)}) async-start(), calls=%async_computation.9 | async-start | bytes 4325376 | tf_op jit(solution)/shard_map/all_gather | solution.py:1143
  15.6 69.9 %collective-permute-start.1 = (f32[2,512]{1,0:T(2,128)S(1)}, f32[2,512]{1,0:T(2,128)S(1)}, u32[]{:S(2)}, u32[]{:S(2)}) collective-permute-start(f32[2,512]{1,0:T(2,128)S(1)} %copy-done.12), channel_id=1, source_target_pairs={{0,0},{1,8},{2,16},{3,24},{8,1},{9,9},{10,17},{11,25},{16,2},{17,1... | collective-permute-start | bytes 12296 | tf_op jit(solution)/shard_map/ppermute | solution.py:265
  20.1 66.6 %collective-permute-start = (f32[128,512]{1,0:T(8,128)S(1)}, f32[128,512]{1,0:T(8,128)S(1)}, u32[]{:S(2)}, u32[]{:S(2)}) collective-permute-start(f32[128,512]{1,0:T(8,128)S(1)} %copy-done.8), channel_id=1, source_target_pairs={{0,0},{1,8},{2,16},{3,24},{8,1},{9,9},{10,17},{11,25},{16,2},{17,1... | collective-permute-start | bytes 786440 | tf_op jit(solution)/shard_map/ppermute | solution.py:265
  23.3 62.8 %collective-permute-start.2 = (f32[2,512]{1,0:T(2,128)S(1)}, f32[2,512]{1,0:T(2,128)S(1)}, u32[]{:S(2)}, u32[]{:S(2)}) collective-permute-start(f32[2,512]{1,0:T(2,128)S(1)} %copy-done.13), channel_id=1, source_target_pairs={{0,0},{1,8},{2,16},{3,24},{8,1},{9,9},{10,17},{11,25},{16,2},{17,1... | collective-permute-start | bytes 12296 | tf_op jit(solution)/shard_map/ppermute | solution.py:265
  27.7 344.9 %collective-permute-start.4 = (f32[128,512]{1,0:T(8,128)}, f32[128,512]{1,0:T(8,128)}, u32[]{:S(2)}, u32[]{:S(2)}) collective-permute-start(f32[128,512]{1,0:T(8,128)} %param.9), channel_id=1, source_target_pairs={{0,0},{1,8},{2,16},{3,24},{8,1},{9,9},{10,17},{11,25},{16,2},{17,1... | collective-permute-start | bytes 786440 | tf_op jit(solution)/shard_map/ppermute | solution.py:265
  31.0 1.4 copy-start
  32.2 11.7 %copy-start.1 = (bf16[2,256,512]{2,1,0:T(8,128)(2,1)S(1)}, bf16[2,256,512]{2,1,0:T(8,128)(2,1)}, u32[]{:S(2)}) copy-start(bf16[2,256,512]{2,1,0:T(8,128)(2,1)} %param.11) | copy-start | bytes 1572868
  32.3 678.5 %reduce-scatter.13.cloned.1.call-start = ((), (), s32[]{:S(2)}) async-start(), calls=%async_computation.12 | async-start | bytes 786432 | tf_op jit(solution)/shard_map/reduce_scatter | solution.py:269
  86.7 0.7 copy-start.10
  594.5 55.8 %copy-start.14 = (bf16[512,512]{1,0:T(8,128)(2,1)S(1)}, bf16[512,512]{1,0:T(8,128)(2,1)}, u32[]{:S(2)}) copy-start(bf16[512,512]{1,0:T(8,128)(2,1)} %get-tuple-element.71) | copy-start | bytes 1572868
  650.4 2.5 copy-start.15
  650.4 2.5 copy-start.16
  652.8 2.2 copy-start.7
  652.8 2.2 copy-start.18
  652.8 2.2 copy-start.19
  652.8 58.0 %reduce-scatter.15.cloned.1.call-start = ((), (), s32[]{:S(2)}) async-start(), calls=%async_computation.13 | async-start | bytes 786432 | tf_op jit(solution)/shard_map/reduce_scatter | solution.py:269
  654.2 58.7 %reduce-scatter.9.cloned.1.call-start = ((), (), s32[]{:S(2)}) async-start(), calls=%async_computation.10 | async-start | bytes 983040 | tf_op jit(solution)/shard_map/reduce_scatter | solution.py:269
  654.9 2.4 copy-start.6
  655.0 2.4 copy-start.17
  655.0 2.4 copy-start.20
  656.6 69.0 %reduce-scatter.11.cloned.1.call-start = ((), (), s32[]{:S(2)}) async-start(), calls=%async_computation.11 | async-start | bytes 983040 | tf_op jit(solution)/shard_map/reduce_scatter | solution.py:269
  657.3 1.7 copy-start.3
  658.9 94.2 %reduce-scatter.23.cloned.1.call-start = ((), (), s32[]{:S(2)}) async-start(), calls=%async_computation.17 | async-start | bytes 2162688 | tf_op jit(solution)/shard_map/reduce_scatter | solution.py:269
  659.0 3.4 copy-start.2
  662.3 117.7 %reduce-scatter.21.cloned.1.call-start = ((), (), s32[]{:S(2)}) async-start(), calls=%async_computation.16 | async-start | bytes 2162688 | tf_op jit(solution)/shard_map/reduce_scatter | solution.py:269
  665.5 0.6 copy-start.5
  665.6 157.3 %reduce-scatter.17.cloned.1.call-start = ((), (), s32[]{:S(2)}) async-start(), calls=%async_computation.14 | async-start | bytes 4325376 | tf_op jit(solution)/shard_map/reduce_scatter | solution.py:269
  671.6 0.7 copy-start.4
  671.6 1.1 copy-start.21
  671.6 194.5 %reduce-scatter.19.cloned.1.call-start = ((), (), s32[]{:S(2)}) async-start(), calls=%async_computation.15 | async-start | bytes 4325376 | tf_op jit(solution)/shard_map/reduce_scatter | solution.py:269
  677.8 3.0 copy-start.11
  677.8 8.9 %copy-start.9 = (f32[128,512]{1,0:T(8,128)S(1)}, f32[128,512]{1,0:T(8,128)}, u32[]{:S(2)}) copy-start(f32[128,512]{1,0:T(8,128)} %get-tuple-element.49) | copy-start | bytes 786436
  680.8 30.0 %collective-permute-start.5 = (f32[128,512]{1,0:T(8,128)S(1)}, f32[128,512]{1,0:T(8,128)S(1)}, u32[]{:S(2)}, u32[]{:S(2)}) collective-permute-start(f32[128,512]{1,0:T(8,128)S(1)} %copy-done.11), channel_id=1, source_target_pairs={{0,0},{1,8},{2,16},{3,24},{8,1},{9,9},{10,17},{11,25},{16,2},{17,1... | collective-permute-start | bytes 786440 | tf_op jit(solution)/shard_map/ppermute | solution.py:265
  686.8 24.0 %collective-permute-start.3 = (f32[128,512]{1,0:T(8,128)S(1)}, f32[128,512]{1,0:T(8,128)S(1)}, u32[]{:S(2)}, u32[]{:S(2)}) collective-permute-start(f32[128,512]{1,0:T(8,128)S(1)} %copy-done.9), channel_id=1, source_target_pairs={{0,0},{1,8},{2,16},{3,24},{8,1},{9,9},{10,17},{11,25},{16,2},{17,1... | collective-permute-start | bytes 786440 | tf_op jit(solution)/shard_map/ppermute | solution.py:265
  702.7 7.4 collective-permute-start.6
Sparse Core Ops, SparseCore 0:
  10.1 27.0 all-gather.14
  39.3 60.0 all-gather.10
  101.4 26.9 all-gather.16
  130.5 41.9 all-gather.12
  652.9 17.8 reduce-scatter.12
  673.5 14.6 reduce-scatter.14
  690.4 16.3 reduce-scatter.8
  709.6 15.9 reduce-scatter.10
  728.4 24.6 reduce-scatter.22
  755.3 24.6 reduce-scatter.20
  782.3 40.5 reduce-scatter.16
  825.5 40.5 reduce-scatter.18

commit v4 on v3

--- a/solution.py
+++ b/solution.py
@@ -265,17 +265,6 @@
     return lax.ppermute(values, ("z", "y", "c"), pairs)
 
 
-def pair_grad(left, right):
-    return lax.psum_scatter(
-        lax.dot_general(
-            left, right, (((0,), (0,)), ((), ())), preferred_element_type=jnp.float32
-        ).astype(jnp.bfloat16),
-        "x",
-        scatter_dimension=0,
-        tiled=True,
-    ).astype(jnp.float32)
-
-
 MESH_ID = pl.DeviceIdType.MESH
 ROWS = 16
 SKEW = 2
@@ -297,6 +286,60 @@
 
 def transposed_dot(left, right):
     return lax.dot_general(left, right, (((1,), (1,)), ((), ())), preferred_element_type=jnp.float32)
+
+
+class Side:
+    def __init__(self, send, recv):
+        self.peer = {"x": 1 - lax.axis_index("x")}
+        self.send, self.recv, self.copies = send, recv, []
+
+    def start(self, source, target):
+        at = len(self.copies)
+        copy = remote(source, target, self.send.at[at], self.recv.at[at], self.peer)
+        copy.start()
+        self.copies.append(copy)
+        return copy
+
+    def later(self, source, target):
+        at = len(self.copies)
+        copy = remote(source, target, self.send.at[at], self.recv.at[at], self.peer)
+        self.copies.append(copy)
+        return copy
+
+    def finish(self, taken=()):
+        for copy in self.copies:
+            copy.wait_send()
+            if not any(copy is item for item in taken):
+                copy.wait_recv()
+
+
+def remote(src, dst, send, recv, device):
+    return pltpu.make_async_remote_copy(
+        src_ref=src, dst_ref=dst, send_sem=send, recv_sem=recv, device_id=device, device_id_type=MESH_ID
+    )
+
+
+def halves(features):
+    half = features // 2
+    x = lax.axis_index("x")
+    own = pl.ds(pl.multiple_of(x * half, half), half)
+    other = pl.ds(pl.multiple_of((1 - x) * half, half), half)
+    return own, other
+
+
+def flip(block):
+    return jnp.transpose(block.astype(jnp.float32)).astype(jnp.bfloat16)
+
+
+def grad_tile(turned, features, right, cols, kept, given):
+    own, other = halves(features)
+    value = right[:, cols]
+    kept[:, cols] = jnp.dot(turned[own, :], value, preferred_element_type=jnp.float32).astype(jnp.bfloat16)
+    given[:, cols] = jnp.dot(turned[other, :], value, preferred_element_type=jnp.float32).astype(jnp.bfloat16)
+
+
+def sem(*shape):
+    return pltpu.SemaphoreType.DMA(shape)
 
 
 class Line:
@@ -326,8 +369,9 @@
         def _():
             pl.semaphore_signal(barrier, 1, device_id={"z": self.z + 1}, device_id_type=MESH_ID)
 
+        pl.semaphore_signal(barrier, 1, device_id={"x": 1 - self.x}, device_id_type=MESH_ID)
         inner = jnp.where(self.z > 0, 1, 0) + jnp.where(self.z < self.depth - 1, 1, 0)
-        pl.semaphore_wait(barrier, 3 + inner)
+        pl.semaphore_wait(barrier, 4 + inner)
 
     def place(self, stream):
         return self.z if stream == 0 else self.depth - 1 - self.z
@@ -351,7 +395,7 @@
     span = GROUP_CHUNKS * ROWS
     half_groups = groups // 2
 
-    def run(line, taken, prepare, finish, second, close, product, carried, chain_out, chain_in, wide, own_part, rs_out, rs_in,
+    def run(line, taken, begin, prepare, beside, finish, second, settle, close, product, carried, chain_out, chain_in, wide, own_part, rs_out, rs_in,
             ag_s, ag_r, ch_s, ch_r, bc_s, bc_r, rs_s, rs_r):
         line.greet()
         gather = [
@@ -367,6 +411,7 @@
         ]
         for copy in gather:
             copy.start()
+        begin()
         gather[0].wait_recv()
         prepare(pl.multiple_of(line.y * 2 * tok, 2 * tok))
 
@@ -413,6 +458,7 @@
                 gather[2].wait_recv()
                 prepare(pl.multiple_of((1 - line.y) * 2 * tok, 2 * tok))
 
+            beside(i)
             for stream in (0, 1):
                 place = line.place(stream)
                 chunk = i - SKEW * place
@@ -511,6 +557,7 @@
                     copy.wait_send()
             return 0
 
+        settle()
         for slot in range(3):
             for part in range(half_groups):
                 pltpu.make_async_remote_copy(
@@ -551,15 +598,27 @@
 TILE = 256
 
 
-def ffn_forward(hidden, gain, weight_gu, weight_down, depth):
+def ffn_forward(hidden, gain, gu_own, gu_peer, down_own, shipped, depth):
     tok, features = hidden.shape
-    width = weight_down.shape[1]
+    width = down_own.shape[1]
     run, scratch = make_line(tok, depth, 2 * width, width, True, False, features)
-
-    def kernel(h_ref, gain_ref, w1_ref, w2_ref, out_ref, taken, kept, wide, scaled, product, carried, chain_out, chain_in,
-               own_part, rs_out, rs_in, *sems):
+    count = len(shipped)
+
+    def kernel(h_ref, gain_ref, w1_own, w1_peer, w2_own, *rest):
+        leave, rest = rest[:count], rest[count:]
+        (out_ref, normed_t, kept, wide, w2_peer), rest = rest[:5], rest[5:]
+        landed, rest = rest[:count], rest[count:]
+        (taken, scaled, pieces, side_s, side_r, product, carried, chain_out, chain_in, own_part, rs_out, rs_in), sems = (
+            rest[:12], rest[12:])
         line = Line(tok, depth)
+        side = Side(side_s, side_r)
+        own, other = halves(features)
         taken[pl.ds(line.own, tok), :] = h_ref[...].astype(jnp.bfloat16)
+
+        def begin():
+            side.start(w2_own, w2_peer)
+            for source, target in zip(leave, landed):
+                side.start(source, target)
 
         def prepare(row):
             rows = pl.ds(row, 2 * tok)
@@ -569,10 +628,17 @@
 
             def tile(j, _):
                 cols = pl.ds(pl.multiple_of(j * TILE, TILE), TILE)
-                product[rows, cols] = jnp.dot(scaled[...], w1_ref[:, cols], preferred_element_type=jnp.float32)
+                product[rows, cols] = jnp.dot(
+                    scaled[:, own], w1_own[:, cols], preferred_element_type=jnp.float32
+                ) + jnp.dot(scaled[:, other], w1_peer[:, cols], preferred_element_type=jnp.float32)
                 return 0
 
             lax.fori_loop(0, 2 * width // TILE, tile, 0)
+
+        def beside(i):
+            @pl.when(i == SKEW * (depth - 1))
+            def _():
+                side.copies[0].wait_recv()
 
         def finish(row, at, total, extra):
             factor = lax.rsqrt(extra / D + EPS)
@@ -585,54 +651,103 @@
             wide[pl.ds(row, ROWS), width:] = spread(factor)
 
         def second(row, span):
-            return transposed_dot(wide[pl.ds(row, span), :width], w2_ref[...])
+            value = wide[pl.ds(row, span), :width]
+            pieces[:, own] = transposed_dot(value, w2_own[...])
+            pieces[:, other] = transposed_dot(value, w2_peer[...])
+            return pieces[...]
+
+        def settle():
+            normed = taken[...].astype(jnp.float32) * unspread(wide[:, width:]) * gain_ref[...]
+            normed_t[...] = jnp.transpose(normed).astype(jnp.bfloat16)
 
         def close():
             total = own_part[...]
             for slot in range(3):
                 total = total + rs_in[slot].astype(jnp.float32)
             out_ref[...] = h_ref[...] + total
-
-        run(line, taken, prepare, finish, second, close, product, carried, chain_out, chain_in, wide, own_part, rs_out, rs_in,
-            *sems)
-
+            side.finish(side.copies[:1])
+
+        run(line, taken, begin, prepare, beside, finish, second, settle, close, product, carried, chain_out, chain_in, wide,
+            own_part, rs_out, rs_in, *sems)
+
+    low, full = jnp.bfloat16, jnp.float32
     shapes = (
-        jax.ShapeDtypeStruct((tok, features), jnp.float32),
-        jax.ShapeDtypeStruct((4 * tok, features), jnp.bfloat16),
-        jax.ShapeDtypeStruct((2 * tok, 2 * width), jnp.float32),
-        jax.ShapeDtypeStruct((4 * tok, width + EXTRA), jnp.bfloat16),
-    )
-    return pl.pallas_call(
+        jax.ShapeDtypeStruct((tok, features), full),
+        jax.ShapeDtypeStruct((features, 4 * tok), low),
+        jax.ShapeDtypeStruct((2 * tok, 2 * width), full),
+        jax.ShapeDtypeStruct((4 * tok, width + EXTRA), low),
+        jax.ShapeDtypeStruct(down_own.shape, low),
+    ) + tuple(jax.ShapeDtypeStruct(item.shape, item.dtype) for item in shipped)
+    inside, outside = pl.BlockSpec(memory_space=pltpu.VMEM), pl.BlockSpec(memory_space=pl.ANY)
+    out = pl.pallas_call(
         kernel,
         out_shape=shapes,
-        in_specs=[pl.BlockSpec(memory_space=pltpu.VMEM)] * 4,
-        out_specs=[pl.BlockSpec(memory_space=pltpu.VMEM)] * 4,
-        scratch_shapes=[pltpu.VMEM((2 * tok, features), jnp.bfloat16)] + scratch,
-        compiler_params=pltpu.CompilerParams(collective_id=1, has_side_effects=True, vmem_limit_bytes=60 << 20),
+        in_specs=[inside] * 5 + [outside] * count,
+        out_specs=[inside] * 5 + [outside] * count,
+        scratch_shapes=[
+            pltpu.VMEM((4 * tok, features), low),
+            pltpu.VMEM((2 * tok, features), low),
+            pltpu.VMEM((GROUP_CHUNKS * ROWS, features), full),
+            sem(1 + count), sem(1 + count),
+        ] + scratch,
+        compiler_params=pltpu.CompilerParams(
+            collective_id=1 if count else 5, has_side_effects=True, vmem_limit_bytes=60 << 20
+        ),
         cost_estimate=pl.CostEstimate(flops=60_000_000_000, bytes_accessed=8_000_000, transcendentals=0),
         name="ffn_forward",
-    )(hidden, gain.reshape(1, -1), weight_gu, weight_down)
-
-
-def ffn_backward(grad, hidden, gain, kept, wide_forward, weight_gu, weight_down, depth):
+    )(hidden, gain.reshape(1, -1), gu_own, gu_peer, down_own, *shipped)
+    return out[:5], out[5:]
+
+
+def ffn_backward(grad, hidden, gain, kept, wide_forward, gu_own, gu_peer, down_own, down_peer, shipped, depth):
     tok, features = hidden.shape
-    width = weight_down.shape[1]
+    width = down_own.shape[1]
     run, scratch = make_line(tok, depth, width, 2 * width, False, True, features)
-
-    def kernel(dy_ref, h_ref, gain_ref, kept_ref, before_ref, w1_ref, w2_ref, out_ref, taken, wide, gain_out, product, carried,
-               chain_out, chain_in, own_part, rs_out, rs_in, *sems):
+    count = len(shipped)
+    first_tile = SKEW + 1
+    tiles = width // EXTRA
+
+    def kernel(dy_ref, h_ref, gain_ref, kept_ref, before_ref, w1_own, w1_peer, w2_own, w2_peer, *rest):
+        leave, rest = rest[:count], rest[count:]
+        (out_ref, wide, gain_out, down_kept, down_got), rest = rest[:5], rest[5:]
+        landed, rest = rest[:count], rest[count:]
+        (taken, turned, down_given, pieces, side_s, side_r, product, carried, chain_out, chain_in, own_part, rs_out,
+         rs_in), sems = rest[:13], rest[13:]
         line = Line(tok, depth)
+        side = Side(side_s, side_r)
+        own, other = halves(features)
         taken[pl.ds(line.own, tok), :] = dy_ref[...].astype(jnp.bfloat16)
+        give = side.later(down_given, down_got)
+
+        def begin():
+            for source, target in zip(leave, landed):
+                side.start(source, target)
 
         def prepare(row):
             rows = pl.ds(row, 2 * tok)
 
             def tile(j, _):
-                cols = pl.ds(pl.multiple_of(j * 128, 128), 128)
-                product[rows, cols] = jnp.dot(taken[rows, :], w2_ref[:, cols], preferred_element_type=jnp.float32)
+                cols = pl.ds(pl.multiple_of(j * EXTRA, EXTRA), EXTRA)
+                product[rows, cols] = jnp.dot(
+                    taken[rows, own], w2_own[:, cols], preferred_element_type=jnp.float32
+                ) + jnp.dot(taken[rows, other], w2_peer[:, cols], preferred_element_type=jnp.float32)
                 return 0
 
-            lax.fori_loop(0, width // 128, tile, 0)
+            lax.fori_loop(0, width // EXTRA, tile, 0)
+
+        def beside(i):
+            @pl.when(i == first_tile)
+            def _():
+                turned[...] = flip(taken[...])
+
+            @pl.when((i >= first_tile) & (i < first_tile + tiles))
+            def _():
+                cols = pl.ds(pl.multiple_of((i - first_tile) * EXTRA, EXTRA), EXTRA)
+                grad_tile(turned, features, before_ref, cols, down_kept, down_given)
+
+            @pl.when(i == first_tile + tiles)
+            def _():
+                give.start()
 
         def finish(row, at, total, extra):
             gate = kept_ref[pl.ds(at, ROWS), :width]
@@ -647,7 +762,10 @@
             wide[pl.ds(row, ROWS), 2 * width :] = spread(inner)
 
         def second(row, span):
-            return transposed_dot(wide[pl.ds(row, span), : 2 * width], w1_ref[...])
+            value = wide[pl.ds(row, span), : 2 * width]
+            pieces[:, own] = transposed_dot(value, w1_own[...])
+            pieces[:, other] = transposed_dot(value, w1_peer[...])
+            return pieces[...]
 
         def close():
             total = own_part[...]
@@ -659,26 +777,39 @@
             normed = h_ref[...] * factor
             gain_out[...] = jnp.broadcast_to(jnp.sum(total * normed, axis=0, keepdims=True), gain_out.shape)
             out_ref[...] = dy_ref[...] + factor * (total * gain_ref[...] - normed * (inner / D))
-
-        run(line, taken, prepare, finish, second, close, product, carried, chain_out, chain_in, wide, own_part, rs_out, rs_in,
-            *sems)
-
+            side.finish()
+
+        run(line, taken, begin, prepare, beside, finish, second, lambda: None, close, product, carried, chain_out, chain_in,
+            wide, own_part, rs_out, rs_in, *sems)
+
+    low, full = jnp.bfloat16, jnp.float32
     shapes = (
-        jax.ShapeDtypeStruct((tok, features), jnp.float32),
-        jax.ShapeDtypeStruct((4 * tok, features), jnp.bfloat16),
-        jax.ShapeDtypeStruct((4 * tok, 2 * width + EXTRA), jnp.bfloat16),
-        jax.ShapeDtypeStruct((8, features), jnp.float32),
-    )
-    return pl.pallas_call(
+        jax.ShapeDtypeStruct((tok, features), full),
+        jax.ShapeDtypeStruct((4 * tok, 2 * width + EXTRA), low),
+        jax.ShapeDtypeStruct((8, features), full),
+        jax.ShapeDtypeStruct(down_own.shape, low),
+        jax.ShapeDtypeStruct(down_own.shape, low),
+    ) + tuple(jax.ShapeDtypeStruct(item.shape, item.dtype) for item in shipped)
+    inside, outside = pl.BlockSpec(memory_space=pltpu.VMEM), pl.BlockSpec(memory_space=pl.ANY)
+    out = pl.pallas_call(
         kernel,
         out_shape=shapes,
-        in_specs=[pl.BlockSpec(memory_space=pltpu.VMEM)] * 7,
-        out_specs=[pl.BlockSpec(memory_space=pltpu.VMEM)] * 4,
-        scratch_shapes=scratch,
-        compiler_params=pltpu.CompilerParams(collective_id=2, has_side_effects=True, vmem_limit_bytes=60 << 20),
+        in_specs=[inside] * 9 + [outside] * count,
+        out_specs=[inside] * 5 + [outside] * count,
+        scratch_shapes=[
+            pltpu.VMEM((4 * tok, features), low),
+            pltpu.VMEM((features, 4 * tok), low),
+            pltpu.VMEM(down_own.shape, low),
+            pltpu.VMEM((GROUP_CHUNKS * ROWS, features), full),
+            sem(1 + count), sem(1 + count),
+        ] + scratch,
+        compiler_params=pltpu.CompilerParams(
+            collective_id=2 if count else 6, has_side_effects=True, vmem_limit_bytes=60 << 20
+        ),
         cost_estimate=pl.CostEstimate(flops=60_000_000_000, bytes_accessed=8_000_000, transcendentals=0),
         name="ffn_backward",
-    )(grad, hidden, gain.reshape(1, -1), kept, wide_forward, weight_gu, weight_down)
+    )(grad, hidden, gain.reshape(1, -1), kept, wide_forward, gu_own, gu_peer, down_own, down_peer, *shipped)
+    return out[:5], out[5:]
 
 
 def to_row(column):
@@ -743,12 +874,6 @@
         pl.semaphore_wait(barrier, 3 + 2 * self.depth - 1)
 
 
-def remote(src, dst, send, recv, device):
-    return pltpu.make_async_remote_copy(
-        src_ref=src, dst_ref=dst, send_sem=send, recv_sem=recv, device_id=device, device_id_type=MESH_ID
-    )
-
-
 def start_gather(square, taken, send, recv):
     copies = [
         remote(taken.at[pl.ds(square.own, square.tok)], taken.at[pl.ds(square.own, square.tok)], send.at[at], recv.at[at], peer)
@@ -759,7 +884,7 @@
     return copies
 
 
-def line_sum(square, gather, product, own, own_row, outs, ins, row_outs, row_ins, send, recv, row_send, row_recv):
+def line_sum(square, gather, product, own, own_row, outs, ins, row_outs, row_ins, send, recv, row_send, row_recv, between):
     tok, depth = square.tok, square.depth
 
     def one(order):
@@ -794,6 +919,7 @@
     gather[1].wait_recv()
     gather[2].wait_recv()
     sent += [one(2), one(3)]
+    between()
     for slot in range(depth - 1):
         remote(outs.at[0], ins.at[slot], send.at[0], recv.at[slot], {"z": square.z}).wait_recv()
         if row_ins is not None:
@@ -816,7 +942,7 @@
     return sent
 
 
-def grid_sum(square, array, rows, second, own, outs, ins, row_ins, arrive, row_arrive, send, recv, row_send, row_recv):
+def grid_sum(square, array, rows, second, settle, own, outs, ins, row_ins, arrive, row_arrive, send, recv, row_send, row_recv):
     tok, depth = square.tok, square.depth
     sent = []
     for step in range(depth):
@@ -846,6 +972,7 @@
                 row_copy.start()
 
         sent.append((away, copy, row_copy))
+    settle()
     for slot in range(depth - 1):
         remote(outs.at[0], ins.at[slot], send.at[0], recv.at[slot], square.peers[0]).wait_recv()
         if row_ins is not None:
@@ -863,35 +990,55 @@
                 row_copy.wait_send()
 
 
-def sem(*shape):
-    return pltpu.SemaphoreType.DMA(shape)
-
-
-def attention_forward(hidden, gain, weight_qkv, weight_out, cosine, sine, depth):
+def attention_forward(hidden, gain, qkv_own, out_own, qkv_peer, out_peer, shipped, cosine, sine, depth):
     tok, features = hidden.shape
-    cols = weight_qkv.shape[1]
+    cols = qkv_own.shape[1]
+    fetch = qkv_peer is None
+    extra = 2 if fetch else 0
+    count = len(shipped)
+    sides = extra + 2 * count
     query_cols = GROUP * HEAD
     seq = 2 * depth * tok
     pairs = query_cols // EXTRA
     scale = 1.0 / math.sqrt(HEAD)
 
-    def kernel(h_ref, gain_ref, wqkv_ref, wo_ref, cos_ref, sin_ref, out_ref, taken, queries, kv, lse, mixed, factors,
-               own, own_row, z_out, z_in, zr_out, zr_in, values_t, g_own, g_out, g_in,
-               ag_s, ag_r, zs_s, zs_r, zr_s, zr_r, kv_s, kv_r, zg_s, zg_r, zgr_s, zgr_r, gs_s, gs_r):
+    def kernel(h_ref, gain_ref, wqkv_own, wo_own, cos_ref, sin_ref, *rest):
+        if not fetch:
+            (wqkv_peer, wo_peer), rest = rest[:2], rest[2:]
+        leave, rest = rest[:count], rest[count:]
+        (out_ref, normed_t, queries, kv, lse, mixed, factors), rest = rest[:7], rest[7:]
+        if fetch:
+            (wqkv_peer, wo_peer), rest = rest[:2], rest[2:]
+        landed, rest = rest[:count], rest[count:]
+        (taken, scaled, pieces, own, own_row, z_out, z_in, zr_out, zr_in, values_t, g_own, g_out, g_in,
+         ag_s, ag_r, zs_s, zs_r, zr_s, zr_r, kv_s, kv_r, zg_s, zg_r, zgr_s, zgr_r, gs_s, gs_r), rest = rest[:27], rest[27:]
         square = Square(tok, depth)
+        side = Side(*rest) if sides else None
+        mine, other = halves(features)
         taken[pl.ds(square.own, tok), :] = h_ref[...].astype(jnp.bfloat16)
         square.greet()
         gather = start_gather(square, taken, ag_s, ag_r)
+        urgent = []
+        if fetch:
+            urgent = [side.start(wqkv_own, wqkv_peer), side.start(wo_own, wo_peer)]
+        held = []
+        for source, target in zip(leave, landed):
+            half = source.shape[0] // 2
+            side.start(source.at[pl.ds(0, half)], target.at[pl.ds(0, half)])
+            held.append(side.later(source.at[pl.ds(half, half)], target.at[pl.ds(half, half)]))
+        for copy in urgent[:1]:
+            copy.wait_recv()
 
         def product(row):
             block = taken[pl.ds(row, tok), :].astype(jnp.float32)
-            scaled = (block * gain_ref[...]).astype(jnp.bfloat16)
+            scaled[...] = (block * gain_ref[...]).astype(jnp.bfloat16)
             return (
-                jnp.dot(scaled, wqkv_ref[...], preferred_element_type=jnp.float32),
+                jnp.dot(scaled[:, mine], wqkv_own[...], preferred_element_type=jnp.float32)
+                + jnp.dot(scaled[:, other], wqkv_peer[...], preferred_element_type=jnp.float32),
                 jnp.sum(block * block, axis=1, keepdims=True),
             )
 
-        sent = line_sum(square, gather, product, own, own_row, z_out, z_in, zr_out, zr_in, zs_s, zs_r, zr_s, zr_r)
+        sent = line_sum(square, gather, product, own, own_row, z_out, z_in, zr_out, zr_in, zs_s, zs_r, zr_s, zr_r, lambda: None)
         total, squares = own[...], own_row[...]
         for slot in range(depth - 1):
             total = total + z_in[slot].astype(jnp.float32)
@@ -909,6 +1056,8 @@
             spreads.append(copy)
         for copy in spreads:
             copy.wait_recv()
+        for copy in held:
+            copy.start()
         keys, both = twice(kv[...])
         values_t[...] = jnp.transpose(both).astype(jnp.bfloat16)
         keys = keys.astype(jnp.bfloat16)
@@ -931,10 +1080,22 @@
         lax.fori_loop(0, pairs, pair, 0)
         given = line_gather(square, mixed, factors, zg_s, zg_r, zgr_s, zgr_r)
 
+        for copy in urgent[1:]:
+            copy.wait_recv()
+
         def second(row):
-            return transposed_dot(mixed[pl.ds(row, tok), :], wo_ref[...])
-
-        sums = grid_sum(square, mixed, factors, second, g_own, g_out, g_in, None, zg_r, zgr_r, gs_s, gs_r, None, None)
+            value = mixed[pl.ds(row, tok), :]
+            pieces[:, mine] = transposed_dot(value, wo_own[...])
+            pieces[:, other] = transposed_dot(value, wo_peer[...])
+            return pieces[...]
+
+        def settle():
+            for block in range(depth):
+                rows = pl.ds(block * tok, tok)
+                normed = taken[rows, :].astype(jnp.float32) * to_column(factors[block]) * gain_ref[...]
+                normed_t[:, rows] = jnp.transpose(normed).astype(jnp.bfloat16)
+
+        sums = grid_sum(square, mixed, factors, second, settle, g_own, g_out, g_in, None, zg_r, zgr_r, gs_s, gs_r, None, None)
         total = g_own[...]
         for slot in range(depth - 1):
             total = total + g_in[slot].astype(jnp.float32)
@@ -943,23 +1104,33 @@
         drain(sums)
         for copy in gather + spreads + given:
             copy.wait_send()
+        if side:
+            side.finish(urgent)
 
     low, full = jnp.bfloat16, jnp.float32
     shapes = (
         jax.ShapeDtypeStruct((tok, features), full),
-        jax.ShapeDtypeStruct((depth * tok, features), low),
+        jax.ShapeDtypeStruct((features, depth * tok), low),
         jax.ShapeDtypeStruct((tok, query_cols), low),
         jax.ShapeDtypeStruct((seq, 2 * HEAD), low),
         jax.ShapeDtypeStruct((pairs, 8, 2 * tok), full),
         jax.ShapeDtypeStruct((depth * tok, query_cols), low),
         jax.ShapeDtypeStruct((depth, 8, tok), full),
     )
-    return pl.pallas_call(
+    if fetch:
+        shapes += (jax.ShapeDtypeStruct(qkv_own.shape, low), jax.ShapeDtypeStruct(out_own.shape, low))
+    shapes += tuple(jax.ShapeDtypeStruct(item.shape, item.dtype) for item in shipped)
+    inside, outside = pl.BlockSpec(memory_space=pltpu.VMEM), pl.BlockSpec(memory_space=pl.ANY)
+    peers = () if fetch else (qkv_peer, out_peer)
+    out = pl.pallas_call(
         kernel,
         out_shape=shapes,
-        in_specs=[pl.BlockSpec(memory_space=pltpu.VMEM)] * 6,
-        out_specs=[pl.BlockSpec(memory_space=pltpu.VMEM)] * 7,
+        in_specs=[inside] * (6 + len(peers)) + [outside] * count,
+        out_specs=[inside] * (7 + extra) + [outside] * count,
         scratch_shapes=[
+            pltpu.VMEM((depth * tok, features), low),
+            pltpu.VMEM((tok, features), low),
+            pltpu.VMEM((tok, features), full),
             pltpu.VMEM((tok, cols), full),
             pltpu.VMEM((8, tok), full),
             pltpu.VMEM((depth, tok, cols), low),
@@ -973,34 +1144,69 @@
             sem(3), sem(3), sem(depth), sem(depth - 1), sem(depth), sem(depth - 1),
             sem(2 * depth - 1), sem(2 * depth - 1), sem(depth - 1), sem(depth - 1), sem(depth - 1), sem(depth - 1),
             sem(depth), sem(depth - 1),
-        ],
-        compiler_params=pltpu.CompilerParams(collective_id=3, has_side_effects=True, vmem_limit_bytes=60 << 20),
+        ] + ([sem(sides), sem(sides)] if sides else []),
+        compiler_params=pltpu.CompilerParams(
+            collective_id=3 if fetch else 7, has_side_effects=True, vmem_limit_bytes=60 << 20
+        ),
         cost_estimate=pl.CostEstimate(flops=50_000_000_000, bytes_accessed=8_000_000, transcendentals=0),
         name="attention_forward",
-    )(hidden, gain.reshape(1, -1), weight_qkv, weight_out, cosine, sine)
-
-
-def attention_backward(grad, hidden, gain, weight_qkv, weight_out, cosine, sine, queries, kv, lse, factors, depth):
+    )(hidden, gain.reshape(1, -1), qkv_own, out_own, cosine, sine, *peers, *shipped)
+    peers = out[7:9] if fetch else peers
+    return out[:7], peers, out[7 + extra :]
+
+
+def attention_backward(
+    grad, hidden, gain, qkv_own, qkv_peer, out_own, out_peer, cosine, sine, queries, kv, lse, factors, mixed, normed_a, normed_f,
+    grad_gu, depth,
+):
     tok, features = hidden.shape
-    cols = weight_qkv.shape[1]
+    cols = qkv_own.shape[1]
+    wide = grad_gu.shape[1] - EXTRA
     query_cols = GROUP * HEAD
     seq = 2 * depth * tok
     pairs = query_cols // EXTRA
     scale = 1.0 / math.sqrt(HEAD)
 
-    def kernel(dy_ref, h_ref, gain_ref, wqkv_ref, wo_ref, cos_ref, sin_ref, q_ref, kv_ref, lse_ref, factor_ref,
-               out_ref, taken, spun, gain_out,
-               own, heads, z_out, z_in, keys_t, dk, dv, kv_out, kv_own, kv_in, dq, inner_rows, g_own, g_out, g_in, g_rows,
-               ag_s, ag_r, zs_s, zs_r, kv_s, kv_r, zg_s, zg_r, zgr_s, zgr_r, gs_s, gs_r, gr_s, gr_r):
+    def kernel(dy_ref, h_ref, gain_ref, wqkv_own, wqkv_peer, wo_own, wo_peer, cos_ref, sin_ref, q_ref, kv_ref, lse_ref,
+               factor_ref, mixed_ref, normed_a_ref, normed_f_ref, gu_ref,
+               out_ref, gain_out, gu_kept, gu_got, out_kept, out_got, qkv_kept, qkv_given,
+               taken, spun, turned, pieces, gu_given, out_given,
+               own, heads, z_out, z_in, keys_t, dk, dv, kv_out, kv_in, dq, inner_rows, g_own, g_out, g_in, g_rows,
+               ag_s, ag_r, zs_s, zs_r, kv_s, kv_r, zg_s, zg_r, zgr_s, zgr_r, gs_s, gs_r, gr_s, gr_r, side_s, side_r):
         square = Square(tok, depth)
+        side = Side(side_s, side_r)
+        mine, other = halves(features)
         taken[pl.ds(square.own, tok), :] = dy_ref[...].astype(jnp.bfloat16)
         square.greet()
         gather = start_gather(square, taken, ag_s, ag_r)
 
+        def gu_tiles(start, stop):
+            def tile(j, _):
+                grad_tile(normed_f_ref, features, gu_ref, pl.ds(pl.multiple_of(j * EXTRA, EXTRA), EXTRA), gu_kept, gu_given)
+                return 0
+
+            lax.fori_loop(start, stop, tile, 0)
+
+        middle = wide // EXTRA // 2
+        gu_tiles(0, middle)
+        front, rest = pl.ds(0, middle * EXTRA), pl.ds(middle * EXTRA, wide - middle * EXTRA)
+        side.start(gu_given.at[:, front], gu_got.at[:, front])
+
+        def between():
+            turned[...] = flip(taken[...])
+            for t in range(query_cols // EXTRA):
+                grad_tile(turned, features, mixed_ref, pl.ds(t * EXTRA, EXTRA), out_kept, out_given)
+            side.start(out_given, out_got)
+            gu_tiles(middle, wide // EXTRA)
+
         def product(row):
-            return jnp.dot(taken[pl.ds(row, tok), :], wo_ref[...], preferred_element_type=jnp.float32), None
-
-        sent = line_sum(square, gather, product, own, None, z_out, z_in, None, None, zs_s, zs_r, None, None)
+            rows = pl.ds(row, tok)
+            value = jnp.dot(taken[rows, mine], wo_own[...], preferred_element_type=jnp.float32) + jnp.dot(
+                taken[rows, other], wo_peer[...], preferred_element_type=jnp.float32
+            )
+            return value, None
+
+        sent = line_sum(square, gather, product, own, None, z_out, z_in, None, None, zs_s, zs_r, None, None, between)
         total = own[...]
         for slot in range(depth - 1):
             total = total + z_in[slot].astype(jnp.float32)
@@ -1054,6 +1260,7 @@
         total_kv = dk[here, :]
         for copy in spreads:
             copy.wait_recv()
+        side.start(gu_given.at[:, rest], gu_got.at[:, rest])
         for slot in range(2 * depth - 1):
             total_kv = total_kv + kv_in[slot].astype(jnp.float32)
         inner = jnp.sum(dq[...] * q_ref[...].astype(jnp.float32), axis=1, keepdims=True) + jnp.sum(
@@ -1065,10 +1272,17 @@
         given = line_gather(square, spun, inner_rows, zg_s, zg_r, zgr_s, zgr_r)
 
         def second(row):
-            return transposed_dot(spun[pl.ds(row, tok), :], wqkv_ref[...])
+            value = spun[pl.ds(row, tok), :]
+            pieces[:, mine] = transposed_dot(value, wqkv_own[...])
+            pieces[:, other] = transposed_dot(value, wqkv_peer[...])
+            return pieces[...]
+
+        def settle():
+            for t in range(cols // EXTRA):
+                grad_tile(normed_a_ref, features, spun, pl.ds(t * EXTRA, EXTRA), qkv_kept, qkv_given)
 
         sums = grid_sum(
-            square, spun, inner_rows, second, g_own, g_out, g_in, g_rows, zg_r, zgr_r, gs_s, gs_r, gr_s, gr_r
+            square, spun, inner_rows, second, settle, g_own, g_out, g_in, g_rows, zg_r, zgr_r, gs_s, gs_r, gr_s, gr_r
         )
         total = g_own[...]
         inner = inner_rows[square.g]
@@ -1083,20 +1297,31 @@
         drain(sums)
         for copy in gather + spreads + given:
             copy.wait_send()
+        side.finish()
 
     low, full = jnp.bfloat16, jnp.float32
     shapes = (
         jax.ShapeDtypeStruct((tok, features), full),
-        jax.ShapeDtypeStruct((depth * tok, features), low),
-        jax.ShapeDtypeStruct((depth * tok, cols), low),
         jax.ShapeDtypeStruct((8, features), full),
+        jax.ShapeDtypeStruct((features // 2, wide), low),
+        jax.ShapeDtypeStruct((features // 2, wide), low),
+        jax.ShapeDtypeStruct(out_own.shape, low),
+        jax.ShapeDtypeStruct(out_own.shape, low),
+        jax.ShapeDtypeStruct(qkv_own.shape, low),
+        jax.ShapeDtypeStruct(qkv_own.shape, low),
     )
     return pl.pallas_call(
         kernel,
         out_shape=shapes,
-        in_specs=[pl.BlockSpec(memory_space=pltpu.VMEM)] * 11,
-        out_specs=[pl.BlockSpec(memory_space=pltpu.VMEM)] * 4,
+        in_specs=[pl.BlockSpec(memory_space=pltpu.VMEM)] * 17,
+        out_specs=[pl.BlockSpec(memory_space=pltpu.VMEM)] * 8,
         scratch_shapes=[
+            pltpu.VMEM((depth * tok, features), low),
+            pltpu.VMEM((depth * tok, cols), low),
+            pltpu.VMEM((features, depth * tok), low),
+            pltpu.VMEM((tok, features), full),
+            pltpu.VMEM((features // 2, wide), low),
+            pltpu.VMEM(out_own.shape, low),
             pltpu.VMEM((tok, query_cols), full),
             pltpu.VMEM((tok, query_cols), low),
             pltpu.VMEM((depth, tok, query_cols), low),
@@ -1105,7 +1330,6 @@
             pltpu.VMEM((seq, 2 * HEAD), full),
             pltpu.VMEM((seq, 2 * HEAD), full),
             pltpu.VMEM((seq, 2 * HEAD), low),
-            pltpu.VMEM((tok, 2 * HEAD), full),
             pltpu.VMEM((2 * depth - 1, tok, 2 * HEAD), low),
             pltpu.VMEM((tok, query_cols), full),
             pltpu.VMEM((depth, 8, tok), full),
@@ -1115,12 +1339,13 @@
             pltpu.VMEM((depth - 1, 8, tok), full),
             sem(3), sem(3), sem(depth), sem(depth - 1),
             sem(2 * depth - 1), sem(2 * depth - 1), sem(depth - 1), sem(depth - 1), sem(depth - 1), sem(depth - 1),
-            sem(depth), sem(depth - 1), sem(depth), sem(depth - 1),
+            sem(depth), sem(depth - 1), sem(depth), sem(depth - 1), sem(3), sem(3),
         ],
         compiler_params=pltpu.CompilerParams(collective_id=4, has_side_effects=True, vmem_limit_bytes=60 << 20),
         cost_estimate=pl.CostEstimate(flops=50_000_000_000, bytes_accessed=8_000_000, transcendentals=0),
         name="attention_backward",
-    )(grad, hidden, gain.reshape(1, -1), weight_qkv, weight_out, cosine, sine, queries, kv, lse, factors)
+    )(grad, hidden, gain.reshape(1, -1), qkv_own, qkv_peer, out_own, out_peer, cosine, sine, queries, kv, lse, factors, mixed,
+      normed_a, normed_f, grad_gu)
 
 
 def stationary(stream, grad_out, wqkv, wo, wgu, wd, gain_attn, gain_ffn):
@@ -1140,47 +1365,55 @@
     sine = jnp.concatenate(
         [jnp.tile(jnp.concatenate([-sine, sine], axis=1), (1, turns)), jnp.zeros((tok, head), jnp.float32)], axis=1
     )
-    whole = lambda shard: lax.all_gather(shard, "x", axis=0, tiled=True)
     current = swap_grid(stream, depth)
     grad_now = swap_grid(grad_out, depth)
     gain_a = swap_grid(gain_attn, depth)
     gain_f = swap_grid(gain_ffn, depth)
+    own_qkv = [wqkv[index].reshape(count_rows, -1) for index in range(layers)]
+    own_out = [wo[index] for index in range(layers)]
+    own_gu = [wgu[index].reshape(count_rows, -1) for index in range(layers)]
+    own_down = [wd[index] for index in range(layers)]
+    peer_qkv, peer_out, peer_gu, peer_down = ([None] * layers for _ in range(4))
     saved = []
     for index in range(layers):
-        weight_qkv = whole(wqkv[index].reshape(count_rows, -1))
-        weight_out = whole(wo[index])
-        weight_gu = whole(wgu[index].reshape(count_rows, -1))
-        weight_down = whole(wd[index])
         before = current
-        hidden_in, xfull, queries, kv, lse, mixed_full, factors = attention_forward(
-            before, gain_a[index], weight_qkv, weight_out, cosine, sine, depth
-        )
-        current, hfull, kept, active = ffn_forward(hidden_in, gain_f[index], weight_gu, weight_down, depth)
-        saved.append(
-            (weight_qkv, weight_out, weight_gu, weight_down, before, xfull, queries, kv, lse, mixed_full, factors,
-             hidden_in, hfull, kept, active)
-        )
+        (hidden_in, normed_a, queries, kv, lse, mixed, factors), (peer_qkv[index], peer_out[index]), landed = attention_forward(
+            before, gain_a[index], own_qkv[index], own_out[index], peer_qkv[index], peer_out[index],
+            [] if index else own_gu[:1], cosine, sine, depth
+        )
+        if landed:
+            peer_gu[0] = landed[0]
+        follow = index + 1
+        shipped = [own_qkv[follow], own_out[follow], own_gu[follow]] if follow < layers else []
+        (current, normed_f, kept, active, peer_down[index]), landed = ffn_forward(
+            hidden_in, gain_f[index], own_gu[index], peer_gu[index], own_down[index], shipped, depth
+        )
+        if landed:
+            peer_qkv[follow], peer_out[follow], peer_gu[follow] = landed
+        saved.append((before, normed_a, queries, kv, lse, mixed, factors, hidden_in, normed_f, kept, active))
     list_qkv, list_out, list_gu, list_down, list_ga, list_gf = ([], [], [], [], [], [])
+    pending = []
+    add = lambda kept, got: kept.astype(jnp.float32) + got.astype(jnp.float32)
     for index in reversed(range(layers)):
-        (weight_qkv, weight_out, weight_gu, weight_down, before, xfull, queries, kv, lse, mixed_full, factors,
-         hidden_in, hfull, kept, active) = saved[index]
-        width = weight_down.shape[1]
-        grad_hidden, grad_full, grad_gu, gain_f_grad = ffn_backward(
-            grad_now, hidden_in, gain_f[index], kept, active, weight_gu, weight_down, depth
-        )
-        list_down.append(pair_grad(grad_full, active[:, :width]))
-        factor_f = jnp.sum(active[:, width:].astype(jnp.float32), axis=1, keepdims=True)
-        hnormed = (hfull.astype(jnp.float32) * factor_f * gain_f[index]).astype(jnp.bfloat16)
-        list_gu.append(pair_grad(hnormed, grad_gu[:, : 2 * width]).reshape(count_rows, 2, -1))
+        before, normed_a, queries, kv, lse, mixed, factors, hidden_in, normed_f, kept, active = saved[index]
+        (grad_hidden, grad_gu, gain_f_grad, down_kept, down_got), landed = ffn_backward(
+            grad_now, hidden_in, gain_f[index], kept, active, own_gu[index], peer_gu[index], own_down[index],
+            peer_down[index], pending[-1:], depth
+        )
+        if landed:
+            list_qkv.append(add(qkv_kept, landed[0]))
+        list_down.append(add(down_kept, down_got))
         list_gf.append(gain_f_grad[0])
-        grad_now, hidden_full, grad_qkv, gain_a_grad = attention_backward(
-            grad_hidden, before, gain_a[index], weight_qkv, weight_out, cosine, sine, queries, kv, lse, factors, depth
-        )
-        list_out.append(pair_grad(hidden_full, mixed_full))
-        factor_a = factors[:, 0, :].reshape(-1, 1)
-        xnormed = (xfull.astype(jnp.float32) * factor_a * gain_a[index]).astype(jnp.bfloat16)
-        list_qkv.append(pair_grad(xnormed, grad_qkv).reshape(count_rows, 1, -1))
+        (grad_now, gain_a_grad, gu_kept, gu_got, out_kept, out_got, qkv_kept, qkv_given) = attention_backward(
+            grad_hidden, before, gain_a[index], own_qkv[index], peer_qkv[index], own_out[index], peer_out[index],
+            cosine, sine, queries, kv, lse, factors, mixed, normed_a, normed_f, grad_gu, depth
+        )
+        pending.append(qkv_given)
+        list_gu.append(add(gu_kept, gu_got).reshape(count_rows, 2, -1))
+        list_out.append(add(out_kept, out_got))
         list_ga.append(gain_a_grad[0])
+    list_qkv.append(add(qkv_kept, lax.ppermute(qkv_given, "x", [(0, 1), (1, 0)])))
+    list_qkv = [item.reshape(count_rows, 1, -1) for item in list_qkv]
     gains = lax.psum(jnp.concatenate([jnp.stack(list_ga[::-1]), jnp.stack(list_gf[::-1])]), ("x", "y", "c"))
     gains = swap_grid(gains, depth)
     return (

time: 895 us -> 674 us (0.75)
  waiting for transfers between devices: 147 us -> 1.54 us
  blocking collectives: 65 us -> 13.6 us
  matrix products: 23.8 us -> 0 us
  between operations: 15.1 us -> 1.39 us
    reduce_scatter x8 -> x0, waiting for transfers between devices: 143 us -> none  [pair_grad(): lax.psum_scatter(lax.dot_general(left, right, (((0,), (0,)), ((), ())), p...]
    all_gather x4 -> x0, blocking collectives: 51 us -> none  [stationary(): whole = lambda shard: lax.all_gather(shard, 'x', axis=0, tiled=True)]
    dot_general x8 -> x0, matrix products: 23.8 us -> none  [pair_grad(): lax.dot_general(left, right, (((0,), (0,)), ((), ())), preferred_element_...]
  transfers between devices with their start and end apart: 19 -> 8, of which waited for: 6 -> 1; matrix products, arithmetic and copies ran while one was open for 5% -> 6% of each run, Pallas kernels for 32% -> 86%
where the time goes in v4:
time: 674 us; the launch traced here: 662 us
  Pallas kernels  569 us (84%)
  local copies, waits for them, and re-layouts  32.2 us (5%)
  starting transfers between devices  28.7 us (4%)
  other arithmetic  15.5 us (2%)
  blocking collectives  13.6 us (2%)
    pallas_call x2, Pallas kernels, ffn_backward(): pl.pallas_call(kernel, out_shape=shapes, in_specs=[inside] * 9 + [outside...  170 us
    pallas_call x2, Pallas kernels, ffn_forward(): pl.pallas_call(kernel, out_shape=shapes, in_specs=[inside] * 5 + [outside...  169 us
    pallas_call x2, Pallas kernels, attention_backward(): pl.pallas_call(kernel, out_shape=shapes, in_specs=[pl.BlockSpec(memory_sp...  116 us
    pallas_call x2, Pallas kernels, attention_forward(): pl.pallas_call(kernel, out_shape=shapes, in_specs=[inside] * (6 + len(pee...  113 us
    ppermute x7, starting transfers between devices, swap_grid(): return lax.ppermute(values, ('z', 'y', 'c'), pairs)  26.5 us
    psum x1, blocking collectives, stationary(): lax.psum(jnp.concatenate([jnp.stack(list_ga[::-1]), jnp.stack(list_gf[::-...  13.6 us
  transfers between devices with their start and end apart: 8, of which 1 were waited for; matrix products, arithmetic and copies ran while one was open for 6% of the time, Pallas kernels for 86%

profile of v4, /device:TPU:4, one launch (start us, length us, event | category | flops | bytes accessed | tf_op | source)
XLA Modules:
  0.0 662.4 jit_solution(570695264041448188)
XLA Ops:
  0.7 4.6 collective-permute-start.1
  5.2 3.2 collective-permute-start.2
  8.4 4.4 collective-permute-start
  12.9 3.2 collective-permute-start.4
  16.1 1.9 slice_bitcast_fusion.4
  18.0 0.9 slice_bitcast_fusion.2
  18.9 1.2 slice_bitcast_fusion
  20.1 1.1 copy-done.2
  21.2 2.0 fusion.1
  23.3 0.1 fusion
  23.5 0.2 copy.18
  23.6 0.8 tile.8
  24.4 1.1 copy.17
  25.5 1.3 copy.21
  26.8 1.3 copy.20
  28.0 0.8 concatenate.14.sin_ref
  28.8 0.8 concatenate.12.cos_ref
  29.6 0.0 collective-permute-done.1
  29.6 0.6 fusion.4
  30.2 0.0 collective-permute-done.2
  30.2 0.6 fusion.3
  30.8 1.5 collective-permute-done.h_ref
  32.3 56.3 %attention_forward.2 = (f32[128,512]{1,0:T(8,128)}, bf16[512,512]{1,0:T(8,128)(2,1)}, bf16[128,512]{1,0:T(8,128)(2,1)}, bf16[1024,128]{1,0:T(8,128)(2,1)}, f32[4...) custom-call(f32[128,512]{1,0:T(8,128)} %collective-permute-done.h_re, ...), custom_call_target="tpu_custom_call" | custom-call | flops 49999998976 | bytes 8000000 | tf_op jit(solution)/shard_map/attention_forward/pallas_call | solution.py:1125
  88.6 85.6 %ffn_forward.2 = (f32[128,512]{1,0:T(8,128)}, bf16[512,512]{1,0:T(8,128)(2,1)}, f32[256,2816]{1,0:T(8,128)}, bf16[512,1536]{1,0:T(8,128)(2,1)}, bf16[256,1408]{1...) custom-call(f32[128,512]{1,0:T(8,128)} %get-tuple-element.65.h_ref, ...), custom_call_target="tpu_custom_call" | custom-call | flops 60000002048 | bytes 8000000 | tf_op jit(solution)/shard_map/ffn_forward/pallas_call | solution.py:682
  174.2 57.0 %attention_forward.3 = (f32[128,512]{1,0:T(8,128)}, bf16[512,512]{1,0:T(8,128)(2,1)}, bf16[128,512]{1,0:T(8,128)(2,1)}, bf16[1024,128]{1,0:T(8,128)(2,1)}, f32[4...) custom-call(f32[128,512]{1,0:T(8,128)} %get-tuple-element.67.h_ref, ...), custom_call_target="tpu_custom_call" | custom-call | flops 49999998976 | bytes 8000000 | tf_op jit(solution)/shard_map/attention_forward/pallas_call | solution.py:1125
  231.2 83.8 %ffn_forward.3 = (f32[128,512]{1,0:T(8,128)}, bf16[512,512]{1,0:T(8,128)(2,1)}, f32[256,2816]{1,0:T(8,128)}, bf16[512,1536]{1,0:T(8,128)(2,1)}, bf16[256,1408]{1,0:T(8,128)(2,1)}) custom-call(f32[128,512]{1,0:T(8,128)} %get-tuple-element.70.h_ref, f32[1,512]{1,0:T(1,128)} %get-tuple-element.148.gain_ref, bf16[256,2816]{1,0:T(8,128)(2,1)} %bitcast.38, ...), custom_call_target="tpu_custom_call" | custom-call | flops 60000002048 | bytes 8000000 | tf_op jit(solution)/shard_map/ffn_forward/pallas_call | solution.py:682
  315.0 1.9 collective-permute-start.3
  316.9 0.0 collective-permute-done.4.dy_ref
  316.9 85.2 %ffn_backward.2 = (f32[128,512]{1,0:T(8,128)}, bf16[512,2944]{1,0:T(8,128)(2,1)}, f32[8,512]{1,0:T(8,128)}, bf16[256,1408]{1,0:T(8,128)(2,1)}, bf16[256,1408]{1,0:T(8,128)(2,1)}) custom-call(f32[128,512]{1,0:T(8,128)} %collective-permute-done.4.dy_ref, f32[128,512]{1,0:T(8,128)} %get-tuple-element.70.h_ref, f32[1,512]{1,0:T(1,128)} %get-tuple-element.148.gain_ref, ...), custom_call_target="tpu_custom_call" | custom-call | flops 60000002048 | bytes 8000000 | tf_op jit(solution)/shard_map/ffn_backward/pallas_call | solution.py:794
  402.2 57.9 %attention_backward.2 = (f32[128,512]{1,0:T(8,128)}, f32[8,512]{1,0:T(8,128)}, bf16[256,2816]{1,0:T(8,128)(2,1)}, bf16[256,2816]{1,0:T(8,128)(2,1)}, bf16[256,51...) custom-call(f32[128,512]{1,0:T(8,128)} %get-tuple-element.76.dy_ref, ...), custom_call_target="tpu_custom_call" | custom-call | flops 49999998976 | bytes 8000000 | tf_op jit(solution)/shard_map/attention_backward/pallas_call | solution.py:1313
  460.1 85.3 %ffn_backward.3 = (f32[128,512]{1,0:T(8,128)}, bf16[512,2944]{1,0:T(8,128)(2,1)}, f32[8,512]{1,0:T(8,128)}, bf16[256,1408]{1,0:T(8,128)(2,1)}, bf16[256,1408]{1,0:T(8,128)(2,1)}, /*index=5*/bf16[256,640]{1,0:T(8,128)(2,1)}) custom-call(f32[128,512]{1,0:T(8,128)} %get-tuple-element.85.dy_ref, f32[128,512]{1,0:T(8,128)} %get-tuple-element.65.h_ref, ...), custom_call_target="tpu_custom_call" | custom-call | flops 60000002048 | bytes 8000000 | tf_op jit(solution)/shard_map/ffn_backward/pallas_call | solution.py:794
  545.3 58.4 %attention_backward.3 = (f32[128,512]{1,0:T(8,128)}, f32[8,512]{1,0:T(8,128)}, bf16[256,2816]{1,0:T(8,128)(2,1)}, bf16[256,2816]{1,0:T(8,128)(2,1)}, bf16[256,51...) custom-call(f32[128,512]{1,0:T(8,128)} %get-tuple-element.90.dy_ref, ...), custom_call_target="tpu_custom_call" | custom-call | flops 49999998976 | bytes 8000000 | tf_op jit(solution)/shard_map/attention_backward/pallas_call | solution.py:1313
  603.7 0.7 slice.70
  604.5 0.7 slice.72
  605.2 0.7 slice.71
  605.9 0.7 slice.73
  606.6 13.6 %psum.7 = f32[4,512]{1,0:T(4,128)S(1)} all-reduce(f32[4,512]{1,0:T(4,128)S(1)} %pad_maximum_fusion.5), channel_id=1, replica_groups=mesh['z'=4,'x'=2,'y'=2,'c'=2] {'x','y','c'}, use_global_device_ids=true, to_apply=%region_0.0 | all-reduce | flops 2048 | bytes 16384 | tf_op jit(solution)/shard_map/psum | solution.py:1417
  620.2 7.0 %collective-permute-start.7 = (f32[4,512]{1,0:T(4,128)S(1)}, f32[4,512]{1,0:T(4,128)S(1)}, u32[]{:S(2)}, u32[]{:S(2)}) collective-permute-start(f32[4,512]{1,0:T(4,128)S(1)} %psum.7), channel_id=1, source_target_pairs={{0,0},{1,8},{2,16},{3,24},{8,1},{9,9},{10,17},{11,25},{16,2},{17,1... | collective-permute-start | bytes 24584 | tf_op jit(solution)/shard_map/ppermute | solution.py:265
  627.2 2.2 collective-permute-start.5
  629.3 2.2 collective-permute-start.6
  631.5 2.1 convert_add_fusion.1
  633.6 2.8 stack_reshape.14
  636.4 2.1 convert_add_fusion
  638.5 2.8 stack_reshape.15
  641.3 0.1 add_bitcast_fusion.2
  641.4 1.0 copy-done.4
  642.4 1.8 add_bitcast_fusion
  644.2 0.0 copy-start.1
  644.3 1.8 pad_maximum_fusion.1
  646.0 1.1 copy-done
  647.1 0.9 copy-done.1
  648.0 5.2 pad_maximum_fusion
  653.2 0.2 add_bitcast_fusion.4
  653.4 1.0 pad_maximum_fusion.3
  654.4 0.0 collective-permute-done.7
  654.4 0.6 fusion.2
  655.0 0.0 collective-permute-done.3
  655.0 0.0 collective-permute-done.5
  655.0 0.0 collective-permute-done.6
  655.0 1.0 add_bitcast_fusion.3
  656.1 0.1 pad_maximum_fusion.2
  656.2 2.4 copy.19
  658.6 1.7 copy.24
  660.2 1.7 copy.25
  (26 shorter events, 0.1 us)
Async XLA Ops:
  0.6 17.4 %copy-start.5 = (bf16[2,256,1,640]{3,1,2,0:T(8,128)(2,1)S(1)}, bf16[2,256,1,640]{3,1,2,0:T(8,128)(2,1)}, u32[]{:S(2)}) copy-start(bf16[2,256,1,640]{3,1,2,0:T(8,128)(2,1)} %param.10) | copy-start | bytes 1966084
  0.6 18.3 %copy-start.3 = (bf16[2,256,1408]{2,1,0:T(8,128)(2,1)S(1)}, bf16[2,256,1408]{2,1,0:T(8,128)(2,1)}, u32[]{:S(2)}) copy-start(bf16[2,256,1408]{2,1,0:T(8,128)(2,1)} %param.13) | copy-start | bytes 4325380
  0.7 28.9 %collective-permute-start.1 = (f32[2,512]{1,0:T(2,128)}, f32[2,512]{1,0:T(2,128)S(1)}, u32[]{:S(2)}, u32[]{:S(2)}) collective-permute-start(f32[2,512]{1,0:T(2,128)} %param.14), channel_id=1, source_target_pairs={{0,0},{1,8},{2,16},{3,24},{8,1},{9,9},{10,17},{11,25},{16,2},{17,1... | collective-permute-start | bytes 12296 | tf_op jit(solution)/shard_map/ppermute | solution.py:265
  5.2 24.9 %collective-permute-start.2 = (f32[2,512]{1,0:T(2,128)}, f32[2,512]{1,0:T(2,128)S(1)}, u32[]{:S(2)}, u32[]{:S(2)}) collective-permute-start(f32[2,512]{1,0:T(2,128)} %param.15), channel_id=1, source_target_pairs={{0,0},{1,8},{2,16},{3,24},{8,1},{9,9},{10,17},{11,25},{16,2},{17,1... | collective-permute-start | bytes 12296 | tf_op jit(solution)/shard_map/ppermute | solution.py:265
  8.4 23.8 %collective-permute-start = (f32[128,512]{1,0:T(8,128)}, f32[128,512]{1,0:T(8,128)}, u32[]{:S(2)}, u32[]{:S(2)}) collective-permute-start(f32[128,512]{1,0:T(8,128)} %param.8), channel_id=1, source_target_pairs={{0,0},{1,8},{2,16},{3,24},{8,1},{9,9},{10,17},{11,25},{16,2},{17,1... | collective-permute-start | bytes 786440 | tf_op jit(solution)/shard_map/ppermute | solution.py:265
  12.9 304.0 %collective-permute-start.4 = (f32[128,512]{1,0:T(8,128)}, f32[128,512]{1,0:T(8,128)}, u32[]{:S(2)}, u32[]{:S(2)}) collective-permute-start(f32[128,512]{1,0:T(8,128)} %param.9), channel_id=1, source_target_pairs={{0,0},{1,8},{2,16},{3,24},{8,1},{9,9},{10,17},{11,25},{16,2},{17,1... | collective-permute-start | bytes 786440 | tf_op jit(solution)/shard_map/ppermute | solution.py:265
  18.9 2.3 copy-start.2
  315.0 340.0 %collective-permute-start.3 = (f32[128,512]{1,0:T(8,128)}, f32[128,512]{1,0:T(8,128)}, u32[]{:S(2)}, u32[]{:S(2)}) collective-permute-start(f32[128,512]{1,0:T(8,128)} %get-tuple-element.72), channel_id=1, source_target_pairs={{0,0},{1,8},{2,16},{3,24},{8,1},{9,9},{10,17},{11,25},{16,2},{17,1... | collective-permute-start | bytes 786440 | tf_op jit(solution)/shard_map/ppermute | solution.py:265
  620.2 34.2 %collective-permute-start.7 = (f32[4,512]{1,0:T(4,128)S(1)}, f32[4,512]{1,0:T(4,128)S(1)}, u32[]{:S(2)}, u32[]{:S(2)}) collective-permute-start(f32[4,512]{1,0:T(4,128)S(1)} %psum.7), channel_id=1, source_target_pairs={{0,0},{1,8},{2,16},{3,24},{8,1},{9,9},{10,17},{11,25},{16,2},{17,1... | collective-permute-start | bytes 24584 | tf_op jit(solution)/shard_map/ppermute | solution.py:265
  627.2 27.9 %collective-permute-start.5 = (f32[128,512]{1,0:T(8,128)}, f32[128,512]{1,0:T(8,128)}, u32[]{:S(2)}, u32[]{:S(2)}) collective-permute-start(f32[128,512]{1,0:T(8,128)} %get-tuple-element.101), channel_id=1, source_target_pairs={{0,0},{1,8},{2,16},{3,24},{8,1},{9,9},{10,17},{11,25},{16,2},{17,1... | collective-permute-start | bytes 786440 | tf_op jit(solution)/shard_map/ppermute | solution.py:265
  629.3 25.7 %collective-permute-start.6 = (bf16[256,640]{1,0:T(8,128)(2,1)}, bf16[256,640]{1,0:T(8,128)(2,1)}, u32[]{:S(2)}, u32[]{:S(2)}) collective-permute-start(bf16[256,640]{1,0:T(8,128)(2,1)} %get-tuple-element.103), channel_id=1, source_target_pairs={{0,4},{4,0},{1,5},{5,1},{2,6},{6,2},{3,7},{7,3},{8,12},{12,8},{9,1... | collective-permute-start | bytes 983048 | tf_op jit(solution)/shard_map/ppermute | solution.py:1415
  638.5 2.8 copy-start.7
  638.5 2.8 copy-start.8
  641.3 1.1 copy-start.4
  644.2 2.9 copy-start
  644.2 3.7 copy-start.1
  648.0 5.2 copy-start.9
  648.0 5.2 copy-start.10
  648.0 5.2 copy-start.11
  648.0 5.2 copy-start.12
  653.4 1.7 copy-start.6

commit v5 on v4

--- a/solution.py
+++ b/solution.py
@@ -267,7 +267,7 @@
 
 MESH_ID = pl.DeviceIdType.MESH
 ROWS = 16
-SKEW = 2
+SKEW = 3
 GROUP_CHUNKS = 4
 EXTRA = 128
 
@@ -598,7 +598,7 @@
 TILE = 256
 
 
-def ffn_forward(hidden, gain, gu_own, gu_peer, down_own, shipped, depth):
+def ffn_forward(hidden, gain, gu_own, gu_peer, down_own, shipped, depth, ident):
     tok, features = hidden.shape
     width = down_own.shape[1]
     run, scratch = make_line(tok, depth, 2 * width, width, True, False, features)
@@ -691,7 +691,7 @@
             sem(1 + count), sem(1 + count),
         ] + scratch,
         compiler_params=pltpu.CompilerParams(
-            collective_id=1 if count else 5, has_side_effects=True, vmem_limit_bytes=60 << 20
+            collective_id=ident, has_side_effects=True, vmem_limit_bytes=60 << 20
         ),
         cost_estimate=pl.CostEstimate(flops=60_000_000_000, bytes_accessed=8_000_000, transcendentals=0),
         name="ffn_forward",
@@ -699,7 +699,9 @@
     return out[:5], out[5:]
 
 
-def ffn_backward(grad, hidden, gain, kept, wide_forward, gu_own, gu_peer, down_own, down_peer, shipped, depth):
+def ffn_backward(
+    grad, hidden, gain, kept, wide_forward, gu_own, gu_peer, down_own, down_peer, shipped, stacks, index, layers, depth, ident
+):
     tok, features = hidden.shape
     width = down_own.shape[1]
     run, scratch = make_line(tok, depth, width, 2 * width, False, True, features)
@@ -709,15 +711,17 @@
 
     def kernel(dy_ref, h_ref, gain_ref, kept_ref, before_ref, w1_own, w1_peer, w2_own, w2_peer, *rest):
         leave, rest = rest[:count], rest[count:]
-        (out_ref, wide, gain_out, down_kept, down_got), rest = rest[:5], rest[5:]
+        rest = rest[len(stacks):]
+        (out_ref, wide, gain_out, kept_all, got_all), rest = rest[:5], rest[5:]
         landed, rest = rest[:count], rest[count:]
-        (taken, turned, down_given, pieces, side_s, side_r, product, carried, chain_out, chain_in, own_part, rs_out,
-         rs_in), sems = rest[:13], rest[13:]
+        (taken, turned, down_kept, down_given, keep_s, pieces, side_s, side_r, product, carried, chain_out, chain_in, own_part,
+         rs_out, rs_in), sems = rest[:15], rest[15:]
         line = Line(tok, depth)
         side = Side(side_s, side_r)
         own, other = halves(features)
         taken[pl.ds(line.own, tok), :] = dy_ref[...].astype(jnp.bfloat16)
-        give = side.later(down_given, down_got)
+        give = side.later(down_given, got_all.at[index])
+        keep = pltpu.make_async_copy(down_kept, kept_all.at[index], keep_s)
 
         def begin():
             for source, target in zip(leave, landed):
@@ -748,6 +752,7 @@
             @pl.when(i == first_tile + tiles)
             def _():
                 give.start()
+                keep.start()
 
         def finish(row, at, total, extra):
             gate = kept_ref[pl.ds(at, ROWS), :width]
@@ -777,6 +782,7 @@
             normed = h_ref[...] * factor
             gain_out[...] = jnp.broadcast_to(jnp.sum(total * normed, axis=0, keepdims=True), gain_out.shape)
             out_ref[...] = dy_ref[...] + factor * (total * gain_ref[...] - normed * (inner / D))
+            keep.wait()
             side.finish()
 
         run(line, taken, begin, prepare, beside, finish, second, lambda: None, close, product, carried, chain_out, chain_in,
@@ -787,28 +793,31 @@
         jax.ShapeDtypeStruct((tok, features), full),
         jax.ShapeDtypeStruct((4 * tok, 2 * width + EXTRA), low),
         jax.ShapeDtypeStruct((8, features), full),
-        jax.ShapeDtypeStruct(down_own.shape, low),
-        jax.ShapeDtypeStruct(down_own.shape, low),
+        jax.ShapeDtypeStruct((layers,) + down_own.shape, low),
+        jax.ShapeDtypeStruct((layers,) + down_own.shape, low),
     ) + tuple(jax.ShapeDtypeStruct(item.shape, item.dtype) for item in shipped)
     inside, outside = pl.BlockSpec(memory_space=pltpu.VMEM), pl.BlockSpec(memory_space=pl.ANY)
     out = pl.pallas_call(
         kernel,
         out_shape=shapes,
-        in_specs=[inside] * 9 + [outside] * count,
-        out_specs=[inside] * 5 + [outside] * count,
+        in_specs=[inside] * 9 + [outside] * (count + len(stacks)),
+        out_specs=[inside] * 3 + [outside] * (2 + count),
+        input_output_aliases={9 + count + at: 3 + at for at in range(len(stacks))},
         scratch_shapes=[
             pltpu.VMEM((4 * tok, features), low),
             pltpu.VMEM((features, 4 * tok), low),
             pltpu.VMEM(down_own.shape, low),
+            pltpu.VMEM(down_own.shape, low),
+            pltpu.SemaphoreType.DMA,
             pltpu.VMEM((GROUP_CHUNKS * ROWS, features), full),
             sem(1 + count), sem(1 + count),
         ] + scratch,
         compiler_params=pltpu.CompilerParams(
-            collective_id=2 if count else 6, has_side_effects=True, vmem_limit_bytes=60 << 20
+            collective_id=ident, has_side_effects=True, vmem_limit_bytes=60 << 20
         ),
         cost_estimate=pl.CostEstimate(flops=60_000_000_000, bytes_accessed=8_000_000, transcendentals=0),
         name="ffn_backward",
-    )(grad, hidden, gain.reshape(1, -1), kept, wide_forward, gu_own, gu_peer, down_own, down_peer, *shipped)
+    )(grad, hidden, gain.reshape(1, -1), kept, wide_forward, gu_own, gu_peer, down_own, down_peer, *shipped, *stacks)
     return out[:5], out[5:]
 
 
@@ -927,19 +936,23 @@
     return sent
 
 
-def line_gather(square, array, rows, send, recv, row_send, row_recv):
+def send_part(square, array, part, send, recv):
+    lanes = pl.ds(pl.multiple_of(part * EXTRA, EXTRA), EXTRA)
+    here = array.at[pl.ds(square.mine, square.tok), lanes]
     depth = square.depth
-    sent = []
-    for step in range(1, depth):
-        peer = {"z": lax.rem(square.z + step, depth)}
-        here = array.at[pl.ds(square.mine, square.tok)]
-        copy = remote(here, here, send.at[step - 1], recv.at[depth - 1 - step], peer)
-        line = rows.at[square.z]
-        row_copy = remote(line, line, row_send.at[step - 1], row_recv.at[depth - 1 - step], peer)
-        copy.start()
-        row_copy.start()
-        sent += [copy, row_copy]
-    return sent
+    return [
+        remote(here, here, send.at[step - 1, part], recv.at[depth - 1 - step, part], {"z": lax.rem(square.z + step, depth)})
+        for step in range(1, depth)
+    ]
+
+
+def send_row(square, rows, send, recv):
+    line = rows.at[square.z]
+    depth = square.depth
+    return [
+        remote(line, line, send.at[step - 1], recv.at[depth - 1 - step], {"z": lax.rem(square.z + step, depth)})
+        for step in range(1, depth)
+    ]
 
 
 def grid_sum(square, array, rows, second, settle, own, outs, ins, row_ins, arrive, row_arrive, send, recv, row_send, row_recv):
@@ -948,8 +961,9 @@
     for step in range(depth):
         block = lax.rem(square.z + step, depth)
         if step:
-            rows_of = pl.ds(pl.multiple_of(block * tok, tok), tok)
-            remote(array.at[rows_of], array.at[rows_of], send.at[0], arrive.at[step - 1], {"z": square.z}).wait_recv()
+            for part in range(array.shape[1] // EXTRA):
+                rows_of = array.at[pl.ds(pl.multiple_of(block * tok, tok), tok), pl.ds(part * EXTRA, EXTRA)]
+                remote(rows_of, rows_of, send.at[0], arrive.at[step - 1, part], {"z": square.z}).wait_recv()
             remote(rows.at[block], rows.at[block], send.at[0], row_arrive.at[step - 1], {"z": square.z}).wait_recv()
         value = second(pl.multiple_of(block * tok, tok))
         away = lax.rem(block - square.g + depth, depth)
@@ -990,7 +1004,7 @@
                 row_copy.wait_send()
 
 
-def attention_forward(hidden, gain, qkv_own, out_own, qkv_peer, out_peer, shipped, cosine, sine, depth):
+def attention_forward(hidden, gain, qkv_own, out_own, qkv_peer, out_peer, shipped, cosine, sine, depth, ident):
     tok, features = hidden.shape
     cols = qkv_own.shape[1]
     fetch = qkv_peer is None
@@ -1045,6 +1059,9 @@
             squares = squares + zr_in[slot]
         factor_row = lax.rsqrt(squares / D + EPS)
         factors[square.z] = factor_row
+        given = send_row(square, factors, zgr_s, zgr_r)
+        for copy in given:
+            copy.start()
         turned = turn(total * to_column(factor_row), cos_ref[...], sin_ref[...])
         here = pl.ds(pl.multiple_of(square.row * tok, tok), tok)
         kv[here, :] = turned[:, query_cols:].astype(jnp.bfloat16)
@@ -1075,10 +1092,12 @@
             probs = (expo * (1.0 / denom)).astype(jnp.bfloat16)
             out_t = jnp.dot(values_t[...], probs, preferred_element_type=jnp.float32)
             mixed[pl.ds(square.mine, tok), lanes] = join_pair(out_t, tok).astype(jnp.bfloat16)
+            for copy in send_part(square, mixed, t, zg_s, zg_r):
+                copy.start()
             return 0
 
         lax.fori_loop(0, pairs, pair, 0)
-        given = line_gather(square, mixed, factors, zg_s, zg_r, zgr_s, zgr_r)
+        given += [copy for part in range(pairs) for copy in send_part(square, mixed, part, zg_s, zg_r)]
 
         for copy in urgent[1:]:
             copy.wait_recv()
@@ -1142,11 +1161,11 @@
             pltpu.VMEM((depth, tok, features), low),
             pltpu.VMEM((depth - 1, tok, features), low),
             sem(3), sem(3), sem(depth), sem(depth - 1), sem(depth), sem(depth - 1),
-            sem(2 * depth - 1), sem(2 * depth - 1), sem(depth - 1), sem(depth - 1), sem(depth - 1), sem(depth - 1),
+            sem(2 * depth - 1), sem(2 * depth - 1), sem(depth - 1, pairs), sem(depth - 1, pairs), sem(depth - 1), sem(depth - 1),
             sem(depth), sem(depth - 1),
         ] + ([sem(sides), sem(sides)] if sides else []),
         compiler_params=pltpu.CompilerParams(
-            collective_id=3 if fetch else 7, has_side_effects=True, vmem_limit_bytes=60 << 20
+            collective_id=ident, has_side_effects=True, vmem_limit_bytes=60 << 20
         ),
         cost_estimate=pl.CostEstimate(flops=50_000_000_000, bytes_accessed=8_000_000, transcendentals=0),
         name="attention_forward",
@@ -1157,7 +1176,7 @@
 
 def attention_backward(
     grad, hidden, gain, qkv_own, qkv_peer, out_own, out_peer, cosine, sine, queries, kv, lse, factors, mixed, normed_a, normed_f,
-    grad_gu, depth,
+    grad_gu, stacks, index, layers, depth, ident,
 ):
     tok, features = hidden.shape
     cols = qkv_own.shape[1]
@@ -1168,11 +1187,11 @@
     scale = 1.0 / math.sqrt(HEAD)
 
     def kernel(dy_ref, h_ref, gain_ref, wqkv_own, wqkv_peer, wo_own, wo_peer, cos_ref, sin_ref, q_ref, kv_ref, lse_ref,
-               factor_ref, mixed_ref, normed_a_ref, normed_f_ref, gu_ref,
-               out_ref, gain_out, gu_kept, gu_got, out_kept, out_got, qkv_kept, qkv_given,
-               taken, spun, turned, pieces, gu_given, out_given,
+               factor_ref, mixed_ref, normed_a_ref, normed_f_ref, gu_ref, *rest_refs):
+        (out_ref, gain_out, qkv_given, gu_kept_all, gu_got_all, out_kept_all, out_got_all, qkv_kept_all,
+               taken, spun, turned, pieces, gu_kept, gu_given, out_kept, out_given, qkv_kept, keep_s,
                own, heads, z_out, z_in, keys_t, dk, dv, kv_out, kv_in, dq, inner_rows, g_own, g_out, g_in, g_rows,
-               ag_s, ag_r, zs_s, zs_r, kv_s, kv_r, zg_s, zg_r, zgr_s, zgr_r, gs_s, gs_r, gr_s, gr_r, side_s, side_r):
+               ag_s, ag_r, zs_s, zs_r, kv_s, kv_r, zg_s, zg_r, zgr_s, zgr_r, gs_s, gs_r, gr_s, gr_r, side_s, side_r) = rest_refs[len(stacks):]
         square = Square(tok, depth)
         side = Side(side_s, side_r)
         mine, other = halves(features)
@@ -1187,17 +1206,29 @@
 
             lax.fori_loop(start, stop, tile, 0)
 
-        middle = wide // EXTRA // 2
+        gu_got = gu_got_all.at[index]
+        keeps = [
+            pltpu.make_async_copy(gu_kept, gu_kept_all.at[index], keep_s.at[0]),
+            pltpu.make_async_copy(out_kept, out_kept_all.at[index], keep_s.at[1]),
+            pltpu.make_async_copy(qkv_kept, qkv_kept_all.at[index], keep_s.at[2]),
+        ]
+        every = wide // EXTRA
+        middle, late = every // 2, every * 3 // 4
         gu_tiles(0, middle)
-        front, rest = pl.ds(0, middle * EXTRA), pl.ds(middle * EXTRA, wide - middle * EXTRA)
+        front, rest = pl.ds(0, middle * EXTRA), pl.ds(late * EXTRA, wide - late * EXTRA)
+        inner_part = pl.ds(middle * EXTRA, (late - middle) * EXTRA)
         side.start(gu_given.at[:, front], gu_got.at[:, front])
 
         def between():
             turned[...] = flip(taken[...])
             for t in range(query_cols // EXTRA):
                 grad_tile(turned, features, mixed_ref, pl.ds(t * EXTRA, EXTRA), out_kept, out_given)
-            side.start(out_given, out_got)
-            gu_tiles(middle, wide // EXTRA)
+            side.start(out_given, out_got_all.at[index])
+            gu_tiles(middle, late)
+            side.start(gu_given.at[:, inner_part], gu_got.at[:, inner_part])
+            gu_tiles(late, every)
+            keeps[0].start()
+            keeps[1].start()
 
         def product(row):
             rows = pl.ds(row, tok)
@@ -1231,10 +1262,17 @@
             grad_scores = (probs * (grad_probs - delta)).astype(jnp.bfloat16)
             dk[...] += jnp.dot(grad_scores, query, preferred_element_type=jnp.float32)
             dv[...] += jnp.dot(probs.astype(jnp.bfloat16), head, preferred_element_type=jnp.float32)
-            turned = jnp.dot(keys_t[...], grad_scores, preferred_element_type=jnp.float32)
-            dq[:, lanes] = join_pair(turned, tok) * scale
+            back = jnp.dot(keys_t[...], grad_scores, preferred_element_type=jnp.float32)
+            value = join_pair(back, tok) * scale
+            dq[...] += jnp.broadcast_to(
+                jnp.sum(value * q_ref[:, lanes].astype(jnp.float32), axis=1, keepdims=True), dq.shape
+            )
+            spun[pl.ds(square.mine, tok), lanes] = turn(value, cos_ref[:, lanes], -sin_ref[:, lanes]).astype(jnp.bfloat16)
+            for copy in send_part(square, spun, t, zg_s, zg_r):
+                copy.start()
             return 0
 
+        dq[...] = jnp.zeros_like(dq)
         lax.fori_loop(0, pairs, pair, 0)
         lane = lax.broadcasted_iota(jnp.int32, (seq, EXTRA), 1)
         left = dk[...]
@@ -1263,13 +1301,15 @@
         side.start(gu_given.at[:, rest], gu_got.at[:, rest])
         for slot in range(2 * depth - 1):
             total_kv = total_kv + kv_in[slot].astype(jnp.float32)
-        inner = jnp.sum(dq[...] * q_ref[...].astype(jnp.float32), axis=1, keepdims=True) + jnp.sum(
-            total_kv * kv_ref[here, :].astype(jnp.float32), axis=1, keepdims=True
-        )
+        spun[pl.ds(square.mine, tok), query_cols:] = turn(
+            total_kv, cos_ref[:, query_cols:], -sin_ref[:, query_cols:]
+        ).astype(jnp.bfloat16)
+        inner = dq[:, :1] + jnp.sum(total_kv * kv_ref[here, :].astype(jnp.float32), axis=1, keepdims=True)
         inner_rows[square.z] = to_row(inner)
-        whole = jnp.concatenate([dq[...], total_kv], axis=1)
-        spun[pl.ds(square.mine, tok), :] = turn(whole, cos_ref[...], -sin_ref[...]).astype(jnp.bfloat16)
-        given = line_gather(square, spun, inner_rows, zg_s, zg_r, zgr_s, zgr_r)
+        given = send_part(square, spun, pairs, zg_s, zg_r) + send_row(square, inner_rows, zgr_s, zgr_r)
+        for copy in given:
+            copy.start()
+        given += [copy for part in range(pairs) for copy in send_part(square, spun, part, zg_s, zg_r)]
 
         def second(row):
             value = spun[pl.ds(row, tok), :]
@@ -1280,6 +1320,7 @@
         def settle():
             for t in range(cols // EXTRA):
                 grad_tile(normed_a_ref, features, spun, pl.ds(t * EXTRA, EXTRA), qkv_kept, qkv_given)
+            keeps[2].start()
 
         sums = grid_sum(
             square, spun, inner_rows, second, settle, g_own, g_out, g_in, g_rows, zg_r, zgr_r, gs_s, gs_r, gr_s, gr_r
@@ -1297,31 +1338,39 @@
         drain(sums)
         for copy in gather + spreads + given:
             copy.wait_send()
+        for copy in keeps:
+            copy.wait()
         side.finish()
 
     low, full = jnp.bfloat16, jnp.float32
     shapes = (
         jax.ShapeDtypeStruct((tok, features), full),
         jax.ShapeDtypeStruct((8, features), full),
-        jax.ShapeDtypeStruct((features // 2, wide), low),
-        jax.ShapeDtypeStruct((features // 2, wide), low),
-        jax.ShapeDtypeStruct(out_own.shape, low),
-        jax.ShapeDtypeStruct(out_own.shape, low),
         jax.ShapeDtypeStruct(qkv_own.shape, low),
-        jax.ShapeDtypeStruct(qkv_own.shape, low),
+        jax.ShapeDtypeStruct((layers, features // 2, wide), low),
+        jax.ShapeDtypeStruct((layers, features // 2, wide), low),
+        jax.ShapeDtypeStruct((layers,) + out_own.shape, low),
+        jax.ShapeDtypeStruct((layers,) + out_own.shape, low),
+        jax.ShapeDtypeStruct((layers,) + qkv_own.shape, low),
     )
+    inside, outside = pl.BlockSpec(memory_space=pltpu.VMEM), pl.BlockSpec(memory_space=pl.ANY)
     return pl.pallas_call(
         kernel,
         out_shape=shapes,
-        in_specs=[pl.BlockSpec(memory_space=pltpu.VMEM)] * 17,
-        out_specs=[pl.BlockSpec(memory_space=pltpu.VMEM)] * 8,
+        in_specs=[inside] * 17 + [outside] * len(stacks),
+        out_specs=[inside] * 3 + [outside] * 5,
+        input_output_aliases={17 + at: 3 + at for at in range(len(stacks))},
         scratch_shapes=[
             pltpu.VMEM((depth * tok, features), low),
             pltpu.VMEM((depth * tok, cols), low),
             pltpu.VMEM((features, depth * tok), low),
             pltpu.VMEM((tok, features), full),
             pltpu.VMEM((features // 2, wide), low),
+            pltpu.VMEM((features // 2, wide), low),
             pltpu.VMEM(out_own.shape, low),
+            pltpu.VMEM(out_own.shape, low),
+            pltpu.VMEM(qkv_own.shape, low),
+            sem(3),
             pltpu.VMEM((tok, query_cols), full),
             pltpu.VMEM((tok, query_cols), low),
             pltpu.VMEM((depth, tok, query_cols), low),
@@ -1331,21 +1380,134 @@
             pltpu.VMEM((seq, 2 * HEAD), full),
             pltpu.VMEM((seq, 2 * HEAD), low),
             pltpu.VMEM((2 * depth - 1, tok, 2 * HEAD), low),
-            pltpu.VMEM((tok, query_cols), full),
+            pltpu.VMEM((tok, EXTRA), full),
             pltpu.VMEM((depth, 8, tok), full),
             pltpu.VMEM((tok, features), full),
             pltpu.VMEM((depth, tok, features), low),
             pltpu.VMEM((depth - 1, tok, features), low),
             pltpu.VMEM((depth - 1, 8, tok), full),
             sem(3), sem(3), sem(depth), sem(depth - 1),
-            sem(2 * depth - 1), sem(2 * depth - 1), sem(depth - 1), sem(depth - 1), sem(depth - 1), sem(depth - 1),
-            sem(depth), sem(depth - 1), sem(depth), sem(depth - 1), sem(3), sem(3),
+            sem(2 * depth - 1), sem(2 * depth - 1), sem(depth - 1, pairs + 1), sem(depth - 1, pairs + 1), sem(depth - 1),
+            sem(depth - 1), sem(depth), sem(depth - 1), sem(depth), sem(depth - 1), sem(4), sem(4),
         ],
-        compiler_params=pltpu.CompilerParams(collective_id=4, has_side_effects=True, vmem_limit_bytes=60 << 20),
+        compiler_params=pltpu.CompilerParams(collective_id=ident, has_side_effects=True, vmem_limit_bytes=60 << 20),
         cost_estimate=pl.CostEstimate(flops=50_000_000_000, bytes_accessed=8_000_000, transcendentals=0),
         name="attention_backward",
     )(grad, hidden, gain.reshape(1, -1), qkv_own, qkv_peer, out_own, out_peer, cosine, sine, queries, kv, lse, factors, mixed,
-      normed_a, normed_f, grad_gu)
+      normed_a, normed_f, grad_gu, *stacks)
+
+
+def finish(grad, gains, qkv_given, depth, ident):
+    tok, features = grad.shape
+    count = len(gains)
+    members = 2 * depth
+
+    def kernel(grad_ref, *rest):
+        gain_refs, rest = rest[:count], rest[count:]
+        (given, out_ref, gain_out, got, packed, parts, sent, home, part_s, part_r, move_s, move_r, side_s, side_r) = rest
+        z, x = lax.axis_index("z"), lax.axis_index("x")
+        y, c = lax.axis_index("y"), lax.axis_index("c")
+        g = 2 * y + c
+        barrier = pltpu.get_barrier_semaphore()
+        self_at = x * depth + g
+
+        def source(slot):
+            return {"z": g, "x": slot // depth, "y": (slot % depth) // 2, "c": slot % 2}
+
+        def target(at):
+            return {"z": at // 2, "x": at % 2, "y": z // 2, "c": lax.rem(z, 2)}
+
+        def is_source_me(slot):
+            return (z == g) & (slot == self_at)
+
+        def is_target_me(at):
+            return (z == g) & (at == 2 * z + x)
+
+        for slot in range(members):
+
+            @pl.when(jnp.logical_not(is_source_me(slot)))
+            def _():
+                pl.semaphore_signal(barrier, 1, device_id=source(slot), device_id_type=MESH_ID)
+
+        pl.semaphore_signal(barrier, 1, device_id={"x": 1 - x}, device_id_type=MESH_ID)
+        for at, ref in enumerate(gain_refs):
+            packed[at : at + 1, :] = ref[:1, :]
+        sent[...] = grad_ref[...].astype(jnp.bfloat16)
+        pl.semaphore_wait(barrier, members + 1 - jnp.where(z == g, 1, 0))
+        side = Side(side_s, side_r)
+        side.start(given, got)
+        move = remote(sent, home, move_s, move_r, {"z": g, "y": z // 2, "c": lax.rem(z, 2)})
+
+        @pl.when(z != g)
+        def _():
+            move.start()
+
+        def part(at):
+            return remote(packed, parts.at[self_at], part_s.at[at], part_r.at[self_at], target(at))
+
+        for at in range(members):
+
+            @pl.when(jnp.logical_not(is_target_me(at)))
+            def _():
+                part(at).start()
+
+        @pl.when(z == g)
+        def _():
+            parts[self_at] = packed[...]
+
+        for slot in range(members):
+
+            @pl.when(jnp.logical_not(is_source_me(slot)))
+            def _():
+                remote(packed, parts.at[slot], part_s.at[0], part_r.at[slot], target(0)).wait_recv()
+
+        total = parts[0]
+        for slot in range(1, members):
+            total = total + parts[slot]
+        gain_out[...] = total
+
+        @pl.when(z == g)
+        def _():
+            out_ref[...] = grad_ref[...]
+
+        @pl.when(z != g)
+        def _():
+            move.wait_recv()
+            out_ref[...] = home[...].astype(jnp.float32)
+            move.wait_send()
+
+        for at in range(members):
+
+            @pl.when(jnp.logical_not(is_target_me(at)))
+            def _():
+                part(at).wait_send()
+
+        side.finish()
+
+    low, full = jnp.bfloat16, jnp.float32
+    inside, outside = pl.BlockSpec(memory_space=pltpu.VMEM), pl.BlockSpec(memory_space=pl.ANY)
+    return pl.pallas_call(
+        kernel,
+        out_shape=(
+            jax.ShapeDtypeStruct((tok, features), full),
+            jax.ShapeDtypeStruct((count, features), full),
+            jax.ShapeDtypeStruct(qkv_given.shape, low),
+        ),
+        in_specs=[inside] * (1 + count) + [outside],
+        out_specs=[inside, inside, outside],
+        scratch_shapes=[
+            pltpu.VMEM((count, features), full),
+            pltpu.VMEM((members, count, features), full),
+            pltpu.VMEM((tok, features), low),
+            pltpu.VMEM((tok, features), low),
+            sem(members), sem(members),
+            pltpu.SemaphoreType.DMA, pltpu.SemaphoreType.DMA,
+            sem(1), sem(1),
+        ],
+        compiler_params=pltpu.CompilerParams(collective_id=ident, has_side_effects=True),
+        cost_estimate=pl.CostEstimate(flops=5_000_000_000, bytes_accessed=1_000_000, transcendentals=0),
+        name="finish",
+    )(grad, *gains, qkv_given)
 
 
 def stationary(stream, grad_out, wqkv, wo, wgu, wd, gain_attn, gain_ffn):
@@ -1356,15 +1518,13 @@
     head = HEAD
     row = lax.axis_index("z") * 2 + lax.axis_index("x")
     query_pos = row * tok + jnp.arange(tok, dtype=jnp.int32)
-    freq = THETA ** (-(jnp.arange(head // 2, dtype=jnp.float32) * 2.0 / head))
+    lane = jnp.arange((GROUP + 2) * head, dtype=jnp.int32)
+    half = head // 2
+    freq = THETA ** (-((lane % half).astype(jnp.float32) * 2.0 / head))
     angle = query_pos.astype(jnp.float32)[:, None] * freq[None, :]
-    cosine = jnp.cos(angle)
-    sine = jnp.sin(angle)
-    turns = GROUP + 1
-    cosine = jnp.concatenate([jnp.tile(cosine, (1, 2 * turns)), jnp.ones((tok, head), jnp.float32)], axis=1)
-    sine = jnp.concatenate(
-        [jnp.tile(jnp.concatenate([-sine, sine], axis=1), (1, turns)), jnp.zeros((tok, head), jnp.float32)], axis=1
-    )
+    rotated = (lane < (GROUP + 1) * head)[None, :]
+    cosine = jnp.where(rotated, jnp.cos(angle), 1.0)
+    sine = jnp.where(rotated, jnp.where((lane % head < half)[None, :], -1.0, 1.0) * jnp.sin(angle), 0.0)
     current = swap_grid(stream, depth)
     grad_now = swap_grid(grad_out, depth)
     gain_a = swap_grid(gain_attn, depth)
@@ -1379,50 +1539,45 @@
         before = current
         (hidden_in, normed_a, queries, kv, lse, mixed, factors), (peer_qkv[index], peer_out[index]), landed = attention_forward(
             before, gain_a[index], own_qkv[index], own_out[index], peer_qkv[index], peer_out[index],
-            [] if index else own_gu[:1], cosine, sine, depth
+            [] if index else own_gu[:1], cosine, sine, depth, 4 * index
         )
         if landed:
             peer_gu[0] = landed[0]
         follow = index + 1
         shipped = [own_qkv[follow], own_out[follow], own_gu[follow]] if follow < layers else []
         (current, normed_f, kept, active, peer_down[index]), landed = ffn_forward(
-            hidden_in, gain_f[index], own_gu[index], peer_gu[index], own_down[index], shipped, depth
+            hidden_in, gain_f[index], own_gu[index], peer_gu[index], own_down[index], shipped, depth, 4 * index + 1
         )
         if landed:
             peer_qkv[follow], peer_out[follow], peer_gu[follow] = landed
         saved.append((before, normed_a, queries, kv, lse, mixed, factors, hidden_in, normed_f, kept, active))
-    list_qkv, list_out, list_gu, list_down, list_ga, list_gf = ([], [], [], [], [], [])
-    pending = []
-    add = lambda kept, got: kept.astype(jnp.float32) + got.astype(jnp.float32)
+    list_ga, list_gf, got_qkv, pending, down_stack, rest_stack = ([], [], [], [], [], [])
     for index in reversed(range(layers)):
         before, normed_a, queries, kv, lse, mixed, factors, hidden_in, normed_f, kept, active = saved[index]
-        (grad_hidden, grad_gu, gain_f_grad, down_kept, down_got), landed = ffn_backward(
+        (grad_hidden, grad_gu, gain_f_grad, *down_stack), landed = ffn_backward(
             grad_now, hidden_in, gain_f[index], kept, active, own_gu[index], peer_gu[index], own_down[index],
-            peer_down[index], pending[-1:], depth
+            peer_down[index], pending[-1:], down_stack, index, layers, depth, 4 * index + 2
         )
-        if landed:
-            list_qkv.append(add(qkv_kept, landed[0]))
-        list_down.append(add(down_kept, down_got))
-        list_gf.append(gain_f_grad[0])
-        (grad_now, gain_a_grad, gu_kept, gu_got, out_kept, out_got, qkv_kept, qkv_given) = attention_backward(
+        got_qkv.extend(landed)
+        list_gf.append(gain_f_grad)
+        (grad_now, gain_a_grad, qkv_given, *rest_stack) = attention_backward(
             grad_hidden, before, gain_a[index], own_qkv[index], peer_qkv[index], own_out[index], peer_out[index],
-            cosine, sine, queries, kv, lse, factors, mixed, normed_a, normed_f, grad_gu, depth
+            cosine, sine, queries, kv, lse, factors, mixed, normed_a, normed_f, grad_gu, rest_stack, index, layers, depth,
+            4 * index + 3
         )
         pending.append(qkv_given)
-        list_gu.append(add(gu_kept, gu_got).reshape(count_rows, 2, -1))
-        list_out.append(add(out_kept, out_got))
-        list_ga.append(gain_a_grad[0])
-    list_qkv.append(add(qkv_kept, lax.ppermute(qkv_given, "x", [(0, 1), (1, 0)])))
-    list_qkv = [item.reshape(count_rows, 1, -1) for item in list_qkv]
-    gains = lax.psum(jnp.concatenate([jnp.stack(list_ga[::-1]), jnp.stack(list_gf[::-1])]), ("x", "y", "c"))
-    gains = swap_grid(gains, depth)
+        list_ga.append(gain_a_grad)
+    grad_in, gains, last_qkv = finish(grad_now, list_ga[::-1] + list_gf[::-1], qkv_given, depth, 4 * layers)
+    got_qkv.append(last_qkv)
+    gu_kept, gu_got, out_kept, out_got, qkv_kept = rest_stack
+    add = lambda kept, got: kept.astype(jnp.float32) + got.astype(jnp.float32)
     return (
         swap_grid(current, depth),
-        swap_grid(grad_now, depth),
-        jnp.stack(list_qkv[::-1]),
-        jnp.stack(list_out[::-1]),
-        jnp.stack(list_gu[::-1]),
-        jnp.stack(list_down[::-1]),
+        grad_in,
+        add(qkv_kept, jnp.stack(got_qkv[::-1])).reshape(layers, count_rows, 1, -1),
+        add(out_kept, out_got),
+        add(gu_kept, gu_got).reshape(layers, count_rows, 2, -1),
+        add(*down_stack),
         gains[:layers],
         gains[layers:],
     )

time: 674 us -> 641 us (0.951)
  blocking collectives: 13.6 us -> 0 us
  starting transfers between devices: 28.7 us -> 17.3 us
    pallas_call x2 -> x3, Pallas kernels: 116 us -> 134 us  [the longest x2 117 us: attention_backward(): pl.pallas_call(kernel, out_shape=shapes, in_specs=[inside] * 17 + [outsid...]
    psum x1 -> x0, blocking collectives: 13.6 us -> none  [stationary(): lax.psum(jnp.concatenate([jnp.stack(list_ga[::-1]), jnp.stack(list_gf[::-...]
    another operation x8 -> x0, other arithmetic: 11.2 us -> none  [the longest x1 5.2 us: stationary(): jnp.stack(list_gu[::-1])]
    ppermute x7 -> x5, starting transfers between devices: 26.5 us -> 17.3 us  [swap_grid(): return lax.ppermute(values, ('z', 'y', 'c'), pairs)]
    reshape x0 -> x1, local copies, waits for them, and re-layouts: none -> 7.94 us  [stationary(): add(gu_kept, gu_got).reshape(layers, count_rows, 2, -1)]
    pallas_call x2, Pallas kernels: 169 us -> 161 us  [ffn_forward(): pl.pallas_call(kernel, out_shape=shapes, in_specs=[inside] * 5 + [outside...]
    another operation x6 -> x0, local copies, waits for them, and re-layouts: 7.62 us -> none  [the longest x2 5.57 us: stationary(): jnp.stack(list_gu[::-1])]
  transfers between devices with their start and end apart: 8 -> 5, of which waited for: 1 -> 1; matrix products, arithmetic and copies ran while one was open for 6% -> 5% of each run, Pallas kernels for 86% -> 91%
where the time goes in v5:
time: 641 us; the launch traced here: 630 us
  Pallas kernels  574 us (90%)
  local copies, waits for them, and re-layouts  25.9 us (4%)
  starting transfers between devices  17.3 us (3%)
  other arithmetic  9.69 us (2%)
    pallas_call x2, Pallas kernels, ffn_backward(): pl.pallas_call(kernel, out_shape=shapes, in_specs=[inside] * 9 + [outside...  166 us
    pallas_call x2, Pallas kernels, ffn_forward(): pl.pallas_call(kernel, out_shape=shapes, in_specs=[inside] * 5 + [outside...  161 us
    pallas_call x2, Pallas kernels, attention_backward(): pl.pallas_call(kernel, out_shape=shapes, in_specs=[inside] * 17 + [outsid...  117 us
    pallas_call x2, Pallas kernels, attention_forward(): pl.pallas_call(kernel, out_shape=shapes, in_specs=[inside] * (6 + len(pee...  112 us
    ppermute x5, starting transfers between devices, swap_grid(): return lax.ppermute(values, ('z', 'y', 'c'), pairs)  17.3 us
    pallas_call x1, Pallas kernels, finish(): pl.pallas_call(kernel, out_shape=(jax.ShapeDtypeStruct((tok, features), f...  17 us
  transfers between devices with their start and end apart: 5, of which 1 were waited for; matrix products, arithmetic and copies ran while one was open for 5% of the time, Pallas kernels for 91%

profile of v5, /device:TPU:4, one launch (start us, length us, event | category | flops | bytes accessed | tf_op | source)
XLA Modules:
  0.0 629.7 jit_solution(11150291619892983744)
XLA Ops:
  0.6 0.0 copy-start.3
  0.6 4.6 collective-permute-start.1
  5.2 3.2 collective-permute-start.2
  8.4 4.4 collective-permute-start
  12.9 3.2 collective-permute-start.4
  16.1 1.9 slice_bitcast_fusion.4
  18.0 2.0 slice_bitcast_fusion.2
  20.0 0.0 copy-done.3
  20.0 0.0 copy-start
  20.0 1.2 slice_bitcast_fusion
  21.2 1.1 copy-done
  22.3 2.0 fusion.15
  24.4 2.1 fusion.2
  26.5 1.3 copy.25
  27.7 1.3 copy.24
  29.0 0.0 collective-permute-done.1
  29.0 0.6 fusion.18
  29.6 0.0 collective-permute-done.2
  29.6 0.5 fusion.17
  30.1 2.0 collective-permute-done.h_ref
  32.2 0.0 copy-start.11
  32.2 0.7 copy-done.11
  32.9 55.5 %attention_forward.2 = (f32[128,512]{1,0:T(8,128)}, bf16[512,512]{1,0:T(8,128)(2,1)}, bf16[128,512]{1,0:T(8,128)(2,1)}, bf16[1024,128]{1,0:T(8,128)(2,1)}, f32[4...) custom-call(f32[128,512]{1,0:T(8,128)} %copy-done.11, ...), custom_call_target="tpu_custom_call" | custom-call | flops 49999998976 | bytes 8000000 | tf_op jit(solution)/shard_map/attention_forward/pallas_call | solution.py:1144
  88.4 80.9 %ffn_forward.2 = (f32[128,512]{1,0:T(8,128)}, bf16[512,512]{1,0:T(8,128)(2,1)}, f32[256,2816]{1,0:T(8,128)}, bf16[512,1536]{1,0:T(8,128)(2,1)}, bf16[256,1408]{1...) custom-call(f32[128,512]{1,0:T(8,128)} %get-tuple-element.68.h_ref, ...), custom_call_target="tpu_custom_call" | custom-call | flops 60000002048 | bytes 8000000 | tf_op jit(solution)/shard_map/ffn_forward/pallas_call | solution.py:682
  169.3 56.3 %attention_forward.3 = (f32[128,512]{1,0:T(8,128)}, bf16[512,512]{1,0:T(8,128)(2,1)}, bf16[128,512]{1,0:T(8,128)(2,1)}, bf16[1024,128]{1,0:T(8,128)(2,1)}, f32[4...) custom-call(f32[128,512]{1,0:T(8,128)} %get-tuple-element.70.h_ref, ...), custom_call_target="tpu_custom_call" | custom-call | flops 49999998976 | bytes 8000000 | tf_op jit(solution)/shard_map/attention_forward/pallas_call | solution.py:1144
  225.6 80.5 %ffn_forward.3 = (f32[128,512]{1,0:T(8,128)}, bf16[512,512]{1,0:T(8,128)(2,1)}, f32[256,2816]{1,0:T(8,128)}, bf16[512,1536]{1,0:T(8,128)(2,1)}, bf16[256,1408]{1,0:T(8,128)(2,1)}) custom-call(f32[128,512]{1,0:T(8,128)} %get-tuple-element.73.h_ref, f32[1,512]{1,0:T(1,128)} %get-tuple-element.148.gain_ref, bf16[256,2816]{1,0:T(8,128)(2,1)} %bitcast.28, ...), custom_call_target="tpu_custom_call" | custom-call | flops 60000002048 | bytes 8000000 | tf_op jit(solution)/shard_map/ffn_forward/pallas_call | solution.py:682
  306.2 1.9 collective-permute-start.3
  308.1 0.0 collective-permute-done.4.dy_ref
  308.1 84.1 %ffn_backward.2 = (f32[128,512]{1,0:T(8,128)}, bf16[512,2944]{1,0:T(8,128)(2,1)}, f32[8,512]{1,0:T(8,128)}, bf16[2,256,1408]{2,1,0:T(8,128)(2,1)}, bf16[2,256,1408]{2,1,0:T(8,128)(2,1)}) custom-call(f32[128,512]{1,0:T(8,128)} %collective-permute-done.4.dy_ref, f32[128,512]{1,0:T(8,128)} %get-tuple-element.73.h_ref, f32[1,512]{1,0:T(1,128)} %get-tuple-element.148.gain_ref, ...), custom_call_target="tpu_custom_call" | custom-call | flops 60000002048 | bytes 8000000 | tf_op jit(solution)/shard_map/ffn_backward/pallas_call | solution.py:800
  392.2 58.9 %attention_backward.2 = (f32[128,512]{1,0:T(8,128)}, f32[8,512]{1,0:T(8,128)}, bf16[256,640]{1,0:T(8,128)(2,1)}, bf16[2,256,2816]{2,1,0:T(8,128)(2,1)}, bf16[2,2...) custom-call(f32[128,512]{1,0:T(8,128)} %get-tuple-element.79.dy_ref,, ...), custom_call_target="tpu_custom_call" | custom-call | flops 49999998976 | bytes 8000000 | tf_op jit(solution)/shard_map/attention_backward/pallas_call | solution.py:1357
  451.1 82.3 %ffn_backward.3 = (f32[128,512]{1,0:T(8,128)}, bf16[512,2944]{1,0:T(8,128)(2,1)}, f32[8,512]{1,0:T(8,128)}, bf16[2,256,1408]{2,1,0:T(8,128)(2,1)}, bf16[2,256,14...) custom-call(f32[128,512]{1,0:T(8,128)} %get-tuple-element.88.dy_ref, ...), custom_call_target="tpu_custom_call", output_to_operand_aliasing={{3}: (10, {}), {4}: (11, {})} | custom-call | flops 60000002048 | bytes 8000000 | tf_op jit(solution)/shard_map/ffn_backward/pallas_call | solution.py:800
  533.4 58.1 %attention_backward.3 = (f32[128,512]{1,0:T(8,128)}, f32[8,512]{1,0:T(8,128)}, bf16[256,640]{1,0:T(8,128)(2,1)}, bf16[2,256,2816]{2,1,0:T(8,128)(2,1)}, bf16[2,2...) custom-call(f32[128,512]{1,0:T(8,128)} %get-tuple-element.95.dy_ref,, ...), custom_call_target="tpu_custom_call", output_to_operand_aliasing={{3}: (17, {}), {4}: (18, {}), {5}: (19, {}), {6}: (20, {}),... | custom-call | flops 49999998976 | bytes 8000000 | tf_op jit(solution)/shard_map/attention_backward/pallas_call | solution.py:1357
  591.5 0.0 copy-start.6
  591.5 0.0 copy-start.2
  591.5 17.0 %finish.1 = (f32[128,512]{1,0:T(8,128)}, f32[4,512]{1,0:T(4,128)}, bf16[256,640]{1,0:T(8,128)(2,1)}) custom-call(f32[128,512]{1,0:T(8,128)} %get-tuple-element.111.grad_ref, f32[8,512]{1,0:T(8,128)} %get-tuple-element.112.rest_0_, f32[8,512]{1,0:T(8,128)} %get-tuple-element.113.rest_1_, f32[8,512]{1,0:T(8,128)} %get-tuple-element.114.rest_2_, ...), custom_call_target="tpu_custom_call" | custom-call | flops 5000000000 | bytes 1000000 | tf_op jit(solution)/shard_map/finish/pallas_call | solution.py:1489
  608.5 0.0 copy-done.6
  608.5 0.0 copy-start.1
  608.5 1.4 add_bitcast_fusion
  609.9 0.0 copy-start.10
  609.9 2.4 copy.23
  612.3 0.0 copy-done.10
  612.3 0.6 fusion.16
  612.9 0.0 copy-done.2
  612.9 0.0 copy-done.1
  612.9 3.2 convert_add_fusion
  616.1 0.0 copy-start.4
  616.1 0.0 copy-start.5
  616.1 7.9 %reshape.57 = f32[2,256,2,1408]{3,2,1,0:T(2,128)} reshape(f32[2,256,2816]{2,1,0:T(8,128)} %convert_add_fusion) | data formatting | bytes 11534336 | tf_op jit(solution)/shard_map/reshape | solution.py:1579
  624.1 0.0 copy-done.4
  624.1 0.0 copy-done.5
  624.1 0.0 copy-start.7
  624.1 0.0 copy-start.8
  624.1 1.9 convert_add_fusion.1
  625.9 0.0 copy-start.9
  625.9 0.0 copy-done.7
  625.9 0.0 copy-done.8
  625.9 1.1 convert_add_fusion.2
  627.1 0.0 collective-permute-done.3
  627.1 1.7 copy.35
  628.8 0.0 copy-done.9
  628.8 0.7 copy.36
  (3 shorter events, 0.0 us)
Async XLA Ops:
  0.6 19.4 %copy-start.3 = (bf16[2,256,1408]{2,1,0:T(8,128)(2,1)S(1)}, bf16[2,256,1408]{2,1,0:T(8,128)(2,1)}, u32[]{:S(2)}) copy-start(bf16[2,256,1408]{2,1,0:T(8,128)(2,1)} %param.13) | copy-start | bytes 4325380
  0.6 28.4 %collective-permute-start.1 = (f32[2,512]{1,0:T(2,128)}, f32[2,512]{1,0:T(2,128)S(1)}, u32[]{:S(2)}, u32[]{:S(2)}) collective-permute-start(f32[2,512]{1,0:T(2,128)} %param.14), channel_id=1, source_target_pairs={{0,0},{1,8},{2,16},{3,24},{8,1},{9,9},{10,17},{11,25},{16,2},{17,1... | collective-permute-start | bytes 12296 | tf_op jit(solution)/shard_map/ppermute | solution.py:265
  5.2 24.4 %collective-permute-start.2 = (f32[2,512]{1,0:T(2,128)}, f32[2,512]{1,0:T(2,128)S(1)}, u32[]{:S(2)}, u32[]{:S(2)}) collective-permute-start(f32[2,512]{1,0:T(2,128)} %param.15), channel_id=1, source_target_pairs={{0,0},{1,8},{2,16},{3,24},{8,1},{9,9},{10,17},{11,25},{16,2},{17,1... | collective-permute-start | bytes 12296 | tf_op jit(solution)/shard_map/ppermute | solution.py:265
  8.4 23.7 %collective-permute-start = (f32[128,512]{1,0:T(8,128)}, f32[128,512]{1,0:T(8,128)S(1)}, u32[]{:S(2)}, u32[]{:S(2)}) collective-permute-start(f32[128,512]{1,0:T(8,128)} %param.8), channel_id=1, source_target_pairs={{0,0},{1,8},{2,16},{3,24},{8,1},{9,9},{10,17},{11,25},{16,2},{17,1... | collective-permute-start | bytes 786440 | tf_op jit(solution)/shard_map/ppermute | solution.py:265
  12.9 295.2 %collective-permute-start.4 = (f32[128,512]{1,0:T(8,128)}, f32[128,512]{1,0:T(8,128)}, u32[]{:S(2)}, u32[]{:S(2)}) collective-permute-start(f32[128,512]{1,0:T(8,128)} %param.9), channel_id=1, source_target_pairs={{0,0},{1,8},{2,16},{3,24},{8,1},{9,9},{10,17},{11,25},{16,2},{17,1... | collective-permute-start | bytes 786440 | tf_op jit(solution)/shard_map/ppermute | solution.py:265
  20.0 2.3 copy-start
  32.2 0.7 copy-start.11
  306.2 320.9 %collective-permute-start.3 = (f32[128,512]{1,0:T(8,128)}, f32[128,512]{1,0:T(8,128)}, u32[]{:S(2)}, u32[]{:S(2)}) collective-permute-start(f32[128,512]{1,0:T(8,128)} %get-tuple-element.75), channel_id=1, source_target_pairs={{0,0},{1,8},{2,16},{3,24},{8,1},{9,9},{10,17},{11,25},{16,2},{17,1... | collective-permute-start | bytes 786440 | tf_op jit(solution)/shard_map/ppermute | solution.py:265
  591.5 17.0 %copy-start.6 = (bf16[2,256,640]{2,1,0:T(8,128)(2,1)S(1)}, bf16[2,256,640]{2,1,0:T(8,128)(2,1)}, u32[]{:S(2)}) copy-start(bf16[2,256,640]{2,1,0:T(8,128)(2,1)} %get-tuple-element.118) | copy-start | bytes 1966084
  591.5 21.4 %copy-start.2 = (bf16[2,256,2816]{2,1,0:T(8,128)(2,1)S(1)}, bf16[2,256,2816]{2,1,0:T(8,128)(2,1)}, u32[]{:S(2)}) copy-start(bf16[2,256,2816]{2,1,0:T(8,128)(2,1)} %get-tuple-element.124) | copy-start | bytes 8650756
  608.5 4.4 copy-start.1
  609.9 2.4 copy-start.10
  616.1 7.9 %copy-start.4 = (bf16[2,256,1408]{2,1,0:T(8,128)(2,1)S(1)}, bf16[2,256,1408]{2,1,0:T(8,128)(2,1)}, u32[]{:S(2)}) copy-start(bf16[2,256,1408]{2,1,0:T(8,128)(2,1)} %get-tuple-element.125) | copy-start | bytes 4325380
  616.1 7.9 %copy-start.5 = (bf16[2,256,1408]{2,1,0:T(8,128)(2,1)S(1)}, bf16[2,256,1408]{2,1,0:T(8,128)(2,1)}, u32[]{:S(2)}) copy-start(bf16[2,256,1408]{2,1,0:T(8,128)(2,1)} %get-tuple-element.126) | copy-start | bytes 4325380
  624.1 1.9 copy-start.7
  624.1 1.9 copy-start.8
  625.9 2.8 copy-start.9

commit v6 on v5

--- a/solution.py
+++ b/solution.py
@@ -342,6 +342,122 @@
     return pltpu.SemaphoreType.DMA(shape)
 
 
+class Link:
+    def __init__(self, part, at, shape, dtype):
+        self.part, self.at, self.shape, self.dtype = part, at, shape, dtype
+
+
+class Part:
+    def __init__(self, kernel, operands, shapes, staged_in, staged_out, scratch, aliases, flops, name):
+        self.kernel, self.operands, self.shapes = kernel, operands, shapes
+        self.staged_in, self.staged_out, self.scratch = staged_in, staged_out, scratch
+        self.aliases, self.flops, self.name = aliases, flops, name
+
+    def link(self, at, part=0):
+        return Link(part, at, self.shapes[at].shape, self.shapes[at].dtype)
+
+
+class Done:
+    def start(self):
+        pass
+
+    def wait(self):
+        pass
+
+
+class Later:
+    def __init__(self, copy):
+        self.start = copy.start
+
+    def wait(self):
+        pass
+
+
+def launch(parts, greet, ident):
+    operands, aliases, shapes, scratch = [], {}, [], []
+    for part in parts:
+        base = len(shapes)
+        for at, item in enumerate(part.operands):
+            if not isinstance(item, Link):
+                if at in part.aliases:
+                    aliases[len(operands)] = base + part.aliases[at]
+                operands.append(item)
+        shapes += part.shapes
+        for item in part.operands[: part.staged_in]:
+            if not (isinstance(item, Link) and item.at < parts[item.part].staged_out):
+                scratch.append(pltpu.VMEM(item.shape, item.dtype))
+        scratch += [pltpu.VMEM(item.shape, item.dtype) for item in part.shapes[: part.staged_out]]
+        scratch += [sem(part.staged_in), sem(part.staged_out)] + part.scratch
+
+    def body(*refs):
+        given, made, rest = refs[: len(operands)], refs[len(operands) : len(operands) + len(shapes)], list(
+            refs[len(operands) + len(shapes) :]
+        )
+        given, made = list(given), list(made)
+        ready, results, held = [], [], []
+        for part in parts:
+            outs = [made.pop(0) for _ in part.shapes]
+            inner, sources, late = [], [], []
+            for at, item in enumerate(part.operands):
+                if isinstance(item, Link):
+                    staged, whole = results[item.part]
+                    near = item.at < parts[item.part].staged_out
+                    source = None if near else whole[item.at]
+                    late.append(at)
+                else:
+                    near, source = False, given.pop(0)
+                if at >= part.staged_in:
+                    inner.append(source)
+                elif near:
+                    inner.append(staged[item.at])
+                    source = None
+                else:
+                    inner.append(rest.pop(0))
+                sources.append(source)
+            results_in = [rest.pop(0) for _ in range(part.staged_out)]
+            load_s, store_s = rest.pop(0), rest.pop(0)
+            own = [rest.pop(0) for _ in part.scratch]
+            loads = [
+                Done() if sources[k] is None else pltpu.make_async_copy(sources[k], inner[k], load_s.at[k])
+                for k in range(part.staged_in)
+            ]
+            stores = [pltpu.make_async_copy(results_in[k], outs[k], store_s.at[k]) for k in range(part.staged_out)]
+            for k, copy in enumerate(loads):
+                if k not in late:
+                    copy.start()
+            results.append((results_in, outs))
+            ready.append((loads, stores, late, inner, results_in + outs[part.staged_out :], own))
+        for at, part in enumerate(parts):
+            loads, stores, late, inner, outs, own = ready[at]
+            for k in late:
+                if k < part.staged_in:
+                    loads[k].start()
+            last = at == len(parts) - 1
+            if not last:
+                held += stores
+                stores = [Later(copy) for copy in stores]
+            part.kernel(loads, stores, greet if at == 0 else lambda: None, *inner, *outs, *own)
+        for copy in held:
+            copy.wait()
+
+    outside = pl.BlockSpec(memory_space=pl.ANY)
+    out = pl.pallas_call(
+        body,
+        out_shape=tuple(shapes),
+        in_specs=[outside] * len(operands),
+        out_specs=[outside] * len(shapes),
+        input_output_aliases=aliases,
+        scratch_shapes=scratch,
+        compiler_params=pltpu.CompilerParams(collective_id=ident, has_side_effects=True, vmem_limit_bytes=62 << 20),
+        cost_estimate=pl.CostEstimate(
+            flops=sum(part.flops for part in parts), bytes_accessed=8_000_000, transcendentals=0
+        ),
+        name="_".join(part.name for part in parts),
+    )(*operands)
+    out = list(out)
+    return [[out.pop(0) for _ in part.shapes] for part in parts]
+
+
 class Line:
     def __init__(self, tok, depth):
         self.z, self.x = lax.axis_index("z"), lax.axis_index("x")
@@ -356,23 +472,6 @@
             {"y": 1 - self.y, "c": 1 - self.c},
         )
 
-    def greet(self):
-        barrier = pltpu.get_barrier_semaphore()
-        for peer in self.peers:
-            pl.semaphore_signal(barrier, 1, device_id=peer, device_id_type=MESH_ID)
-
-        @pl.when(self.z > 0)
-        def _():
-            pl.semaphore_signal(barrier, 1, device_id={"z": self.z - 1}, device_id_type=MESH_ID)
-
-        @pl.when(self.z < self.depth - 1)
-        def _():
-            pl.semaphore_signal(barrier, 1, device_id={"z": self.z + 1}, device_id_type=MESH_ID)
-
-        pl.semaphore_signal(barrier, 1, device_id={"x": 1 - self.x}, device_id_type=MESH_ID)
-        inner = jnp.where(self.z > 0, 1, 0) + jnp.where(self.z < self.depth - 1, 1, 0)
-        pl.semaphore_wait(barrier, 4 + inner)
-
     def place(self, stream):
         return self.z if stream == 0 else self.depth - 1 - self.z
 
@@ -395,9 +494,9 @@
     span = GROUP_CHUNKS * ROWS
     half_groups = groups // 2
 
-    def run(line, taken, begin, prepare, beside, finish, second, settle, close, product, carried, chain_out, chain_in, wide, own_part, rs_out, rs_in,
+    def run(line, greet, taken, begin, prepare, beside, finish, second, settle, close, product, carried, chain_out, chain_in, wide, own_part, rs_out, rs_in,
             ag_s, ag_r, ch_s, ch_r, bc_s, bc_r, rs_s, rs_r):
-        line.greet()
+        greet()
         gather = [
             pltpu.make_async_remote_copy(
                 src_ref=taken.at[pl.ds(line.own, tok)],
@@ -598,13 +697,13 @@
 TILE = 256
 
 
-def ffn_forward(hidden, gain, gu_own, gu_peer, down_own, shipped, depth, ident):
+def ffn_forward(hidden, gain, gu_own, gu_peer, down_own, shipped, depth):
     tok, features = hidden.shape
     width = down_own.shape[1]
     run, scratch = make_line(tok, depth, 2 * width, width, True, False, features)
     count = len(shipped)
 
-    def kernel(h_ref, gain_ref, w1_own, w1_peer, w2_own, *rest):
+    def kernel(loads, stores, greet, h_ref, gain_ref, w1_own, w1_peer, w2_own, *rest):
         leave, rest = rest[:count], rest[count:]
         (out_ref, normed_t, kept, wide, w2_peer), rest = rest[:5], rest[5:]
         landed, rest = rest[:count], rest[count:]
@@ -613,9 +712,13 @@
         line = Line(tok, depth)
         side = Side(side_s, side_r)
         own, other = halves(features)
+        loads[0].wait()
         taken[pl.ds(line.own, tok), :] = h_ref[...].astype(jnp.bfloat16)
+        at_end = (line.z == 0) | (line.z == depth - 1)
 
         def begin():
+            for copy in loads[1:]:
+                copy.wait()
             side.start(w2_own, w2_peer)
             for source, target in zip(leave, landed):
                 side.start(source, target)
@@ -639,6 +742,7 @@
             @pl.when(i == SKEW * (depth - 1))
             def _():
                 side.copies[0].wait_recv()
+                stores[4].start()
 
         def finish(row, at, total, extra):
             factor = lax.rsqrt(extra / D + EPS)
@@ -657,17 +761,31 @@
             return pieces[...]
 
         def settle():
+            stores[3].start()
+
+            @pl.when(at_end)
+            def _():
+                stores[2].start()
+
             normed = taken[...].astype(jnp.float32) * unspread(wide[:, width:]) * gain_ref[...]
             normed_t[...] = jnp.transpose(normed).astype(jnp.bfloat16)
+            stores[1].start()
 
         def close():
             total = own_part[...]
             for slot in range(3):
                 total = total + rs_in[slot].astype(jnp.float32)
             out_ref[...] = h_ref[...] + total
+            stores[0].start()
             side.finish(side.copies[:1])
-
-        run(line, taken, begin, prepare, beside, finish, second, settle, close, product, carried, chain_out, chain_in, wide,
+            for at in (0, 1, 3, 4):
+                stores[at].wait()
+
+            @pl.when(at_end)
+            def _():
+                stores[2].wait()
+
+        run(line, greet, taken, begin, prepare, beside, finish, second, settle, close, product, carried, chain_out, chain_in, wide,
             own_part, rs_out, rs_in, *sems)
 
     low, full = jnp.bfloat16, jnp.float32
@@ -678,29 +796,20 @@
         jax.ShapeDtypeStruct((4 * tok, width + EXTRA), low),
         jax.ShapeDtypeStruct(down_own.shape, low),
     ) + tuple(jax.ShapeDtypeStruct(item.shape, item.dtype) for item in shipped)
-    inside, outside = pl.BlockSpec(memory_space=pltpu.VMEM), pl.BlockSpec(memory_space=pl.ANY)
-    out = pl.pallas_call(
-        kernel,
-        out_shape=shapes,
-        in_specs=[inside] * 5 + [outside] * count,
-        out_specs=[inside] * 5 + [outside] * count,
-        scratch_shapes=[
+    return Part(
+        kernel, (hidden, gain.reshape(1, -1), gu_own, gu_peer, down_own, *shipped), shapes, 5, 5,
+        [
             pltpu.VMEM((4 * tok, features), low),
             pltpu.VMEM((2 * tok, features), low),
             pltpu.VMEM((GROUP_CHUNKS * ROWS, features), full),
             sem(1 + count), sem(1 + count),
         ] + scratch,
-        compiler_params=pltpu.CompilerParams(
-            collective_id=ident, has_side_effects=True, vmem_limit_bytes=60 << 20
-        ),
-        cost_estimate=pl.CostEstimate(flops=60_000_000_000, bytes_accessed=8_000_000, transcendentals=0),
-        name="ffn_forward",
-    )(hidden, gain.reshape(1, -1), gu_own, gu_peer, down_own, *shipped)
-    return out[:5], out[5:]
+        {}, 60_000_000_000, "ffn_forward",
+    )
 
 
 def ffn_backward(
-    grad, hidden, gain, kept, wide_forward, gu_own, gu_peer, down_own, down_peer, shipped, stacks, index, layers, depth, ident
+    grad, hidden, gain, kept, wide_forward, gu_own, gu_peer, down_own, down_peer, shipped, stacks, index, layers, depth
 ):
     tok, features = hidden.shape
     width = down_own.shape[1]
@@ -709,7 +818,7 @@
     first_tile = SKEW + 1
     tiles = width // EXTRA
 
-    def kernel(dy_ref, h_ref, gain_ref, kept_ref, before_ref, w1_own, w1_peer, w2_own, w2_peer, *rest):
+    def kernel(loads, stores, greet, dy_ref, h_ref, gain_ref, kept_ref, before_ref, w1_own, w1_peer, w2_own, w2_peer, *rest):
         leave, rest = rest[:count], rest[count:]
         rest = rest[len(stacks):]
         (out_ref, wide, gain_out, kept_all, got_all), rest = rest[:5], rest[5:]
@@ -719,6 +828,7 @@
         line = Line(tok, depth)
         side = Side(side_s, side_r)
         own, other = halves(features)
+        loads[0].wait()
         taken[pl.ds(line.own, tok), :] = dy_ref[...].astype(jnp.bfloat16)
         give = side.later(down_given, got_all.at[index])
         keep = pltpu.make_async_copy(down_kept, kept_all.at[index], keep_s)
@@ -726,6 +836,8 @@
         def begin():
             for source, target in zip(leave, landed):
                 side.start(source, target)
+            loads[7].wait()
+            loads[8].wait()
 
         def prepare(row):
             rows = pl.ds(row, 2 * tok)
@@ -740,6 +852,11 @@
             lax.fori_loop(0, width // EXTRA, tile, 0)
 
         def beside(i):
+            @pl.when(i == 1)
+            def _():
+                for copy in loads[1:7]:
+                    copy.wait()
+
             @pl.when(i == first_tile)
             def _():
                 turned[...] = flip(taken[...])
@@ -772,6 +889,9 @@
             pieces[:, other] = transposed_dot(value, w1_peer[...])
             return pieces[...]
 
+        def settle():
+            stores[1].start()
+
         def close():
             total = own_part[...]
             inner = unspread(wide[pl.ds(line.own, tok), 2 * width :])
@@ -782,10 +902,14 @@
             normed = h_ref[...] * factor
             gain_out[...] = jnp.broadcast_to(jnp.sum(total * normed, axis=0, keepdims=True), gain_out.shape)
             out_ref[...] = dy_ref[...] + factor * (total * gain_ref[...] - normed * (inner / D))
+            stores[2].start()
+            stores[0].start()
             keep.wait()
             side.finish()
-
-        run(line, taken, begin, prepare, beside, finish, second, lambda: None, close, product, carried, chain_out, chain_in,
+            for copy in stores:
+                copy.wait()
+
+        run(line, greet, taken, begin, prepare, beside, finish, second, settle, close, product, carried, chain_out, chain_in,
             wide, own_part, rs_out, rs_in, *sems)
 
     low, full = jnp.bfloat16, jnp.float32
@@ -796,14 +920,11 @@
         jax.ShapeDtypeStruct((layers,) + down_own.shape, low),
         jax.ShapeDtypeStruct((layers,) + down_own.shape, low),
     ) + tuple(jax.ShapeDtypeStruct(item.shape, item.dtype) for item in shipped)
-    inside, outside = pl.BlockSpec(memory_space=pltpu.VMEM), pl.BlockSpec(memory_space=pl.ANY)
-    out = pl.pallas_call(
+    return Part(
         kernel,
-        out_shape=shapes,
-        in_specs=[inside] * 9 + [outside] * (count + len(stacks)),
-        out_specs=[inside] * 3 + [outside] * (2 + count),
-        input_output_aliases={9 + count + at: 3 + at for at in range(len(stacks))},
-        scratch_shapes=[
+        (grad, hidden, gain.reshape(1, -1), kept, wide_forward, gu_own, gu_peer, down_own, down_peer, *shipped, *stacks),
+        shapes, 9, 3,
+        [
             pltpu.VMEM((4 * tok, features), low),
             pltpu.VMEM((features, 4 * tok), low),
             pltpu.VMEM(down_own.shape, low),
@@ -812,13 +933,8 @@
             pltpu.VMEM((GROUP_CHUNKS * ROWS, features), full),
             sem(1 + count), sem(1 + count),
         ] + scratch,
-        compiler_params=pltpu.CompilerParams(
-            collective_id=ident, has_side_effects=True, vmem_limit_bytes=60 << 20
-        ),
-        cost_estimate=pl.CostEstimate(flops=60_000_000_000, bytes_accessed=8_000_000, transcendentals=0),
-        name="ffn_backward",
-    )(grad, hidden, gain.reshape(1, -1), kept, wide_forward, gu_own, gu_peer, down_own, down_peer, *shipped, *stacks)
-    return out[:5], out[5:]
+        {9 + count + at: 3 + at for at in range(len(stacks))}, 60_000_000_000, "ffn_backward",
+    )
 
 
 def to_row(column):
@@ -1004,7 +1120,7 @@
                 row_copy.wait_send()
 
 
-def attention_forward(hidden, gain, qkv_own, out_own, qkv_peer, out_peer, shipped, cosine, sine, depth, ident):
+def attention_forward(hidden, gain, qkv_own, out_own, qkv_peer, out_peer, shipped, cosine, sine, depth):
     tok, features = hidden.shape
     cols = qkv_own.shape[1]
     fetch = qkv_peer is None
@@ -1016,7 +1132,7 @@
     pairs = query_cols // EXTRA
     scale = 1.0 / math.sqrt(HEAD)
 
-    def kernel(h_ref, gain_ref, wqkv_own, wo_own, cos_ref, sin_ref, *rest):
+    def kernel(loads, stores, greet, h_ref, gain_ref, wqkv_own, wo_own, cos_ref, sin_ref, *rest):
         if not fetch:
             (wqkv_peer, wo_peer), rest = rest[:2], rest[2:]
         leave, rest = rest[:count], rest[count:]
@@ -1029,19 +1145,24 @@
         square = Square(tok, depth)
         side = Side(*rest) if sides else None
         mine, other = halves(features)
+        loads[0].wait()
         taken[pl.ds(square.own, tok), :] = h_ref[...].astype(jnp.bfloat16)
-        square.greet()
+        greet()
         gather = start_gather(square, taken, ag_s, ag_r)
+        for copy in loads[1:]:
+            copy.wait()
         urgent = []
         if fetch:
             urgent = [side.start(wqkv_own, wqkv_peer), side.start(wo_own, wo_peer)]
         held = []
         for source, target in zip(leave, landed):
-            half = source.shape[0] // 2
-            side.start(source.at[pl.ds(0, half)], target.at[pl.ds(0, half)])
-            held.append(side.later(source.at[pl.ds(half, half)], target.at[pl.ds(half, half)]))
+            most = source.shape[0] // 2
+            rest_of = pl.ds(most, source.shape[0] - most)
+            side.start(source.at[pl.ds(0, most)], target.at[pl.ds(0, most)])
+            held.append(side.later(source.at[rest_of], target.at[rest_of]))
         for copy in urgent[:1]:
             copy.wait_recv()
+            stores[7].start()
 
         def product(row):
             block = taken[pl.ds(row, tok), :].astype(jnp.float32)
@@ -1062,10 +1183,17 @@
         given = send_row(square, factors, zgr_s, zgr_r)
         for copy in given:
             copy.start()
-        turned = turn(total * to_column(factor_row), cos_ref[...], sin_ref[...])
+        first = lax.broadcasted_iota(jnp.int32, (tok, EXTRA), 1) < HEAD
+        cosine_row, sine_row = cos_ref[...], sin_ref[...]
+        turned = turn(
+            total * to_column(factor_row),
+            jnp.concatenate([cosine_row] * pairs + [jnp.where(first, cosine_row, 1.0)], axis=1),
+            jnp.concatenate([sine_row] * pairs + [jnp.where(first, sine_row, 0.0)], axis=1),
+        )
         here = pl.ds(pl.multiple_of(square.row * tok, tok), tok)
         kv[here, :] = turned[:, query_cols:].astype(jnp.bfloat16)
         queries[...] = turned[:, :query_cols].astype(jnp.bfloat16)
+        stores[2].start()
         spreads = []
         for step in range(1, 2 * depth):
             copy = remote(kv.at[here], kv.at[here], kv_s.at[step - 1], kv_r.at[2 * depth - 1 - step], square.row_peer(step))
@@ -1073,6 +1201,7 @@
             spreads.append(copy)
         for copy in spreads:
             copy.wait_recv()
+        stores[3].start()
         for copy in held:
             copy.start()
         keys, both = twice(kv[...])
@@ -1099,8 +1228,10 @@
         lax.fori_loop(0, pairs, pair, 0)
         given += [copy for part in range(pairs) for copy in send_part(square, mixed, part, zg_s, zg_r)]
 
+        stores[4].start()
         for copy in urgent[1:]:
             copy.wait_recv()
+            stores[8].start()
 
         def second(row):
             value = mixed[pl.ds(row, tok), :]
@@ -1109,22 +1240,28 @@
             return pieces[...]
 
         def settle():
+            stores[5].start()
+            stores[6].start()
             for block in range(depth):
                 rows = pl.ds(block * tok, tok)
                 normed = taken[rows, :].astype(jnp.float32) * to_column(factors[block]) * gain_ref[...]
                 normed_t[:, rows] = jnp.transpose(normed).astype(jnp.bfloat16)
+            stores[1].start()
 
         sums = grid_sum(square, mixed, factors, second, settle, g_own, g_out, g_in, None, zg_r, zgr_r, gs_s, gs_r, None, None)
         total = g_own[...]
         for slot in range(depth - 1):
             total = total + g_in[slot].astype(jnp.float32)
         out_ref[...] = h_ref[...] + total
+        stores[0].start()
         drain(sent)
         drain(sums)
         for copy in gather + spreads + given:
             copy.wait_send()
         if side:
             side.finish(urgent)
+        for copy in stores:
+            copy.wait()
 
     low, full = jnp.bfloat16, jnp.float32
     shapes = (
@@ -1139,14 +1276,11 @@
     if fetch:
         shapes += (jax.ShapeDtypeStruct(qkv_own.shape, low), jax.ShapeDtypeStruct(out_own.shape, low))
     shapes += tuple(jax.ShapeDtypeStruct(item.shape, item.dtype) for item in shipped)
-    inside, outside = pl.BlockSpec(memory_space=pltpu.VMEM), pl.BlockSpec(memory_space=pl.ANY)
     peers = () if fetch else (qkv_peer, out_peer)
-    out = pl.pallas_call(
-        kernel,
-        out_shape=shapes,
-        in_specs=[inside] * (6 + len(peers)) + [outside] * count,
-        out_specs=[inside] * (7 + extra) + [outside] * count,
-        scratch_shapes=[
+    operands = (hidden, gain.reshape(1, -1), qkv_own, out_own, cosine, sine, *peers, *shipped)
+    return Part(
+        kernel, operands, shapes, 6 + len(peers), 7 + extra,
+        [
             pltpu.VMEM((depth * tok, features), low),
             pltpu.VMEM((tok, features), low),
             pltpu.VMEM((tok, features), full),
@@ -1164,19 +1298,13 @@
             sem(2 * depth - 1), sem(2 * depth - 1), sem(depth - 1, pairs), sem(depth - 1, pairs), sem(depth - 1), sem(depth - 1),
             sem(depth), sem(depth - 1),
         ] + ([sem(sides), sem(sides)] if sides else []),
-        compiler_params=pltpu.CompilerParams(
-            collective_id=ident, has_side_effects=True, vmem_limit_bytes=60 << 20
-        ),
-        cost_estimate=pl.CostEstimate(flops=50_000_000_000, bytes_accessed=8_000_000, transcendentals=0),
-        name="attention_forward",
-    )(hidden, gain.reshape(1, -1), qkv_own, out_own, cosine, sine, *peers, *shipped)
-    peers = out[7:9] if fetch else peers
-    return out[:7], peers, out[7 + extra :]
+        {}, 50_000_000_000, "attention_forward",
+    )
 
 
 def attention_backward(
     grad, hidden, gain, qkv_own, qkv_peer, out_own, out_peer, cosine, sine, queries, kv, lse, factors, mixed, normed_a, normed_f,
-    grad_gu, stacks, index, layers, depth, ident,
+    grad_gu, stacks, index, layers, depth,
 ):
     tok, features = hidden.shape
     cols = qkv_own.shape[1]
@@ -1186,7 +1314,7 @@
     pairs = query_cols // EXTRA
     scale = 1.0 / math.sqrt(HEAD)
 
-    def kernel(dy_ref, h_ref, gain_ref, wqkv_own, wqkv_peer, wo_own, wo_peer, cos_ref, sin_ref, q_ref, kv_ref, lse_ref,
+    def kernel(loads, stores, greet, dy_ref, h_ref, gain_ref, wqkv_own, wqkv_peer, wo_own, wo_peer, cos_ref, sin_ref, q_ref, kv_ref, lse_ref,
                factor_ref, mixed_ref, normed_a_ref, normed_f_ref, gu_ref, *rest_refs):
         (out_ref, gain_out, qkv_given, gu_kept_all, gu_got_all, out_kept_all, out_got_all, qkv_kept_all,
                taken, spun, turned, pieces, gu_kept, gu_given, out_kept, out_given, qkv_kept, keep_s,
@@ -1195,9 +1323,12 @@
         square = Square(tok, depth)
         side = Side(side_s, side_r)
         mine, other = halves(features)
+        loads[0].wait()
         taken[pl.ds(square.own, tok), :] = dy_ref[...].astype(jnp.bfloat16)
-        square.greet()
+        greet()
         gather = start_gather(square, taken, ag_s, ag_r)
+        for copy in loads[1:]:
+            copy.wait()
 
         def gu_tiles(start, stop):
             def tile(j, _):
@@ -1267,7 +1398,7 @@
             dq[...] += jnp.broadcast_to(
                 jnp.sum(value * q_ref[:, lanes].astype(jnp.float32), axis=1, keepdims=True), dq.shape
             )
-            spun[pl.ds(square.mine, tok), lanes] = turn(value, cos_ref[:, lanes], -sin_ref[:, lanes]).astype(jnp.bfloat16)
+            spun[pl.ds(square.mine, tok), lanes] = turn(value, cos_ref[...], -sin_ref[...]).astype(jnp.bfloat16)
             for copy in send_part(square, spun, t, zg_s, zg_r):
                 copy.start()
             return 0
@@ -1301,8 +1432,9 @@
         side.start(gu_given.at[:, rest], gu_got.at[:, rest])
         for slot in range(2 * depth - 1):
             total_kv = total_kv + kv_in[slot].astype(jnp.float32)
+        first = lax.broadcasted_iota(jnp.int32, (tok, EXTRA), 1) < HEAD
         spun[pl.ds(square.mine, tok), query_cols:] = turn(
-            total_kv, cos_ref[:, query_cols:], -sin_ref[:, query_cols:]
+            total_kv, jnp.where(first, cos_ref[...], 1.0), jnp.where(first, -sin_ref[...], 0.0)
         ).astype(jnp.bfloat16)
         inner = dq[:, :1] + jnp.sum(total_kv * kv_ref[here, :].astype(jnp.float32), axis=1, keepdims=True)
         inner_rows[square.z] = to_row(inner)
@@ -1321,6 +1453,7 @@
             for t in range(cols // EXTRA):
                 grad_tile(normed_a_ref, features, spun, pl.ds(t * EXTRA, EXTRA), qkv_kept, qkv_given)
             keeps[2].start()
+            stores[2].start()
 
         sums = grid_sum(
             square, spun, inner_rows, second, settle, g_own, g_out, g_in, g_rows, zg_r, zgr_r, gs_s, gs_r, gr_s, gr_r
@@ -1334,11 +1467,13 @@
         normed = h_ref[...] * factor
         gain_out[...] = jnp.broadcast_to(jnp.sum(total * normed, axis=0, keepdims=True), gain_out.shape)
         out_ref[...] = dy_ref[...] + factor * (total * gain_ref[...] - normed * (to_column(inner) / D))
+        stores[0].start()
+        stores[1].start()
         drain(sent)
         drain(sums)
         for copy in gather + spreads + given:
             copy.wait_send()
-        for copy in keeps:
+        for copy in keeps + stores:
             copy.wait()
         side.finish()
 
@@ -1353,14 +1488,13 @@
         jax.ShapeDtypeStruct((layers,) + out_own.shape, low),
         jax.ShapeDtypeStruct((layers,) + qkv_own.shape, low),
     )
-    inside, outside = pl.BlockSpec(memory_space=pltpu.VMEM), pl.BlockSpec(memory_space=pl.ANY)
-    return pl.pallas_call(
-        kernel,
-        out_shape=shapes,
-        in_specs=[inside] * 17 + [outside] * len(stacks),
-        out_specs=[inside] * 3 + [outside] * 5,
-        input_output_aliases={17 + at: 3 + at for at in range(len(stacks))},
-        scratch_shapes=[
+    operands = (
+        grad, hidden, gain.reshape(1, -1), qkv_own, qkv_peer, out_own, out_peer, cosine, sine, queries, kv, lse, factors,
+        mixed, normed_a, normed_f, grad_gu, *stacks,
+    )
+    return Part(
+        kernel, operands, shapes, 17, 3,
+        [
             pltpu.VMEM((depth * tok, features), low),
             pltpu.VMEM((depth * tok, cols), low),
             pltpu.VMEM((features, depth * tok), low),
@@ -1390,19 +1524,16 @@
             sem(2 * depth - 1), sem(2 * depth - 1), sem(depth - 1, pairs + 1), sem(depth - 1, pairs + 1), sem(depth - 1),
             sem(depth - 1), sem(depth), sem(depth - 1), sem(depth), sem(depth - 1), sem(4), sem(4),
         ],
-        compiler_params=pltpu.CompilerParams(collective_id=ident, has_side_effects=True, vmem_limit_bytes=60 << 20),
-        cost_estimate=pl.CostEstimate(flops=50_000_000_000, bytes_accessed=8_000_000, transcendentals=0),
-        name="attention_backward",
-    )(grad, hidden, gain.reshape(1, -1), qkv_own, qkv_peer, out_own, out_peer, cosine, sine, queries, kv, lse, factors, mixed,
-      normed_a, normed_f, grad_gu, *stacks)
-
-
-def finish(grad, gains, qkv_given, depth, ident):
+        {17 + at: 3 + at for at in range(len(stacks))}, 50_000_000_000, "attention_backward",
+    )
+
+
+def finish(grad, gains, qkv_given, depth):
     tok, features = grad.shape
     count = len(gains)
     members = 2 * depth
 
-    def kernel(grad_ref, *rest):
+    def kernel(loads, stores, greet, grad_ref, *rest):
         gain_refs, rest = rest[:count], rest[count:]
         (given, out_ref, gain_out, got, packed, parts, sent, home, part_s, part_r, move_s, move_r, side_s, side_r) = rest
         z, x = lax.axis_index("z"), lax.axis_index("x")
@@ -1430,6 +1561,8 @@
                 pl.semaphore_signal(barrier, 1, device_id=source(slot), device_id_type=MESH_ID)
 
         pl.semaphore_signal(barrier, 1, device_id={"x": 1 - x}, device_id_type=MESH_ID)
+        for copy in loads:
+            copy.wait()
         for at, ref in enumerate(gain_refs):
             packed[at : at + 1, :] = ref[:1, :]
         sent[...] = grad_ref[...].astype(jnp.bfloat16)
@@ -1465,6 +1598,7 @@
         for slot in range(1, members):
             total = total + parts[slot]
         gain_out[...] = total
+        stores[1].start()
 
         @pl.when(z == g)
         def _():
@@ -1476,6 +1610,7 @@
             out_ref[...] = home[...].astype(jnp.float32)
             move.wait_send()
 
+        stores[0].start()
         for at in range(members):
 
             @pl.when(jnp.logical_not(is_target_me(at)))
@@ -1483,19 +1618,18 @@
                 part(at).wait_send()
 
         side.finish()
+        for copy in stores:
+            copy.wait()
 
     low, full = jnp.bfloat16, jnp.float32
-    inside, outside = pl.BlockSpec(memory_space=pltpu.VMEM), pl.BlockSpec(memory_space=pl.ANY)
-    return pl.pallas_call(
-        kernel,
-        out_shape=(
-            jax.ShapeDtypeStruct((tok, features), full),
-            jax.ShapeDtypeStruct((count, features), full),
-            jax.ShapeDtypeStruct(qkv_given.shape, low),
-        ),
-        in_specs=[inside] * (1 + count) + [outside],
-        out_specs=[inside, inside, outside],
-        scratch_shapes=[
+    shapes = (
+        jax.ShapeDtypeStruct((tok, features), full),
+        jax.ShapeDtypeStruct((count, features), full),
+        jax.ShapeDtypeStruct(qkv_given.shape, low),
+    )
+    return Part(
+        kernel, (grad, *gains, qkv_given), shapes, 1 + count, 2,
+        [
             pltpu.VMEM((count, features), full),
             pltpu.VMEM((members, count, features), full),
             pltpu.VMEM((tok, features), low),
@@ -1504,10 +1638,8 @@
             pltpu.SemaphoreType.DMA, pltpu.SemaphoreType.DMA,
             sem(1), sem(1),
         ],
-        compiler_params=pltpu.CompilerParams(collective_id=ident, has_side_effects=True),
-        cost_estimate=pl.CostEstimate(flops=5_000_000_000, bytes_accessed=1_000_000, transcendentals=0),
-        name="finish",
-    )(grad, *gains, qkv_given)
+        {}, 5_000_000_000, "finish",
+    )
 
 
 def stationary(stream, grad_out, wqkv, wo, wgu, wd, gain_attn, gain_ffn):
@@ -1518,17 +1650,17 @@
     head = HEAD
     row = lax.axis_index("z") * 2 + lax.axis_index("x")
     query_pos = row * tok + jnp.arange(tok, dtype=jnp.int32)
-    lane = jnp.arange((GROUP + 2) * head, dtype=jnp.int32)
+    lane = jnp.arange(EXTRA, dtype=jnp.int32)
     half = head // 2
     freq = THETA ** (-((lane % half).astype(jnp.float32) * 2.0 / head))
     angle = query_pos.astype(jnp.float32)[:, None] * freq[None, :]
-    rotated = (lane < (GROUP + 1) * head)[None, :]
-    cosine = jnp.where(rotated, jnp.cos(angle), 1.0)
-    sine = jnp.where(rotated, jnp.where((lane % head < half)[None, :], -1.0, 1.0) * jnp.sin(angle), 0.0)
+    cosine = jnp.cos(angle)
+    sine = jnp.where((lane % head < half)[None, :], -1.0, 1.0) * jnp.sin(angle)
     current = swap_grid(stream, depth)
     grad_now = swap_grid(grad_out, depth)
-    gain_a = swap_grid(gain_attn, depth)
-    gain_f = swap_grid(gain_ffn, depth)
+    gains = swap_grid(jnp.concatenate([gain_attn, gain_ffn]), depth)
+    gain_a, gain_f = gains[:layers], gains[layers:]
+    greet = lambda: Square(tok, depth).greet()
     own_qkv = [wqkv[index].reshape(count_rows, -1) for index in range(layers)]
     own_out = [wo[index] for index in range(layers)]
     own_gu = [wgu[index].reshape(count_rows, -1) for index in range(layers)]
@@ -1537,37 +1669,47 @@
     saved = []
     for index in range(layers):
         before = current
-        (hidden_in, normed_a, queries, kv, lse, mixed, factors), (peer_qkv[index], peer_out[index]), landed = attention_forward(
-            before, gain_a[index], own_qkv[index], own_out[index], peer_qkv[index], peer_out[index],
-            [] if index else own_gu[:1], cosine, sine, depth, 4 * index
-        )
-        if landed:
-            peer_gu[0] = landed[0]
+        first = index == 0
         follow = index + 1
         shipped = [own_qkv[follow], own_out[follow], own_gu[follow]] if follow < layers else []
-        (current, normed_f, kept, active, peer_down[index]), landed = ffn_forward(
-            hidden_in, gain_f[index], own_gu[index], peer_gu[index], own_down[index], shipped, depth, 4 * index + 1
+        attend = attention_forward(
+            before, gain_a[index], own_qkv[index], own_out[index], peer_qkv[index], peer_out[index],
+            own_gu[:1] if first else [], cosine, sine, depth
         )
-        if landed:
-            peer_qkv[follow], peer_out[follow], peer_gu[follow] = landed
+        feed = ffn_forward(
+            attend.link(0), gain_f[index], own_gu[index], attend.link(len(attend.shapes) - 1) if first else peer_gu[index],
+            own_down[index], shipped, depth
+        )
+        made, fed = launch([attend, feed], greet, 2 * index)
+        hidden_in, normed_a, queries, kv, lse, mixed, factors = made[:7]
+        if first:
+            peer_qkv[0], peer_out[0], peer_gu[0] = made[7:]
+        current, normed_f, kept, active, peer_down[index] = fed[:5]
+        if shipped:
+            peer_qkv[follow], peer_out[follow], peer_gu[follow] = fed[5:]
         saved.append((before, normed_a, queries, kv, lse, mixed, factors, hidden_in, normed_f, kept, active))
     list_ga, list_gf, got_qkv, pending, down_stack, rest_stack = ([], [], [], [], [], [])
     for index in reversed(range(layers)):
         before, normed_a, queries, kv, lse, mixed, factors, hidden_in, normed_f, kept, active = saved[index]
-        (grad_hidden, grad_gu, gain_f_grad, *down_stack), landed = ffn_backward(
+        feed = ffn_backward(
             grad_now, hidden_in, gain_f[index], kept, active, own_gu[index], peer_gu[index], own_down[index],
-            peer_down[index], pending[-1:], down_stack, index, layers, depth, 4 * index + 2
+            peer_down[index], pending[-1:], down_stack, index, layers, depth
         )
-        got_qkv.extend(landed)
-        list_gf.append(gain_f_grad)
-        (grad_now, gain_a_grad, qkv_given, *rest_stack) = attention_backward(
-            grad_hidden, before, gain_a[index], own_qkv[index], peer_qkv[index], own_out[index], peer_out[index],
-            cosine, sine, queries, kv, lse, factors, mixed, normed_a, normed_f, grad_gu, rest_stack, index, layers, depth,
-            4 * index + 3
+        attend = attention_backward(
+            feed.link(0), before, gain_a[index], own_qkv[index], peer_qkv[index], own_out[index], peer_out[index],
+            cosine, sine, queries, kv, lse, factors, mixed, normed_a, normed_f, feed.link(1), rest_stack, index, layers,
+            depth
         )
+        fed, made = launch([feed, attend], greet, 2 * index + 1)
+        down_stack = fed[3:5]
+        got_qkv.extend(fed[5:])
+        list_gf.append(fed[2])
+        (grad_now, gain_a_grad, qkv_given, *rest_stack) = made
         pending.append(qkv_given)
         list_ga.append(gain_a_grad)
-    grad_in, gains, last_qkv = finish(grad_now, list_ga[::-1] + list_gf[::-1], qkv_given, depth, 4 * layers)
+    ((grad_in, gains, last_qkv),) = launch(
+        [finish(grad_now, list_ga[::-1] + list_gf[::-1], qkv_given, depth)], None, 2 * layers
+    )
     got_qkv.append(last_qkv)
     gu_kept, gu_got, out_kept, out_got, qkv_kept = rest_stack
     add = lambda kept, got: kept.astype(jnp.float32) + got.astype(jnp.float32)

time: 641 us -> 595 us (0.928); the launches traced: 630 us -> 591 us
  Pallas kernels: 574 us -> 536 us
    pallas_call x9 -> x5, Pallas kernels: 574 us -> 536 us  [launch(): pl.pallas_call(body, out_shape=tuple(shapes), in_specs=[outside] * len(op...]
    ppermute x5 -> x4, starting transfers between devices: 17.3 us -> 14 us  [swap_grid(): return lax.ppermute(values, ('z', 'y', 'c'), pairs)]
  transfers between devices with their start and end apart: 5 -> 4, of which waited for: 1 -> 1; matrix products, arithmetic and copies ran while one was open for 5% -> 5% of each run, Pallas kernels for 91% -> 91%
where the time goes in v6:
time: 595 us; the launch traced here: 591 us
  Pallas kernels  536 us (90%)
  local copies, waits for them, and re-layouts  25.4 us (4%)
  starting transfers between devices  14 us (2%)
  other arithmetic  11.1 us (2%)
    pallas_call x5, Pallas kernels, launch(): pl.pallas_call(body, out_shape=tuple(shapes), in_specs=[outside] * len(op...  536 us
    ppermute x4, starting transfers between devices, swap_grid(): return lax.ppermute(values, ('z', 'y', 'c'), pairs)  14 us
  transfers between devices with their start and end apart: 4, of which 1 were waited for; matrix products, arithmetic and copies ran while one was open for 5% of the time, Pallas kernels for 91%

profile of v6, /device:TPU:4, one launch (start us, length us, event | category | flops | bytes accessed | tf_op | source)
XLA Modules:
  0.0 591.0 jit_solution(6553820107593487268)
XLA Ops:
  0.6 0.0 copy-start.2
  0.6 0.8 pad_maximum_fusion
  1.5 4.4 collective-permute-start.1
  5.9 3.2 collective-permute-start
  9.1 4.4 collective-permute-start.3
  13.6 1.9 slice_bitcast_fusion.4
  15.5 2.0 slice_bitcast_fusion.2
  17.4 0.0 copy-done.2
  17.4 0.0 copy-start
  17.4 1.2 slice_bitcast_fusion
  18.6 1.1 copy-done
  19.8 2.0 fusion.5
  21.8 1.0 fusion
  22.8 1.3 copy.25
  24.1 1.3 copy.24
  25.3 0.0 collective-permute-done.1
  25.3 0.6 fusion.7
  25.9 4.0 collective-permute-done.refs_0_.refs_12_
  29.9 0.0 copy-start.11
  29.9 0.7 copy-done.11
  30.6 131.4 %attention_forward_ffn_forward.2 = (f32[128,512]{1,0:T(8,128)}, bf16[512,512]{1,0:T(8,128)(2,1)}, bf16[128,512]{1,0:T(8,128)(2,1)}, bf16[1024,128]{1,0:T(8,128)(...) custom-call(f32[128,512]{1,0:T(8,128)} %copy-done.11, ...), custom_call_target="tpu_custom_call" | custom-call | flops 109999996928 | bytes 8000000 | tf_op jit(solution)/shard_map/attention_forward_ffn_forward/pallas_call | solution.py:444
  162.0 131.7 %attention_forward_ffn_forward.3 = (f32[128,512]{1,0:T(8,128)}, bf16[512,512]{1,0:T(8,128)(2,1)}, bf16[128,512]{1,0:T(8,128)(2,1)}, bf16[1024,128]{1,0:T(8,128)(...) custom-call(f32[128,512]{1,0:T(8,128)} %get-tuple-element.64.refs_0_, ...), custom_call_target="tpu_custom_call" | custom-call | flops 109999996928 | bytes 8000000 | tf_op jit(solution)/shard_map/attention_forward_ffn_forward/pallas_call | solution.py:444
  293.7 1.9 collective-permute-start.2
  295.6 0.0 collective-permute-done.3.refs_0_
  295.6 129.6 %ffn_backward_attention_backward.2 = (f32[128,512]{1,0:T(8,128)}, bf16[512,2944]{1,0:T(8,128)(2,1)}, f32[8,512]{1,0:T(8,128)}, bf16[2,256,1408]{2,1,0:T(8,128)(2...) custom-call(f32[128,512]{1,0:T(8,128)} %collective-permute-done.3.re, ...), custom_call_target="tpu_custom_call" | custom-call | flops 109999996928 | bytes 8000000 | tf_op jit(solution)/shard_map/ffn_backward_attention_backward/pallas_call | solution.py:444
  425.2 126.5 %ffn_backward_attention_backward.3 = (f32[128,512]{1,0:T(8,128)}, bf16[512,2944]{1,0:T(8,128)(2,1)}, f32[8,512]{1,0:T(8,128)}, bf16[2,256,1408]{2,1,0:T(8,128)(2...) custom-call(f32[128,512]{1,0:T(8,128)} %get-tuple-element.80.refs_0_, ...), custom_call_target="tpu_custom_call", output_to_operand_aliasing={{3}: (10, {}), {4}: (11, {}), {9}: (27, {}), {10}: (28, {})... | custom-call | flops 109999996928 | bytes 8000000 | tf_op jit(solution)/shard_map/ffn_backward_attention_backward/pallas_call | solution.py:444
  551.7 0.0 copy-start.5
  551.7 0.0 copy-start.8
  551.7 16.6 %finish.1 = (f32[128,512]{1,0:T(8,128)}, f32[4,512]{1,0:T(4,128)}, bf16[256,640]{1,0:T(8,128)(2,1)}) custom-call(f32[128,512]{1,0:T(8,128)} %get-tuple-element.103.refs_0_, f32[8,512]{1,0:T(8,128)} %get-tuple-element.104.refs_1_, f32[8,512]{1,0:T(8,128)} %get-tuple-element.105.refs_2_, f32[8,512]{1,0:T(8,128)} %get-tuple-element.106.refs_3_, ...), custom_call_target="tpu_custom_call" | custom-call | flops 5000000000 | bytes 8000000 | tf_op jit(solution)/shard_map/finish/pallas_call | solution.py:444
  568.3 0.0 copy-done.5
  568.3 0.0 copy-done.8
  568.3 0.0 copy-start.1
  568.4 1.3 add_bitcast_fusion
  569.6 0.0 copy-start.10
  569.6 2.4 copy.23
  572.0 0.0 copy-done.10
  572.0 0.6 fusion.6
  572.6 0.0 copy-done.1
  572.6 5.0 convert_add_fusion
  577.7 0.0 copy-start.3
  577.7 0.0 copy-start.4
  577.7 7.9 %reshape.53 = f32[2,256,2,1408]{3,2,1,0:T(2,128)} reshape(f32[2,256,2816]{2,1,0:T(8,128)} %convert_add_fusion) | data formatting | bytes 11534336 | tf_op jit(solution)/shard_map/reshape | solution.py:1721
  585.6 0.0 copy-done.3
  585.6 0.0 copy-done.4
  585.6 0.0 copy-start.6
  585.6 0.0 copy-start.7
  585.6 1.9 convert_add_fusion.1
  587.5 0.0 copy-start.9
  587.5 0.0 copy-done.6
  587.5 0.0 copy-done.7
  587.5 1.1 convert_add_fusion.2
  588.6 0.0 collective-permute-done.2
  588.6 1.7 copy.35
  590.3 0.0 copy-done.9
  590.3 0.7 copy.36
  (2 shorter events, 0.0 us)
Async XLA Ops:
  0.6 16.8 %copy-start.2 = (bf16[2,256,1408]{2,1,0:T(8,128)(2,1)S(1)}, bf16[2,256,1408]{2,1,0:T(8,128)(2,1)}, u32[]{:S(2)}) copy-start(bf16[2,256,1408]{2,1,0:T(8,128)(2,1)} %param.13) | copy-start | bytes 4325380
  1.5 23.9 %collective-permute-start.1 = (f32[4,512]{1,0:T(4,128)S(1)}, f32[4,512]{1,0:T(4,128)S(1)}, u32[]{:S(2)}, u32[]{:S(2)}) collective-permute-start(f32[4,512]{1,0:T(4,128)S(1)} %pad_maximum_fusion), channel_id=1, source_target_pairs={{0,0},{1,8},{2,16},{3,24},{8,1},{9,9},{10,17},{11,25},{16,2},{17,1... | collective-permute-start | bytes 24584 | tf_op jit(solution)/shard_map/ppermute | solution.py:265
  5.9 24.0 %collective-permute-start = (f32[128,512]{1,0:T(8,128)}, f32[128,512]{1,0:T(8,128)S(1)}, u32[]{:S(2)}, u32[]{:S(2)}) collective-permute-start(f32[128,512]{1,0:T(8,128)} %param.8), channel_id=1, source_target_pairs={{0,0},{1,8},{2,16},{3,24},{8,1},{9,9},{10,17},{11,25},{16,2},{17,1... | collective-permute-start | bytes 786440 | tf_op jit(solution)/shard_map/ppermute | solution.py:265
  9.1 286.5 %collective-permute-start.3 = (f32[128,512]{1,0:T(8,128)}, f32[128,512]{1,0:T(8,128)}, u32[]{:S(2)}, u32[]{:S(2)}) collective-permute-start(f32[128,512]{1,0:T(8,128)} %param.9), channel_id=1, source_target_pairs={{0,0},{1,8},{2,16},{3,24},{8,1},{9,9},{10,17},{11,25},{16,2},{17,1... | collective-permute-start | bytes 786440 | tf_op jit(solution)/shard_map/ppermute | solution.py:265
  17.4 2.3 copy-start
  29.9 0.7 copy-start.11
  293.7 295.0 %collective-permute-start.2 = (f32[128,512]{1,0:T(8,128)}, f32[128,512]{1,0:T(8,128)}, u32[]{:S(2)}, u32[]{:S(2)}) collective-permute-start(f32[128,512]{1,0:T(8,128)} %get-tuple-element.68), channel_id=1, source_target_pairs={{0,0},{1,8},{2,16},{3,24},{8,1},{9,9},{10,17},{11,25},{16,2},{17,1... | collective-permute-start | bytes 786440 | tf_op jit(solution)/shard_map/ppermute | solution.py:265
  551.7 16.6 %copy-start.5 = (bf16[2,256,640]{2,1,0:T(8,128)(2,1)S(1)}, bf16[2,256,640]{2,1,0:T(8,128)(2,1)}, u32[]{:S(2)}) copy-start(bf16[2,256,640]{2,1,0:T(8,128)(2,1)} %get-tuple-element.110) | copy-start | bytes 1966084
  551.7 16.6 %copy-start.8 = (bf16[256,640]{1,0:T(8,128)(2,1)S(1)}, bf16[256,640]{1,0:T(8,128)(2,1)}, u32[]{:S(2)}) copy-start(bf16[256,640]{1,0:T(8,128)(2,1)} %get-tuple-element.112) | copy-start | bytes 983044
  568.3 4.3 copy-start.1
  569.6 2.4 copy-start.10
  577.7 7.9 %copy-start.3 = (bf16[2,256,1408]{2,1,0:T(8,128)(2,1)S(1)}, bf16[2,256,1408]{2,1,0:T(8,128)(2,1)}, u32[]{:S(2)}) copy-start(bf16[2,256,1408]{2,1,0:T(8,128)(2,1)} %get-tuple-element.117) | copy-start | bytes 4325380
  577.7 7.9 %copy-start.4 = (bf16[2,256,1408]{2,1,0:T(8,128)(2,1)S(1)}, bf16[2,256,1408]{2,1,0:T(8,128)(2,1)}, u32[]{:S(2)}) copy-start(bf16[2,256,1408]{2,1,0:T(8,128)(2,1)} %get-tuple-element.118) | copy-start | bytes 4325380
  585.6 1.9 copy-start.6
  585.6 1.9 copy-start.7
  587.5 2.8 copy-start.9

commit v7 on v6

--- a/solution.py
+++ b/solution.py
@@ -348,10 +348,11 @@
 
 
 class Part:
-    def __init__(self, kernel, operands, shapes, staged_in, staged_out, scratch, aliases, flops, name):
+    def __init__(self, kernel, operands, shapes, staged_in, staged_out, scratch, aliases, flops, name, early=None):
         self.kernel, self.operands, self.shapes = kernel, operands, shapes
         self.staged_in, self.staged_out, self.scratch = staged_in, staged_out, scratch
         self.aliases, self.flops, self.name = aliases, flops, name
+        self.early, self.private = early, ()
 
     def link(self, at, part=0):
         return Link(part, at, self.shapes[at].shape, self.shapes[at].dtype)
@@ -407,10 +408,9 @@
                 else:
                     near, source = False, given.pop(0)
                 if at >= part.staged_in:
-                    inner.append(source)
+                    inner.append(staged[item.at] if near else source)
                 elif near:
                     inner.append(staged[item.at])
-                    source = None
                 else:
                     inner.append(rest.pop(0))
                 sources.append(source)
@@ -421,7 +421,10 @@
                 Done() if sources[k] is None else pltpu.make_async_copy(sources[k], inner[k], load_s.at[k])
                 for k in range(part.staged_in)
             ]
-            stores = [pltpu.make_async_copy(results_in[k], outs[k], store_s.at[k]) for k in range(part.staged_out)]
+            stores = [
+                Done() if k in part.private else pltpu.make_async_copy(results_in[k], outs[k], store_s.at[k])
+                for k in range(part.staged_out)
+            ]
             for k, copy in enumerate(loads):
                 if k not in late:
                     copy.start()
@@ -436,7 +439,11 @@
             if not last:
                 held += stores
                 stores = [Later(copy) for copy in stores]
-            part.kernel(loads, stores, greet if at == 0 else lambda: None, *inner, *outs, *own)
+            hook = lambda: None
+            if not last and parts[at + 1].early:
+                following = ready[at + 1]
+                hook = lambda: parts[at + 1].early(following[0], *following[3], *following[4], *following[5])
+            part.kernel(loads, stores, greet if at == 0 else lambda: None, hook, *inner, *outs, *own)
         for copy in held:
             copy.wait()
 
@@ -494,7 +501,7 @@
     span = GROUP_CHUNKS * ROWS
     half_groups = groups // 2
 
-    def run(line, greet, taken, begin, prepare, beside, finish, second, settle, close, product, carried, chain_out, chain_in, wide, own_part, rs_out, rs_in,
+    def run(line, greet, started, taken, begin, prepare, beside, finish, second, settle, close, product, carried, chain_out, chain_in, wide, own_part, rs_out, rs_in,
             ag_s, ag_r, ch_s, ch_r, bc_s, bc_r, rs_s, rs_r):
         greet()
         gather = [
@@ -508,8 +515,9 @@
             )
             for at, peer in enumerate(line.peers)
         ]
-        for copy in gather:
-            copy.start()
+        if not started:
+            for copy in gather:
+                copy.start()
         begin()
         gather[0].wait_recv()
         prepare(pl.multiple_of(line.y * 2 * tok, 2 * tok))
@@ -701,9 +709,11 @@
     tok, features = hidden.shape
     width = down_own.shape[1]
     run, scratch = make_line(tok, depth, 2 * width, width, True, False, features)
+    chunks = 2 * tok // ROWS
+    started = False
     count = len(shipped)
 
-    def kernel(loads, stores, greet, h_ref, gain_ref, w1_own, w1_peer, w2_own, *rest):
+    def kernel(loads, stores, greet, hook, h_ref, gain_ref, w1_own, w1_peer, w2_own, *rest):
         leave, rest = rest[:count], rest[count:]
         (out_ref, normed_t, kept, wide, w2_peer), rest = rest[:5], rest[5:]
         landed, rest = rest[:count], rest[count:]
@@ -744,6 +754,10 @@
                 side.copies[0].wait_recv()
                 stores[4].start()
 
+            @pl.when(i == chunks // 2)
+            def _():
+                hook()
+
         def finish(row, at, total, extra):
             factor = lax.rsqrt(extra / D + EPS)
             gate = total[:, :width] * factor
@@ -785,7 +799,7 @@
             def _():
                 stores[2].wait()
 
-        run(line, greet, taken, begin, prepare, beside, finish, second, settle, close, product, carried, chain_out, chain_in, wide,
+        run(line, greet, started, taken, begin, prepare, beside, finish, second, settle, close, product, carried, chain_out, chain_in, wide,
             own_part, rs_out, rs_in, *sems)
 
     low, full = jnp.bfloat16, jnp.float32
@@ -809,7 +823,7 @@
 
 
 def ffn_backward(
-    grad, hidden, gain, kept, wide_forward, gu_own, gu_peer, down_own, down_peer, shipped, stacks, index, layers, depth
+    grad, hidden, gain, kept, wide_forward, gu_own, gu_peer, down_own, down_peer, shipped, stacks, index, layers, depth, started
 ):
     tok, features = hidden.shape
     width = down_own.shape[1]
@@ -818,7 +832,7 @@
     first_tile = SKEW + 1
     tiles = width // EXTRA
 
-    def kernel(loads, stores, greet, dy_ref, h_ref, gain_ref, kept_ref, before_ref, w1_own, w1_peer, w2_own, w2_peer, *rest):
+    def kernel(loads, stores, greet, hook, dy_ref, h_ref, gain_ref, kept_ref, before_ref, w1_own, w1_peer, w2_own, w2_peer, *rest):
         leave, rest = rest[:count], rest[count:]
         rest = rest[len(stacks):]
         (out_ref, wide, gain_out, kept_all, got_all), rest = rest[:5], rest[5:]
@@ -828,8 +842,9 @@
         line = Line(tok, depth)
         side = Side(side_s, side_r)
         own, other = halves(features)
-        loads[0].wait()
-        taken[pl.ds(line.own, tok), :] = dy_ref[...].astype(jnp.bfloat16)
+        if not started:
+            loads[0].wait()
+            taken[pl.ds(line.own, tok), :] = dy_ref[...].astype(jnp.bfloat16)
         give = side.later(down_given, got_all.at[index])
         keep = pltpu.make_async_copy(down_kept, kept_all.at[index], keep_s)
 
@@ -909,7 +924,7 @@
             for copy in stores:
                 copy.wait()
 
-        run(line, greet, taken, begin, prepare, beside, finish, second, settle, close, product, carried, chain_out, chain_in,
+        run(line, greet, started, taken, begin, prepare, beside, finish, second, settle, close, product, carried, chain_out, chain_in,
             wide, own_part, rs_out, rs_in, *sems)
 
     low, full = jnp.bfloat16, jnp.float32
@@ -920,20 +935,31 @@
         jax.ShapeDtypeStruct((layers,) + down_own.shape, low),
         jax.ShapeDtypeStruct((layers,) + down_own.shape, low),
     ) + tuple(jax.ShapeDtypeStruct(item.shape, item.dtype) for item in shipped)
+    def early(loads, dy_ref, *rest):
+        line = Line(tok, depth)
+        own = rest[-len(own_scratch) :]
+        taken, ag_s, ag_r = own[0], own[15], own[16]
+        loads[0].wait()
+        here = pl.ds(line.own, tok)
+        taken[here, :] = dy_ref[...].astype(jnp.bfloat16)
+        for at, peer in enumerate(line.peers):
+            remote(taken.at[here], taken.at[here], ag_s.at[at], ag_r.at[at], peer).start()
+
+    own_scratch = [
+        pltpu.VMEM((4 * tok, features), low),
+        pltpu.VMEM((features, 4 * tok), low),
+        pltpu.VMEM(down_own.shape, low),
+        pltpu.VMEM(down_own.shape, low),
+        pltpu.SemaphoreType.DMA,
+        pltpu.VMEM((GROUP_CHUNKS * ROWS, features), full),
+        sem(1 + count), sem(1 + count),
+    ] + scratch
     return Part(
         kernel,
         (grad, hidden, gain.reshape(1, -1), kept, wide_forward, gu_own, gu_peer, down_own, down_peer, *shipped, *stacks),
         shapes, 9, 3,
-        [
-            pltpu.VMEM((4 * tok, features), low),
-            pltpu.VMEM((features, 4 * tok), low),
-            pltpu.VMEM(down_own.shape, low),
-            pltpu.VMEM(down_own.shape, low),
-            pltpu.SemaphoreType.DMA,
-            pltpu.VMEM((GROUP_CHUNKS * ROWS, features), full),
-            sem(1 + count), sem(1 + count),
-        ] + scratch,
-        {9 + count + at: 3 + at for at in range(len(stacks))}, 60_000_000_000, "ffn_backward",
+        own_scratch,
+        {9 + count + at: 3 + at for at in range(len(stacks))}, 60_000_000_000, "ffn_backward", early if started else None,
     )
 
 
@@ -990,13 +1016,13 @@
         at = lax.rem(self.row + step, 2 * self.depth)
         return {"z": at // 2, "x": lax.rem(at, 2)}
 
-    def greet(self):
+    def greet(self, extra=0):
         barrier = pltpu.get_barrier_semaphore()
         for peer in self.peers:
             pl.semaphore_signal(barrier, 1, device_id=peer, device_id_type=MESH_ID)
         for step in range(1, 2 * self.depth):
             pl.semaphore_signal(barrier, 1, device_id=self.row_peer(step), device_id_type=MESH_ID)
-        pl.semaphore_wait(barrier, 3 + 2 * self.depth - 1)
+        pl.semaphore_wait(barrier, 3 + 2 * self.depth - 1 + extra)
 
 
 def start_gather(square, taken, send, recv):
@@ -1132,7 +1158,7 @@
     pairs = query_cols // EXTRA
     scale = 1.0 / math.sqrt(HEAD)
 
-    def kernel(loads, stores, greet, h_ref, gain_ref, wqkv_own, wo_own, cos_ref, sin_ref, *rest):
+    def kernel(loads, stores, greet, hook, h_ref, gain_ref, wqkv_own, wo_own, cos_ref, sin_ref, *rest):
         if not fetch:
             (wqkv_peer, wo_peer), rest = rest[:2], rest[2:]
         leave, rest = rest[:count], rest[count:]
@@ -1314,7 +1340,7 @@
     pairs = query_cols // EXTRA
     scale = 1.0 / math.sqrt(HEAD)
 
-    def kernel(loads, stores, greet, dy_ref, h_ref, gain_ref, wqkv_own, wqkv_peer, wo_own, wo_peer, cos_ref, sin_ref, q_ref, kv_ref, lse_ref,
+    def kernel(loads, stores, greet, hook, dy_ref, h_ref, gain_ref, wqkv_own, wqkv_peer, wo_own, wo_peer, cos_ref, sin_ref, q_ref, kv_ref, lse_ref,
                factor_ref, mixed_ref, normed_a_ref, normed_f_ref, gu_ref, *rest_refs):
         (out_ref, gain_out, qkv_given, gu_kept_all, gu_got_all, out_kept_all, out_got_all, qkv_kept_all,
                taken, spun, turned, pieces, gu_kept, gu_given, out_kept, out_given, qkv_kept, keep_s,
@@ -1454,6 +1480,7 @@
                 grad_tile(normed_a_ref, features, spun, pl.ds(t * EXTRA, EXTRA), qkv_kept, qkv_given)
             keeps[2].start()
             stores[2].start()
+            hook()
 
         sums = grid_sum(
             square, spun, inner_rows, second, settle, g_own, g_out, g_in, g_rows, zg_r, zgr_r, gs_s, gs_r, gr_s, gr_r
@@ -1528,22 +1555,32 @@
     )
 
 
+def greet_last(tok, depth):
+    square = Square(tok, depth)
+    barrier = pltpu.get_barrier_semaphore()
+    for slot in range(2 * depth):
+        here = (square.z == square.g) & (slot == square.x * depth + square.g)
+
+        @pl.when(jnp.logical_not(here))
+        def _():
+            source = {"z": square.g, "x": slot // depth, "y": (slot % depth) // 2, "c": slot % 2}
+            pl.semaphore_signal(barrier, 1, device_id=source, device_id_type=MESH_ID)
+
+    square.greet(2 * depth - jnp.where(square.z == square.g, 1, 0))
+
+
 def finish(grad, gains, qkv_given, depth):
     tok, features = grad.shape
     count = len(gains)
     members = 2 * depth
 
-    def kernel(loads, stores, greet, grad_ref, *rest):
+    def kernel(loads, stores, greet, hook, grad_ref, *rest):
         gain_refs, rest = rest[:count], rest[count:]
         (given, out_ref, gain_out, got, packed, parts, sent, home, part_s, part_r, move_s, move_r, side_s, side_r) = rest
         z, x = lax.axis_index("z"), lax.axis_index("x")
         y, c = lax.axis_index("y"), lax.axis_index("c")
         g = 2 * y + c
-        barrier = pltpu.get_barrier_semaphore()
         self_at = x * depth + g
-
-        def source(slot):
-            return {"z": g, "x": slot // depth, "y": (slot % depth) // 2, "c": slot % 2}
 
         def target(at):
             return {"z": at // 2, "x": at % 2, "y": z // 2, "c": lax.rem(z, 2)}
@@ -1554,21 +1591,13 @@
         def is_target_me(at):
             return (z == g) & (at == 2 * z + x)
 
-        for slot in range(members):
-
-            @pl.when(jnp.logical_not(is_source_me(slot)))
-            def _():
-                pl.semaphore_signal(barrier, 1, device_id=source(slot), device_id_type=MESH_ID)
-
-        pl.semaphore_signal(barrier, 1, device_id={"x": 1 - x}, device_id_type=MESH_ID)
         for copy in loads:
             copy.wait()
         for at, ref in enumerate(gain_refs):
             packed[at : at + 1, :] = ref[:1, :]
         sent[...] = grad_ref[...].astype(jnp.bfloat16)
-        pl.semaphore_wait(barrier, members + 1 - jnp.where(z == g, 1, 0))
         side = Side(side_s, side_r)
-        side.start(given, got)
+        side.later(given, got)
         move = remote(sent, home, move_s, move_r, {"z": g, "y": z // 2, "c": lax.rem(z, 2)})
 
         @pl.when(z != g)
@@ -1627,6 +1656,10 @@
         jax.ShapeDtypeStruct((count, features), full),
         jax.ShapeDtypeStruct(qkv_given.shape, low),
     )
+    def early(loads, *refs):
+        given, got, side_s, side_r = refs[1 + count], refs[4 + count], refs[-2], refs[-1]
+        Side(side_s, side_r).start(given, got)
+
     return Part(
         kernel, (grad, *gains, qkv_given), shapes, 1 + count, 2,
         [
@@ -1638,8 +1671,55 @@
             pltpu.SemaphoreType.DMA, pltpu.SemaphoreType.DMA,
             sem(1), sem(1),
         ],
-        {}, 5_000_000_000, "finish",
+        {}, 5_000_000_000, "finish", early,
     )
+
+
+def combine(rests, downs, got_qkv):
+    gu_kept, gu_got, out_kept, out_got, qkv_kept = rests
+    layers, rows, wide = gu_kept.shape
+    half = wide // 2
+    step = rows // 2
+
+    def kernel(gu_k, gu_g, out_k, out_g, down_k, down_g, qkv_k, *rest):
+        got, (qkv_o, out_o, gu_o, down_o) = rest[:layers], rest[layers:]
+        total = gu_k[0].astype(jnp.float32) + gu_g[0].astype(jnp.float32)
+        gu_o[0, :, 0, :] = total[:, :half]
+        gu_o[0, :, 1, :] = total[:, half:]
+        out_o[...] = out_k[...].astype(jnp.float32) + out_g[...].astype(jnp.float32)
+        down_o[...] = down_k[...].astype(jnp.float32) + down_g[...].astype(jnp.float32)
+        for index in range(layers):
+
+            @pl.when(pl.program_id(0) == index)
+            def _():
+                qkv_o[0, :, 0, :] = qkv_k[0].astype(jnp.float32) + got[index][...].astype(jnp.float32)
+
+    def spec(item):
+        return pl.BlockSpec((1, step, item.shape[2]), lambda layer, at: (layer, at, 0))
+
+    operands = (gu_kept, gu_got, out_kept, out_got, *downs, qkv_kept)
+    cols = qkv_kept.shape[2]
+    full = jnp.float32
+    return pl.pallas_call(
+        kernel,
+        grid=(layers, rows // step),
+        in_specs=[spec(item) for item in operands]
+        + [pl.BlockSpec((step, cols), lambda layer, at: (at, 0)) for _ in range(layers)],
+        out_specs=[
+            pl.BlockSpec((1, step, 1, cols), lambda layer, at: (layer, at, 0, 0)),
+            spec(out_kept),
+            pl.BlockSpec((1, step, 2, half), lambda layer, at: (layer, at, 0, 0)),
+            spec(downs[0]),
+        ],
+        out_shape=[
+            jax.ShapeDtypeStruct((layers, rows, 1, cols), full),
+            jax.ShapeDtypeStruct(out_kept.shape, full),
+            jax.ShapeDtypeStruct((layers, rows, 2, half), full),
+            jax.ShapeDtypeStruct(downs[0].shape, full),
+        ],
+        compiler_params=pltpu.CompilerParams(vmem_limit_bytes=60 << 20),
+        name="combine",
+    )(*operands, *got_qkv)
 
 
 def stationary(stream, grad_out, wqkv, wo, wgu, wd, gain_attn, gain_ffn):
@@ -1670,17 +1750,25 @@
     for index in range(layers):
         before = current
         first = index == 0
+        final = index == layers - 1
         follow = index + 1
-        shipped = [own_qkv[follow], own_out[follow], own_gu[follow]] if follow < layers else []
+        shipped = [] if final else [own_qkv[follow], own_out[follow], own_gu[follow]]
         attend = attention_forward(
             before, gain_a[index], own_qkv[index], own_out[index], peer_qkv[index], peer_out[index],
             own_gu[:1] if first else [], cosine, sine, depth
         )
-        feed = ffn_forward(
-            attend.link(0), gain_f[index], own_gu[index], attend.link(len(attend.shapes) - 1) if first else peer_gu[index],
-            own_down[index], shipped, depth
-        )
-        made, fed = launch([attend, feed], greet, 2 * index)
+        peer = attend.link(len(attend.shapes) - 1) if first else peer_gu[index]
+        feed = ffn_forward(attend.link(0), gain_f[index], own_gu[index], peer, own_down[index], shipped, depth)
+        parts = [attend, feed]
+        if final:
+            feed.private = (2, 3, 4)
+            parts.append(
+                ffn_backward(
+                    grad_now, attend.link(0), gain_f[index], feed.link(2, 1), feed.link(3, 1), own_gu[index], peer,
+                    own_down[index], feed.link(4, 1), [], [], index, layers, depth, True
+                )
+            )
+        made, fed, *back = launch(parts, greet, 2 * index)
         hidden_in, normed_a, queries, kv, lse, mixed, factors = made[:7]
         if first:
             peer_qkv[0], peer_out[0], peer_gu[0] = made[7:]
@@ -1688,41 +1776,32 @@
         if shipped:
             peer_qkv[follow], peer_out[follow], peer_gu[follow] = fed[5:]
         saved.append((before, normed_a, queries, kv, lse, mixed, factors, hidden_in, normed_f, kept, active))
-    list_ga, list_gf, got_qkv, pending, down_stack, rest_stack = ([], [], [], [], [], [])
+    list_ga, list_gf, got_qkv, rest_stack = ([], [], [], [])
+    grad_hidden, grad_gu, gain_f_grad, *down_stack = back[0]
     for index in reversed(range(layers)):
-        before, normed_a, queries, kv, lse, mixed, factors, hidden_in, normed_f, kept, active = saved[index]
-        feed = ffn_backward(
-            grad_now, hidden_in, gain_f[index], kept, active, own_gu[index], peer_gu[index], own_down[index],
-            peer_down[index], pending[-1:], down_stack, index, layers, depth
+        list_gf.append(gain_f_grad)
+        before, normed_a, queries, kv, lse, mixed, factors, _, normed_f, _, _ = saved[index]
+        attend = attention_backward(
+            grad_hidden, before, gain_a[index], own_qkv[index], peer_qkv[index], own_out[index], peer_out[index],
+            cosine, sine, queries, kv, lse, factors, mixed, normed_a, normed_f, grad_gu, rest_stack, index, layers, depth
         )
-        attend = attention_backward(
-            feed.link(0), before, gain_a[index], own_qkv[index], peer_qkv[index], own_out[index], peer_out[index],
-            cosine, sine, queries, kv, lse, factors, mixed, normed_a, normed_f, feed.link(1), rest_stack, index, layers,
-            depth
-        )
-        fed, made = launch([feed, attend], greet, 2 * index + 1)
-        down_stack = fed[3:5]
-        got_qkv.extend(fed[5:])
-        list_gf.append(fed[2])
-        (grad_now, gain_a_grad, qkv_given, *rest_stack) = made
-        pending.append(qkv_given)
-        list_ga.append(gain_a_grad)
-    ((grad_in, gains, last_qkv),) = launch(
-        [finish(grad_now, list_ga[::-1] + list_gf[::-1], qkv_given, depth)], None, 2 * layers
-    )
-    got_qkv.append(last_qkv)
-    gu_kept, gu_got, out_kept, out_got, qkv_kept = rest_stack
-    add = lambda kept, got: kept.astype(jnp.float32) + got.astype(jnp.float32)
-    return (
-        swap_grid(current, depth),
-        grad_in,
-        add(qkv_kept, jnp.stack(got_qkv[::-1])).reshape(layers, count_rows, 1, -1),
-        add(out_kept, out_got),
-        add(gu_kept, gu_got).reshape(layers, count_rows, 2, -1),
-        add(*down_stack),
-        gains[:layers],
-        gains[layers:],
-    )
+        attend.private = (2,)
+        if index:
+            _, _, _, _, _, _, _, hidden_in, _, kept, active = saved[index - 1]
+            feed = ffn_backward(
+                attend.link(0), hidden_in, gain_f[index - 1], kept, active, own_gu[index - 1], peer_gu[index - 1],
+                own_down[index - 1], peer_down[index - 1], [attend.link(2)], down_stack, index - 1, layers, depth, False
+            )
+            made, (grad_hidden, grad_gu, gain_f_grad, *down_stack, landed) = launch([attend, feed], greet, 2 * index + 1)
+            got_qkv.append(landed)
+        else:
+            tail = finish(attend.link(0), [attend.link(1)] + list_ga[::-1] + list_gf[::-1], attend.link(2), depth)
+            made, (grad_in, gains, landed) = launch([attend, tail], lambda: greet_last(tok, depth), 1)
+            got_qkv.append(landed)
+        list_ga.append(made[1])
+        rest_stack = made[3:]
+    grads = combine(rest_stack, down_stack, got_qkv[::-1])
+    return (swap_grid(current, depth), grad_in, *grads, gains[:layers], gains[layers:])
 
 
 def solution(mesh):

time: 595 us -> 579 us (0.973)
  local copies, waits for them, and re-layouts: 25.4 us -> 14.7 us
  other arithmetic: 11.1 us -> 1.82 us
  Pallas kernels: 536 us -> 542 us
    pallas_call x0 -> x1, Pallas kernels: none -> 9.22 us  [combine(): pl.pallas_call(kernel, grid=(layers, rows // step), in_specs=[spec(item)...]
    add x3 -> x0, other arithmetic: 8.03 us -> none  [stationary(): add = lambda kept, got: kept.astype(jnp.float32) + got.astype(jnp.float32)]
    reshape x1 -> x0, local copies, waits for them, and re-layouts: 7.94 us -> none  [stationary(): add(gu_kept, gu_got).reshape(layers, count_rows, 2, -1)]
    pallas_call x5 -> x4, Pallas kernels: 536 us -> 533 us  [launch(): pl.pallas_call(body, out_shape=tuple(shapes), in_specs=[outside] * len(op...]
  transfers between devices with their start and end apart: 4 -> 4, of which waited for: 1 -> 1; matrix products, arithmetic and copies ran while one was open for 5% -> 2% of each run, Pallas kernels for 91% -> 59%
where the time goes in v7:
time: 579 us
  Pallas kernels  542 us (94%)
  local copies, waits for them, and re-layouts  14.7 us (3%)
  starting transfers between devices  14 us (2%)
    pallas_call x4, Pallas kernels, launch(): pl.pallas_call(body, out_shape=tuple(shapes), in_specs=[outside] * len(op...  533 us
    ppermute x4, starting transfers between devices, swap_grid(): return lax.ppermute(values, ('z', 'y', 'c'), pairs)  14 us
  transfers between devices with their start and end apart: 4, of which 1 were waited for; matrix products, arithmetic and copies ran while one was open for 2% of the time, Pallas kernels for 59%

profile of v7, /device:TPU:4, one launch (start us, length us, event | category | flops | bytes accessed | tf_op | source)
XLA Modules:
  0.0 578.5 jit_solution(14514749652807526066)
XLA Ops:
  0.6 0.0 copy-start.2
  0.6 0.0 copy-start.1
  0.7 0.9 pad_maximum_fusion
  1.5 4.4 collective-permute-start.1
  5.9 3.2 collective-permute-start
  9.2 4.4 collective-permute-start.2
  13.6 1.9 slice_bitcast_fusion.4
  15.5 0.0 copy-done.2
  15.5 0.9 slice_bitcast_fusion.2
  16.4 0.0 copy-done.1
  16.4 0.0 copy-start
  16.4 1.2 slice_bitcast_fusion
  17.6 1.1 copy-done
  18.8 2.0 fusion.5
  20.8 1.0 fusion
  21.8 1.3 copy.24
  23.0 1.3 copy.23
  24.3 0.0 collective-permute-done.1
  24.3 0.6 fusion.7
  24.9 5.1 collective-permute-done.refs_0_.refs_1_
  30.0 0.0 copy-start.5
  30.0 0.7 copy-done.5
  30.7 131.3 %attention_forward_ffn_forward.1 = (f32[128,512]{1,0:T(8,128)}, bf16[512,512]{1,0:T(8,128)(2,1)}, bf16[128,512]{1,0:T(8,128)(2,1)}, bf16[1024,128]{1,0:T(8,128)(...) custom-call(f32[128,512]{1,0:T(8,128)} %copy-done.5, ...), custom_call_target="tpu_custom_call" | custom-call | flops 109999996928 | bytes 8000000 | tf_op jit(solution)/shard_map/attention_forward_ffn_forward/pallas_call | solution.py:451
  162.0 0.0 collective-permute-done.2.refs_12_
  162.0 0.0 copy-start.6
  162.0 0.7 copy-done.6
  162.7 203.0 %attention_forward_ffn_forward_ffn_backward.1 = (f32[128,512]{1,0:T(8,128)}, bf16[512,512]{1,0:T(8,128)(2,1)}, bf16[128,512]{1,0:T(8,128)(2,1)}, bf16[1024,128]{...) custom-call(f32[128,512]{1,0:T(8,128)} %get-tuple-element.63.refs_0_, ...), custom_call_target="tpu_custom_call" | custom-call | flops 170000007168 | bytes 8000000 | tf_op jit(solution)/shard_map/attention_forward_ffn_forward_ffn_backward/pallas_call | solution.py:451
  365.7 1.9 collective-permute-start.3
  367.6 130.7 %attention_backward_ffn_backward.1 = (f32[128,512]{1,0:T(8,128)}, f32[8,512]{1,0:T(8,128)}, bf16[256,640]{1,0:T(8,128)(2,1)}, bf16[2,256,2816]{2,1,0:T(8,128)(2,...) custom-call(f32[128,512]{1,0:T(8,128)} %get-tuple-element.68.refs_0_, ...), custom_call_target="tpu_custom_call", output_to_operand_aliasing={{11}: (25, {}), {12}: (26, {})} | custom-call | flops 109999996928 | bytes 8000000 | tf_op jit(solution)/shard_map/attention_backward_ffn_backward/pallas_call | solution.py:451
  498.3 68.0 %attention_backward_finish.1 = (f32[128,512]{1,0:T(8,128)}, f32[8,512]{1,0:T(8,128)}, bf16[256,640]{1,0:T(8,128)(2,1)}, bf16[2,256,2816]{2,1,0:T(8,128)(2,1)}, b...) custom-call(f32[128,512]{1,0:T(8,128)} %get-tuple-element.84.refs_0_, ...), custom_call_target="tpu_custom_call", output_to_operand_aliasing={{3}: (17, {}), {4}: (18, {}), {5}: (19, {}), {6}: (20, {}),... | custom-call | flops 54999998464 | bytes 8000000 | tf_op jit(solution)/shard_map/attention_backward_finish/pallas_call | solution.py:451
  566.3 0.0 copy-start.4
  566.3 0.0 copy-start.3
  566.3 9.2 %combine.1 = (f32[2,256,1,640]{3,2,1,0:T(1,128)}, f32[2,256,512]{2,1,0:T(8,128)}, f32[2,256,2,1408]{3,2,1,0:T(2,128)}, f32[2,256,1408]{2,1,0:T(8,128)}) custom-call(bf16[2,256,2816]{2,1,0:T(8,128)(2,1)} %get-tuple-element.104.gu_k, bf16[2,256,2816]{2,1,0:T(8,128)(2,1)} %get-tuple-element.105.gu_g, bf16[2,256,512]{2,1,0:T(8,128)(2,1)} %get-tuple-element.106.out_k, ...), custom_call_target="tpu_custom_call" | custom-call | tf_op jit(solution)/shard_map/combine/pallas_call | solution.py:1703
  575.6 0.0 copy-done.4
  575.6 0.6 fusion.6
  576.2 0.0 collective-permute-done.3
  576.2 1.7 copy.34
  577.8 0.0 copy-done.3
  577.8 0.7 copy.35
  (2 shorter events, 0.0 us)
Async XLA Ops:
  0.6 14.9 %copy-start.2 = (bf16[2,256,1,640]{3,1,2,0:T(8,128)(2,1)S(1)}, bf16[2,256,1,640]{3,1,2,0:T(8,128)(2,1)}, u32[]{:S(2)}) copy-start(bf16[2,256,1,640]{3,1,2,0:T(8,128)(2,1)} %param.10) | copy-start | bytes 1966084
  0.6 15.8 %copy-start.1 = (bf16[2,256,1408]{2,1,0:T(8,128)(2,1)S(1)}, bf16[2,256,1408]{2,1,0:T(8,128)(2,1)}, u32[]{:S(2)}) copy-start(bf16[2,256,1408]{2,1,0:T(8,128)(2,1)} %param.13) | copy-start | bytes 4325380
  1.5 22.8 %collective-permute-start.1 = (f32[4,512]{1,0:T(4,128)S(1)}, f32[4,512]{1,0:T(4,128)S(1)}, u32[]{:S(2)}, u32[]{:S(2)}) collective-permute-start(f32[4,512]{1,0:T(4,128)S(1)} %pad_maximum_fusion), channel_id=1, source_target_pairs={{0,0},{1,8},{2,16},{3,24},{8,1},{9,9},{10,17},{11,25},{16,2},{17,1... | collective-permute-start | bytes 24584 | tf_op jit(solution)/shard_map/ppermute | solution.py:265
  5.9 24.0 %collective-permute-start = (f32[128,512]{1,0:T(8,128)}, f32[128,512]{1,0:T(8,128)S(1)}, u32[]{:S(2)}, u32[]{:S(2)}) collective-permute-start(f32[128,512]{1,0:T(8,128)} %param.8), channel_id=1, source_target_pairs={{0,0},{1,8},{2,16},{3,24},{8,1},{9,9},{10,17},{11,25},{16,2},{17,1... | collective-permute-start | bytes 786440 | tf_op jit(solution)/shard_map/ppermute | solution.py:265
  9.2 152.8 %collective-permute-start.2 = (f32[128,512]{1,0:T(8,128)}, f32[128,512]{1,0:T(8,128)S(1)}, u32[]{:S(2)}, u32[]{:S(2)}) collective-permute-start(f32[128,512]{1,0:T(8,128)} %param.9), channel_id=1, source_target_pairs={{0,0},{1,8},{2,16},{3,24},{8,1},{9,9},{10,17},{11,25},{16,2},{17,1... | collective-permute-start | bytes 786440 | tf_op jit(solution)/shard_map/ppermute | solution.py:265
  16.4 2.3 copy-start
  30.0 0.7 copy-start.5
  162.0 0.7 copy-start.6
  365.7 210.5 %collective-permute-start.3 = (f32[128,512]{1,0:T(8,128)}, f32[128,512]{1,0:T(8,128)}, u32[]{:S(2)}, u32[]{:S(2)}) collective-permute-start(f32[128,512]{1,0:T(8,128)} %get-tuple-element.67), channel_id=1, source_target_pairs={{0,0},{1,8},{2,16},{3,24},{8,1},{9,9},{10,17},{11,25},{16,2},{17,1... | collective-permute-start | bytes 786440 | tf_op jit(solution)/shard_map/ppermute | solution.py:265
  566.3 9.2 %copy-start.4 = (f32[4,512]{1,0:T(4,128)S(1)}, f32[4,512]{1,0:T(4,128)}, u32[]{:S(2)}) copy-start(f32[4,512]{1,0:T(4,128)} %get-tuple-element.117) | copy-start | bytes 24580
  566.3 11.5 %copy-start.3 = (f32[128,512]{1,0:T(8,128)S(1)}, f32[128,512]{1,0:T(8,128)}, u32[]{:S(2)}) copy-start(f32[128,512]{1,0:T(8,128)} %get-tuple-element.145) | copy-start | bytes 786436

commit v8 on v7

--- a/solution.py
+++ b/solution.py
@@ -268,6 +268,7 @@
 MESH_ID = pl.DeviceIdType.MESH
 ROWS = 16
 SKEW = 3
+OFFSET = 18
 GROUP_CHUNKS = 4
 EXTRA = 128
 
@@ -352,7 +353,7 @@
         self.kernel, self.operands, self.shapes = kernel, operands, shapes
         self.staged_in, self.staged_out, self.scratch = staged_in, staged_out, scratch
         self.aliases, self.flops, self.name = aliases, flops, name
-        self.early, self.private = early, ()
+        self.early, self.private, self.woven = early, (), False
 
     def link(self, at, part=0):
         return Link(part, at, self.shapes[at].shape, self.shapes[at].dtype)
@@ -372,6 +373,23 @@
 
     def wait(self):
         pass
+
+
+def weave(step, count, later_step, later_post, later_count, post):
+    def both(i, _):
+        @pl.when(i < count)
+        def _():
+            step(i, 0)
+
+        @pl.when(i >= OFFSET)
+        def _():
+            later_step(i - OFFSET, 0)
+
+        return 0
+
+    lax.fori_loop(0, OFFSET + later_count, both, 0)
+    post()
+    later_post()
 
 
 def launch(parts, greet, ident):
@@ -430,20 +448,37 @@
                     copy.start()
             results.append((results_in, outs))
             ready.append((loads, stores, late, inner, results_in + outs[part.staged_out :], own))
-        for at, part in enumerate(parts):
+        begun = {}
+
+        def begin(at):
+            part = parts[at]
             loads, stores, late, inner, outs, own = ready[at]
             for k in late:
                 if k < part.staged_in:
                     loads[k].start()
-            last = at == len(parts) - 1
-            if not last:
-                held += stores
-                stores = [Later(copy) for copy in stores]
+            if at < len(parts) - 1:
+                held.extend(copy for copy in stores if not isinstance(copy, Done))
+                stores = [copy if isinstance(copy, Done) else Later(copy) for copy in stores]
             hook = lambda: None
-            if not last and parts[at + 1].early:
+            if at + 2 < len(parts) and parts[at + 2].woven:
+                hook = lambda: begin(at + 2)
+            elif at + 1 < len(parts) and parts[at + 1].early:
                 following = ready[at + 1]
                 hook = lambda: parts[at + 1].early(following[0], *following[3], *following[4], *following[5])
-            part.kernel(loads, stores, greet if at == 0 else lambda: None, hook, *inner, *outs, *own)
+            begun[at] = part.kernel(loads, stores, greet if at == 0 else lambda: None, hook, *inner, *outs, *own)
+
+        for at, part in enumerate(parts):
+            if part.woven:
+                continue
+            begin(at)
+            if begun[at] is None:
+                continue
+            step, post, count = begun[at]
+            if at + 1 < len(parts) and parts[at + 1].woven:
+                weave(step, count, *begun[at + 1], post)
+            else:
+                lax.fori_loop(0, count, step, 0)
+                post()
         for copy in held:
             copy.wait()
 
@@ -501,7 +536,7 @@
     span = GROUP_CHUNKS * ROWS
     half_groups = groups // 2
 
-    def run(line, greet, started, taken, begin, prepare, beside, finish, second, settle, close, product, carried, chain_out, chain_in, wide, own_part, rs_out, rs_in,
+    def run(line, greet, taken, begin, prepare, beside, finish, second, settle, close, product, carried, chain_out, chain_in, wide, own_part, rs_out, rs_in,
             ag_s, ag_r, ch_s, ch_r, bc_s, bc_r, rs_s, rs_r):
         greet()
         gather = [
@@ -515,9 +550,8 @@
             )
             for at, peer in enumerate(line.peers)
         ]
-        if not started:
-            for copy in gather:
-                copy.start()
+        for copy in gather:
+            copy.start()
         begin()
         gather[0].wait_recv()
         prepare(pl.multiple_of(line.y * 2 * tok, 2 * tok))
@@ -565,7 +599,6 @@
                 gather[2].wait_recv()
                 prepare(pl.multiple_of((1 - line.y) * 2 * tok, 2 * tok))
 
-            beside(i)
             for stream in (0, 1):
                 place = line.place(stream)
                 chunk = i - SKEW * place
@@ -607,6 +640,8 @@
                         finish(row, pl.multiple_of(chunk * ROWS, ROWS), total, extra)
                         wide_copy(stream, chunk).start()
 
+            for stream in (0, 1):
+                place = line.place(stream)
                 ready = i - SKEW * (2 * (depth - 1) - place)
 
                 @pl.when((ready >= 0) & (ready < chunks))
@@ -619,6 +654,13 @@
                         def _():
                             wide_copy(stream, ready).start()
 
+            beside(i)
+            for stream in (0, 1):
+                place = line.place(stream)
+                ready = i - SKEW * (2 * (depth - 1) - place)
+
+                @pl.when((ready >= 0) & (ready < chunks))
+                def _():
                     @pl.when(lax.rem(ready, GROUP_CHUNKS) == GROUP_CHUNKS - 1)
                     def _():
                         group = ready // GROUP_CHUNKS
@@ -639,8 +681,6 @@
 
             return 0
 
-        lax.fori_loop(0, chunks + 2 * SKEW * (depth - 1), step, 0)
-
         def drain(i, _):
             for stream in (0, 1):
                 place = line.place(stream)
@@ -664,22 +704,25 @@
                     copy.wait_send()
             return 0
 
-        settle()
-        for slot in range(3):
-            for part in range(half_groups):
-                pltpu.make_async_remote_copy(
-                    src_ref=rs_out.at[0, 0],
-                    dst_ref=rs_in.at[slot, pl.ds(part * span, span)],
-                    send_sem=rs_s.at[0, 0],
-                    recv_sem=rs_r.at[slot, part],
-                    device_id=line.peers[slot],
-                    device_id_type=MESH_ID,
-                ).wait_recv()
-        close()
-        for copy in gather:
-            copy.wait_send()
-        lax.fori_loop(0, chunks, drain, 0)
-        lax.fori_loop(0, groups, drain_sums, 0)
+        def post():
+            settle()
+            for slot in range(3):
+                for part in range(half_groups):
+                    pltpu.make_async_remote_copy(
+                        src_ref=rs_out.at[0, 0],
+                        dst_ref=rs_in.at[slot, pl.ds(part * span, span)],
+                        send_sem=rs_s.at[0, 0],
+                        recv_sem=rs_r.at[slot, part],
+                        device_id=line.peers[slot],
+                        device_id_type=MESH_ID,
+                    ).wait_recv()
+            close()
+            for copy in gather:
+                copy.wait_send()
+            lax.fori_loop(0, chunks, drain, 0)
+            lax.fori_loop(0, groups, drain_sums, 0)
+
+        return step, post, chunks + 2 * SKEW * (depth - 1)
 
     wide_in = width_in + (EXTRA if carry_in else 0)
     scratch = [
@@ -705,17 +748,21 @@
 TILE = 256
 
 
-def ffn_forward(hidden, gain, gu_own, gu_peer, down_own, shipped, depth):
+def ffn_forward(hidden, gain, gu_own, gu_peer, down_own, down_peer, shipped, depth):
     tok, features = hidden.shape
     width = down_own.shape[1]
     run, scratch = make_line(tok, depth, 2 * width, width, True, False, features)
-    chunks = 2 * tok // ROWS
-    started = False
+    fetch = down_peer is None
     count = len(shipped)
+    sides = count + (1 if fetch else 0)
 
     def kernel(loads, stores, greet, hook, h_ref, gain_ref, w1_own, w1_peer, w2_own, *rest):
+        if not fetch:
+            w2_peer, rest = rest[0], rest[1:]
         leave, rest = rest[:count], rest[count:]
-        (out_ref, normed_t, kept, wide, w2_peer), rest = rest[:5], rest[5:]
+        (out_ref, normed_t, kept, wide), rest = rest[:4], rest[4:]
+        if fetch:
+            w2_peer, rest = rest[0], rest[1:]
         landed, rest = rest[:count], rest[count:]
         (taken, scaled, pieces, side_s, side_r, product, carried, chain_out, chain_in, own_part, rs_out, rs_in), sems = (
             rest[:12], rest[12:])
@@ -729,7 +776,8 @@
         def begin():
             for copy in loads[1:]:
                 copy.wait()
-            side.start(w2_own, w2_peer)
+            if fetch:
+                side.start(w2_own, w2_peer)
             for source, target in zip(leave, landed):
                 side.start(source, target)
 
@@ -749,14 +797,12 @@
             lax.fori_loop(0, 2 * width // TILE, tile, 0)
 
         def beside(i):
-            @pl.when(i == SKEW * (depth - 1))
-            def _():
-                side.copies[0].wait_recv()
-                stores[4].start()
-
-            @pl.when(i == chunks // 2)
-            def _():
-                hook()
+            if fetch:
+
+                @pl.when(i == SKEW * (depth - 1))
+                def _():
+                    side.copies[0].wait_recv()
+                    stores[4].start()
 
         def finish(row, at, total, extra):
             factor = lax.rsqrt(extra / D + EPS)
@@ -791,15 +837,15 @@
                 total = total + rs_in[slot].astype(jnp.float32)
             out_ref[...] = h_ref[...] + total
             stores[0].start()
-            side.finish(side.copies[:1])
-            for at in (0, 1, 3, 4):
+            side.finish(side.copies[:1] if fetch else ())
+            for at in (0, 1, 3, 4)[: 4 if fetch else 3]:
                 stores[at].wait()
 
             @pl.when(at_end)
             def _():
                 stores[2].wait()
 
-        run(line, greet, started, taken, begin, prepare, beside, finish, second, settle, close, product, carried, chain_out, chain_in, wide,
+        return run(line, greet, taken, begin, prepare, beside, finish, second, settle, close, product, carried, chain_out, chain_in, wide,
             own_part, rs_out, rs_in, *sems)
 
     low, full = jnp.bfloat16, jnp.float32
@@ -808,29 +854,31 @@
         jax.ShapeDtypeStruct((features, 4 * tok), low),
         jax.ShapeDtypeStruct((2 * tok, 2 * width), full),
         jax.ShapeDtypeStruct((4 * tok, width + EXTRA), low),
-        jax.ShapeDtypeStruct(down_own.shape, low),
-    ) + tuple(jax.ShapeDtypeStruct(item.shape, item.dtype) for item in shipped)
+    ) + ((jax.ShapeDtypeStruct(down_own.shape, low),) if fetch else ()) + tuple(jax.ShapeDtypeStruct(item.shape, item.dtype) for item in shipped)
     return Part(
-        kernel, (hidden, gain.reshape(1, -1), gu_own, gu_peer, down_own, *shipped), shapes, 5, 5,
+        kernel, (hidden, gain.reshape(1, -1), gu_own, gu_peer, down_own, *(() if fetch else (down_peer,)), *shipped), shapes,
+        5 if fetch else 6, 5 if fetch else 4,
         [
             pltpu.VMEM((4 * tok, features), low),
             pltpu.VMEM((2 * tok, features), low),
             pltpu.VMEM((GROUP_CHUNKS * ROWS, features), full),
-            sem(1 + count), sem(1 + count),
+            sem(max(sides, 1)), sem(max(sides, 1)),
         ] + scratch,
         {}, 60_000_000_000, "ffn_forward",
     )
 
 
 def ffn_backward(
-    grad, hidden, gain, kept, wide_forward, gu_own, gu_peer, down_own, down_peer, shipped, stacks, index, layers, depth, started
+    grad, hidden, gain, kept, wide_forward, gu_own, gu_peer, down_own, down_peer, shipped, stacks, index, layers, depth, woven=False
 ):
     tok, features = hidden.shape
     width = down_own.shape[1]
     run, scratch = make_line(tok, depth, width, 2 * width, False, True, features)
     count = len(shipped)
-    first_tile = SKEW + 1
     tiles = width // EXTRA
+    every = 2 if woven else 1
+    first_tile = 2 * tok // ROWS + 2 * SKEW * (depth - 1) - OFFSET if woven else SKEW + 1
+    turns = (tiles + every - 1) // every
 
     def kernel(loads, stores, greet, hook, dy_ref, h_ref, gain_ref, kept_ref, before_ref, w1_own, w1_peer, w2_own, w2_peer, *rest):
         leave, rest = rest[:count], rest[count:]
@@ -842,9 +890,8 @@
         line = Line(tok, depth)
         side = Side(side_s, side_r)
         own, other = halves(features)
-        if not started:
-            loads[0].wait()
-            taken[pl.ds(line.own, tok), :] = dy_ref[...].astype(jnp.bfloat16)
+        loads[0].wait()
+        taken[pl.ds(line.own, tok), :] = dy_ref[...].astype(jnp.bfloat16)
         give = side.later(down_given, got_all.at[index])
         keep = pltpu.make_async_copy(down_kept, kept_all.at[index], keep_s)
 
@@ -876,12 +923,15 @@
             def _():
                 turned[...] = flip(taken[...])
 
-            @pl.when((i >= first_tile) & (i < first_tile + tiles))
-            def _():
-                cols = pl.ds(pl.multiple_of((i - first_tile) * EXTRA, EXTRA), EXTRA)
-                grad_tile(turned, features, before_ref, cols, down_kept, down_given)
-
-            @pl.when(i == first_tile + tiles)
+            for turn_at in range(every):
+                at = (i - first_tile) * every + turn_at
+
+                @pl.when((at >= 0) & (at < tiles))
+                def _():
+                    cols = pl.ds(pl.multiple_of(at * EXTRA, EXTRA), EXTRA)
+                    grad_tile(turned, features, before_ref, cols, down_kept, down_given)
+
+            @pl.when(i == first_tile + turns)
             def _():
                 give.start()
                 keep.start()
@@ -924,7 +974,7 @@
             for copy in stores:
                 copy.wait()
 
-        run(line, greet, started, taken, begin, prepare, beside, finish, second, settle, close, product, carried, chain_out, chain_in,
+        return run(line, greet, taken, begin, prepare, beside, finish, second, settle, close, product, carried, chain_out, chain_in,
             wide, own_part, rs_out, rs_in, *sems)
 
     low, full = jnp.bfloat16, jnp.float32
@@ -935,16 +985,6 @@
         jax.ShapeDtypeStruct((layers,) + down_own.shape, low),
         jax.ShapeDtypeStruct((layers,) + down_own.shape, low),
     ) + tuple(jax.ShapeDtypeStruct(item.shape, item.dtype) for item in shipped)
-    def early(loads, dy_ref, *rest):
-        line = Line(tok, depth)
-        own = rest[-len(own_scratch) :]
-        taken, ag_s, ag_r = own[0], own[15], own[16]
-        loads[0].wait()
-        here = pl.ds(line.own, tok)
-        taken[here, :] = dy_ref[...].astype(jnp.bfloat16)
-        for at, peer in enumerate(line.peers):
-            remote(taken.at[here], taken.at[here], ag_s.at[at], ag_r.at[at], peer).start()
-
     own_scratch = [
         pltpu.VMEM((4 * tok, features), low),
         pltpu.VMEM((features, 4 * tok), low),
@@ -959,7 +999,7 @@
         (grad, hidden, gain.reshape(1, -1), kept, wide_forward, gu_own, gu_peer, down_own, down_peer, *shipped, *stacks),
         shapes, 9, 3,
         own_scratch,
-        {9 + count + at: 3 + at for at in range(len(stacks))}, 60_000_000_000, "ffn_backward", early if started else None,
+        {9 + count + at: 3 + at for at in range(len(stacks))}, 60_000_000_000, "ffn_backward",
     )
 
 
@@ -1199,7 +1239,7 @@
                 jnp.sum(block * block, axis=1, keepdims=True),
             )
 
-        sent = line_sum(square, gather, product, own, own_row, z_out, z_in, zr_out, zr_in, zs_s, zs_r, zr_s, zr_r, lambda: None)
+        sent = line_sum(square, gather, product, own, own_row, z_out, z_in, zr_out, zr_in, zs_s, zs_r, zr_s, zr_r, hook)
         total, squares = own[...], own_row[...]
         for slot in range(depth - 1):
             total = total + z_in[slot].astype(jnp.float32)
@@ -1752,29 +1792,33 @@
         first = index == 0
         final = index == layers - 1
         follow = index + 1
-        shipped = [] if final else [own_qkv[follow], own_out[follow], own_gu[follow]]
+        shipped = [] if final else [own_qkv[follow], own_out[follow], own_gu[follow], own_down[follow]]
         attend = attention_forward(
             before, gain_a[index], own_qkv[index], own_out[index], peer_qkv[index], peer_out[index],
             own_gu[:1] if first else [], cosine, sine, depth
         )
         peer = attend.link(len(attend.shapes) - 1) if first else peer_gu[index]
-        feed = ffn_forward(attend.link(0), gain_f[index], own_gu[index], peer, own_down[index], shipped, depth)
+        feed = ffn_forward(
+            attend.link(0), gain_f[index], own_gu[index], peer, own_down[index], peer_down[index], shipped, depth
+        )
         parts = [attend, feed]
         if final:
-            feed.private = (2, 3, 4)
-            parts.append(
-                ffn_backward(
-                    grad_now, attend.link(0), gain_f[index], feed.link(2, 1), feed.link(3, 1), own_gu[index], peer,
-                    own_down[index], feed.link(4, 1), [], [], index, layers, depth, True
-                )
+            feed.private = (2, 3)
+            back_part = ffn_backward(
+                grad_now, attend.link(0), gain_f[index], feed.link(2, 1), feed.link(3, 1), own_gu[index], peer, own_down[index],
+                feed.link(4, 1) if first else peer_down[index], [], [], index, layers, depth, not first
             )
+            back_part.woven = not first
+            parts.append(back_part)
         made, fed, *back = launch(parts, greet, 2 * index)
         hidden_in, normed_a, queries, kv, lse, mixed, factors = made[:7]
         if first:
             peer_qkv[0], peer_out[0], peer_gu[0] = made[7:]
-        current, normed_f, kept, active, peer_down[index] = fed[:5]
+        current, normed_f, kept, active = fed[:4]
+        if first:
+            peer_down[index] = fed[4]
         if shipped:
-            peer_qkv[follow], peer_out[follow], peer_gu[follow] = fed[5:]
+            peer_qkv[follow], peer_out[follow], peer_gu[follow], peer_down[follow] = fed[-4:]
         saved.append((before, normed_a, queries, kv, lse, mixed, factors, hidden_in, normed_f, kept, active))
     list_ga, list_gf, got_qkv, rest_stack = ([], [], [], [])
     grad_hidden, grad_gu, gain_f_grad, *down_stack = back[0]
@@ -1790,7 +1834,7 @@
             _, _, _, _, _, _, _, hidden_in, _, kept, active = saved[index - 1]
             feed = ffn_backward(
                 attend.link(0), hidden_in, gain_f[index - 1], kept, active, own_gu[index - 1], peer_gu[index - 1],
-                own_down[index - 1], peer_down[index - 1], [attend.link(2)], down_stack, index - 1, layers, depth, False
+                own_down[index - 1], peer_down[index - 1], [attend.link(2)], down_stack, index - 1, layers, depth
             )
             made, (grad_hidden, grad_gu, gain_f_grad, *down_stack, landed) = launch([attend, feed], greet, 2 * index + 1)
             got_qkv.append(landed)

time: 579 us -> 560 us (0.967)
  Pallas kernels: 542 us -> 522 us
    pallas_call x4, Pallas kernels: 533 us -> 513 us  [launch(): pl.pallas_call(body, out_shape=tuple(shapes), in_specs=[outside] * len(op...]
  transfers between devices with their start and end apart: 4 -> 4, of which waited for: 1 -> 1; matrix products, arithmetic and copies ran while one was open for 2% -> 2% of each run, Pallas kernels for 59% -> 61%
where the time goes in v8:
time: 560 us; the launch traced here: 559 us
  Pallas kernels  522 us (93%)
  local copies, waits for them, and re-layouts  14.7 us (3%)
  starting transfers between devices  14 us (2%)
    pallas_call x4, Pallas kernels, launch(): pl.pallas_call(body, out_shape=tuple(shapes), in_specs=[outside] * len(op...  513 us
    ppermute x4, starting transfers between devices, swap_grid(): return lax.ppermute(values, ('z', 'y', 'c'), pairs)  14 us
  transfers between devices with their start and end apart: 4, of which 1 were waited for; matrix products, arithmetic and copies ran while one was open for 2% of the time, Pallas kernels for 61%

profile of v8, /device:TPU:4, one launch (start us, length us, event | category | flops | bytes accessed | tf_op | source)
XLA Modules:
  0.0 558.8 jit_solution(10555374536156586022)
XLA Ops:
  0.6 0.0 copy-start.2
  0.6 0.0 copy-start.1
  0.7 0.9 pad_maximum_fusion
  1.5 4.4 collective-permute-start.1
  5.9 3.2 collective-permute-start
  9.2 4.4 collective-permute-start.2
  13.6 1.9 slice_bitcast_fusion.4
  15.5 0.0 copy-done.2
  15.5 0.9 slice_bitcast_fusion.2
  16.4 0.0 copy-done.1
  16.4 0.0 copy-start
  16.4 1.2 slice_bitcast_fusion
  17.6 1.1 copy-done
  18.8 2.0 fusion.5
  20.8 1.0 fusion
  21.8 1.3 copy.24
  23.0 1.3 copy.23
  24.3 0.0 collective-permute-done.1
  24.3 0.6 fusion.7
  24.9 5.1 collective-permute-done.refs_0_.refs_1_
  30.0 0.0 copy-start.5
  30.0 0.7 copy-done.5
  30.7 134.5 %attention_forward_ffn_forward.1 = (f32[128,512]{1,0:T(8,128)}, bf16[512,512]{1,0:T(8,128)(2,1)}, bf16[128,512]{1,0:T(8,128)(2,1)}, bf16[1024,128]{1,0:T(8,128)(...) custom-call(f32[128,512]{1,0:T(8,128)} %copy-done.5, ...), custom_call_target="tpu_custom_call" | custom-call | flops 109999996928 | bytes 8000000 | tf_op jit(solution)/shard_map/attention_forward_ffn_forward/pallas_call | solution.py:486
  165.2 0.0 collective-permute-done.2.refs_13_
  165.2 0.0 copy-start.6
  165.2 0.7 copy-done.6
  165.9 179.8 %attention_forward_ffn_forward_ffn_backward.1 = (f32[128,512]{1,0:T(8,128)}, bf16[512,512]{1,0:T(8,128)(2,1)}, bf16[128,512]{1,0:T(8,128)(2,1)}, bf16[1024,128]{...) custom-call(f32[128,512]{1,0:T(8,128)} %get-tuple-element.64.refs_0_, ...), custom_call_target="tpu_custom_call" | custom-call | flops 170000007168 | bytes 8000000 | tf_op jit(solution)/shard_map/attention_forward_ffn_forward_ffn_backward/pallas_call | solution.py:486
  345.7 1.9 collective-permute-start.3
  347.6 131.8 %attention_backward_ffn_backward.1 = (f32[128,512]{1,0:T(8,128)}, f32[8,512]{1,0:T(8,128)}, bf16[256,640]{1,0:T(8,128)(2,1)}, bf16[2,256,2816]{2,1,0:T(8,128)(2,...) custom-call(f32[128,512]{1,0:T(8,128)} %get-tuple-element.70.refs_0_, ...), custom_call_target="tpu_custom_call", output_to_operand_aliasing={{11}: (25, {}), {12}: (26, {})} | custom-call | flops 109999996928 | bytes 8000000 | tf_op jit(solution)/shard_map/attention_backward_ffn_backward/pallas_call | solution.py:486
  479.5 67.1 %attention_backward_finish.1 = (f32[128,512]{1,0:T(8,128)}, f32[8,512]{1,0:T(8,128)}, bf16[256,640]{1,0:T(8,128)(2,1)}, bf16[2,256,2816]{2,1,0:T(8,128)(2,1)}, b...) custom-call(f32[128,512]{1,0:T(8,128)} %get-tuple-element.86.refs_0_, ...), custom_call_target="tpu_custom_call", output_to_operand_aliasing={{3}: (17, {}), {4}: (18, {}), {5}: (19, {}), {6}: (20, {}),... | custom-call | flops 54999998464 | bytes 8000000 | tf_op jit(solution)/shard_map/attention_backward_finish/pallas_call | solution.py:486
  546.5 0.0 copy-start.4
  546.6 0.0 copy-start.3
  546.6 9.2 %combine.1 = (f32[2,256,1,640]{3,2,1,0:T(1,128)}, f32[2,256,512]{2,1,0:T(8,128)}, f32[2,256,2,1408]{3,2,1,0:T(2,128)}, f32[2,256,1408]{2,1,0:T(8,128)}) custom-call(bf16[2,256,2816]{2,1,0:T(8,128)(2,1)} %get-tuple-element.106.gu_k, bf16[2,256,2816]{2,1,0:T(8,128)(2,1)} %get-tuple-element.107.gu_g, bf16[2,256,512]{2,1,0:T(8,128)(2,1)} %get-tuple-element.108.out_k, ...), custom_call_target="tpu_custom_call" | custom-call | tf_op jit(solution)/shard_map/combine/pallas_call | solution.py:1743
  555.8 0.0 copy-done.4
  555.8 0.6 fusion.6
  556.4 0.0 collective-permute-done.3
  556.4 1.7 copy.34
  558.1 0.0 copy-done.3
  558.1 0.7 copy.35
  (2 shorter events, 0.0 us)
Async XLA Ops:
  0.6 14.9 %copy-start.2 = (bf16[2,256,1,640]{3,1,2,0:T(8,128)(2,1)S(1)}, bf16[2,256,1,640]{3,1,2,0:T(8,128)(2,1)}, u32[]{:S(2)}) copy-start(bf16[2,256,1,640]{3,1,2,0:T(8,128)(2,1)} %param.10) | copy-start | bytes 1966084
  0.6 15.8 %copy-start.1 = (bf16[2,256,1408]{2,1,0:T(8,128)(2,1)S(1)}, bf16[2,256,1408]{2,1,0:T(8,128)(2,1)}, u32[]{:S(2)}) copy-start(bf16[2,256,1408]{2,1,0:T(8,128)(2,1)} %param.13) | copy-start | bytes 4325380
  1.5 22.8 %collective-permute-start.1 = (f32[4,512]{1,0:T(4,128)S(1)}, f32[4,512]{1,0:T(4,128)S(1)}, u32[]{:S(2)}, u32[]{:S(2)}) collective-permute-start(f32[4,512]{1,0:T(4,128)S(1)} %pad_maximum_fusion), channel_id=1, source_target_pairs={{0,0},{1,8},{2,16},{3,24},{8,1},{9,9},{10,17},{11,25},{16,2},{17,1... | collective-permute-start | bytes 24584 | tf_op jit(solution)/shard_map/ppermute | solution.py:265
  5.9 24.0 %collective-permute-start = (f32[128,512]{1,0:T(8,128)}, f32[128,512]{1,0:T(8,128)S(1)}, u32[]{:S(2)}, u32[]{:S(2)}) collective-permute-start(f32[128,512]{1,0:T(8,128)} %param.8), channel_id=1, source_target_pairs={{0,0},{1,8},{2,16},{3,24},{8,1},{9,9},{10,17},{11,25},{16,2},{17,1... | collective-permute-start | bytes 786440 | tf_op jit(solution)/shard_map/ppermute | solution.py:265
  9.2 156.0 %collective-permute-start.2 = (f32[128,512]{1,0:T(8,128)}, f32[128,512]{1,0:T(8,128)S(1)}, u32[]{:S(2)}, u32[]{:S(2)}) collective-permute-start(f32[128,512]{1,0:T(8,128)} %param.9), channel_id=1, source_target_pairs={{0,0},{1,8},{2,16},{3,24},{8,1},{9,9},{10,17},{11,25},{16,2},{17,1... | collective-permute-start | bytes 786440 | tf_op jit(solution)/shard_map/ppermute | solution.py:265
  16.4 2.3 copy-start
  30.0 0.7 copy-start.5
  165.2 0.7 copy-start.6
  345.7 210.7 %collective-permute-start.3 = (f32[128,512]{1,0:T(8,128)}, f32[128,512]{1,0:T(8,128)}, u32[]{:S(2)}, u32[]{:S(2)}) collective-permute-start(f32[128,512]{1,0:T(8,128)} %get-tuple-element.69), channel_id=1, source_target_pairs={{0,0},{1,8},{2,16},{3,24},{8,1},{9,9},{10,17},{11,25},{16,2},{17,1... | collective-permute-start | bytes 786440 | tf_op jit(solution)/shard_map/ppermute | solution.py:265
  546.5 9.2 %copy-start.4 = (f32[4,512]{1,0:T(4,128)S(1)}, f32[4,512]{1,0:T(4,128)}, u32[]{:S(2)}) copy-start(f32[4,512]{1,0:T(4,128)} %get-tuple-element.119) | copy-start | bytes 24580
  546.6 11.5 %copy-start.3 = (f32[128,512]{1,0:T(8,128)S(1)}, f32[128,512]{1,0:T(8,128)}, u32[]{:S(2)}) copy-start(f32[128,512]{1,0:T(8,128)} %get-tuple-element.147) | copy-start | bytes 786436

commit v9 on v8

--- a/solution.py
+++ b/solution.py
@@ -869,7 +869,7 @@
 
 
 def ffn_backward(
-    grad, hidden, gain, kept, wide_forward, gu_own, gu_peer, down_own, down_peer, shipped, stacks, index, layers, depth, woven=False
+    grad, hidden, gain, kept, wide_forward, gu_own, gu_peer, down_own, down_peer, shipped, depth, woven=False
 ):
     tok, features = hidden.shape
     width = down_own.shape[1]
@@ -882,7 +882,6 @@
 
     def kernel(loads, stores, greet, hook, dy_ref, h_ref, gain_ref, kept_ref, before_ref, w1_own, w1_peer, w2_own, w2_peer, *rest):
         leave, rest = rest[:count], rest[count:]
-        rest = rest[len(stacks):]
         (out_ref, wide, gain_out, kept_all, got_all), rest = rest[:5], rest[5:]
         landed, rest = rest[:count], rest[count:]
         (taken, turned, down_kept, down_given, keep_s, pieces, side_s, side_r, product, carried, chain_out, chain_in, own_part,
@@ -892,8 +891,8 @@
         own, other = halves(features)
         loads[0].wait()
         taken[pl.ds(line.own, tok), :] = dy_ref[...].astype(jnp.bfloat16)
-        give = side.later(down_given, got_all.at[index])
-        keep = pltpu.make_async_copy(down_kept, kept_all.at[index], keep_s)
+        give = side.later(down_given, got_all)
+        keep = pltpu.make_async_copy(down_kept, kept_all, keep_s)
 
         def begin():
             for source, target in zip(leave, landed):
@@ -982,8 +981,8 @@
         jax.ShapeDtypeStruct((tok, features), full),
         jax.ShapeDtypeStruct((4 * tok, 2 * width + EXTRA), low),
         jax.ShapeDtypeStruct((8, features), full),
-        jax.ShapeDtypeStruct((layers,) + down_own.shape, low),
-        jax.ShapeDtypeStruct((layers,) + down_own.shape, low),
+        jax.ShapeDtypeStruct(down_own.shape, low),
+        jax.ShapeDtypeStruct(down_own.shape, low),
     ) + tuple(jax.ShapeDtypeStruct(item.shape, item.dtype) for item in shipped)
     own_scratch = [
         pltpu.VMEM((4 * tok, features), low),
@@ -996,10 +995,10 @@
     ] + scratch
     return Part(
         kernel,
-        (grad, hidden, gain.reshape(1, -1), kept, wide_forward, gu_own, gu_peer, down_own, down_peer, *shipped, *stacks),
+        (grad, hidden, gain.reshape(1, -1), kept, wide_forward, gu_own, gu_peer, down_own, down_peer, *shipped),
         shapes, 9, 3,
         own_scratch,
-        {9 + count + at: 3 + at for at in range(len(stacks))}, 60_000_000_000, "ffn_backward",
+        {}, 60_000_000_000, "ffn_backward",
     )
 
 
@@ -1370,7 +1369,7 @@
 
 def attention_backward(
     grad, hidden, gain, qkv_own, qkv_peer, out_own, out_peer, cosine, sine, queries, kv, lse, factors, mixed, normed_a, normed_f,
-    grad_gu, stacks, index, layers, depth,
+    grad_gu, depth,
 ):
     tok, features = hidden.shape
     cols = qkv_own.shape[1]
@@ -1385,7 +1384,7 @@
         (out_ref, gain_out, qkv_given, gu_kept_all, gu_got_all, out_kept_all, out_got_all, qkv_kept_all,
                taken, spun, turned, pieces, gu_kept, gu_given, out_kept, out_given, qkv_kept, keep_s,
                own, heads, z_out, z_in, keys_t, dk, dv, kv_out, kv_in, dq, inner_rows, g_own, g_out, g_in, g_rows,
-               ag_s, ag_r, zs_s, zs_r, kv_s, kv_r, zg_s, zg_r, zgr_s, zgr_r, gs_s, gs_r, gr_s, gr_r, side_s, side_r) = rest_refs[len(stacks):]
+               ag_s, ag_r, zs_s, zs_r, kv_s, kv_r, zg_s, zg_r, zgr_s, zgr_r, gs_s, gs_r, gr_s, gr_r, side_s, side_r) = rest_refs
         square = Square(tok, depth)
         side = Side(side_s, side_r)
         mine, other = halves(features)
@@ -1403,11 +1402,11 @@
 
             lax.fori_loop(start, stop, tile, 0)
 
-        gu_got = gu_got_all.at[index]
+        gu_got = gu_got_all
         keeps = [
-            pltpu.make_async_copy(gu_kept, gu_kept_all.at[index], keep_s.at[0]),
-            pltpu.make_async_copy(out_kept, out_kept_all.at[index], keep_s.at[1]),
-            pltpu.make_async_copy(qkv_kept, qkv_kept_all.at[index], keep_s.at[2]),
+            pltpu.make_async_copy(gu_kept, gu_kept_all, keep_s.at[0]),
+            pltpu.make_async_copy(out_kept, out_kept_all, keep_s.at[1]),
+            pltpu.make_async_copy(qkv_kept, qkv_kept_all, keep_s.at[2]),
         ]
         every = wide // EXTRA
         middle, late = every // 2, every * 3 // 4
@@ -1420,7 +1419,7 @@
             turned[...] = flip(taken[...])
             for t in range(query_cols // EXTRA):
                 grad_tile(turned, features, mixed_ref, pl.ds(t * EXTRA, EXTRA), out_kept, out_given)
-            side.start(out_given, out_got_all.at[index])
+            side.start(out_given, out_got_all)
             gu_tiles(middle, late)
             side.start(gu_given.at[:, inner_part], gu_got.at[:, inner_part])
             gu_tiles(late, every)
@@ -1549,15 +1548,15 @@
         jax.ShapeDtypeStruct((tok, features), full),
         jax.ShapeDtypeStruct((8, features), full),
         jax.ShapeDtypeStruct(qkv_own.shape, low),
-        jax.ShapeDtypeStruct((layers, features // 2, wide), low),
-        jax.ShapeDtypeStruct((layers, features // 2, wide), low),
-        jax.ShapeDtypeStruct((layers,) + out_own.shape, low),
-        jax.ShapeDtypeStruct((layers,) + out_own.shape, low),
-        jax.ShapeDtypeStruct((layers,) + qkv_own.shape, low),
+        jax.ShapeDtypeStruct((features // 2, wide), low),
+        jax.ShapeDtypeStruct((features // 2, wide), low),
+        jax.ShapeDtypeStruct(out_own.shape, low),
+        jax.ShapeDtypeStruct(out_own.shape, low),
+        jax.ShapeDtypeStruct(qkv_own.shape, low),
     )
     operands = (
         grad, hidden, gain.reshape(1, -1), qkv_own, qkv_peer, out_own, out_peer, cosine, sine, queries, kv, lse, factors,
-        mixed, normed_a, normed_f, grad_gu, *stacks,
+        mixed, normed_a, normed_f, grad_gu,
     )
     return Part(
         kernel, operands, shapes, 17, 3,
@@ -1591,7 +1590,7 @@
             sem(2 * depth - 1), sem(2 * depth - 1), sem(depth - 1, pairs + 1), sem(depth - 1, pairs + 1), sem(depth - 1),
             sem(depth - 1), sem(depth), sem(depth - 1), sem(depth), sem(depth - 1), sem(4), sem(4),
         ],
-        {17 + at: 3 + at for at in range(len(stacks))}, 50_000_000_000, "attention_backward",
+        {}, 50_000_000_000, "attention_backward",
     )
 
 
@@ -1715,51 +1714,57 @@
     )
 
 
-def combine(rests, downs, got_qkv):
-    gu_kept, gu_got, out_kept, out_got, qkv_kept = rests
-    layers, rows, wide = gu_kept.shape
+def combine(halves_of):
+    layers, count = len(halves_of), len(halves_of[0])
+    rows, wide = halves_of[0][0].shape
     half = wide // 2
     step = rows // 2
-
-    def kernel(gu_k, gu_g, out_k, out_g, down_k, down_g, qkv_k, *rest):
-        got, (qkv_o, out_o, gu_o, down_o) = rest[:layers], rest[layers:]
-        total = gu_k[0].astype(jnp.float32) + gu_g[0].astype(jnp.float32)
-        gu_o[0, :, 0, :] = total[:, :half]
-        gu_o[0, :, 1, :] = total[:, half:]
-        out_o[...] = out_k[...].astype(jnp.float32) + out_g[...].astype(jnp.float32)
-        down_o[...] = down_k[...].astype(jnp.float32) + down_g[...].astype(jnp.float32)
+    last = rows // step - 1
+
+    def kernel(*refs):
+        qkv_o, out_o, gu_o, down_o = refs[layers * count :]
         for index in range(layers):
+            gu_k, gu_g, out_k, out_g, down_k, down_g, qkv_k, qkv_g = refs[index * count : (index + 1) * count]
 
             @pl.when(pl.program_id(0) == index)
             def _():
-                qkv_o[0, :, 0, :] = qkv_k[0].astype(jnp.float32) + got[index][...].astype(jnp.float32)
-
-    def spec(item):
-        return pl.BlockSpec((1, step, item.shape[2]), lambda layer, at: (layer, at, 0))
-
-    operands = (gu_kept, gu_got, out_kept, out_got, *downs, qkv_kept)
-    cols = qkv_kept.shape[2]
+                add = lambda kept, got: kept[...].astype(jnp.float32) + got[...].astype(jnp.float32)
+                total = add(gu_k, gu_g)
+                gu_o[0, :, 0, :] = total[:, :half]
+                gu_o[0, :, 1, :] = total[:, half:]
+                out_o[0] = add(out_k, out_g)
+                down_o[0] = add(down_k, down_g)
+                qkv_o[0, :, 0, :] = add(qkv_k, qkv_g)
+
+    def place(index):
+        def at_of(layer, at):
+            return jnp.where(layer == index, at, jnp.where(layer < index, 0, last)), 0
+
+        return at_of
+
     full = jnp.float32
+    sizes = [item.shape[1] for item in halves_of[0]]
+    outer = lambda layer, at: (layer, at, 0)
+    inner = lambda layer, at: (layer, at, 0, 0)
     return pl.pallas_call(
         kernel,
         grid=(layers, rows // step),
-        in_specs=[spec(item) for item in operands]
-        + [pl.BlockSpec((step, cols), lambda layer, at: (at, 0)) for _ in range(layers)],
+        in_specs=[pl.BlockSpec((step, size), place(index)) for index in range(layers) for size in sizes],
         out_specs=[
-            pl.BlockSpec((1, step, 1, cols), lambda layer, at: (layer, at, 0, 0)),
-            spec(out_kept),
-            pl.BlockSpec((1, step, 2, half), lambda layer, at: (layer, at, 0, 0)),
-            spec(downs[0]),
+            pl.BlockSpec((1, step, 1, sizes[6]), inner),
+            pl.BlockSpec((1, step, sizes[2]), outer),
+            pl.BlockSpec((1, step, 2, half), inner),
+            pl.BlockSpec((1, step, sizes[4]), outer),
         ],
         out_shape=[
-            jax.ShapeDtypeStruct((layers, rows, 1, cols), full),
-            jax.ShapeDtypeStruct(out_kept.shape, full),
+            jax.ShapeDtypeStruct((layers, rows, 1, sizes[6]), full),
+            jax.ShapeDtypeStruct((layers, rows, sizes[2]), full),
             jax.ShapeDtypeStruct((layers, rows, 2, half), full),
-            jax.ShapeDtypeStruct(downs[0].shape, full),
+            jax.ShapeDtypeStruct((layers, rows, sizes[4]), full),
         ],
         compiler_params=pltpu.CompilerParams(vmem_limit_bytes=60 << 20),
         name="combine",
-    )(*operands, *got_qkv)
+    )(*(item for items in halves_of for item in items))
 
 
 def stationary(stream, grad_out, wqkv, wo, wgu, wd, gain_attn, gain_ffn):
@@ -1806,7 +1811,7 @@
             feed.private = (2, 3)
             back_part = ffn_backward(
                 grad_now, attend.link(0), gain_f[index], feed.link(2, 1), feed.link(3, 1), own_gu[index], peer, own_down[index],
-                feed.link(4, 1) if first else peer_down[index], [], [], index, layers, depth, not first
+                feed.link(4, 1) if first else peer_down[index], [], depth, not first
             )
             back_part.woven = not first
             parts.append(back_part)
@@ -1820,31 +1825,48 @@
         if shipped:
             peer_qkv[follow], peer_out[follow], peer_gu[follow], peer_down[follow] = fed[-4:]
         saved.append((before, normed_a, queries, kv, lse, mixed, factors, hidden_in, normed_f, kept, active))
-    list_ga, list_gf, got_qkv, rest_stack = ([], [], [], [])
-    grad_hidden, grad_gu, gain_f_grad, *down_stack = back[0]
+    gains_a, gains_f, downs, rests, got_qkv = ({}, {}, {}, {}, {})
+    grad_hidden, grad_gu, gains_f[layers - 1], *downs[layers - 1] = back[0]
+    parts, whose = [], []
     for index in reversed(range(layers)):
-        list_gf.append(gain_f_grad)
         before, normed_a, queries, kv, lse, mixed, factors, _, normed_f, _, _ = saved[index]
         attend = attention_backward(
             grad_hidden, before, gain_a[index], own_qkv[index], peer_qkv[index], own_out[index], peer_out[index],
-            cosine, sine, queries, kv, lse, factors, mixed, normed_a, normed_f, grad_gu, rest_stack, index, layers, depth
+            cosine, sine, queries, kv, lse, factors, mixed, normed_a, normed_f, grad_gu, depth
         )
         attend.private = (2,)
+        at = len(parts)
+        parts.append(attend)
         if index:
             _, _, _, _, _, _, _, hidden_in, _, kept, active = saved[index - 1]
             feed = ffn_backward(
-                attend.link(0), hidden_in, gain_f[index - 1], kept, active, own_gu[index - 1], peer_gu[index - 1],
-                own_down[index - 1], peer_down[index - 1], [attend.link(2)], down_stack, index - 1, layers, depth
+                attend.link(0, at), hidden_in, gain_f[index - 1], kept, active, own_gu[index - 1], peer_gu[index - 1],
+                own_down[index - 1], peer_down[index - 1], [attend.link(2, at)], depth
             )
-            made, (grad_hidden, grad_gu, gain_f_grad, *down_stack, landed) = launch([attend, feed], greet, 2 * index + 1)
-            got_qkv.append(landed)
-        else:
-            tail = finish(attend.link(0), [attend.link(1)] + list_ga[::-1] + list_gf[::-1], attend.link(2), depth)
-            made, (grad_in, gains, landed) = launch([attend, tail], lambda: greet_last(tok, depth), 1)
-            got_qkv.append(landed)
-        list_ga.append(made[1])
-        rest_stack = made[3:]
-    grads = combine(rest_stack, down_stack, got_qkv[::-1])
+            parts.append(feed)
+            whose.append((index, at))
+            grad_hidden, grad_gu = feed.link(0, at + 1), feed.link(1, at + 1)
+            if index > 1:
+                made = launch(parts, greet, 2 * index + 1)
+                for layer, spot in whose:
+                    _, gains_a[layer], _, *rests[layer] = made[spot]
+                    grad_hidden, grad_gu, gains_f[layer - 1], *downs[layer - 1], got_qkv[layer] = made[spot + 1]
+                parts, whose = [], []
+    known_a = [gains_a[layer] for layer in range(1, layers) if layer in gains_a]
+    open_a = [parts[spot].link(1, spot) for _, spot in whose[::-1]]
+    known_f = [gains_f[layer] for layer in range(layers) if layer in gains_f]
+    open_f = [parts[spot + 1].link(2, spot + 1) for _, spot in whose[::-1]]
+    tail = finish(attend.link(0, at), [attend.link(1, at)] + open_a + known_a + open_f + known_f, attend.link(2, at), depth)
+    made = launch(parts + [tail], lambda: greet_last(tok, depth), 1)
+    for layer, spot in whose:
+        rests[layer] = made[spot][3:]
+        *_, kept_down, got_down, got_qkv[layer] = made[spot + 1]
+        downs[layer - 1] = [kept_down, got_down]
+    rests[0] = made[at][3:]
+    grad_in, gains, got_qkv[0] = made[-1]
+    grads = combine([
+        (*rests[layer][:4], *downs[layer], rests[layer][4], got_qkv[layer]) for layer in range(layers)
+    ])
     return (swap_grid(current, depth), grad_in, *grads, gains[:layers], gains[layers:])
 
 

time: 560 us -> 550 us (0.982)
  Pallas kernels: 522 us -> 514 us
    pallas_call x4 -> x3, Pallas kernels: 513 us -> 504 us  [launch(): pl.pallas_call(body, out_shape=tuple(shapes), in_specs=[outside] * len(op...]
where the time goes in v9:
time: 550 us
  Pallas kernels  514 us (93%)
  local copies, waits for them, and re-layouts  14.7 us (3%)
  starting transfers between devices  14 us (3%)
    pallas_call x3, Pallas kernels, launch(): pl.pallas_call(body, out_shape=tuple(shapes), in_specs=[outside] * len(op...  504 us
    ppermute x4, starting transfers between devices, swap_grid(): return lax.ppermute(values, ('z', 'y', 'c'), pairs)  14 us
  transfers between devices with their start and end apart: 4, of which 1 were waited for; matrix products, arithmetic and copies ran while one was open for 2% of the time, Pallas kernels for 61%

profile of v9, /device:TPU:4, one launch (start us, length us, event | category | flops | bytes accessed | tf_op | source)
XLA Modules:
  0.0 549.9 jit_solution(14760563352224171050)
XLA Ops:
  0.6 0.0 copy-start.2
  0.6 0.0 copy-start.1
  0.7 0.9 pad_maximum_fusion
  1.5 4.4 collective-permute-start.1
  5.9 3.2 collective-permute-start
  9.2 4.4 collective-permute-start.2
  13.6 1.9 slice_bitcast_fusion.4
  15.5 0.0 copy-done.2
  15.5 0.9 slice_bitcast_fusion.2
  16.4 0.0 copy-done.1
  16.4 0.0 copy-start
  16.4 1.2 slice_bitcast_fusion
  17.6 1.1 copy-done
  18.8 2.0 fusion.5
  20.8 1.0 fusion
  21.8 1.3 copy.17
  23.0 1.3 copy.16
  24.3 0.0 collective-permute-done.1
  24.3 0.6 fusion.7
  24.9 5.1 collective-permute-done.refs_0_.refs_25_
  30.0 0.0 copy-start.5
  30.0 0.7 copy-done.5
  30.7 134.5 %attention_forward_ffn_forward.1 = (f32[128,512]{1,0:T(8,128)}, bf16[512,512]{1,0:T(8,128)(2,1)}, bf16[128,512]{1,0:T(8,128)(2,1)}, bf16[1024,128]{1,0:T(8,128)(...) custom-call(f32[128,512]{1,0:T(8,128)} %copy-done.5, ...), custom_call_target="tpu_custom_call" | custom-call | flops 109999996928 | bytes 8000000 | tf_op jit(solution)/shard_map/attention_forward_ffn_forward/pallas_call | solution.py:486
  165.2 0.0 collective-permute-done.2.refs_13_
  165.2 0.0 copy-start.6
  165.2 0.7 copy-done.6
  165.9 179.8 %attention_forward_ffn_forward_ffn_backward.1 = (f32[128,512]{1,0:T(8,128)}, bf16[512,512]{1,0:T(8,128)(2,1)}, bf16[128,512]{1,0:T(8,128)(2,1)}, bf16[1024,128]{...) custom-call(f32[128,512]{1,0:T(8,128)} %get-tuple-element.60.refs_0_, ...), custom_call_target="tpu_custom_call" | custom-call | flops 170000007168 | bytes 8000000 | tf_op jit(solution)/shard_map/attention_forward_ffn_forward_ffn_backward/pallas_call | solution.py:486
  345.7 1.9 collective-permute-start.3
  347.6 189.5 %attention_backward_ffn_backward_attention_backward_finish.1 = (f32[128,512]{1,0:T(8,128)}, f32[8,512]{1,0:T(8,128)}, bf16[256,640]{1,0:T(8,128)(2,1)}, bf16[256...) custom-call(f32[128,512]{1,0:T(8,128)} %get-tuple-element.66.refs_0_, ...), custom_call_target="tpu_custom_call" | custom-call | flops 165000003584 | bytes 8000000 | tf_op jit(solution)/shard_map/attention_backward_ffn_backward_attention_backward_finish/pallas_call | solution.py:486
  537.2 0.0 copy-start.4
  537.2 0.0 copy-start.3
  537.2 9.8 %combine.1 = (f32[2,256,1,640]{3,2,1,0:T(1,128)}, f32[2,256,512]{2,1,0:T(8,128)}, f32[2,256,2,1408]{3,2,1,0:T(2,128)}, f32[2,256,1408]{2,1,0:T(8,128)}) custom-call(bf16[256,2816]{1,0:T(8,128)(2,1)} %get-tuple-element.91.refs_0_, bf16[256,2816]{1,0:T(8,128)(2,1)} %get-tuple-element.92.refs_1_, bf16[256,512]{1,0:T(8,128)(2,1)} %get-tuple-element.93.refs_2_, ...), custom_call_target="tpu_custom_call" | custom-call | tf_op jit(solution)/shard_map/combine/pallas_call | solution.py:1749
  547.0 0.0 copy-done.4
  547.0 0.6 fusion.6
  547.6 0.0 collective-permute-done.3
  547.6 1.7 copy.20
  549.2 0.0 copy-done.3
  549.2 0.7 copy.21
  (2 shorter events, 0.0 us)
Async XLA Ops:
  0.6 14.9 %copy-start.2 = (bf16[2,256,1,640]{3,1,2,0:T(8,128)(2,1)S(1)}, bf16[2,256,1,640]{3,1,2,0:T(8,128)(2,1)}, u32[]{:S(2)}) copy-start(bf16[2,256,1,640]{3,1,2,0:T(8,128)(2,1)} %param.10) | copy-start | bytes 1966084
  0.6 15.8 %copy-start.1 = (bf16[2,256,1408]{2,1,0:T(8,128)(2,1)S(1)}, bf16[2,256,1408]{2,1,0:T(8,128)(2,1)}, u32[]{:S(2)}) copy-start(bf16[2,256,1408]{2,1,0:T(8,128)(2,1)} %param.13) | copy-start | bytes 4325380
  1.5 22.8 %collective-permute-start.1 = (f32[4,512]{1,0:T(4,128)S(1)}, f32[4,512]{1,0:T(4,128)S(1)}, u32[]{:S(2)}, u32[]{:S(2)}) collective-permute-start(f32[4,512]{1,0:T(4,128)S(1)} %pad_maximum_fusion), channel_id=1, source_target_pairs={{0,0},{1,8},{2,16},{3,24},{8,1},{9,9},{10,17},{11,25},{16,2},{17,1... | collective-permute-start | bytes 24584 | tf_op jit(solution)/shard_map/ppermute | solution.py:265
  5.9 24.0 %collective-permute-start = (f32[128,512]{1,0:T(8,128)}, f32[128,512]{1,0:T(8,128)S(1)}, u32[]{:S(2)}, u32[]{:S(2)}) collective-permute-start(f32[128,512]{1,0:T(8,128)} %param.8), channel_id=1, source_target_pairs={{0,0},{1,8},{2,16},{3,24},{8,1},{9,9},{10,17},{11,25},{16,2},{17,1... | collective-permute-start | bytes 786440 | tf_op jit(solution)/shard_map/ppermute | solution.py:265
  9.2 156.0 %collective-permute-start.2 = (f32[128,512]{1,0:T(8,128)}, f32[128,512]{1,0:T(8,128)S(1)}, u32[]{:S(2)}, u32[]{:S(2)}) collective-permute-start(f32[128,512]{1,0:T(8,128)} %param.9), channel_id=1, source_target_pairs={{0,0},{1,8},{2,16},{3,24},{8,1},{9,9},{10,17},{11,25},{16,2},{17,1... | collective-permute-start | bytes 786440 | tf_op jit(solution)/shard_map/ppermute | solution.py:265
  16.4 2.3 copy-start
  30.0 0.7 copy-start.5
  165.2 0.7 copy-start.6
  345.7 201.9 %collective-permute-start.3 = (f32[128,512]{1,0:T(8,128)}, f32[128,512]{1,0:T(8,128)}, u32[]{:S(2)}, u32[]{:S(2)}) collective-permute-start(f32[128,512]{1,0:T(8,128)} %get-tuple-element.65), channel_id=1, source_target_pairs={{0,0},{1,8},{2,16},{3,24},{8,1},{9,9},{10,17},{11,25},{16,2},{17,1... | collective-permute-start | bytes 786440 | tf_op jit(solution)/shard_map/ppermute | solution.py:265
  537.2 9.8 %copy-start.4 = (f32[4,512]{1,0:T(4,128)S(1)}, f32[4,512]{1,0:T(4,128)}, u32[]{:S(2)}) copy-start(f32[4,512]{1,0:T(4,128)} %get-tuple-element.111) | copy-start | bytes 24580
  537.2 12.1 %copy-start.3 = (f32[128,512]{1,0:T(8,128)S(1)}, f32[128,512]{1,0:T(8,128)}, u32[]{:S(2)}) copy-start(f32[128,512]{1,0:T(8,128)} %get-tuple-element.139) | copy-start | bytes 786436

commit v10 on v9

--- a/solution.py
+++ b/solution.py
@@ -348,6 +348,12 @@
         self.part, self.at, self.shape, self.dtype = part, at, shape, dtype
 
 
+class Slice:
+    def __init__(self, array, index):
+        self.array, self.index = array, index
+        self.shape, self.dtype = array.shape[1:], array.dtype
+
+
 class Part:
     def __init__(self, kernel, operands, shapes, staged_in, staged_out, scratch, aliases, flops, name, early=None):
         self.kernel, self.operands, self.shapes = kernel, operands, shapes
@@ -400,7 +406,7 @@
             if not isinstance(item, Link):
                 if at in part.aliases:
                     aliases[len(operands)] = base + part.aliases[at]
-                operands.append(item)
+                operands.append(item.array if isinstance(item, Slice) else item)
         shapes += part.shapes
         for item in part.operands[: part.staged_in]:
             if not (isinstance(item, Link) and item.at < parts[item.part].staged_out):
@@ -425,6 +431,8 @@
                     late.append(at)
                 else:
                     near, source = False, given.pop(0)
+                    if isinstance(item, Slice):
+                        source = source.at[item.index]
                 if at >= part.staged_in:
                     inner.append(staged[item.at] if near else source)
                 elif near:
@@ -1185,25 +1193,27 @@
                 row_copy.wait_send()
 
 
-def attention_forward(hidden, gain, qkv_own, out_own, qkv_peer, out_peer, shipped, cosine, sine, depth):
+def attention_forward(hidden, gain, qkv_own, out_own, qkv_peer, out_peer, shipped, freq, cosine, sine, depth):
     tok, features = hidden.shape
     cols = qkv_own.shape[1]
     fetch = qkv_peer is None
-    extra = 2 if fetch else 0
+    extra = 4 if fetch else 0
     count = len(shipped)
-    sides = extra + 2 * count
+    sides = (2 if fetch else 0) + 2 * count
     query_cols = GROUP * HEAD
     seq = 2 * depth * tok
     pairs = query_cols // EXTRA
     scale = 1.0 / math.sqrt(HEAD)
 
-    def kernel(loads, stores, greet, hook, h_ref, gain_ref, wqkv_own, wo_own, cos_ref, sin_ref, *rest):
-        if not fetch:
-            (wqkv_peer, wo_peer), rest = rest[:2], rest[2:]
+    def kernel(loads, stores, greet, hook, h_ref, gain_ref, wqkv_own, wo_own, *rest):
+        if fetch:
+            freq_ref, rest = rest[0], rest[1:]
+        else:
+            (cos_ref, sin_ref, wqkv_peer, wo_peer), rest = rest[:4], rest[4:]
         leave, rest = rest[:count], rest[count:]
         (out_ref, normed_t, queries, kv, lse, mixed, factors), rest = rest[:7], rest[7:]
         if fetch:
-            (wqkv_peer, wo_peer), rest = rest[:2], rest[2:]
+            (wqkv_peer, wo_peer, cos_ref, sin_ref), rest = rest[:4], rest[4:]
         landed, rest = rest[:count], rest[count:]
         (taken, scaled, pieces, own, own_row, z_out, z_in, zr_out, zr_in, values_t, g_own, g_out, g_in,
          ag_s, ag_r, zs_s, zs_r, zr_s, zr_r, kv_s, kv_r, zg_s, zg_r, zgr_s, zgr_r, gs_s, gs_r), rest = rest[:27], rest[27:]
@@ -1225,6 +1235,14 @@
             rest_of = pl.ds(most, source.shape[0] - most)
             side.start(source.at[pl.ds(0, most)], target.at[pl.ds(0, most)])
             held.append(side.later(source.at[rest_of], target.at[rest_of]))
+        if fetch:
+            at = lax.broadcasted_iota(jnp.int32, (tok, EXTRA), 0) + square.row * tok
+            lane = lax.broadcasted_iota(jnp.int32, (tok, EXTRA), 1)
+            angle = at.astype(jnp.float32) * freq_ref[...]
+            cos_ref[...] = jnp.cos(angle)
+            sin_ref[...] = jnp.where(lax.rem(lane, HEAD) < HEAD // 2, -1.0, 1.0) * jnp.sin(angle)
+            stores[9].start()
+            stores[10].start()
         for copy in urgent[:1]:
             copy.wait_recv()
             stores[7].start()
@@ -1340,11 +1358,13 @@
     )
     if fetch:
         shapes += (jax.ShapeDtypeStruct(qkv_own.shape, low), jax.ShapeDtypeStruct(out_own.shape, low))
+        shapes += (jax.ShapeDtypeStruct((tok, EXTRA), full),) * 2
     shapes += tuple(jax.ShapeDtypeStruct(item.shape, item.dtype) for item in shipped)
     peers = () if fetch else (qkv_peer, out_peer)
-    operands = (hidden, gain.reshape(1, -1), qkv_own, out_own, cosine, sine, *peers, *shipped)
+    tables = (freq,) if fetch else (cosine, sine)
+    operands = (hidden, gain.reshape(1, -1), qkv_own, out_own, *tables, *peers, *shipped)
     return Part(
-        kernel, operands, shapes, 6 + len(peers), 7 + extra,
+        kernel, operands, shapes, 4 + len(tables) + len(peers), 7 + extra,
         [
             pltpu.VMEM((depth * tok, features), low),
             pltpu.VMEM((tok, features), low),
@@ -1772,24 +1792,20 @@
     layers = wqkv.shape[0]
     count_rows = wqkv.shape[1]
     depth = lax.axis_size("z")
-    head = HEAD
-    row = lax.axis_index("z") * 2 + lax.axis_index("x")
-    query_pos = row * tok + jnp.arange(tok, dtype=jnp.int32)
+    half = HEAD // 2
     lane = jnp.arange(EXTRA, dtype=jnp.int32)
-    half = head // 2
-    freq = THETA ** (-((lane % half).astype(jnp.float32) * 2.0 / head))
-    angle = query_pos.astype(jnp.float32)[:, None] * freq[None, :]
-    cosine = jnp.cos(angle)
-    sine = jnp.where((lane % head < half)[None, :], -1.0, 1.0) * jnp.sin(angle)
+    freq = (THETA ** (-((lane % half).astype(jnp.float32) * 2.0 / HEAD))).reshape(1, -1)
+    cosine = sine = None
     current = swap_grid(stream, depth)
     grad_now = swap_grid(grad_out, depth)
     gains = swap_grid(jnp.concatenate([gain_attn, gain_ffn]), depth)
     gain_a, gain_f = gains[:layers], gains[layers:]
     greet = lambda: Square(tok, depth).greet()
-    own_qkv = [wqkv[index].reshape(count_rows, -1) for index in range(layers)]
-    own_out = [wo[index] for index in range(layers)]
+    flat_qkv = wqkv.reshape(layers, count_rows, -1)
+    own_qkv = [Slice(flat_qkv, index) for index in range(layers)]
+    own_out = [Slice(wo, index) for index in range(layers)]
     own_gu = [wgu[index].reshape(count_rows, -1) for index in range(layers)]
-    own_down = [wd[index] for index in range(layers)]
+    own_down = [Slice(wd, index) for index in range(layers)]
     peer_qkv, peer_out, peer_gu, peer_down = ([None] * layers for _ in range(4))
     saved = []
     for index in range(layers):
@@ -1800,7 +1816,7 @@
         shipped = [] if final else [own_qkv[follow], own_out[follow], own_gu[follow], own_down[follow]]
         attend = attention_forward(
             before, gain_a[index], own_qkv[index], own_out[index], peer_qkv[index], peer_out[index],
-            own_gu[:1] if first else [], cosine, sine, depth
+            own_gu[:1] if first else [], freq, cosine, sine, depth
         )
         peer = attend.link(len(attend.shapes) - 1) if first else peer_gu[index]
         feed = ffn_forward(
@@ -1818,7 +1834,7 @@
         made, fed, *back = launch(parts, greet, 2 * index)
         hidden_in, normed_a, queries, kv, lse, mixed, factors = made[:7]
         if first:
-            peer_qkv[0], peer_out[0], peer_gu[0] = made[7:]
+            peer_qkv[0], peer_out[0], cosine, sine, peer_gu[0] = made[7:]
         current, normed_f, kept, active = fed[:4]
         if first:
             peer_down[index] = fed[4]

time: 550 us -> 549 us (level)
  transfers between devices with their start and end apart: 4 -> 4, of which waited for: 1 -> 1; matrix products, arithmetic and copies ran while one was open for 2% -> 1% of each run, Pallas kernels for 61% -> 61%
where the time goes in v10:
time: 549 us; the launch traced here: 548 us
  Pallas kernels  512 us (93%)
  starting transfers between devices  14 us (3%)
  local copies, waits for them, and re-layouts  11.2 us (2%)
  waiting for transfers between devices  9 us (2%)
    pallas_call x3, Pallas kernels, launch(): pl.pallas_call(body, out_shape=tuple(shapes), in_specs=[outside] * len(op...  502 us
    ppermute x4, starting transfers between devices, swap_grid(): return lax.ppermute(values, ('z', 'y', 'c'), pairs)  14 us
  transfers between devices with their start and end apart: 4, of which 1 were waited for; matrix products, arithmetic and copies ran while one was open for 1% of the time, Pallas kernels for 61%

profile of v10, /device:TPU:4, one launch (start us, length us, event | category | flops | bytes accessed | tf_op | source)
XLA Modules:
  0.0 548.3 jit_solution(14320490013588511013)
XLA Ops:
  0.6 0.7 pad_maximum_fusion
  1.3 4.4 collective-permute-start.1
  5.8 3.2 collective-permute-start
  9.0 4.4 collective-permute-start.2
  13.4 3.7 fusion.4
  17.2 0.5 fusion.3.refs_4_
  17.7 1.3 copy.17
  18.9 1.3 copy.16
  20.2 0.0 collective-permute-done.1
  20.2 0.6 fusion.6
  20.8 9.0 %collective-permute-done.refs_0_.refs_25_ = f32[128,512]{1,0:T(8,128)S(1)} collective-permute-done((f32[128,512]{1,0:T(8,128)}, f32[128,512]{1,0:T(8,128)S(1)}, u32[]{:S(2)}, u32[]{:S(2)}) %collective-permute-start) | collective-permute-done | bytes 262176 | tf_op jit(solution)/shard_map/ppermute | solution.py:265
  29.8 0.0 copy-start.2
  29.8 0.7 copy-done.2
  30.5 134.5 %attention_forward_ffn_forward.1 = (f32[128,512]{1,0:T(8,128)}, bf16[512,512]{1,0:T(8,128)(2,1)}, bf16[128,512]{1,0:T(8,128)(2,1)}, bf16[1024,128]{1,0:T(8,128)(...) custom-call(f32[128,512]{1,0:T(8,128)} %copy-done.2, ...), custom_call_target="tpu_custom_call" | custom-call | flops 109999996928 | bytes 8000000 | tf_op jit(solution)/shard_map/attention_forward_ffn_forward/pallas_call | solution.py:494
  165.0 0.0 collective-permute-done.2.refs_13_
  165.1 0.0 copy-start.3
  165.1 0.7 copy-done.3
  165.8 179.8 %attention_forward_ffn_forward_ffn_backward.1 = (f32[128,512]{1,0:T(8,128)}, bf16[512,512]{1,0:T(8,128)(2,1)}, bf16[128,512]{1,0:T(8,128)(2,1)}, bf16[1024,128]{...) custom-call(f32[128,512]{1,0:T(8,128)} %get-tuple-element.62.refs_0_, ...), custom_call_target="tpu_custom_call" | custom-call | flops 170000007168 | bytes 8000000 | tf_op jit(solution)/shard_map/attention_forward_ffn_forward_ffn_backward/pallas_call | solution.py:494
  345.6 1.9 collective-permute-start.3
  347.5 188.0 %attention_backward_ffn_backward_attention_backward_finish.1 = (f32[128,512]{1,0:T(8,128)}, f32[8,512]{1,0:T(8,128)}, bf16[256,640]{1,0:T(8,128)(2,1)}, bf16[256...) custom-call(f32[128,512]{1,0:T(8,128)} %get-tuple-element.70.refs_0_, ...), custom_call_target="tpu_custom_call" | custom-call | flops 165000003584 | bytes 8000000 | tf_op jit(solution)/shard_map/attention_backward_ffn_backward_attention_backward_finish/pallas_call | solution.py:494
  535.5 0.0 copy-start.1
  535.5 0.0 copy-start
  535.5 9.8 %combine.1 = (f32[2,256,1,640]{3,2,1,0:T(1,128)}, f32[2,256,512]{2,1,0:T(8,128)}, f32[2,256,2,1408]{3,2,1,0:T(2,128)}, f32[2,256,1408]{2,1,0:T(8,128)}) custom-call(bf16[256,2816]{1,0:T(8,128)(2,1)} %get-tuple-element.95.refs_0_, bf16[256,2816]{1,0:T(8,128)(2,1)} %get-tuple-element.96.refs_1_, bf16[256,512]{1,0:T(8,128)(2,1)} %get-tuple-element.97.refs_2_, ...), custom_call_target="tpu_custom_call" | custom-call | tf_op jit(solution)/shard_map/combine/pallas_call | solution.py:1769
  545.3 0.0 copy-done.1
  545.3 0.6 fusion.5
  545.9 0.0 collective-permute-done.3
  545.9 1.7 copy.20
  547.6 0.0 copy-done
  547.6 0.7 copy.21
Async XLA Ops:
  1.3 18.9 %collective-permute-start.1 = (f32[4,512]{1,0:T(4,128)S(1)}, f32[4,512]{1,0:T(4,128)S(1)}, u32[]{:S(2)}, u32[]{:S(2)}) collective-permute-start(f32[4,512]{1,0:T(4,128)S(1)} %pad_maximum_fusion), channel_id=1, source_target_pairs={{0,0},{1,8},{2,16},{3,24},{8,1},{9,9},{10,17},{11,25},{16,2},{17,1... | collective-permute-start | bytes 24584 | tf_op jit(solution)/shard_map/ppermute | solution.py:265
  5.8 24.0 %collective-permute-start = (f32[128,512]{1,0:T(8,128)}, f32[128,512]{1,0:T(8,128)S(1)}, u32[]{:S(2)}, u32[]{:S(2)}) collective-permute-start(f32[128,512]{1,0:T(8,128)} %param.8), channel_id=1, source_target_pairs={{0,0},{1,8},{2,16},{3,24},{8,1},{9,9},{10,17},{11,25},{16,2},{17,1... | collective-permute-start | bytes 786440 | tf_op jit(solution)/shard_map/ppermute | solution.py:265
  9.0 156.1 %collective-permute-start.2 = (f32[128,512]{1,0:T(8,128)}, f32[128,512]{1,0:T(8,128)S(1)}, u32[]{:S(2)}, u32[]{:S(2)}) collective-permute-start(f32[128,512]{1,0:T(8,128)} %param.9), channel_id=1, source_target_pairs={{0,0},{1,8},{2,16},{3,24},{8,1},{9,9},{10,17},{11,25},{16,2},{17,1... | collective-permute-start | bytes 786440 | tf_op jit(solution)/shard_map/ppermute | solution.py:265
  29.8 0.7 copy-start.2
  165.1 0.7 copy-start.3
  345.6 200.3 %collective-permute-start.3 = (f32[128,512]{1,0:T(8,128)}, f32[128,512]{1,0:T(8,128)}, u32[]{:S(2)}, u32[]{:S(2)}) collective-permute-start(f32[128,512]{1,0:T(8,128)} %get-tuple-element.69), channel_id=1, source_target_pairs={{0,0},{1,8},{2,16},{3,24},{8,1},{9,9},{10,17},{11,25},{16,2},{17,1... | collective-permute-start | bytes 786440 | tf_op jit(solution)/shard_map/ppermute | solution.py:265
  535.5 9.8 %copy-start.1 = (f32[4,512]{1,0:T(4,128)S(1)}, f32[4,512]{1,0:T(4,128)}, u32[]{:S(2)}) copy-start(f32[4,512]{1,0:T(4,128)} %get-tuple-element.115) | copy-start | bytes 24580
  535.5 12.1 %copy-start = (f32[128,512]{1,0:T(8,128)S(1)}, f32[128,512]{1,0:T(8,128)}, u32[]{:S(2)}) copy-start(f32[128,512]{1,0:T(8,128)} %get-tuple-element.133) | copy-start | bytes 786436
